TPU v7x, 8 devices: a whole 2x2x1 slice. The times are simulated.
8 devices in a mesh: dp: 8 (over z, y, x, core).
Axes of the slice: x: 2, y: 2, z: 1, core: 2. Of those that a mesh axis runs over, the one named last changes fastest.
Arguments:
- grad_rows: bfloat16 [8, 25530368], P('dp')
- master: float32 [25530368], P('dp')
- mom_first: float32 [25530368], P('dp')
- mom_second: float32 [25530368], P('dp')
- decay_mask: int32 [25530368], P('dp')
- learn_rate: float32 [1], replicated
Outputs:
- output 1: bfloat16 [25530368], replicated
- output 2: float32 [25530368], P('dp')
- output 3: float32 [25530368], P('dp')
- output 4: float32 [25530368], P('dp')
- output 5: float32 [1], replicated
All inputs are finite; a program needn't handle non-finite values.
Results may differ from a plain program's by a relative error of at most 0.001.
Values are sent between devices in bfloat16 or wider.
A program may use at most 1 GiB of HBM per device.

v0:
```python
import functools

import jax
import jax.numpy as jnp
from jax import lax
from jax.experimental import pallas as pl
from jax.experimental.pallas import tpu as pltpu
from jax.sharding import PartitionSpec as P


BETA_FIRST = 0.9
BETA_SECOND = 0.95
ADAM_EPS = 1e-8
CLIP_EPS = 1e-6
WEIGHT_DECAY = 0.1
ADAM_STEP = 10

MESH = pl.DeviceIdType.MESH
LANES = 128
CHUNK_ROWS = 384
HALF_ROWS = CHUNK_ROWS // 2
SLOTS = 4
VMEM_LIMIT = 20 << 20
PARTS = 8
ADAM_ROWS = 1560
TILE_ROWS = 120


def places():
    me = lax.axis_index("dp")
    core = me % 2
    part = me + 1 - 2 * core
    along_x = me + 2 - 4 * ((me // 2) % 2)
    along_y = me + 4 - 8 * (me // 4)
    return me, part, along_x, along_y


def meet(peers):
    barrier = pltpu.get_barrier_semaphore()
    for peer in peers:
        pl.semaphore_signal(barrier, inc=1, device_id=(peer,), device_id_type=MESH)
    pl.semaphore_wait(barrier, len(peers))


def stay(array):
    return pltpu.with_memory_space_constraint(array, pltpu.VMEM)


def remote(src, dst, send_sem, recv_sem, device):
    return pltpu.make_async_remote_copy(
        src_ref=src, dst_ref=dst, send_sem=send_sem, recv_sem=recv_sem,
        device_id=(device,), device_id_type=MESH)


def reduce_kernel(shard_rows, grad, w, m, g_out, w_out, m_out, norm_out,
                  own, other, x_send, y_send, x_keep, y_keep, mine, x_recv, y_recv,
                  x_fin, y_fin, x_last, y_last, acc, norm_recv,
                  own_sem, part_ssem, part_rsem, x_ssem, x_rsem, y_ssem, y_rsem,
                  xf_ssem, xf_rsem, yf_ssem, yf_rsem, n_ssem, n_rsem, w_sem, m_sem):
    me, part, along_x, along_y = places()
    diag = along_x + along_y - me
    shift = part - me
    blocks = (me, along_x, along_y, diag)
    shard_len = shard_rows * LANES
    full = CHUNK_ROWS * LANES
    chunks = -(-shard_rows // CHUNK_ROWS)
    tail_rows = shard_rows - (chunks - 1) * CHUNK_ROWS
    tail = tail_rows * LANES

    num_dev = grad.shape[1] // shard_len
    others = [(me + k) % num_dev for k in range(1, num_dev)]
    fetches = (pltpu.make_async_copy(w, w_out.at[pl.ds(0, shard_rows)], w_sem),
               pltpu.make_async_copy(m, m_out.at[pl.ds(0, shard_rows)], m_sem))

    meet(others)
    acc[...] = jnp.zeros_like(acc)

    def loads(i, size):
        slot = i % SLOTS
        out = []
        for b, block in enumerate(blocks):
            src = pl.multiple_of(block * shard_len + i * full, LANES)
            out.append(pltpu.make_async_copy(
                grad.at[:, pl.ds(src, size)], own.at[slot, b, :, pl.ds(0, size)], own_sem.at[slot, b]))
        return out

    def swaps(i, size):
        slot = i % SLOTS
        out = []
        for b, block in enumerate(blocks):
            src = pl.multiple_of((block + shift) * shard_len + i * full, LANES)
            out.append(remote(
                grad.at[:, pl.ds(src, size)], other.at[slot, b, :, pl.ds(0, size)],
                part_ssem.at[slot, b], part_rsem.at[slot, b], part))
        return out

    def first_hops(j):
        slot = j % SLOTS
        return (remote(x_send.at[slot], x_recv.at[slot], x_ssem.at[slot], x_rsem.at[slot], along_x),
                remote(y_send.at[slot], y_recv.at[slot], y_ssem.at[slot], y_rsem.at[slot], along_y))

    def last_hops(j):
        slot = j % SLOTS
        return (remote(x_fin.at[slot], x_last.at[slot], xf_ssem.at[slot], xf_rsem.at[slot], along_x),
                remote(y_fin.at[slot], y_last.at[slot], yf_ssem.at[slot], yf_rsem.at[slot], along_y))

    def for_size(i, do):
        @pl.when(i < chunks - 1)
        def _():
            do(full)

        @pl.when(i == chunks - 1)
        def _():
            do(tail)

    def begin(i):
        def do(size):
            for cp in loads(i, size) + swaps(i, size):
                cp.start()

        for_size(i, do)

    def pair_sums(j):
        def do(size):
            for cp in loads(j, size) + swaps(j, size):
                cp.wait()

        for_size(j, do)
        slot = j % SLOTS

        def tile(t, carry):
            for half in range(2):
                row = pl.multiple_of(t * 8, 8)
                col = pl.multiple_of((t + half * (HALF_ROWS // 8)) * 8 * LANES, 8 * LANES)

                def pair(b):
                    a = own[slot, b, :, pl.ds(col, 8 * LANES)].astype(jnp.float32)
                    o = other[slot, b, :, pl.ds(col, 8 * LANES)].astype(jnp.float32)
                    return (a + o).reshape(8, LANES)

                mine[slot, half, pl.ds(row, 8)] = pair(0)
                if half == 0:
                    x_send[slot, 0, pl.ds(row, 8)] = pair(1)
                    y_keep[slot, pl.ds(row, 8)] = pair(2)
                    x_send[slot, 1, pl.ds(row, 8)] = pair(3)
                else:
                    x_keep[slot, pl.ds(row, 8)] = pair(1)
                    y_send[slot, 0, pl.ds(row, 8)] = pair(2)
                    y_send[slot, 1, pl.ds(row, 8)] = pair(3)
            return carry

        lax.fori_loop(0, HALF_ROWS // 8, tile, 0)
        for cp in first_hops(j):
            cp.start()

    def relay(j):
        for cp in first_hops(j):
            cp.wait()
        slot = j % SLOTS
        x_fin[slot] = x_keep[slot] + y_recv[slot, 1]
        y_fin[slot] = y_keep[slot] + x_recv[slot, 1]
        for cp in last_hops(j):
            cp.start()
        mine[slot, 0] = mine[slot, 0] + x_recv[slot, 0]
        mine[slot, 1] = mine[slot, 1] + y_recv[slot, 0]

    def finish(j):
        for cp in last_hops(j):
            cp.wait()
        slot = j % SLOTS
        base = j * CHUNK_ROWS
        left = shard_rows - j * CHUNK_ROWS
        rows = lax.broadcasted_iota(jnp.int32, (8, LANES), 0)

        def tile(t, total):
            row = pl.multiple_of(t * 8, 8)
            top = (mine[slot, 0, pl.ds(row, 8)] + y_last[slot, pl.ds(row, 8)]) * 0.125
            low = (mine[slot, 1, pl.ds(row, 8)] + x_last[slot, pl.ds(row, 8)]) * 0.125
            g_out[pl.ds(pl.multiple_of(base + t * 8, 8), 8)] = top
            g_out[pl.ds(pl.multiple_of(base + HALF_ROWS + t * 8, 8), 8)] = low
            total = total + jnp.where(rows + t * 8 < left, top * top, 0.0)
            return total + jnp.where(rows + (HALF_ROWS + t * 8) < left, low * low, 0.0)

        acc[...] += lax.fori_loop(0, HALF_ROWS // 8, tile, jnp.zeros((8, LANES), jnp.float32))

    def step(i, carry):
        @pl.when(i < chunks)
        def _():
            begin(i)

        @pl.when((i >= 1) & (i < chunks + 1))
        def _():
            pair_sums(i - 1)

        @pl.when((i >= 2) & (i < chunks + 2))
        def _():
            relay(i - 2)

        @pl.when(i == 4)
        def _():
            for cp in fetches:
                cp.start()

        @pl.when(i >= 4)
        def _():
            finish(i - 4)

        return carry

    lax.fori_loop(0, chunks + 4, step, 0)
    norm_recv[me] = acc[...]

    def shares(peer, k):
        return remote(acc, norm_recv.at[me], n_ssem.at[k], n_rsem.at[me], peer)

    for k, peer in enumerate(others):
        shares(peer, k).start()
    for k, peer in enumerate(others):
        shares(peer, k).wait_send()
        remote(acc, norm_recv.at[peer], n_ssem.at[k], n_rsem.at[peer], peer).wait_recv()
    total = norm_recv[0]
    for k in range(1, num_dev):
        total = total + norm_recv[k]
    for cp in fetches:
        cp.wait()
    norm_out[...] = jnp.broadcast_to(jnp.sqrt(jnp.sum(total, keepdims=True)), norm_out.shape)


def reduce_scatter(grad_row, w, m, shard_rows, num_dev):
    f32, bf16 = jnp.float32, jnp.bfloat16
    chunks = -(-shard_rows // CHUNK_ROWS)
    vm, dma = pltpu.VMEM, pltpu.SemaphoreType.DMA
    pair = (SLOTS, 2, HALF_ROWS, LANES)
    one = (SLOTS, HALF_ROWS, LANES)
    raw = (SLOTS, 4, 1, CHUNK_ROWS * LANES)
    state = vm((chunks * CHUNK_ROWS, LANES), f32)
    return pl.pallas_call(
        functools.partial(reduce_kernel, shard_rows),
        out_shape=(state, state, state, jax.ShapeDtypeStruct((8, LANES), f32)),
        in_specs=[pl.BlockSpec(memory_space=pltpu.HBM)] * 3,
        out_specs=(pl.BlockSpec(memory_space=vm),) * 4,
        scratch_shapes=[
            vm(raw, bf16), vm(raw, bf16), vm(pair, f32), vm(pair, f32), vm(one, f32), vm(one, f32),
            vm(pair, f32), vm(pair, f32), vm(pair, f32), vm(one, f32), vm(one, f32), vm(one, f32),
            vm(one, f32), vm((8, LANES), f32),
            vm((num_dev, 8, LANES), f32),
            dma((SLOTS, 4)), dma((SLOTS, 4)), dma((SLOTS, 4)),
            dma((SLOTS,)), dma((SLOTS,)), dma((SLOTS,)), dma((SLOTS,)),
            dma((SLOTS,)), dma((SLOTS,)), dma((SLOTS,)), dma((SLOTS,)),
            dma((num_dev - 1,)), dma((num_dev,)), dma, dma],
        compiler_params=pltpu.CompilerParams(collective_id=0, has_side_effects=True,
                                             vmem_limit_bytes=VMEM_LIMIT),
    )(grad_row, w, m)


def adamw_kernel(lr, norm, g, w, m, v, mask, *rest):
    w_out, m_out, v_out, packed, norm_out = rest[-5:]
    norm_out[0] = norm[0, 0]
    coef = jnp.minimum(1.0, 1.0 / (norm[0:1] + CLIP_EPS))
    rate = lr[0]

    def tile(t, carry):
        at = pl.ds(pl.multiple_of(t * TILE_ROWS, 8), TILE_ROWS)
        h = g[at] * coef
        first = BETA_FIRST * m[at] + (1.0 - BETA_FIRST) * h
        second = BETA_SECOND * v[at] + (1.0 - BETA_SECOND) * h * h
        step_dir = (first * (1.0 / (1.0 - BETA_FIRST ** ADAM_STEP))) / (
            jnp.sqrt(second * (1.0 / (1.0 - BETA_SECOND ** ADAM_STEP))) + ADAM_EPS)
        old = w[at]
        new = old - rate * (step_dir + WEIGHT_DECAY * mask[at].astype(jnp.float32) * old)
        w_out[at] = new
        m_out[at] = first
        v_out[at] = second
        grains = TILE_ROWS // 4
        packed[pl.ds(pl.multiple_of(t * grains, 2), grains)] = new.reshape(grains, 4, LANES).astype(packed.dtype)
        return carry

    lax.fori_loop(0, ADAM_ROWS // TILE_ROWS, tile, 0)


def adamw(part, lr, norm, g, w, m, v, mask, before):
    rows = v.shape[0]
    part_rows = g.shape[0] // PARTS
    steps = part_rows // ADAM_ROWS
    block = pl.BlockSpec((ADAM_ROWS, LANES), lambda i: (i + part * steps, 0))
    state = jax.ShapeDtypeStruct((rows, LANES), jnp.float32)
    blind = [pl.BlockSpec(memory_space=pl.ANY)] * len(before)
    return pl.pallas_call(
        adamw_kernel,
        grid=(steps,),
        out_shape=(state, state, state, jax.ShapeDtypeStruct((part_rows // 4, 4, LANES), jnp.bfloat16),
                   jax.ShapeDtypeStruct((1,), jnp.float32)),
        in_specs=[pl.BlockSpec(memory_space=pltpu.SMEM),
                  pl.BlockSpec((8, LANES), lambda i: (0, 0)),
                  block, block, block, block, block] + blind,
        out_specs=(block, block, block, pl.BlockSpec((ADAM_ROWS // 4, 4, LANES), lambda i: (i, 0, 0)),
                   pl.BlockSpec(memory_space=pltpu.SMEM)),
        input_output_aliases={7 + k: k for k in range(len(before))},
        compiler_params=pltpu.CompilerParams(vmem_limit_bytes=VMEM_LIMIT),
        cost_estimate=pl.CostEstimate(flops=30 * part_rows * LANES * 40, bytes_accessed=20 * part_rows * LANES, transcendentals=0),
    )(lr, norm, stay(g), stay(w), stay(m), v, mask, *before)


def store_kernel(spots, *refs):
    count = len(spots)
    pieces = refs[:count]
    params, buf, in_sem, out_sem = refs[-4:]
    me, part, along_x, along_y = places()
    diag = along_x + along_y - me
    shift = part - me
    blocks = (me, along_x, along_y, diag, me + shift, along_x + shift, along_y + shift, diag + shift)
    loads, stores = [], []
    for k, (which, start, size, grains) in enumerate(spots):
        dst = params.at[pl.ds(blocks[which] * grains + start, size)]
        loads.append(pltpu.make_async_copy(pieces[k].at[pl.ds(0, size)], buf.at[k, pl.ds(0, size)], in_sem.at[k]))
        stores.append(pltpu.make_async_copy(buf.at[k, pl.ds(0, size)], dst, out_sem.at[k]))
    for cp in loads:
        cp.start()
    for cp, out in zip(loads, stores):
        cp.wait()
        out.start()
    for out in stores:
        out.wait()


def store(pieces, spots, before, num_dev, grains):
    count = len(pieces)
    hbm = pl.BlockSpec(memory_space=pltpu.HBM)
    size = pieces[0].shape[0]
    moved = sum(p.size for p in pieces)
    return pl.pallas_call(
        functools.partial(store_kernel, [(which, start, min(size, grains - start), grains) for which, start in spots]),
        out_shape=jax.ShapeDtypeStruct((num_dev * grains, 4, LANES), jnp.bfloat16),
        in_specs=[hbm] * (count + len(before)),
        out_specs=hbm,
        input_output_aliases={count: 0} if before else {},
        scratch_shapes=[pltpu.VMEM((count,) + pieces[0].shape, jnp.bfloat16),
                        pltpu.SemaphoreType.DMA((count,)), pltpu.SemaphoreType.DMA((count,))],
        compiler_params=pltpu.CompilerParams(vmem_limit_bytes=VMEM_LIMIT),
        cost_estimate=pl.CostEstimate(flops=40 * moved, bytes_accessed=4 * moved, transcendentals=0),
    )(*pieces, *before)


def solution(mesh):
    num_dev = mesh.shape["dp"]
    hop = {"core": [(i, i ^ 1) for i in range(num_dev)], "x": [(i, i ^ 2) for i in range(num_dev)],
           "y": [(i, i ^ 4) for i in range(num_dev)]}

    def local_step(grad_row, master, mom_first, mom_second, decay_mask, learn_rate):
        shard_len = master.shape[0]
        rows = shard_len // LANES
        grains = rows // 4
        flat = lambda a: a.reshape(rows, LANES)

        def send(a, along):
            return lax.ppermute(a, "dp", hop[along])

        def put(pieces, spots, whole):
            return (store(pieces, spots, whole, num_dev, grains),)

        g, w, m, norm = reduce_scatter(grad_row, flat(master), flat(mom_first), rows, num_dev)
        state = ()
        whole = ()
        arrived = []
        for p in range(PARTS):
            *state, packed, grad_norm = adamw(
                p, learn_rate, norm, g, w, m, flat(mom_second), flat(decay_mask), state)
            arrived.append((packed, send(packed, "x"), send(packed, "y"),
                            send(packed, "core")))
        size = packed.shape[0]
        far = []
        for p, (packed, from_x, from_y, from_core) in enumerate(arrived):
            far.append(send(from_x, "y") if p % 2 == 0 else send(from_y, "x"))
            pieces = [packed, from_x, from_y, from_core, send(from_x, "core"), send(from_y, "core")]
            whole = put(pieces, [(k, p * size) for k in (0, 1, 2, 4, 5, 6)], whole)
        for p in range(0, PARTS, 2):
            pieces, spots = [], []
            for q in (p, p + 1):
                pieces += [far[q], send(far[q], "core")]
                spots += [(3, q * size), (7, q * size)]
            whole = put(pieces, spots, whole)
        new_w, new_m, new_v = state
        params = whole[0].reshape(num_dev * shard_len)
        return (params, new_w.reshape(shard_len), new_m.reshape(shard_len), new_v.reshape(shard_len),
                grad_norm)

    return jax.shard_map(
        local_step, mesh=mesh,
        in_specs=(P("dp", None), P("dp"), P("dp"), P("dp"), P("dp"), P()),
        out_specs=(P(), P("dp"), P("dp"), P("dp"), P()), check_vma=False)
```

profile of v0, /device:TPU:0, one launch (start us, length us, event | category | flops | bytes accessed | tf_op | source)
XLA Modules:
  0.0 724.9 jit_solution(17267585468147647993)
XLA Ops:
  1.3 424.9 %shard_map.101 = (f32[24960,128]{1,0:T(8,128)S(1)}, f32[24960,128]{1,0:T(8,128)S(1)}, f32[24960,128]{1,0:T(8,128)S(1)}, f32[8,128]{1,0:T(8,128)}) custom-call(bf16[1,25530368]{1,0:T(2,128)(2,1)} %grad.1, f32[24932,128]{1,0:T(8,128)} %bitcast.28, f32[24932,128]{1,0:T(8,128)} %bitcast.29), custom_call_target="tpu_custom_call" | custom-call | tf_op jit(solution)/shard_map/pallas_call | solution.py:237
  426.2 4.9 shard_map.102
  431.1 5.0 shard_map.103
  436.1 5.0 shard_map.104
  441.1 5.0 shard_map.105
  446.1 4.9 shard_map.106
  451.0 5.0 shard_map.107
  456.0 5.0 shard_map.108
  461.0 5.1 shard_map.109
  466.2 1.4 collective-permute-start.24
  468.4 1.3 collective-permute-start.28
  469.7 0.9 copy-done.8
  471.2 15.9 %collective-permute-done.24.refs_1_ = bf16[780,4,128]{2,1,0:T(4,128)(2,1)S(1)} collective-permute-done((bf16[780,4,128]{2,1,0:T(4,128)(2,1)}, bf16[780,4,128]{2,1,0:T(4,128)(2,1)S(1)}, u32[]{:S(2)}, u32[]{:S(2)}) %collective-permute-start.24) | collective-permute-done | bytes 798752 | tf_op jit(solution)/shard_map/ppermute | solution.py:356
  487.1 1.4 collective-permute-done.3.refs_2_
  489.2 1.0 copy-done.14
  490.1 1.3 collective-permute-start.9
  491.4 14.2 %collective-permute-done.28.refs_2_ = bf16[780,4,128]{2,1,0:T(4,128)(2,1)S(1)} collective-permute-done((bf16[780,4,128]{2,1,0:T(4,128)(2,1)S(1)}, bf16[780,4,128]{2,1,0:T(4,128)(2,1)S(1)}, u32[]{:S(2)}, u32[]{:S(2)}) %collective-permute-start.28) | collective-permute-done | bytes 798752 | tf_op jit(solution)/shard_map/ppermute | solution.py:356
  506.4 1.2 collective-permute-start.6
  507.6 13.8 %collective-permute-done.32.refs_1_ = bf16[780,4,128]{2,1,0:T(4,128)(2,1)S(1)} collective-permute-done((bf16[780,4,128]{2,1,0:T(4,128)(2,1)S(1)}, bf16[780,4,128]{2,1,0:T(4,128)(2,1)S(1)}, u32[]{:S(2)}, u32[]{:S(2)}) %collective-permute-start.32) | collective-permute-done | bytes 798752 | tf_op jit(solution)/shard_map/ppermute | solution.py:356
  521.4 1.4 collective-permute-done.9.refs_2_
  523.4 1.3 collective-permute-start.15
  524.7 15.2 %collective-permute-done.36.refs_2_ = bf16[780,4,128]{2,1,0:T(4,128)(2,1)S(1)} collective-permute-done((bf16[780,4,128]{2,1,0:T(4,128)(2,1)S(1)}, bf16[780,4,128]{2,1,0:T(4,128)(2,1)S(1)}, u32[]{:S(2)}, u32[]{:S(2)}) %collective-permute-start.36) | collective-permute-done | bytes 798752 | tf_op jit(solution)/shard_map/ppermute | solution.py:356
  540.6 1.2 collective-permute-start.12
  541.8 13.8 %collective-permute-done.40.refs_1_ = bf16[780,4,128]{2,1,0:T(4,128)(2,1)S(1)} collective-permute-done((bf16[780,4,128]{2,1,0:T(4,128)(2,1)S(1)}, bf16[780,4,128]{2,1,0:T(4,128)(2,1)S(1)}, u32[]{:S(2)}, u32[]{:S(2)}) %collective-permute-start.40) | collective-permute-done | bytes 798752 | tf_op jit(solution)/shard_map/ppermute | solution.py:356
  555.6 1.4 collective-permute-done.15.refs_2_
  557.6 1.3 collective-permute-start.21
  558.9 15.2 %collective-permute-done.44.refs_2_ = bf16[780,4,128]{2,1,0:T(4,128)(2,1)S(1)} collective-permute-done((bf16[780,4,128]{2,1,0:T(4,128)(2,1)S(1)}, bf16[780,4,128]{2,1,0:T(4,128)(2,1)S(1)}, u32[]{:S(2)}, u32[]{:S(2)}) %collective-permute-start.44) | collective-permute-done | bytes 798752 | tf_op jit(solution)/shard_map/ppermute | solution.py:356
  574.9 1.2 collective-permute-start.18
  576.0 13.8 %collective-permute-done.48.refs_1_ = bf16[780,4,128]{2,1,0:T(4,128)(2,1)S(1)} collective-permute-done((bf16[780,4,128]{2,1,0:T(4,128)(2,1)S(1)}, bf16[780,4,128]{2,1,0:T(4,128)(2,1)S(1)}, u32[]{:S(2)}, u32[]{:S(2)}) %collective-permute-start.48) | collective-permute-done | bytes 798752 | tf_op jit(solution)/shard_map/ppermute | solution.py:356
  589.8 0.9 copy-done.10
  591.2 1.4 collective-permute-start.4
  592.6 0.9 copy-done.12
  593.5 13.9 %collective-permute-done.52.refs_2_ = bf16[780,4,128]{2,1,0:T(4,128)(2,1)S(1)} collective-permute-done((bf16[780,4,128]{2,1,0:T(4,128)(2,1)S(1)}, bf16[780,4,128]{2,1,0:T(4,128)(2,1)S(1)}, u32[]{:S(2)}, u32[]{:S(2)}) %collective-permute-start.52) | collective-permute-done | bytes 798752 | tf_op jit(solution)/shard_map/ppermute | solution.py:356
  607.5 0.9 copy-done.16
  608.9 1.0 copy-done.20
  610.6 0.9 copy-done.18
  611.5 0.9 copy-done.22
  612.4 11.2 %collective-permute-done.4.refs_2_ = bf16[780,4,128]{2,1,0:T(4,128)(2,1)} collective-permute-done((bf16[780,4,128]{2,1,0:T(4,128)(2,1)S(1)}, bf16[780,4,128]{2,1,0:T(4,128)(2,1)}, u32[]{:S(2)}, u32[]{:S(2)}) %collective-permute-start.4) | collective-permute-done | bytes 798752 | tf_op jit(solution)/shard_map/ppermute | solution.py:356
  623.6 0.9 copy-done.24
  624.5 1.4 collective-permute-start.10
  625.9 0.9 copy-done.26
  627.0 2.7 collective-permute-done.1.refs_0_
  630.7 14.1 %collective-permute-done.10.refs_2_ = bf16[780,4,128]{2,1,0:T(4,128)(2,1)} collective-permute-done((bf16[780,4,128]{2,1,0:T(4,128)(2,1)S(1)}, bf16[780,4,128]{2,1,0:T(4,128)(2,1)}, u32[]{:S(2)}, u32[]{:S(2)}) %collective-permute-start.10) | collective-permute-done | bytes 798752 | tf_op jit(solution)/shard_map/ppermute | solution.py:356
  644.8 1.4 collective-permute-start.16
  646.4 3.6 collective-permute-done.7.refs_0_
  651.0 14.0 %collective-permute-done.16.refs_2_ = bf16[780,4,128]{2,1,0:T(4,128)(2,1)S(1)} collective-permute-done((bf16[780,4,128]{2,1,0:T(4,128)(2,1)S(1)}, bf16[780,4,128]{2,1,0:T(4,128)(2,1)S(1)}, u32[]{:S(2)}, u32[]{:S(2)}) %collective-permute-start.16) | collective-permute-done | bytes 798752 | tf_op jit(solution)/shard_map/ppermute | solution.py:356
  665.0 1.4 collective-permute-start.22
  667.2 3.6 collective-permute-done.13.refs_0_
  671.3 13.9 %collective-permute-done.22.refs_2_ = bf16[780,4,128]{2,1,0:T(4,128)(2,1)S(1)} collective-permute-done((bf16[780,4,128]{2,1,0:T(4,128)(2,1)S(1)}, bf16[780,4,128]{2,1,0:T(4,128)(2,1)S(1)}, u32[]{:S(2)}, u32[]{:S(2)}) %collective-permute-start.22) | collective-permute-done | bytes 798752 | tf_op jit(solution)/shard_map/ppermute | solution.py:356
  685.3 0.9 copy-done.30
  686.2 1.2 collective-permute-done.19.refs_0_
  687.4 0.9 copy-done.32
  689.8 2.7 shard_map.110.refs_6_
  692.5 2.7 shard_map.111.refs_6_
  695.3 2.7 shard_map.112.refs_6_
  698.1 2.7 shard_map.113.refs_6_
  700.8 2.7 shard_map.114.refs_6_
  703.6 3.0 shard_map.115.refs_6_
  707.4 3.0 shard_map.116.refs_6_
  711.5 2.6 shard_map.117.refs_4_
  714.2 2.0 shard_map.118.refs_4_
  716.2 2.9 shard_map.119.refs_4_
  719.1 2.9 shard_map.120.refs_4_
  722.1 2.9 shard_map.121
  (137 shorter events, 14.7 us)
Async XLA Ops:
  460.9 7.4 %copy-start.7 = (bf16[780,4,128]{2,1,0:T(4,128)(2,1)S(1)}, bf16[780,4,128]{2,1,0:T(4,128)(2,1)}, u32[]{:S(2)}) copy-start(bf16[780,4,128]{2,1,0:T(4,128)(2,1)} %get-tuple-element.64.refs_0_) | copy-start | bytes 2396164
  460.9 26.2 %copy-start.6 = (bf16[780,4,128]{2,1,0:T(4,128)(2,1)S(1)}, bf16[780,4,128]{2,1,0:T(4,128)(2,1)}, u32[]{:S(2)}) copy-start(bf16[780,4,128]{2,1,0:T(4,128)(2,1)} %get-tuple-element.70.refs_0_) | copy-start | bytes 2396164
  461.0 44.7 %copy-start.4 = (bf16[780,4,128]{2,1,0:T(4,128)(2,1)S(1)}, bf16[780,4,128]{2,1,0:T(4,128)(2,1)}, u32[]{:S(2)}) copy-start(bf16[780,4,128]{2,1,0:T(4,128)(2,1)} %get-tuple-element.69.refs_0_) | copy-start | bytes 2396164
  461.0 60.4 %copy-start.3 = (bf16[780,4,128]{2,1,0:T(4,128)(2,1)S(1)}, bf16[780,4,128]{2,1,0:T(4,128)(2,1)}, u32[]{:S(2)}) copy-start(bf16[780,4,128]{2,1,0:T(4,128)(2,1)} %get-tuple-element.72.refs_0_) | copy-start | bytes 2396164
  461.0 78.9 %copy-start.2 = (bf16[780,4,128]{2,1,0:T(4,128)(2,1)S(1)}, bf16[780,4,128]{2,1,0:T(4,128)(2,1)}, u32[]{:S(2)}) copy-start(bf16[780,4,128]{2,1,0:T(4,128)(2,1)} %get-tuple-element.71.refs_0_) | copy-start | bytes 2396164
  461.0 94.6 %copy-start.1 = (bf16[780,4,128]{2,1,0:T(4,128)(2,1)S(1)}, bf16[780,4,128]{2,1,0:T(4,128)(2,1)}, u32[]{:S(2)}) copy-start(bf16[780,4,128]{2,1,0:T(4,128)(2,1)} %get-tuple-element.74.refs_0_) | copy-start | bytes 2396164
  461.0 113.1 %copy-start = (bf16[780,4,128]{2,1,0:T(4,128)(2,1)S(1)}, bf16[780,4,128]{2,1,0:T(4,128)(2,1)}, u32[]{:S(2)}) copy-start(bf16[780,4,128]{2,1,0:T(4,128)(2,1)} %get-tuple-element.73.refs_0_) | copy-start | bytes 2396164
  466.1 3.5 collective-permute-start.25
  466.2 20.9 %collective-permute-start.24 = (bf16[780,4,128]{2,1,0:T(4,128)(2,1)}, bf16[780,4,128]{2,1,0:T(4,128)(2,1)S(1)}, u32[]{:S(2)}, u32[]{:S(2)}) collective-permute-start(bf16[780,4,128]{2,1,0:T(4,128)(2,1)} %get-tuple-element.68.refs_0_), channel_id=1, source_target_pairs={{0,2},{1,3},{2,0},{3,1},{4,6},{5,7},{6,4},{7,5}} | collective-permute-start | bytes 2396168 | tf_op jit(solution)/shard_map/ppermute | solution.py:356
  467.6 20.9 %collective-permute-start.3 = (bf16[780,4,128]{2,1,0:T(4,128)(2,1)}, bf16[780,4,128]{2,1,0:T(4,128)(2,1)S(1)}, u32[]{:S(2)}, u32[]{:S(2)}) collective-permute-start(bf16[780,4,128]{2,1,0:T(4,128)(2,1)} %get-tuple-element.68.refs_0_), channel_id=1, source_target_pairs={{0,4},{1,5},{2,6},{3,7},{4,0},{5,1},{6,2},{7,3}} | collective-permute-start | bytes 2396168 | tf_op jit(solution)/shard_map/ppermute | solution.py:356
  468.4 20.8 %collective-permute-start.29 = (bf16[780,4,128]{2,1,0:T(4,128)(2,1)S(1)}, bf16[780,4,128]{2,1,0:T(4,128)(2,1)S(1)}, u32[]{:S(2)}, u32[]{:S(2)}) collective-permute-start(bf16[780,4,128]{2,1,0:T(4,128)(2,1)S(1)} %copy-done.7), channel_id=1, source_target_pairs={{0,1},{1,0},{2,3},{3,2},{4,5},{5,4},{6,7},{7,6}} | collective-permute-start | bytes 2396168 | tf_op jit(solution)/shard_map/ppermute | solution.py:356
  468.4 37.3 %collective-permute-start.28 = (bf16[780,4,128]{2,1,0:T(4,128)(2,1)S(1)}, bf16[780,4,128]{2,1,0:T(4,128)(2,1)S(1)}, u32[]{:S(2)}, u32[]{:S(2)}) collective-permute-start(bf16[780,4,128]{2,1,0:T(4,128)(2,1)S(1)} %copy-done.7), channel_id=1, source_target_pairs={{0,4},{1,5},{2,6},{3,7},{4,0},{5,1},{6,2},{7,3}} | collective-permute-start | bytes 2396168 | tf_op jit(solution)/shard_map/ppermute | solution.py:356
  470.5 35.1 %collective-permute-start = (bf16[780,4,128]{2,1,0:T(4,128)(2,1)S(1)}, bf16[780,4,128]{2,1,0:T(4,128)(2,1)S(1)}, u32[]{:S(2)}, u32[]{:S(2)}) collective-permute-start(bf16[780,4,128]{2,1,0:T(4,128)(2,1)S(1)} %copy-done.7), channel_id=1, source_target_pairs={{0,2},{1,3},{2,0},{3,1},{4,6},{5,7},{6,4},{7,5}} | collective-permute-start | bytes 2396168 | tf_op jit(solution)/shard_map/ppermute | solution.py:356
  487.1 19.3 %collective-permute-start.33 = (bf16[780,4,128]{2,1,0:T(4,128)(2,1)S(1)}, bf16[780,4,128]{2,1,0:T(4,128)(2,1)S(1)}, u32[]{:S(2)}, u32[]{:S(2)}) collective-permute-start(bf16[780,4,128]{2,1,0:T(4,128)(2,1)S(1)} %copy-done.6), channel_id=1, source_target_pairs={{0,1},{1,0},{2,3},{3,2},{4,5},{5,4},{6,7},{7,6}} | collective-permute-start | bytes 2396168 | tf_op jit(solution)/shard_map/ppermute | solution.py:356
  488.5 32.9 %collective-permute-start.32 = (bf16[780,4,128]{2,1,0:T(4,128)(2,1)S(1)}, bf16[780,4,128]{2,1,0:T(4,128)(2,1)S(1)}, u32[]{:S(2)}, u32[]{:S(2)}) collective-permute-start(bf16[780,4,128]{2,1,0:T(4,128)(2,1)S(1)} %copy-done.6), channel_id=1, source_target_pairs={{0,2},{1,3},{2,0},{3,1},{4,6},{5,7},{6,4},{7,5}} | collective-permute-start | bytes 2396168 | tf_op jit(solution)/shard_map/ppermute | solution.py:356
  490.1 32.6 %collective-permute-start.9 = (bf16[780,4,128]{2,1,0:T(4,128)(2,1)S(1)}, bf16[780,4,128]{2,1,0:T(4,128)(2,1)S(1)}, u32[]{:S(2)}, u32[]{:S(2)}) collective-permute-start(bf16[780,4,128]{2,1,0:T(4,128)(2,1)S(1)} %copy-done.6), channel_id=1, source_target_pairs={{0,4},{1,5},{2,6},{3,7},{4,0},{5,1},{6,2},{7,3}} | collective-permute-start | bytes 2396168 | tf_op jit(solution)/shard_map/ppermute | solution.py:356
  505.6 17.8 %collective-permute-start.37 = (bf16[780,4,128]{2,1,0:T(4,128)(2,1)S(1)}, bf16[780,4,128]{2,1,0:T(4,128)(2,1)S(1)}, u32[]{:S(2)}, u32[]{:S(2)}) collective-permute-start(bf16[780,4,128]{2,1,0:T(4,128)(2,1)S(1)} %copy-done.4), channel_id=1, source_target_pairs={{0,1},{1,0},{2,3},{3,2},{4,5},{5,4},{6,7},{7,6}} | collective-permute-start | bytes 2396168 | tf_op jit(solution)/shard_map/ppermute | solution.py:356
  505.6 34.2 %collective-permute-start.36 = (bf16[780,4,128]{2,1,0:T(4,128)(2,1)S(1)}, bf16[780,4,128]{2,1,0:T(4,128)(2,1)S(1)}, u32[]{:S(2)}, u32[]{:S(2)}) collective-permute-start(bf16[780,4,128]{2,1,0:T(4,128)(2,1)S(1)} %copy-done.4), channel_id=1, source_target_pairs={{0,4},{1,5},{2,6},{3,7},{4,0},{5,1},{6,2},{7,3}} | collective-permute-start | bytes 2396168 | tf_op jit(solution)/shard_map/ppermute | solution.py:356
  506.4 33.5 %collective-permute-start.6 = (bf16[780,4,128]{2,1,0:T(4,128)(2,1)S(1)}, bf16[780,4,128]{2,1,0:T(4,128)(2,1)S(1)}, u32[]{:S(2)}, u32[]{:S(2)}) collective-permute-start(bf16[780,4,128]{2,1,0:T(4,128)(2,1)S(1)} %copy-done.4), channel_id=1, source_target_pairs={{0,2},{1,3},{2,0},{3,1},{4,6},{5,7},{6,4},{7,5}} | collective-permute-start | bytes 2396168 | tf_op jit(solution)/shard_map/ppermute | solution.py:356
  521.4 19.3 %collective-permute-start.41 = (bf16[780,4,128]{2,1,0:T(4,128)(2,1)S(1)}, bf16[780,4,128]{2,1,0:T(4,128)(2,1)S(1)}, u32[]{:S(2)}, u32[]{:S(2)}) collective-permute-start(bf16[780,4,128]{2,1,0:T(4,128)(2,1)S(1)} %copy-done.3), channel_id=1, source_target_pairs={{0,1},{1,0},{2,3},{3,2},{4,5},{5,4},{6,7},{7,6}} | collective-permute-start | bytes 2396168 | tf_op jit(solution)/shard_map/ppermute | solution.py:356
  522.7 32.9 %collective-permute-start.40 = (bf16[780,4,128]{2,1,0:T(4,128)(2,1)S(1)}, bf16[780,4,128]{2,1,0:T(4,128)(2,1)S(1)}, u32[]{:S(2)}, u32[]{:S(2)}) collective-permute-start(bf16[780,4,128]{2,1,0:T(4,128)(2,1)S(1)} %copy-done.3), channel_id=1, source_target_pairs={{0,2},{1,3},{2,0},{3,1},{4,6},{5,7},{6,4},{7,5}} | collective-permute-start | bytes 2396168 | tf_op jit(solution)/shard_map/ppermute | solution.py:356
  523.4 33.6 %collective-permute-start.15 = (bf16[780,4,128]{2,1,0:T(4,128)(2,1)S(1)}, bf16[780,4,128]{2,1,0:T(4,128)(2,1)S(1)}, u32[]{:S(2)}, u32[]{:S(2)}) collective-permute-start(bf16[780,4,128]{2,1,0:T(4,128)(2,1)S(1)} %copy-done.3), channel_id=1, source_target_pairs={{0,4},{1,5},{2,6},{3,7},{4,0},{5,1},{6,2},{7,3}} | collective-permute-start | bytes 2396168 | tf_op jit(solution)/shard_map/ppermute | solution.py:356
  539.9 17.8 %collective-permute-start.45 = (bf16[780,4,128]{2,1,0:T(4,128)(2,1)S(1)}, bf16[780,4,128]{2,1,0:T(4,128)(2,1)S(1)}, u32[]{:S(2)}, u32[]{:S(2)}) collective-permute-start(bf16[780,4,128]{2,1,0:T(4,128)(2,1)S(1)} %copy-done.2), channel_id=1, source_target_pairs={{0,1},{1,0},{2,3},{3,2},{4,5},{5,4},{6,7},{7,6}} | collective-permute-start | bytes 2396168 | tf_op jit(solution)/shard_map/ppermute | solution.py:356
  539.9 34.2 %collective-permute-start.44 = (bf16[780,4,128]{2,1,0:T(4,128)(2,1)S(1)}, bf16[780,4,128]{2,1,0:T(4,128)(2,1)S(1)}, u32[]{:S(2)}, u32[]{:S(2)}) collective-permute-start(bf16[780,4,128]{2,1,0:T(4,128)(2,1)S(1)} %copy-done.2), channel_id=1, source_target_pairs={{0,4},{1,5},{2,6},{3,7},{4,0},{5,1},{6,2},{7,3}} | collective-permute-start | bytes 2396168 | tf_op jit(solution)/shard_map/ppermute | solution.py:356
  540.6 33.5 %collective-permute-start.12 = (bf16[780,4,128]{2,1,0:T(4,128)(2,1)S(1)}, bf16[780,4,128]{2,1,0:T(4,128)(2,1)S(1)}, u32[]{:S(2)}, u32[]{:S(2)}) collective-permute-start(bf16[780,4,128]{2,1,0:T(4,128)(2,1)S(1)} %copy-done.2), channel_id=1, source_target_pairs={{0,2},{1,3},{2,0},{3,1},{4,6},{5,7},{6,4},{7,5}} | collective-permute-start | bytes 2396168 | tf_op jit(solution)/shard_map/ppermute | solution.py:356
  555.6 19.3 %collective-permute-start.49 = (bf16[780,4,128]{2,1,0:T(4,128)(2,1)S(1)}, bf16[780,4,128]{2,1,0:T(4,128)(2,1)S(1)}, u32[]{:S(2)}, u32[]{:S(2)}) collective-permute-start(bf16[780,4,128]{2,1,0:T(4,128)(2,1)S(1)} %copy-done.1), channel_id=1, source_target_pairs={{0,1},{1,0},{2,3},{3,2},{4,5},{5,4},{6,7},{7,6}} | collective-permute-start | bytes 2396168 | tf_op jit(solution)/shard_map/ppermute | solution.py:356
  557.0 32.9 %collective-permute-start.48 = (bf16[780,4,128]{2,1,0:T(4,128)(2,1)S(1)}, bf16[780,4,128]{2,1,0:T(4,128)(2,1)S(1)}, u32[]{:S(2)}, u32[]{:S(2)}) collective-permute-start(bf16[780,4,128]{2,1,0:T(4,128)(2,1)S(1)} %copy-done.1), channel_id=1, source_target_pairs={{0,2},{1,3},{2,0},{3,1},{4,6},{5,7},{6,4},{7,5}} | collective-permute-start | bytes 2396168 | tf_op jit(solution)/shard_map/ppermute | solution.py:356
  557.6 33.6 %collective-permute-start.21 = (bf16[780,4,128]{2,1,0:T(4,128)(2,1)S(1)}, bf16[780,4,128]{2,1,0:T(4,128)(2,1)S(1)}, u32[]{:S(2)}, u32[]{:S(2)}) collective-permute-start(bf16[780,4,128]{2,1,0:T(4,128)(2,1)S(1)} %copy-done.1), channel_id=1, source_target_pairs={{0,4},{1,5},{2,6},{3,7},{4,0},{5,1},{6,2},{7,3}} | collective-permute-start | bytes 2396168 | tf_op jit(solution)/shard_map/ppermute | solution.py:356
  574.1 17.1 %collective-permute-start.53 = (bf16[780,4,128]{2,1,0:T(4,128)(2,1)S(1)}, bf16[780,4,128]{2,1,0:T(4,128)(2,1)S(1)}, u32[]{:S(2)}, u32[]{:S(2)}) collective-permute-start(bf16[780,4,128]{2,1,0:T(4,128)(2,1)S(1)} %copy-done), channel_id=1, source_target_pairs={{0,1},{1,0},{2,3},{3,2},{4,5},{5,4},{6,7},{7,6}} | collective-permute-start | bytes 2396168 | tf_op jit(solution)/shard_map/ppermute | solution.py:356
  574.1 33.4 %collective-permute-start.52 = (bf16[780,4,128]{2,1,0:T(4,128)(2,1)S(1)}, bf16[780,4,128]{2,1,0:T(4,128)(2,1)S(1)}, u32[]{:S(2)}, u32[]{:S(2)}) collective-permute-start(bf16[780,4,128]{2,1,0:T(4,128)(2,1)S(1)} %copy-done), channel_id=1, source_target_pairs={{0,4},{1,5},{2,6},{3,7},{4,0},{5,1},{6,2},{7,3}} | collective-permute-start | bytes 2396168 | tf_op jit(solution)/shard_map/ppermute | solution.py:356
  574.9 33.5 %collective-permute-start.18 = (bf16[780,4,128]{2,1,0:T(4,128)(2,1)S(1)}, bf16[780,4,128]{2,1,0:T(4,128)(2,1)S(1)}, u32[]{:S(2)}, u32[]{:S(2)}) collective-permute-start(bf16[780,4,128]{2,1,0:T(4,128)(2,1)S(1)} %copy-done), channel_id=1, source_target_pairs={{0,2},{1,3},{2,0},{3,1},{4,6},{5,7},{6,4},{7,5}} | collective-permute-start | bytes 2396168 | tf_op jit(solution)/shard_map/ppermute | solution.py:356
  589.8 19.0 %collective-permute-start.26 = (bf16[780,4,128]{2,1,0:T(4,128)(2,1)S(1)}, bf16[780,4,128]{2,1,0:T(4,128)(2,1)S(1)}, u32[]{:S(2)}, u32[]{:S(2)}) collective-permute-start(bf16[780,4,128]{2,1,0:T(4,128)(2,1)S(1)} %collective-permute-done.24.refs_1_), channel_id=1, source_target_pairs={{0,1},{1,0},{2,3},{3,2},{4,5},{5,4},{6,7},{7,6}} | collective-permute-start | bytes 2396168 | tf_op jit(solution)/shard_map/ppermute | solution.py:356
  591.2 20.3 %collective-permute-start.27 = (bf16[780,4,128]{2,1,0:T(4,128)(2,1)S(1)}, bf16[780,4,128]{2,1,0:T(4,128)(2,1)S(1)}, u32[]{:S(2)}, u32[]{:S(2)}) collective-permute-start(bf16[780,4,128]{2,1,0:T(4,128)(2,1)S(1)} %collective-permute-done.3.refs_2_), channel_id=1, source_target_pairs={{0,1},{1,0},{2,3},{3,2},{4,5},{5,4},{6,7},{7,6}} | collective-permute-start | bytes 2396168 | tf_op jit(solution)/shard_map/ppermute | solution.py:356
  591.2 32.4 %collective-permute-start.4 = (bf16[780,4,128]{2,1,0:T(4,128)(2,1)S(1)}, bf16[780,4,128]{2,1,0:T(4,128)(2,1)}, u32[]{:S(2)}, u32[]{:S(2)}) collective-permute-start(bf16[780,4,128]{2,1,0:T(4,128)(2,1)S(1)} %collective-permute-done.3.refs_2_), channel_id=1, source_target_pairs={{0,2},{1,3},{2,0},{3,1},{4,6},{5,7},{6,4},{7,5}} | collective-permute-start | bytes 2396168 | tf_op jit(solution)/shard_map/ppermute | solution.py:356
  607.5 16.1 %collective-permute-start.31 = (bf16[780,4,128]{2,1,0:T(4,128)(2,1)S(1)}, bf16[780,4,128]{2,1,0:T(4,128)(2,1)S(1)}, u32[]{:S(2)}, u32[]{:S(2)}) collective-permute-start(bf16[780,4,128]{2,1,0:T(4,128)(2,1)S(1)} %collective-permute-done.28.refs_2_), channel_id=1, source_target_pairs={{0,1},{1,0},{2,3},{3,2},{4,5},{5,4},{6,7},{7,6}} | collective-permute-start | bytes 2396168 | tf_op jit(solution)/shard_map/ppermute | solution.py:356
  608.4 17.5 %collective-permute-start.30 = (bf16[780,4,128]{2,1,0:T(4,128)(2,1)S(1)}, bf16[780,4,128]{2,1,0:T(4,128)(2,1)S(1)}, u32[]{:S(2)}, u32[]{:S(2)}) collective-permute-start(bf16[780,4,128]{2,1,0:T(4,128)(2,1)S(1)} %collective-permute-done.refs_1_), channel_id=1, source_target_pairs={{0,1},{1,0},{2,3},{3,2},{4,5},{5,4},{6,7},{7,6}} | collective-permute-start | bytes 2396168 | tf_op jit(solution)/shard_map/ppermute | solution.py:356
  609.9 19.8 %collective-permute-start.1 = (bf16[780,4,128]{2,1,0:T(4,128)(2,1)S(1)}, bf16[780,4,128]{2,1,0:T(4,128)(2,1)}, u32[]{:S(2)}, u32[]{:S(2)}) collective-permute-start(bf16[780,4,128]{2,1,0:T(4,128)(2,1)S(1)} %collective-permute-done.refs_1_), channel_id=1, source_target_pairs={{0,4},{1,5},{2,6},{3,7},{4,0},{5,1},{6,2},{7,3}} | collective-permute-start | bytes 2396168 | tf_op jit(solution)/shard_map/ppermute | solution.py:356
  612.4 17.3 %collective-permute-start.34 = (bf16[780,4,128]{2,1,0:T(4,128)(2,1)S(1)}, bf16[780,4,128]{2,1,0:T(4,128)(2,1)S(1)}, u32[]{:S(2)}, u32[]{:S(2)}) collective-permute-start(bf16[780,4,128]{2,1,0:T(4,128)(2,1)S(1)} %collective-permute-done.32.refs_1_), channel_id=1, source_target_pairs={{0,1},{1,0},{2,3},{3,2},{4,5},{5,4},{6,7},{7,6}} | collective-permute-start | bytes 2396168 | tf_op jit(solution)/shard_map/ppermute | solution.py:356
  623.6 6.9 collective-permute-start.35
  624.5 20.3 %collective-permute-start.10 = (bf16[780,4,128]{2,1,0:T(4,128)(2,1)S(1)}, bf16[780,4,128]{2,1,0:T(4,128)(2,1)}, u32[]{:S(2)}, u32[]{:S(2)}) collective-permute-start(bf16[780,4,128]{2,1,0:T(4,128)(2,1)S(1)} %collective-permute-done.9.refs_2_), channel_id=1, source_target_pairs={{0,2},{1,3},{2,0},{3,1},{4,6},{5,7},{6,4},{7,5}} | collective-permute-start | bytes 2396168 | tf_op jit(solution)/shard_map/ppermute | solution.py:356
  626.8 18.1 %collective-permute-start.39 = (bf16[780,4,128]{2,1,0:T(4,128)(2,1)S(1)}, bf16[780,4,128]{2,1,0:T(4,128)(2,1)S(1)}, u32[]{:S(2)}, u32[]{:S(2)}) collective-permute-start(bf16[780,4,128]{2,1,0:T(4,128)(2,1)S(1)} %collective-permute-done.36.refs_2_), channel_id=1, source_target_pairs={{0,1},{1,0},{2,3},{3,2},{4,5},{5,4},{6,7},{7,6}} | collective-permute-start | bytes 2396168 | tf_op jit(solution)/shard_map/ppermute | solution.py:356
  629.7 16.5 %collective-permute-start.38 = (bf16[780,4,128]{2,1,0:T(4,128)(2,1)S(1)}, bf16[780,4,128]{2,1,0:T(4,128)(2,1)S(1)}, u32[]{:S(2)}, u32[]{:S(2)}) collective-permute-start(bf16[780,4,128]{2,1,0:T(4,128)(2,1)S(1)} %collective-permute-done.6.refs_1_), channel_id=1, source_target_pairs={{0,1},{1,0},{2,3},{3,2},{4,5},{5,4},{6,7},{7,6}} | collective-permute-start | bytes 2396168 | tf_op jit(solution)/shard_map/ppermute | solution.py:356
  629.7 20.3 %collective-permute-start.7 = (bf16[780,4,128]{2,1,0:T(4,128)(2,1)S(1)}, bf16[780,4,128]{2,1,0:T(4,128)(2,1)}, u32[]{:S(2)}, u32[]{:S(2)}) collective-permute-start(bf16[780,4,128]{2,1,0:T(4,128)(2,1)S(1)} %collective-permute-done.6.refs_1_), channel_id=1, source_target_pairs={{0,4},{1,5},{2,6},{3,7},{4,0},{5,1},{6,2},{7,3}} | collective-permute-start | bytes 2396168 | tf_op jit(solution)/shard_map/ppermute | solution.py:356
  630.4 19.6 %collective-permute-start.42 = (bf16[780,4,128]{2,1,0:T(4,128)(2,1)S(1)}, bf16[780,4,128]{2,1,0:T(4,128)(2,1)S(1)}, u32[]{:S(2)}, u32[]{:S(2)}) collective-permute-start(bf16[780,4,128]{2,1,0:T(4,128)(2,1)S(1)} %collective-permute-done.40.refs_1_), channel_id=1, source_target_pairs={{0,1},{1,0},{2,3},{3,2},{4,5},{5,4},{6,7},{7,6}} | collective-permute-start | bytes 2396168 | tf_op jit(solution)/shard_map/ppermute | solution.py:356
  644.8 6.0 collective-permute-start.43
  644.8 20.2 %collective-permute-start.16 = (bf16[780,4,128]{2,1,0:T(4,128)(2,1)S(1)}, bf16[780,4,128]{2,1,0:T(4,128)(2,1)S(1)}, u32[]{:S(2)}, u32[]{:S(2)}) collective-permute-start(bf16[780,4,128]{2,1,0:T(4,128)(2,1)S(1)} %collective-permute-done.15.refs_2_), channel_id=1, source_target_pairs={{0,2},{1,3},{2,0},{3,1},{4,6},{5,7},{6,4},{7,5}} | collective-permute-start | bytes 2396168 | tf_op jit(solution)/shard_map/ppermute | solution.py:356
  646.2 18.8 %collective-permute-start.47 = (bf16[780,4,128]{2,1,0:T(4,128)(2,1)S(1)}, bf16[780,4,128]{2,1,0:T(4,128)(2,1)S(1)}, u32[]{:S(2)}, u32[]{:S(2)}) collective-permute-start(bf16[780,4,128]{2,1,0:T(4,128)(2,1)S(1)} %collective-permute-done.44.refs_2_), channel_id=1, source_target_pairs={{0,1},{1,0},{2,3},{3,2},{4,5},{5,4},{6,7},{7,6}} | collective-permute-start | bytes 2396168 | tf_op jit(solution)/shard_map/ppermute | solution.py:356
  650.0 16.4 %collective-permute-start.46 = (bf16[780,4,128]{2,1,0:T(4,128)(2,1)S(1)}, bf16[780,4,128]{2,1,0:T(4,128)(2,1)S(1)}, u32[]{:S(2)}, u32[]{:S(2)}) collective-permute-start(bf16[780,4,128]{2,1,0:T(4,128)(2,1)S(1)} %collective-permute-done.12.refs_1_), channel_id=1, source_target_pairs={{0,1},{1,0},{2,3},{3,2},{4,5},{5,4},{6,7},{7,6}} | collective-permute-start | bytes 2396168 | tf_op jit(solution)/shard_map/ppermute | solution.py:356
  650.0 20.8 %collective-permute-start.13 = (bf16[780,4,128]{2,1,0:T(4,128)(2,1)S(1)}, bf16[780,4,128]{2,1,0:T(4,128)(2,1)}, u32[]{:S(2)}, u32[]{:S(2)}) collective-permute-start(bf16[780,4,128]{2,1,0:T(4,128)(2,1)S(1)} %collective-permute-done.12.refs_1_), channel_id=1, source_target_pairs={{0,4},{1,5},{2,6},{3,7},{4,0},{5,1},{6,2},{7,3}} | collective-permute-start | bytes 2396168 | tf_op jit(solution)/shard_map/ppermute | solution.py:356
  650.8 20.0 %collective-permute-start.50 = (bf16[780,4,128]{2,1,0:T(4,128)(2,1)S(1)}, bf16[780,4,128]{2,1,0:T(4,128)(2,1)S(1)}, u32[]{:S(2)}, u32[]{:S(2)}) collective-permute-start(bf16[780,4,128]{2,1,0:T(4,128)(2,1)S(1)} %collective-permute-done.48.refs_1_), channel_id=1, source_target_pairs={{0,1},{1,0},{2,3},{3,2},{4,5},{5,4},{6,7},{7,6}} | collective-permute-start | bytes 2396168 | tf_op jit(solution)/shard_map/ppermute | solution.py:356
  665.0 27.5 %copy-start.28 = (bf16[780,4,128]{2,1,0:T(4,128)(2,1)}, bf16[780,4,128]{2,1,0:T(4,128)(2,1)S(1)}, u32[]{:S(2)}) copy-start(bf16[780,4,128]{2,1,0:T(4,128)(2,1)S(1)} %collective-permute-done.16.refs_2_) | copy-start | bytes 2396164
  665.0 6.3 collective-permute-start.51
  665.0 20.2 %collective-permute-start.22 = (bf16[780,4,128]{2,1,0:T(4,128)(2,1)S(1)}, bf16[780,4,128]{2,1,0:T(4,128)(2,1)S(1)}, u32[]{:S(2)}, u32[]{:S(2)}) collective-permute-start(bf16[780,4,128]{2,1,0:T(4,128)(2,1)S(1)} %collective-permute-done.21.refs_2_), channel_id=1, source_target_pairs={{0,2},{1,3},{2,0},{3,1},{4,6},{5,7},{6,4},{7,5}} | collective-permute-start | bytes 2396168 | tf_op jit(solution)/shard_map/ppermute | solution.py:356
  666.4 20.9 %collective-permute-start.19 = (bf16[780,4,128]{2,1,0:T(4,128)(2,1)S(1)}, bf16[780,4,128]{2,1,0:T(4,128)(2,1)S(1)}, u32[]{:S(2)}, u32[]{:S(2)}) collective-permute-start(bf16[780,4,128]{2,1,0:T(4,128)(2,1)S(1)} %collective-permute-done.18.refs_1_), channel_id=1, source_target_pairs={{0,4},{1,5},{2,6},{3,7},{4,0},{5,1},{6,2},{7,3}} | collective-permute-start | bytes 2396168 | tf_op jit(solution)/shard_map/ppermute | solution.py:356
  670.8 17.5 %collective-permute-start.55 = (bf16[780,4,128]{2,1,0:T(4,128)(2,1)S(1)}, bf16[780,4,128]{2,1,0:T(4,128)(2,1)S(1)}, u32[]{:S(2)}, u32[]{:S(2)}) collective-permute-start(bf16[780,4,128]{2,1,0:T(4,128)(2,1)S(1)} %collective-permute-done.52.refs_2_), channel_id=1, source_target_pairs={{0,1},{1,0},{2,3},{3,2},{4,5},{5,4},{6,7},{7,6}} | collective-permute-start | bytes 2396168 | tf_op jit(solution)/shard_map/ppermute | solution.py:356
  670.8 18.0 %collective-permute-start.54 = (bf16[780,4,128]{2,1,0:T(4,128)(2,1)S(1)}, bf16[780,4,128]{2,1,0:T(4,128)(2,1)S(1)}, u32[]{:S(2)}, u32[]{:S(2)}) collective-permute-start(bf16[780,4,128]{2,1,0:T(4,128)(2,1)S(1)} %collective-permute-done.18.refs_1_), channel_id=1, source_target_pairs={{0,1},{1,0},{2,3},{3,2},{4,5},{5,4},{6,7},{7,6}} | collective-permute-start | bytes 2396168 | tf_op jit(solution)/shard_map/ppermute | solution.py:356
  671.3 17.5 %collective-permute-start.17 = (bf16[780,4,128]{2,1,0:T(4,128)(2,1)S(1)}, bf16[780,4,128]{2,1,0:T(4,128)(2,1)S(1)}, u32[]{:S(2)}, u32[]{:S(2)}) collective-permute-start(bf16[780,4,128]{2,1,0:T(4,128)(2,1)S(1)} %collective-permute-done.16.refs_2_), channel_id=1, source_target_pairs={{0,1},{1,0},{2,3},{3,2},{4,5},{5,4},{6,7},{7,6}} | collective-permute-start | bytes 2396168 | tf_op jit(solution)/shard_map/ppermute | solution.py:356
  685.3 4.0 collective-permute-start.23
  687.4 2.3 collective-permute-start.20
  688.3 27.9 %collective-permute-start.14 = (bf16[780,4,128]{2,1,0:T(4,128)(2,1)}, bf16[780,4,128]{2,1,0:T(4,128)(2,1)}, u32[]{:S(2)}, u32[]{:S(2)}) collective-permute-start(bf16[780,4,128]{2,1,0:T(4,128)(2,1)} %collective-permute-done.13.refs_0_), channel_id=1, source_target_pairs={{0,1},{1,0},{2,3},{3,2},{4,5},{5,4},{6,7},{7,6}} | collective-permute-start | bytes 2396168 | tf_op jit(solution)/shard_map/ppermute | solution.py:356
  688.8 30.4 %collective-permute-start.11 = (bf16[780,4,128]{2,1,0:T(4,128)(2,1)}, bf16[780,4,128]{2,1,0:T(4,128)(2,1)}, u32[]{:S(2)}, u32[]{:S(2)}) collective-permute-start(bf16[780,4,128]{2,1,0:T(4,128)(2,1)} %collective-permute-done.10.refs_2_), channel_id=1, source_target_pairs={{0,1},{1,0},{2,3},{3,2},{4,5},{5,4},{6,7},{7,6}} | collective-permute-start | bytes 2396168 | tf_op jit(solution)/shard_map/ppermute | solution.py:356
  688.8 30.3 %collective-permute-start.8 = (bf16[780,4,128]{2,1,0:T(4,128)(2,1)}, bf16[780,4,128]{2,1,0:T(4,128)(2,1)}, u32[]{:S(2)}, u32[]{:S(2)}) collective-permute-start(bf16[780,4,128]{2,1,0:T(4,128)(2,1)} %collective-permute-done.7.refs_0_), channel_id=1, source_target_pairs={{0,1},{1,0},{2,3},{3,2},{4,5},{5,4},{6,7},{7,6}} | collective-permute-start | bytes 2396168 | tf_op jit(solution)/shard_map/ppermute | solution.py:356
  689.3 32.7 %collective-permute-start.5 = (bf16[780,4,128]{2,1,0:T(4,128)(2,1)}, bf16[780,4,128]{2,1,0:T(4,128)(2,1)}, u32[]{:S(2)}, u32[]{:S(2)}) collective-permute-start(bf16[780,4,128]{2,1,0:T(4,128)(2,1)} %collective-permute-done.4.refs_2_), channel_id=1, source_target_pairs={{0,1},{1,0},{2,3},{3,2},{4,5},{5,4},{6,7},{7,6}} | collective-permute-start | bytes 2396168 | tf_op jit(solution)/shard_map/ppermute | solution.py:356
  689.7 32.4 %collective-permute-start.2 = (bf16[780,4,128]{2,1,0:T(4,128)(2,1)}, bf16[780,4,128]{2,1,0:T(4,128)(2,1)}, u32[]{:S(2)}, u32[]{:S(2)}) collective-permute-start(bf16[780,4,128]{2,1,0:T(4,128)(2,1)} %collective-permute-done.1.refs_0_), channel_id=1, source_target_pairs={{0,1},{1,0},{2,3},{3,2},{4,5},{5,4},{6,7},{7,6}} | collective-permute-start | bytes 2396168 | tf_op jit(solution)/shard_map/ppermute | solution.py:356
  (26 other events, 54.4 us)
where the time goes:
time: 725 us
  Pallas kernels  498 us (69%)
  waiting for transfers between devices  185 us (26%)
  starting transfers between devices  27.6 us (4%)
  local copies, waits for them, and re-layouts  12.7 us (2%)
    pallas_call x1, Pallas kernels, reduce_scatter(): pl.pallas_call(functools.partial(reduce_kernel, shard_rows), out_shape=(s...  425 us
    ppermute x56, waiting for transfers between devices, send(): return lax.ppermute(a, 'dp', hop[along])  185 us
    pallas_call x8, Pallas kernels, adamw(): pl.pallas_call(adamw_kernel, grid=(steps,), out_shape=(state, state, stat...  39.9 us
    pallas_call x12, Pallas kernels, store(): pl.pallas_call(functools.partial(store_kernel, [(which, start, min(size,...  33 us
    ppermute x56, starting transfers between devices, send(): return lax.ppermute(a, 'dp', hop[along])  27.6 us
  transfers between devices with their start and end apart: 56, of which 21 were waited for; matrix products, arithmetic and copies ran while one was open for 0% of the time, Pallas kernels for 4%

commit v1 on v0

--- a/solution.py
+++ b/solution.py
@@ -17,12 +17,12 @@
 
 MESH = pl.DeviceIdType.MESH
 LANES = 128
-CHUNK_ROWS = 384
+CHUNK_ROWS = 240
 HALF_ROWS = CHUNK_ROWS // 2
 SLOTS = 4
 VMEM_LIMIT = 20 << 20
-PARTS = 8
-ADAM_ROWS = 1560
+ADAM_ROWS = 960
+PARTS = (1, 2, 4, 4, 4, 4, 3, 2, 1, 1)
 TILE_ROWS = 120
 
 
@@ -72,7 +72,6 @@
     fetches = (pltpu.make_async_copy(w, w_out.at[pl.ds(0, shard_rows)], w_sem),
                pltpu.make_async_copy(m, m_out.at[pl.ds(0, shard_rows)], m_sem))
 
-    meet(others)
     acc[...] = jnp.zeros_like(acc)
 
     def loads(i, size):
@@ -113,9 +112,15 @@
         def _():
             do(tail)
 
+    for cp in loads(0, full):
+        cp.start()
+    meet(others)
+    for cp in swaps(0, full):
+        cp.start()
+
     def begin(i):
         def do(size):
-            for cp in loads(i, size) + swaps(i, size):
+            for cp in swaps(i, size) + loads(i, size):
                 cp.start()
 
         for_size(i, do)
@@ -184,7 +189,7 @@
         acc[...] += lax.fori_loop(0, HALF_ROWS // 8, tile, jnp.zeros((8, LANES), jnp.float32))
 
     def step(i, carry):
-        @pl.when(i < chunks)
+        @pl.when((i >= 1) & (i < chunks))
         def _():
             begin(i)
 
@@ -278,11 +283,10 @@
     lax.fori_loop(0, ADAM_ROWS // TILE_ROWS, tile, 0)
 
 
-def adamw(part, lr, norm, g, w, m, v, mask, before):
+def adamw(first, steps, lr, norm, g, w, m, v, mask, before):
     rows = v.shape[0]
-    part_rows = g.shape[0] // PARTS
-    steps = part_rows // ADAM_ROWS
-    block = pl.BlockSpec((ADAM_ROWS, LANES), lambda i: (i + part * steps, 0))
+    part_rows = steps * ADAM_ROWS
+    block = pl.BlockSpec((ADAM_ROWS, LANES), lambda i: (i + first, 0))
     state = jax.ShapeDtypeStruct((rows, LANES), jnp.float32)
     blind = [pl.BlockSpec(memory_space=pl.ANY)] * len(before)
     return pl.pallas_call(
@@ -326,15 +330,16 @@
 def store(pieces, spots, before, num_dev, grains):
     count = len(pieces)
     hbm = pl.BlockSpec(memory_space=pltpu.HBM)
-    size = pieces[0].shape[0]
+    room = max(p.shape[0] for p in pieces)
     moved = sum(p.size for p in pieces)
     return pl.pallas_call(
-        functools.partial(store_kernel, [(which, start, min(size, grains - start), grains) for which, start in spots]),
+        functools.partial(store_kernel, [(which, start, min(p.shape[0], grains - start), grains)
+                                         for p, (which, start) in zip(pieces, spots)]),
         out_shape=jax.ShapeDtypeStruct((num_dev * grains, 4, LANES), jnp.bfloat16),
         in_specs=[hbm] * (count + len(before)),
         out_specs=hbm,
         input_output_aliases={count: 0} if before else {},
-        scratch_shapes=[pltpu.VMEM((count,) + pieces[0].shape, jnp.bfloat16),
+        scratch_shapes=[pltpu.VMEM((count, room, 4, LANES), jnp.bfloat16),
                         pltpu.SemaphoreType.DMA((count,)), pltpu.SemaphoreType.DMA((count,))],
         compiler_params=pltpu.CompilerParams(vmem_limit_bytes=VMEM_LIMIT),
         cost_estimate=pl.CostEstimate(flops=40 * moved, bytes_accessed=4 * moved, transcendentals=0),
@@ -362,22 +367,23 @@
         state = ()
         whole = ()
         arrived = []
-        for p in range(PARTS):
+        firsts = [sum(PARTS[:p]) for p in range(len(PARTS))]
+        for p, steps in enumerate(PARTS):
             *state, packed, grad_norm = adamw(
-                p, learn_rate, norm, g, w, m, flat(mom_second), flat(decay_mask), state)
+                firsts[p], steps, learn_rate, norm, g, w, m, flat(mom_second), flat(decay_mask), state)
             arrived.append((packed, send(packed, "x"), send(packed, "y"),
                             send(packed, "core")))
-        size = packed.shape[0]
+        starts = [first * ADAM_ROWS // 4 for first in firsts]
         far = []
         for p, (packed, from_x, from_y, from_core) in enumerate(arrived):
             far.append(send(from_x, "y") if p % 2 == 0 else send(from_y, "x"))
             pieces = [packed, from_x, from_y, from_core, send(from_x, "core"), send(from_y, "core")]
-            whole = put(pieces, [(k, p * size) for k in (0, 1, 2, 4, 5, 6)], whole)
-        for p in range(0, PARTS, 2):
+            whole = put(pieces, [(k, starts[p]) for k in (0, 1, 2, 4, 5, 6)], whole)
+        for p in range(0, len(PARTS), 2):
             pieces, spots = [], []
             for q in (p, p + 1):
                 pieces += [far[q], send(far[q], "core")]
-                spots += [(3, q * size), (7, q * size)]
+                spots += [(3, starts[q]), (7, starts[q])]
             whole = put(pieces, spots, whole)
         new_w, new_m, new_v = state
         params = whole[0].reshape(num_dev * shard_len)

time: 725 us -> 761 us (1.050)
  Pallas kernels: 498 us -> 527 us
    pallas_call x12 -> x15, Pallas kernels: 33 us -> 51.6 us  [store(): pl.pallas_call(functools.partial(store_kernel, [(which, start, min(p.shap...]
    pallas_call x8 -> x10, Pallas kernels: 39.9 us -> 47.9 us  [adamw(): pl.pallas_call(adamw_kernel, grid=(steps,), out_shape=(state, state, stat...]
    ppermute x56 -> x70, starting transfers between devices: 27.6 us -> 35.1 us  [send(): return lax.ppermute(a, 'dp', hop[along])]
    ppermute x56 -> x70, waiting for transfers between devices: 185 us -> 182 us  [send(): return lax.ppermute(a, 'dp', hop[along])]
  transfers between devices with their start and end apart: 56 -> 70, of which waited for: 21 -> 32; matrix products, arithmetic and copies ran while one was open for 0% -> 0% of each run, Pallas kernels for 4% -> 12%
where the time goes in v1:
time: 761 us; the launch traced here: 760 us
  Pallas kernels  527 us (69%)
  waiting for transfers between devices  182 us (24%)
  starting transfers between devices  35.1 us (5%)
  local copies, waits for them, and re-layouts  14.2 us (2%)
    pallas_call x1, Pallas kernels, reduce_scatter(): pl.pallas_call(functools.partial(reduce_kernel, shard_rows), out_shape=(s...  427 us
    ppermute x70, waiting for transfers between devices, send(): return lax.ppermute(a, 'dp', hop[along])  182 us
    pallas_call x15, Pallas kernels, store(): pl.pallas_call(functools.partial(store_kernel, [(which, start, min(p.shap...  51.6 us
    pallas_call x10, Pallas kernels, adamw(): pl.pallas_call(adamw_kernel, grid=(steps,), out_shape=(state, state, stat...  47.9 us
    ppermute x70, starting transfers between devices, send(): return lax.ppermute(a, 'dp', hop[along])  35.1 us
  transfers between devices with their start and end apart: 70, of which 32 were waited for; matrix products, arithmetic and copies ran while one was open for 0% of the time, Pallas kernels for 12%

profile of v1, /device:TPU:0, one launch (start us, length us, event | category | flops | bytes accessed | tf_op | source)
XLA Modules:
  0.0 760.1 jit_solution(10404453229244344546)
XLA Ops:
  1.3 427.2 %shard_map.101 = (f32[24960,128]{1,0:T(8,128)S(1)}, f32[24960,128]{1,0:T(8,128)S(1)}, f32[24960,128]{1,0:T(8,128)S(1)}, f32[8,128]{1,0:T(8,128)}) custom-call(bf16[1,25530368]{1,0:T(2,128)(2,1)} %grad.1, f32[24932,128]{1,0:T(8,128)} %bitcast.32, f32[24932,128]{1,0:T(8,128)} %bitcast.33), custom_call_target="tpu_custom_call" | custom-call | tf_op jit(solution)/shard_map/pallas_call | solution.py:242
  428.4 3.0 shard_map.102
  431.4 1.4 collective-permute-start.24
  433.4 3.7 shard_map.103
  437.1 6.4 shard_map.104
  443.5 6.4 shard_map.105
  449.9 6.4 shard_map.106
  456.4 6.4 shard_map.107
  462.8 5.6 shard_map.108
  468.5 3.7 shard_map.109
  472.2 3.0 shard_map.110
  475.1 1.5 collective-permute-start
  477.3 3.1 shard_map.111
  480.6 1.4 collective-permute-start.30
  482.6 1.1 collective-permute-done.refs_1_
  483.7 1.5 collective-permute-start.3
  486.4 3.2 collective-permute-done.30.refs_1_
  489.6 1.8 collective-permute-done.3.refs_2_
  491.4 1.5 collective-permute-start.27
  494.3 1.4 collective-permute-start.9
  495.6 4.5 collective-permute-done.62.refs_1_
  500.1 5.4 collective-permute-done.27.refs_2_
  506.0 4.2 collective-permute-done.38.refs_1_
  510.9 3.0 collective-permute-done.9.refs_2_
  513.9 1.5 collective-permute-start.6
  517.4 1.4 collective-permute-start.42
  519.4 5.7 collective-permute-done.25.refs_0_
  525.7 12.4 %collective-permute-done.4.refs_2_ = bf16[240,4,128]{2,1,0:T(4,128)(2,1)} collective-permute-done((bf16[240,4,128]{2,1,0:T(4,128)(2,1)S(1)}, bf16[240,4,128]{2,1,0:T(4,128)(2,1)}, u32[]{:S(2)}, u32[]{:S(2)}) %collective-permute-start.4) | collective-permute-done | bytes 245792 | tf_op jit(solution)/shard_map/ppermute | solution.py:361
  538.1 1.4 collective-permute-start.18
  539.6 5.9 collective-permute-done.1.refs_0_
  549.4 1.4 collective-permute-start.54
  551.5 11.3 %collective-permute-done.18.refs_1_ = bf16[960,4,128]{2,1,0:T(4,128)(2,1)S(1)} collective-permute-done((bf16[960,4,128]{2,1,0:T(4,128)(2,1)S(1)}, bf16[960,4,128]{2,1,0:T(4,128)(2,1)S(1)}, u32[]{:S(2)}, u32[]{:S(2)}) %collective-permute-start.18) | collective-permute-done | bytes 983072 | tf_op jit(solution)/shard_map/ppermute | solution.py:361
  562.8 7.4 collective-permute-done.58.refs_2_
  570.7 1.5 collective-permute-start.50
  572.2 11.6 %collective-permute-done.54.refs_1_ = bf16[960,4,128]{2,1,0:T(4,128)(2,1)S(1)} collective-permute-done((bf16[960,4,128]{2,1,0:T(4,128)(2,1)S(1)}, bf16[960,4,128]{2,1,0:T(4,128)(2,1)S(1)}, u32[]{:S(2)}, u32[]{:S(2)}) %collective-permute-start.54) | collective-permute-done | bytes 983072 | tf_op jit(solution)/shard_map/ppermute | solution.py:361
  583.8 7.4 collective-permute-done.21.refs_2_
  591.8 1.5 collective-permute-start.15
  593.3 11.6 %collective-permute-done.12.refs_1_ = bf16[960,4,128]{2,1,0:T(4,128)(2,1)S(1)} collective-permute-done((bf16[960,4,128]{2,1,0:T(4,128)(2,1)S(1)}, bf16[960,4,128]{2,1,0:T(4,128)(2,1)S(1)}, u32[]{:S(2)}, u32[]{:S(2)}) %collective-permute-start.12) | collective-permute-done | bytes 983072 | tf_op jit(solution)/shard_map/ppermute | solution.py:361
  604.9 7.4 collective-permute-done.50.refs_2_
  613.6 11.0 %collective-permute-done.46.refs_1_ = bf16[960,4,128]{2,1,0:T(4,128)(2,1)S(1)} collective-permute-done((bf16[960,4,128]{2,1,0:T(4,128)(2,1)S(1)}, bf16[960,4,128]{2,1,0:T(4,128)(2,1)S(1)}, u32[]{:S(2)}, u32[]{:S(2)}) %collective-permute-start.46) | collective-permute-done | bytes 983072 | tf_op jit(solution)/shard_map/ppermute | solution.py:361
  624.6 7.1 collective-permute-done.15.refs_2_
  634.0 1.4 collective-permute-start.10
  637.3 8.5 %collective-permute-done.28.refs_2_ = bf16[480,4,128]{2,1,0:T(4,128)(2,1)S(1)} collective-permute-done((bf16[480,4,128]{2,1,0:T(4,128)(2,1)S(1)}, bf16[480,4,128]{2,1,0:T(4,128)(2,1)S(1)}, u32[]{:S(2)}, u32[]{:S(2)}) %collective-permute-start.28) | collective-permute-done | bytes 491552 | tf_op jit(solution)/shard_map/ppermute | solution.py:361
  647.3 6.7 collective-permute-done.10.refs_2_
  658.4 1.1 collective-permute-done.7.refs_0_
  661.0 1.0 collective-permute-start.19
  665.4 19.3 %collective-permute-done.22.refs_2_ = bf16[960,4,128]{2,1,0:T(4,128)(2,1)S(1)} collective-permute-done((bf16[960,4,128]{2,1,0:T(4,128)(2,1)S(1)}, bf16[960,4,128]{2,1,0:T(4,128)(2,1)S(1)}, u32[]{:S(2)}, u32[]{:S(2)}) %collective-permute-start.22) | collective-permute-done | bytes 983072 | tf_op jit(solution)/shard_map/ppermute | solution.py:361
  684.6 1.0 collective-permute-done.19.refs_0_
  685.7 19.6 %collective-permute-done.16.refs_2_ = bf16[960,4,128]{2,1,0:T(4,128)(2,1)S(1)} collective-permute-done((bf16[960,4,128]{2,1,0:T(4,128)(2,1)S(1)}, bf16[960,4,128]{2,1,0:T(4,128)(2,1)S(1)}, u32[]{:S(2)}, u32[]{:S(2)}) %collective-permute-start.16) | collective-permute-done | bytes 983072 | tf_op jit(solution)/shard_map/ppermute | solution.py:361
  707.9 2.4 shard_map.112.refs_6_
  710.4 3.6 shard_map.113.refs_6_
  714.0 4.5 shard_map.114.refs_6_
  718.5 4.5 shard_map.115.refs_6_
  723.1 4.5 shard_map.116.refs_6_
  727.7 4.5 shard_map.117.refs_6_
  732.3 4.1 shard_map.118.refs_6_
  736.4 3.6 shard_map.119.refs_6_
  740.1 3.1 shard_map.120.refs_6_
  743.3 3.0 shard_map.121.refs_4_
  746.4 2.5 shard_map.122.refs_4_
  748.9 3.2 shard_map.123.refs_4_
  752.2 3.2 shard_map.124.refs_4_
  755.4 2.6 shard_map.125.refs_4_
  758.0 2.1 shard_map.126
  (202 shorter events, 33.6 us)
Async XLA Ops:
  431.4 49.1 %collective-permute-start.24 = (bf16[240,4,128]{2,1,0:T(4,128)(2,1)}, bf16[240,4,128]{2,1,0:T(4,128)(2,1)}, u32[]{:S(2)}, u32[]{:S(2)}) collective-permute-start(bf16[240,4,128]{2,1,0:T(4,128)(2,1)} %get-tuple-element.89.refs_0_), channel_id=1, source_target_pairs={{0,2},{1,3},{2,0},{3,1},{4,6},{5,7},{6,4},{7,5}} | collective-permute-start | bytes 737288 | tf_op jit(solution)/shard_map/ppermute | solution.py:361
  432.8 47.7 %collective-permute-start.66 = (bf16[240,4,128]{2,1,0:T(4,128)(2,1)}, bf16[240,4,128]{2,1,0:T(4,128)(2,1)}, u32[]{:S(2)}, u32[]{:S(2)}) collective-permute-start(bf16[240,4,128]{2,1,0:T(4,128)(2,1)} %get-tuple-element.89.refs_0_), channel_id=1, source_target_pairs={{0,4},{1,5},{2,6},{3,7},{4,0},{5,1},{6,2},{7,3}} | collective-permute-start | bytes 737288 | tf_op jit(solution)/shard_map/ppermute | solution.py:361
  433.4 48.6 %collective-permute-start.67 = (bf16[240,4,128]{2,1,0:T(4,128)(2,1)}, bf16[240,4,128]{2,1,0:T(4,128)(2,1)}, u32[]{:S(2)}, u32[]{:S(2)}) collective-permute-start(bf16[240,4,128]{2,1,0:T(4,128)(2,1)} %get-tuple-element.89.refs_0_), channel_id=1, source_target_pairs={{0,1},{1,0},{2,3},{3,2},{4,5},{5,4},{6,7},{7,6}} | collective-permute-start | bytes 737288 | tf_op jit(solution)/shard_map/ppermute | solution.py:361
  475.1 8.6 %collective-permute-start = (bf16[240,4,128]{2,1,0:T(4,128)(2,1)}, bf16[240,4,128]{2,1,0:T(4,128)(2,1)S(1)}, u32[]{:S(2)}, u32[]{:S(2)}) collective-permute-start(bf16[240,4,128]{2,1,0:T(4,128)(2,1)} %get-tuple-element.78.refs_0_), channel_id=1, source_target_pairs={{0,2},{1,3},{2,0},{3,1},{4,6},{5,7},{6,4},{7,5}} | collective-permute-start | bytes 737288 | tf_op jit(solution)/shard_map/ppermute | solution.py:361
  476.6 8.6 %collective-permute-start.34 = (bf16[240,4,128]{2,1,0:T(4,128)(2,1)}, bf16[240,4,128]{2,1,0:T(4,128)(2,1)S(1)}, u32[]{:S(2)}, u32[]{:S(2)}) collective-permute-start(bf16[240,4,128]{2,1,0:T(4,128)(2,1)} %get-tuple-element.78.refs_0_), channel_id=1, source_target_pairs={{0,4},{1,5},{2,6},{3,7},{4,0},{5,1},{6,2},{7,3}} | collective-permute-start | bytes 737288 | tf_op jit(solution)/shard_map/ppermute | solution.py:361
  480.5 4.7 collective-permute-start.35
  480.6 9.1 %collective-permute-start.30 = (bf16[240,4,128]{2,1,0:T(4,128)(2,1)}, bf16[240,4,128]{2,1,0:T(4,128)(2,1)S(1)}, u32[]{:S(2)}, u32[]{:S(2)}) collective-permute-start(bf16[240,4,128]{2,1,0:T(4,128)(2,1)} %get-tuple-element.82.refs_0_), channel_id=1, source_target_pairs={{0,2},{1,3},{2,0},{3,1},{4,6},{5,7},{6,4},{7,5}} | collective-permute-start | bytes 737288 | tf_op jit(solution)/shard_map/ppermute | solution.py:361
  482.0 18.2 %collective-permute-start.62 = (bf16[480,4,128]{2,1,0:T(4,128)(2,1)S(1)}, bf16[480,4,128]{2,1,0:T(4,128)(2,1)S(1)}, u32[]{:S(2)}, u32[]{:S(2)}) collective-permute-start(bf16[480,4,128]{2,1,0:T(4,128)(2,1)S(1)} %copy-done.19), channel_id=1, source_target_pairs={{0,2},{1,3},{2,0},{3,1},{4,6},{5,7},{6,4},{7,5}} | collective-permute-start | bytes 1474568 | tf_op jit(solution)/shard_map/ppermute | solution.py:361
  483.7 7.7 %collective-permute-start.3 = (bf16[240,4,128]{2,1,0:T(4,128)(2,1)}, bf16[240,4,128]{2,1,0:T(4,128)(2,1)S(1)}, u32[]{:S(2)}, u32[]{:S(2)}) collective-permute-start(bf16[240,4,128]{2,1,0:T(4,128)(2,1)} %get-tuple-element.82.refs_0_), channel_id=1, source_target_pairs={{0,4},{1,5},{2,6},{3,7},{4,0},{5,1},{6,2},{7,3}} | collective-permute-start | bytes 737288 | tf_op jit(solution)/shard_map/ppermute | solution.py:361
  485.2 7.7 %collective-permute-start.31 = (bf16[240,4,128]{2,1,0:T(4,128)(2,1)}, bf16[240,4,128]{2,1,0:T(4,128)(2,1)S(1)}, u32[]{:S(2)}, u32[]{:S(2)}) collective-permute-start(bf16[240,4,128]{2,1,0:T(4,128)(2,1)} %get-tuple-element.82.refs_0_), channel_id=1, source_target_pairs={{0,1},{1,0},{2,3},{3,2},{4,5},{5,4},{6,7},{7,6}} | collective-permute-start | bytes 737288 | tf_op jit(solution)/shard_map/ppermute | solution.py:361
  485.9 7.7 %collective-permute-start.68 = (bf16[240,4,128]{2,1,0:T(4,128)(2,1)}, bf16[240,4,128]{2,1,0:T(4,128)(2,1)S(1)}, u32[]{:S(2)}, u32[]{:S(2)}) collective-permute-start(bf16[240,4,128]{2,1,0:T(4,128)(2,1)} %collective-permute-done.24.refs_1_), channel_id=1, source_target_pairs={{0,1},{1,0},{2,3},{3,2},{4,5},{5,4},{6,7},{7,6}} | collective-permute-start | bytes 737288 | tf_op jit(solution)/shard_map/ppermute | solution.py:361
  489.6 4.7 collective-permute-start.69
  491.4 14.1 %collective-permute-start.27 = (bf16[480,4,128]{2,1,0:T(4,128)(2,1)S(1)}, bf16[480,4,128]{2,1,0:T(4,128)(2,1)S(1)}, u32[]{:S(2)}, u32[]{:S(2)}) collective-permute-start(bf16[480,4,128]{2,1,0:T(4,128)(2,1)S(1)} %copy-done.19), channel_id=1, source_target_pairs={{0,4},{1,5},{2,6},{3,7},{4,0},{5,1},{6,2},{7,3}} | collective-permute-start | bytes 1474568 | tf_op jit(solution)/shard_map/ppermute | solution.py:361
  493.6 11.9 %collective-permute-start.63 = (bf16[480,4,128]{2,1,0:T(4,128)(2,1)S(1)}, bf16[480,4,128]{2,1,0:T(4,128)(2,1)S(1)}, u32[]{:S(2)}, u32[]{:S(2)}) collective-permute-start(bf16[480,4,128]{2,1,0:T(4,128)(2,1)S(1)} %copy-done.19), channel_id=1, source_target_pairs={{0,1},{1,0},{2,3},{3,2},{4,5},{5,4},{6,7},{7,6}} | collective-permute-start | bytes 1474568 | tf_op jit(solution)/shard_map/ppermute | solution.py:361
  493.6 16.6 %collective-permute-start.38 = (bf16[480,4,128]{2,1,0:T(4,128)(2,1)S(1)}, bf16[480,4,128]{2,1,0:T(4,128)(2,1)S(1)}, u32[]{:S(2)}, u32[]{:S(2)}) collective-permute-start(bf16[480,4,128]{2,1,0:T(4,128)(2,1)S(1)} %copy-done.20), channel_id=1, source_target_pairs={{0,2},{1,3},{2,0},{3,1},{4,6},{5,7},{6,4},{7,5}} | collective-permute-start | bytes 1474568 | tf_op jit(solution)/shard_map/ppermute | solution.py:361
  494.3 19.6 %collective-permute-start.9 = (bf16[480,4,128]{2,1,0:T(4,128)(2,1)S(1)}, bf16[480,4,128]{2,1,0:T(4,128)(2,1)S(1)}, u32[]{:S(2)}, u32[]{:S(2)}) collective-permute-start(bf16[480,4,128]{2,1,0:T(4,128)(2,1)S(1)} %copy-done.20), channel_id=1, source_target_pairs={{0,4},{1,5},{2,6},{3,7},{4,0},{5,1},{6,2},{7,3}} | collective-permute-start | bytes 1474568 | tf_op jit(solution)/shard_map/ppermute | solution.py:361
  500.1 13.7 %collective-permute-start.39 = (bf16[480,4,128]{2,1,0:T(4,128)(2,1)S(1)}, bf16[480,4,128]{2,1,0:T(4,128)(2,1)S(1)}, u32[]{:S(2)}, u32[]{:S(2)}) collective-permute-start(bf16[480,4,128]{2,1,0:T(4,128)(2,1)S(1)} %copy-done.20), channel_id=1, source_target_pairs={{0,1},{1,0},{2,3},{3,2},{4,5},{5,4},{6,7},{7,6}} | collective-permute-start | bytes 1474568 | tf_op jit(solution)/shard_map/ppermute | solution.py:361
  505.5 9.8 %collective-permute-start.36 = (bf16[240,4,128]{2,1,0:T(4,128)(2,1)S(1)}, bf16[240,4,128]{2,1,0:T(4,128)(2,1)S(1)}, u32[]{:S(2)}, u32[]{:S(2)}) collective-permute-start(bf16[240,4,128]{2,1,0:T(4,128)(2,1)S(1)} %collective-permute-done.refs_1_), channel_id=1, source_target_pairs={{0,1},{1,0},{2,3},{3,2},{4,5},{5,4},{6,7},{7,6}} | collective-permute-start | bytes 737288 | tf_op jit(solution)/shard_map/ppermute | solution.py:361
  505.5 11.2 %collective-permute-start.37 = (bf16[240,4,128]{2,1,0:T(4,128)(2,1)S(1)}, bf16[240,4,128]{2,1,0:T(4,128)(2,1)S(1)}, u32[]{:S(2)}, u32[]{:S(2)}) collective-permute-start(bf16[240,4,128]{2,1,0:T(4,128)(2,1)S(1)} %collective-permute-done.34.refs_2_), channel_id=1, source_target_pairs={{0,1},{1,0},{2,3},{3,2},{4,5},{5,4},{6,7},{7,6}} | collective-permute-start | bytes 737288 | tf_op jit(solution)/shard_map/ppermute | solution.py:361
  510.2 8.6 %collective-permute-start.32 = (bf16[240,4,128]{2,1,0:T(4,128)(2,1)S(1)}, bf16[240,4,128]{2,1,0:T(4,128)(2,1)S(1)}, u32[]{:S(2)}, u32[]{:S(2)}) collective-permute-start(bf16[240,4,128]{2,1,0:T(4,128)(2,1)S(1)} %collective-permute-done.30.refs_1_), channel_id=1, source_target_pairs={{0,1},{1,0},{2,3},{3,2},{4,5},{5,4},{6,7},{7,6}} | collective-permute-start | bytes 737288 | tf_op jit(solution)/shard_map/ppermute | solution.py:361
  513.9 5.0 collective-permute-start.33
  513.9 32.3 %collective-permute-start.6 = (bf16[720,4,128]{2,1,0:T(4,128)(2,1)S(1)}, bf16[720,4,128]{2,1,0:T(4,128)(2,1)S(1)}, u32[]{:S(2)}, u32[]{:S(2)}) collective-permute-start(bf16[720,4,128]{2,1,0:T(4,128)(2,1)S(1)} %copy-done.8), channel_id=1, source_target_pairs={{0,2},{1,3},{2,0},{3,1},{4,6},{5,7},{6,4},{7,5}} | collective-permute-start | bytes 2211848 | tf_op jit(solution)/shard_map/ppermute | solution.py:361
  516.1 9.0 %collective-permute-start.25 = (bf16[240,4,128]{2,1,0:T(4,128)(2,1)}, bf16[240,4,128]{2,1,0:T(4,128)(2,1)S(1)}, u32[]{:S(2)}, u32[]{:S(2)}) collective-permute-start(bf16[240,4,128]{2,1,0:T(4,128)(2,1)} %collective-permute-done.24.refs_1_), channel_id=1, source_target_pairs={{0,4},{1,5},{2,6},{3,7},{4,0},{5,1},{6,2},{7,3}} | collective-permute-start | bytes 737288 | tf_op jit(solution)/shard_map/ppermute | solution.py:361
  517.4 28.7 %collective-permute-start.42 = (bf16[720,4,128]{2,1,0:T(4,128)(2,1)S(1)}, bf16[720,4,128]{2,1,0:T(4,128)(2,1)S(1)}, u32[]{:S(2)}, u32[]{:S(2)}) collective-permute-start(bf16[720,4,128]{2,1,0:T(4,128)(2,1)S(1)} %copy-done.8), channel_id=1, source_target_pairs={{0,4},{1,5},{2,6},{3,7},{4,0},{5,1},{6,2},{7,3}} | collective-permute-start | bytes 2211848 | tf_op jit(solution)/shard_map/ppermute | solution.py:361
  518.8 28.5 %collective-permute-start.43 = (bf16[720,4,128]{2,1,0:T(4,128)(2,1)S(1)}, bf16[720,4,128]{2,1,0:T(4,128)(2,1)S(1)}, u32[]{:S(2)}, u32[]{:S(2)}) collective-permute-start(bf16[720,4,128]{2,1,0:T(4,128)(2,1)S(1)} %copy-done.8), channel_id=1, source_target_pairs={{0,1},{1,0},{2,3},{3,2},{4,5},{5,4},{6,7},{7,6}} | collective-permute-start | bytes 2211848 | tf_op jit(solution)/shard_map/ppermute | solution.py:361
  518.8 19.3 %collective-permute-start.4 = (bf16[240,4,128]{2,1,0:T(4,128)(2,1)S(1)}, bf16[240,4,128]{2,1,0:T(4,128)(2,1)}, u32[]{:S(2)}, u32[]{:S(2)}) collective-permute-start(bf16[240,4,128]{2,1,0:T(4,128)(2,1)S(1)} %collective-permute-done.3.refs_2_), channel_id=1, source_target_pairs={{0,2},{1,3},{2,0},{3,1},{4,6},{5,7},{6,4},{7,5}} | collective-permute-start | bytes 737288 | tf_op jit(solution)/shard_map/ppermute | solution.py:361
  525.1 20.4 %collective-permute-start.1 = (bf16[240,4,128]{2,1,0:T(4,128)(2,1)S(1)}, bf16[240,4,128]{2,1,0:T(4,128)(2,1)}, u32[]{:S(2)}, u32[]{:S(2)}) collective-permute-start(bf16[240,4,128]{2,1,0:T(4,128)(2,1)S(1)} %collective-permute-done.refs_1_), channel_id=1, source_target_pairs={{0,4},{1,5},{2,6},{3,7},{4,0},{5,1},{6,2},{7,3}} | collective-permute-start | bytes 737288 | tf_op jit(solution)/shard_map/ppermute | solution.py:361
  538.1 24.6 %collective-permute-start.18 = (bf16[960,4,128]{2,1,0:T(4,128)(2,1)S(1)}, bf16[960,4,128]{2,1,0:T(4,128)(2,1)S(1)}, u32[]{:S(2)}, u32[]{:S(2)}) collective-permute-start(bf16[960,4,128]{2,1,0:T(4,128)(2,1)S(1)} %copy-done), channel_id=1, source_target_pairs={{0,2},{1,3},{2,0},{3,1},{4,6},{5,7},{6,4},{7,5}} | collective-permute-start | bytes 2949128 | tf_op jit(solution)/shard_map/ppermute | solution.py:361
  545.5 24.6 %collective-permute-start.58 = (bf16[960,4,128]{2,1,0:T(4,128)(2,1)S(1)}, bf16[960,4,128]{2,1,0:T(4,128)(2,1)S(1)}, u32[]{:S(2)}, u32[]{:S(2)}) collective-permute-start(bf16[960,4,128]{2,1,0:T(4,128)(2,1)S(1)} %copy-done), channel_id=1, source_target_pairs={{0,4},{1,5},{2,6},{3,7},{4,0},{5,1},{6,2},{7,3}} | collective-permute-start | bytes 2949128 | tf_op jit(solution)/shard_map/ppermute | solution.py:361
  546.1 3.3 collective-permute-start.64
  549.1 21.7 %collective-permute-start.59 = (bf16[960,4,128]{2,1,0:T(4,128)(2,1)S(1)}, bf16[960,4,128]{2,1,0:T(4,128)(2,1)S(1)}, u32[]{:S(2)}, u32[]{:S(2)}) collective-permute-start(bf16[960,4,128]{2,1,0:T(4,128)(2,1)S(1)} %copy-done), channel_id=1, source_target_pairs={{0,1},{1,0},{2,3},{3,2},{4,5},{5,4},{6,7},{7,6}} | collective-permute-start | bytes 2949128 | tf_op jit(solution)/shard_map/ppermute | solution.py:361
  549.4 34.4 %collective-permute-start.54 = (bf16[960,4,128]{2,1,0:T(4,128)(2,1)S(1)}, bf16[960,4,128]{2,1,0:T(4,128)(2,1)S(1)}, u32[]{:S(2)}, u32[]{:S(2)}) collective-permute-start(bf16[960,4,128]{2,1,0:T(4,128)(2,1)S(1)} %copy-done.1), channel_id=1, source_target_pairs={{0,2},{1,3},{2,0},{3,1},{4,6},{5,7},{6,4},{7,5}} | collective-permute-start | bytes 2949128 | tf_op jit(solution)/shard_map/ppermute | solution.py:361
  550.9 40.3 %collective-permute-start.21 = (bf16[960,4,128]{2,1,0:T(4,128)(2,1)S(1)}, bf16[960,4,128]{2,1,0:T(4,128)(2,1)S(1)}, u32[]{:S(2)}, u32[]{:S(2)}) collective-permute-start(bf16[960,4,128]{2,1,0:T(4,128)(2,1)S(1)} %copy-done.1), channel_id=1, source_target_pairs={{0,4},{1,5},{2,6},{3,7},{4,0},{5,1},{6,2},{7,3}} | collective-permute-start | bytes 2949128 | tf_op jit(solution)/shard_map/ppermute | solution.py:361
  562.8 29.0 %collective-permute-start.55 = (bf16[960,4,128]{2,1,0:T(4,128)(2,1)S(1)}, bf16[960,4,128]{2,1,0:T(4,128)(2,1)S(1)}, u32[]{:S(2)}, u32[]{:S(2)}) collective-permute-start(bf16[960,4,128]{2,1,0:T(4,128)(2,1)S(1)} %copy-done.1), channel_id=1, source_target_pairs={{0,1},{1,0},{2,3},{3,2},{4,5},{5,4},{6,7},{7,6}} | collective-permute-start | bytes 2949128 | tf_op jit(solution)/shard_map/ppermute | solution.py:361
  570.1 34.8 %collective-permute-start.12 = (bf16[960,4,128]{2,1,0:T(4,128)(2,1)S(1)}, bf16[960,4,128]{2,1,0:T(4,128)(2,1)S(1)}, u32[]{:S(2)}, u32[]{:S(2)}) collective-permute-start(bf16[960,4,128]{2,1,0:T(4,128)(2,1)S(1)} %copy-done.2), channel_id=1, source_target_pairs={{0,2},{1,3},{2,0},{3,1},{4,6},{5,7},{6,4},{7,5}} | collective-permute-start | bytes 2949128 | tf_op jit(solution)/shard_map/ppermute | solution.py:361
  570.7 41.5 %collective-permute-start.50 = (bf16[960,4,128]{2,1,0:T(4,128)(2,1)S(1)}, bf16[960,4,128]{2,1,0:T(4,128)(2,1)S(1)}, u32[]{:S(2)}, u32[]{:S(2)}) collective-permute-start(bf16[960,4,128]{2,1,0:T(4,128)(2,1)S(1)} %copy-done.2), channel_id=1, source_target_pairs={{0,4},{1,5},{2,6},{3,7},{4,0},{5,1},{6,2},{7,3}} | collective-permute-start | bytes 2949128 | tf_op jit(solution)/shard_map/ppermute | solution.py:361
  583.8 29.3 %collective-permute-start.51 = (bf16[960,4,128]{2,1,0:T(4,128)(2,1)S(1)}, bf16[960,4,128]{2,1,0:T(4,128)(2,1)S(1)}, u32[]{:S(2)}, u32[]{:S(2)}) collective-permute-start(bf16[960,4,128]{2,1,0:T(4,128)(2,1)S(1)} %copy-done.2), channel_id=1, source_target_pairs={{0,1},{1,0},{2,3},{3,2},{4,5},{5,4},{6,7},{7,6}} | collective-permute-start | bytes 2949128 | tf_op jit(solution)/shard_map/ppermute | solution.py:361
  591.2 33.4 %collective-permute-start.46 = (bf16[960,4,128]{2,1,0:T(4,128)(2,1)S(1)}, bf16[960,4,128]{2,1,0:T(4,128)(2,1)S(1)}, u32[]{:S(2)}, u32[]{:S(2)}) collective-permute-start(bf16[960,4,128]{2,1,0:T(4,128)(2,1)S(1)} %copy-done.3), channel_id=1, source_target_pairs={{0,2},{1,3},{2,0},{3,1},{4,6},{5,7},{6,4},{7,5}} | collective-permute-start | bytes 2949128 | tf_op jit(solution)/shard_map/ppermute | solution.py:361
  591.8 39.9 %collective-permute-start.15 = (bf16[960,4,128]{2,1,0:T(4,128)(2,1)S(1)}, bf16[960,4,128]{2,1,0:T(4,128)(2,1)S(1)}, u32[]{:S(2)}, u32[]{:S(2)}) collective-permute-start(bf16[960,4,128]{2,1,0:T(4,128)(2,1)S(1)} %copy-done.3), channel_id=1, source_target_pairs={{0,4},{1,5},{2,6},{3,7},{4,0},{5,1},{6,2},{7,3}} | collective-permute-start | bytes 2949128 | tf_op jit(solution)/shard_map/ppermute | solution.py:361
  604.9 27.4 %collective-permute-start.47 = (bf16[960,4,128]{2,1,0:T(4,128)(2,1)S(1)}, bf16[960,4,128]{2,1,0:T(4,128)(2,1)S(1)}, u32[]{:S(2)}, u32[]{:S(2)}) collective-permute-start(bf16[960,4,128]{2,1,0:T(4,128)(2,1)S(1)} %copy-done.3), channel_id=1, source_target_pairs={{0,1},{1,0},{2,3},{3,2},{4,5},{5,4},{6,7},{7,6}} | collective-permute-start | bytes 2949128 | tf_op jit(solution)/shard_map/ppermute | solution.py:361
  612.3 21.0 %collective-permute-start.40 = (bf16[480,4,128]{2,1,0:T(4,128)(2,1)S(1)}, bf16[480,4,128]{2,1,0:T(4,128)(2,1)S(1)}, u32[]{:S(2)}, u32[]{:S(2)}) collective-permute-start(bf16[480,4,128]{2,1,0:T(4,128)(2,1)S(1)} %collective-permute-done.38.refs_1_), channel_id=1, source_target_pairs={{0,1},{1,0},{2,3},{3,2},{4,5},{5,4},{6,7},{7,6}} | collective-permute-start | bytes 1474568 | tf_op jit(solution)/shard_map/ppermute | solution.py:361
  613.1 23.2 %collective-permute-start.41 = (bf16[480,4,128]{2,1,0:T(4,128)(2,1)S(1)}, bf16[480,4,128]{2,1,0:T(4,128)(2,1)S(1)}, u32[]{:S(2)}, u32[]{:S(2)}) collective-permute-start(bf16[480,4,128]{2,1,0:T(4,128)(2,1)S(1)} %collective-permute-done.9.refs_2_), channel_id=1, source_target_pairs={{0,1},{1,0},{2,3},{3,2},{4,5},{5,4},{6,7},{7,6}} | collective-permute-start | bytes 1474568 | tf_op jit(solution)/shard_map/ppermute | solution.py:361
  624.6 29.4 %collective-permute-start.44 = (bf16[720,4,128]{2,1,0:T(4,128)(2,1)S(1)}, bf16[720,4,128]{2,1,0:T(4,128)(2,1)S(1)}, u32[]{:S(2)}, u32[]{:S(2)}) collective-permute-start(bf16[720,4,128]{2,1,0:T(4,128)(2,1)S(1)} %collective-permute-done.6.refs_1_), channel_id=1, source_target_pairs={{0,1},{1,0},{2,3},{3,2},{4,5},{5,4},{6,7},{7,6}} | collective-permute-start | bytes 2211848 | tf_op jit(solution)/shard_map/ppermute | solution.py:361
  631.7 14.1 %collective-permute-start.28 = (bf16[480,4,128]{2,1,0:T(4,128)(2,1)S(1)}, bf16[480,4,128]{2,1,0:T(4,128)(2,1)S(1)}, u32[]{:S(2)}, u32[]{:S(2)}) collective-permute-start(bf16[480,4,128]{2,1,0:T(4,128)(2,1)S(1)} %collective-permute-done.27.refs_2_), channel_id=1, source_target_pairs={{0,2},{1,3},{2,0},{3,1},{4,6},{5,7},{6,4},{7,5}} | collective-permute-start | bytes 1474568 | tf_op jit(solution)/shard_map/ppermute | solution.py:361
  632.3 23.9 %collective-permute-start.45 = (bf16[720,4,128]{2,1,0:T(4,128)(2,1)S(1)}, bf16[720,4,128]{2,1,0:T(4,128)(2,1)S(1)}, u32[]{:S(2)}, u32[]{:S(2)}) collective-permute-start(bf16[720,4,128]{2,1,0:T(4,128)(2,1)S(1)} %collective-permute-done.42.refs_2_), channel_id=1, source_target_pairs={{0,1},{1,0},{2,3},{3,2},{4,5},{5,4},{6,7},{7,6}} | collective-permute-start | bytes 2211848 | tf_op jit(solution)/shard_map/ppermute | solution.py:361
  634.0 20.0 %collective-permute-start.10 = (bf16[480,4,128]{2,1,0:T(4,128)(2,1)S(1)}, bf16[480,4,128]{2,1,0:T(4,128)(2,1)}, u32[]{:S(2)}, u32[]{:S(2)}) collective-permute-start(bf16[480,4,128]{2,1,0:T(4,128)(2,1)S(1)} %collective-permute-done.9.refs_2_), channel_id=1, source_target_pairs={{0,2},{1,3},{2,0},{3,1},{4,6},{5,7},{6,4},{7,5}} | collective-permute-start | bytes 1474568 | tf_op jit(solution)/shard_map/ppermute | solution.py:361
  637.0 22.4 %collective-permute-start.60 = (bf16[960,4,128]{2,1,0:T(4,128)(2,1)S(1)}, bf16[960,4,128]{2,1,0:T(4,128)(2,1)S(1)}, u32[]{:S(2)}, u32[]{:S(2)}) collective-permute-start(bf16[960,4,128]{2,1,0:T(4,128)(2,1)S(1)} %collective-permute-done.18.refs_1_), channel_id=1, source_target_pairs={{0,1},{1,0},{2,3},{3,2},{4,5},{5,4},{6,7},{7,6}} | collective-permute-start | bytes 2949128 | tf_op jit(solution)/shard_map/ppermute | solution.py:361
  645.8 13.7 %collective-permute-start.7 = (bf16[720,4,128]{2,1,0:T(4,128)(2,1)S(1)}, bf16[720,4,128]{2,1,0:T(4,128)(2,1)}, u32[]{:S(2)}, u32[]{:S(2)}) collective-permute-start(bf16[720,4,128]{2,1,0:T(4,128)(2,1)S(1)} %collective-permute-done.6.refs_1_), channel_id=1, source_target_pairs={{0,4},{1,5},{2,6},{3,7},{4,0},{5,1},{6,2},{7,3}} | collective-permute-start | bytes 2211848 | tf_op jit(solution)/shard_map/ppermute | solution.py:361
  654.0 6.0 collective-permute-start.61
  658.0 3.0 collective-permute-start.57
  659.5 4.4 collective-permute-start.53
  660.0 5.3 collective-permute-start.48
  660.0 24.6 %collective-permute-start.22 = (bf16[960,4,128]{2,1,0:T(4,128)(2,1)S(1)}, bf16[960,4,128]{2,1,0:T(4,128)(2,1)S(1)}, u32[]{:S(2)}, u32[]{:S(2)}) collective-permute-start(bf16[960,4,128]{2,1,0:T(4,128)(2,1)S(1)} %collective-permute-done.21.refs_2_), channel_id=1, source_target_pairs={{0,2},{1,3},{2,0},{3,1},{4,6},{5,7},{6,4},{7,5}} | collective-permute-start | bytes 2949128 | tf_op jit(solution)/shard_map/ppermute | solution.py:361
  661.0 24.6 %collective-permute-start.19 = (bf16[960,4,128]{2,1,0:T(4,128)(2,1)S(1)}, bf16[960,4,128]{2,1,0:T(4,128)(2,1)S(1)}, u32[]{:S(2)}, u32[]{:S(2)}) collective-permute-start(bf16[960,4,128]{2,1,0:T(4,128)(2,1)S(1)} %collective-permute-done.18.refs_1_), channel_id=1, source_target_pairs={{0,4},{1,5},{2,6},{3,7},{4,0},{5,1},{6,2},{7,3}} | collective-permute-start | bytes 2949128 | tf_op jit(solution)/shard_map/ppermute | solution.py:361
  662.4 42.8 %collective-permute-start.16 = (bf16[960,4,128]{2,1,0:T(4,128)(2,1)S(1)}, bf16[960,4,128]{2,1,0:T(4,128)(2,1)S(1)}, u32[]{:S(2)}, u32[]{:S(2)}) collective-permute-start(bf16[960,4,128]{2,1,0:T(4,128)(2,1)S(1)} %collective-permute-done.15.refs_2_), channel_id=1, source_target_pairs={{0,2},{1,3},{2,0},{3,1},{4,6},{5,7},{6,4},{7,5}} | collective-permute-start | bytes 2949128 | tf_op jit(solution)/shard_map/ppermute | solution.py:361
  663.8 42.2 %collective-permute-start.13 = (bf16[960,4,128]{2,1,0:T(4,128)(2,1)S(1)}, bf16[960,4,128]{2,1,0:T(4,128)(2,1)}, u32[]{:S(2)}, u32[]{:S(2)}) collective-permute-start(bf16[960,4,128]{2,1,0:T(4,128)(2,1)S(1)} %collective-permute-done.12.refs_1_), channel_id=1, source_target_pairs={{0,4},{1,5},{2,6},{3,7},{4,0},{5,1},{6,2},{7,3}} | collective-permute-start | bytes 2949128 | tf_op jit(solution)/shard_map/ppermute | solution.py:361
  665.3 40.8 %collective-permute-start.49 = (bf16[960,4,128]{2,1,0:T(4,128)(2,1)S(1)}, bf16[960,4,128]{2,1,0:T(4,128)(2,1)S(1)}, u32[]{:S(2)}, u32[]{:S(2)}) collective-permute-start(bf16[960,4,128]{2,1,0:T(4,128)(2,1)S(1)} %collective-permute-done.15.refs_2_), channel_id=1, source_target_pairs={{0,1},{1,0},{2,3},{3,2},{4,5},{5,4},{6,7},{7,6}} | collective-permute-start | bytes 2949128 | tf_op jit(solution)/shard_map/ppermute | solution.py:361
  684.6 21.9 %collective-permute-start.23 = (bf16[960,4,128]{2,1,0:T(4,128)(2,1)S(1)}, bf16[960,4,128]{2,1,0:T(4,128)(2,1)S(1)}, u32[]{:S(2)}, u32[]{:S(2)}) collective-permute-start(bf16[960,4,128]{2,1,0:T(4,128)(2,1)S(1)} %collective-permute-done.22.refs_2_), channel_id=1, source_target_pairs={{0,1},{1,0},{2,3},{3,2},{4,5},{5,4},{6,7},{7,6}} | collective-permute-start | bytes 2949128 | tf_op jit(solution)/shard_map/ppermute | solution.py:361
  685.7 20.9 %collective-permute-start.20 = (bf16[960,4,128]{2,1,0:T(4,128)(2,1)S(1)}, bf16[960,4,128]{2,1,0:T(4,128)(2,1)S(1)}, u32[]{:S(2)}, u32[]{:S(2)}) collective-permute-start(bf16[960,4,128]{2,1,0:T(4,128)(2,1)S(1)} %collective-permute-done.19.refs_0_), channel_id=1, source_target_pairs={{0,1},{1,0},{2,3},{3,2},{4,5},{5,4},{6,7},{7,6}} | collective-permute-start | bytes 2949128 | tf_op jit(solution)/shard_map/ppermute | solution.py:361
  706.0 46.1 %collective-permute-start.14 = (bf16[960,4,128]{2,1,0:T(4,128)(2,1)}, bf16[960,4,128]{2,1,0:T(4,128)(2,1)}, u32[]{:S(2)}, u32[]{:S(2)}) collective-permute-start(bf16[960,4,128]{2,1,0:T(4,128)(2,1)} %collective-permute-done.13.refs_0_), channel_id=1, source_target_pairs={{0,1},{1,0},{2,3},{3,2},{4,5},{5,4},{6,7},{7,6}} | collective-permute-start | bytes 2949128 | tf_op jit(solution)/shard_map/ppermute | solution.py:361
  706.0 49.4 %collective-permute-start.8 = (bf16[720,4,128]{2,1,0:T(4,128)(2,1)}, bf16[720,4,128]{2,1,0:T(4,128)(2,1)}, u32[]{:S(2)}, u32[]{:S(2)}) collective-permute-start(bf16[720,4,128]{2,1,0:T(4,128)(2,1)} %collective-permute-done.7.refs_0_), channel_id=1, source_target_pairs={{0,1},{1,0},{2,3},{3,2},{4,5},{5,4},{6,7},{7,6}} | collective-permute-start | bytes 2211848 | tf_op jit(solution)/shard_map/ppermute | solution.py:361
  706.5 48.8 %collective-permute-start.11 = (bf16[480,4,128]{2,1,0:T(4,128)(2,1)}, bf16[480,4,128]{2,1,0:T(4,128)(2,1)}, u32[]{:S(2)}, u32[]{:S(2)}) collective-permute-start(bf16[480,4,128]{2,1,0:T(4,128)(2,1)} %collective-permute-done.10.refs_2_), channel_id=1, source_target_pairs={{0,1},{1,0},{2,3},{3,2},{4,5},{5,4},{6,7},{7,6}} | collective-permute-start | bytes 1474568 | tf_op jit(solution)/shard_map/ppermute | solution.py:361
  706.5 51.5 %collective-permute-start.5 = (bf16[240,4,128]{2,1,0:T(4,128)(2,1)}, bf16[240,4,128]{2,1,0:T(4,128)(2,1)}, u32[]{:S(2)}, u32[]{:S(2)}) collective-permute-start(bf16[240,4,128]{2,1,0:T(4,128)(2,1)} %collective-permute-done.4.refs_2_), channel_id=1, source_target_pairs={{0,1},{1,0},{2,3},{3,2},{4,5},{5,4},{6,7},{7,6}} | collective-permute-start | bytes 737288 | tf_op jit(solution)/shard_map/ppermute | solution.py:361
  707.8 50.2 %collective-permute-start.2 = (bf16[240,4,128]{2,1,0:T(4,128)(2,1)}, bf16[240,4,128]{2,1,0:T(4,128)(2,1)}, u32[]{:S(2)}, u32[]{:S(2)}) collective-permute-start(bf16[240,4,128]{2,1,0:T(4,128)(2,1)} %collective-permute-done.1.refs_0_), channel_id=1, source_target_pairs={{0,1},{1,0},{2,3},{3,2},{4,5},{5,4},{6,7},{7,6}} | collective-permute-start | bytes 737288 | tf_op jit(solution)/shard_map/ppermute | solution.py:361
  (56 other events, 768.8 us)

commit v2 on v1

--- a/solution.py
+++ b/solution.py
@@ -17,7 +17,7 @@
 
 MESH = pl.DeviceIdType.MESH
 LANES = 128
-CHUNK_ROWS = 240
+CHUNK_ROWS = 384
 HALF_ROWS = CHUNK_ROWS // 2
 SLOTS = 4
 VMEM_LIMIT = 20 << 20
@@ -305,7 +305,7 @@
     )(lr, norm, stay(g), stay(w), stay(m), v, mask, *before)
 
 
-def store_kernel(spots, *refs):
+def store_kernel(spots, direct, *refs):
     count = len(spots)
     pieces = refs[:count]
     params, buf, in_sem, out_sem = refs[-4:]
@@ -316,30 +316,36 @@
     loads, stores = [], []
     for k, (which, start, size, grains) in enumerate(spots):
         dst = params.at[pl.ds(blocks[which] * grains + start, size)]
-        loads.append(pltpu.make_async_copy(pieces[k].at[pl.ds(0, size)], buf.at[k, pl.ds(0, size)], in_sem.at[k]))
-        stores.append(pltpu.make_async_copy(buf.at[k, pl.ds(0, size)], dst, out_sem.at[k]))
+        src = pieces[k].at[pl.ds(0, size)]
+        if not direct:
+            loads.append(pltpu.make_async_copy(src, buf.at[k, pl.ds(0, size)], in_sem.at[k]))
+            src = buf.at[k, pl.ds(0, size)]
+        stores.append(pltpu.make_async_copy(src, dst, out_sem.at[k]))
     for cp in loads:
         cp.start()
-    for cp, out in zip(loads, stores):
-        cp.wait()
+    for k, out in enumerate(stores):
+        if not direct:
+            loads[k].wait()
         out.start()
     for out in stores:
         out.wait()
 
 
-def store(pieces, spots, before, num_dev, grains):
+def store(pieces, spots, before, num_dev, grains, direct):
     count = len(pieces)
+    if direct:
+        pieces = [stay(p) for p in pieces]
     hbm = pl.BlockSpec(memory_space=pltpu.HBM)
     room = max(p.shape[0] for p in pieces)
     moved = sum(p.size for p in pieces)
     return pl.pallas_call(
         functools.partial(store_kernel, [(which, start, min(p.shape[0], grains - start), grains)
-                                         for p, (which, start) in zip(pieces, spots)]),
+                                         for p, (which, start) in zip(pieces, spots)], direct),
         out_shape=jax.ShapeDtypeStruct((num_dev * grains, 4, LANES), jnp.bfloat16),
-        in_specs=[hbm] * (count + len(before)),
+        in_specs=[pl.BlockSpec(memory_space=pltpu.VMEM) if direct else hbm] * count + [hbm] * len(before),
         out_specs=hbm,
         input_output_aliases={count: 0} if before else {},
-        scratch_shapes=[pltpu.VMEM((count, room, 4, LANES), jnp.bfloat16),
+        scratch_shapes=[pltpu.VMEM((1, 2, 4, LANES) if direct else (count, room, 4, LANES), jnp.bfloat16),
                         pltpu.SemaphoreType.DMA((count,)), pltpu.SemaphoreType.DMA((count,))],
         compiler_params=pltpu.CompilerParams(vmem_limit_bytes=VMEM_LIMIT),
         cost_estimate=pl.CostEstimate(flops=40 * moved, bytes_accessed=4 * moved, transcendentals=0),
@@ -360,8 +366,8 @@
         def send(a, along):
             return lax.ppermute(a, "dp", hop[along])
 
-        def put(pieces, spots, whole):
-            return (store(pieces, spots, whole, num_dev, grains),)
+        def put(pieces, spots, whole, direct=False):
+            return (store(pieces, spots, whole, num_dev, grains, direct),)
 
         g, w, m, norm = reduce_scatter(grad_row, flat(master), flat(mom_first), rows, num_dev)
         state = ()
@@ -384,7 +390,7 @@
             for q in (p, p + 1):
                 pieces += [far[q], send(far[q], "core")]
                 spots += [(3, starts[q]), (7, starts[q])]
-            whole = put(pieces, spots, whole)
+            whole = put(pieces, spots, whole, p + 2 == len(PARTS))
         new_w, new_m, new_v = state
         params = whole[0].reshape(num_dev * shard_len)
         return (params, new_w.reshape(shard_len), new_m.reshape(shard_len), new_v.reshape(shard_len),

time: 761 us -> 759 us (level)
  no operation moved by 1% of the time
where the time goes in v2:
time: 759 us; the launch traced here: 758 us
  Pallas kernels  525 us (69%)
  waiting for transfers between devices  182 us (24%)
  starting transfers between devices  35.2 us (5%)
  local copies, waits for them, and re-layouts  14.2 us (2%)
    pallas_call x1, Pallas kernels, reduce_scatter(): pl.pallas_call(functools.partial(reduce_kernel, shard_rows), out_shape=(s...  425 us
    ppermute x70, waiting for transfers between devices, send(): return lax.ppermute(a, 'dp', hop[along])  182 us
    pallas_call x15, Pallas kernels, store(): pl.pallas_call(functools.partial(store_kernel, [(which, start, min(p.shap...  51.8 us
    pallas_call x10, Pallas kernels, adamw(): pl.pallas_call(adamw_kernel, grid=(steps,), out_shape=(state, state, stat...  47.9 us
    ppermute x70, starting transfers between devices, send(): return lax.ppermute(a, 'dp', hop[along])  35.2 us
  transfers between devices with their start and end apart: 70, of which 32 were waited for; matrix products, arithmetic and copies ran while one was open for 0% of the time, Pallas kernels for 12%

profile of v2, /device:TPU:0, one launch (start us, length us, event | category | flops | bytes accessed | tf_op | source)
XLA Modules:
  0.0 758.0 jit_solution(6842584680816834736)
XLA Ops:
  1.3 424.9 %shard_map.101 = (f32[24960,128]{1,0:T(8,128)S(1)}, f32[24960,128]{1,0:T(8,128)S(1)}, f32[24960,128]{1,0:T(8,128)S(1)}, f32[8,128]{1,0:T(8,128)}) custom-call(bf16[1,25530368]{1,0:T(2,128)(2,1)} %grad.1, f32[24932,128]{1,0:T(8,128)} %bitcast.32, f32[24932,128]{1,0:T(8,128)} %bitcast.33), custom_call_target="tpu_custom_call" | custom-call | tf_op jit(solution)/shard_map/pallas_call | solution.py:242
  426.2 3.0 shard_map.102
  429.2 1.4 collective-permute-start.24
  431.3 3.7 shard_map.103
  435.0 6.4 shard_map.104
  441.5 6.4 shard_map.105
  447.9 6.4 shard_map.106
  454.3 6.4 shard_map.107
  460.8 5.6 shard_map.108
  466.4 3.7 shard_map.109
  470.1 3.0 shard_map.110
  473.1 1.2 collective-permute-start
  475.1 3.1 shard_map.111
  478.3 1.4 collective-permute-start.30
  480.4 1.4 collective-permute-done.refs_1_
  481.7 1.3 collective-permute-start.3
  484.2 3.1 collective-permute-done.30.refs_1_
  487.4 2.0 collective-permute-done.3.refs_2_
  489.4 1.3 collective-permute-start.27
  492.0 1.3 collective-permute-start.9
  493.3 4.6 collective-permute-done.62.refs_1_
  497.9 5.6 collective-permute-done.27.refs_2_
  504.0 4.0 collective-permute-done.38.refs_1_
  508.7 3.0 collective-permute-done.9.refs_2_
  511.7 1.3 collective-permute-start.6
  515.2 1.3 collective-permute-start.42
  517.3 5.5 collective-permute-done.25.refs_0_
  523.5 12.5 %collective-permute-done.4.refs_2_ = bf16[240,4,128]{2,1,0:T(4,128)(2,1)} collective-permute-done((bf16[240,4,128]{2,1,0:T(4,128)(2,1)S(1)}, bf16[240,4,128]{2,1,0:T(4,128)(2,1)}, u32[]{:S(2)}, u32[]{:S(2)}) %collective-permute-start.4) | collective-permute-done | bytes 245792 | tf_op jit(solution)/shard_map/ppermute | solution.py:367
  536.0 1.2 collective-permute-start.18
  537.3 5.9 collective-permute-done.1.refs_0_
  547.2 1.3 collective-permute-start.54
  549.3 11.3 %collective-permute-done.18.refs_1_ = bf16[960,4,128]{2,1,0:T(4,128)(2,1)S(1)} collective-permute-done((bf16[960,4,128]{2,1,0:T(4,128)(2,1)S(1)}, bf16[960,4,128]{2,1,0:T(4,128)(2,1)S(1)}, u32[]{:S(2)}, u32[]{:S(2)}) %collective-permute-start.18) | collective-permute-done | bytes 983072 | tf_op jit(solution)/shard_map/ppermute | solution.py:367
  560.6 7.2 collective-permute-done.58.refs_2_
  568.6 1.3 collective-permute-start.50
  569.9 11.8 %collective-permute-done.54.refs_1_ = bf16[960,4,128]{2,1,0:T(4,128)(2,1)S(1)} collective-permute-done((bf16[960,4,128]{2,1,0:T(4,128)(2,1)S(1)}, bf16[960,4,128]{2,1,0:T(4,128)(2,1)S(1)}, u32[]{:S(2)}, u32[]{:S(2)}) %collective-permute-start.54) | collective-permute-done | bytes 983072 | tf_op jit(solution)/shard_map/ppermute | solution.py:367
  581.7 7.2 collective-permute-done.21.refs_2_
  589.7 1.3 collective-permute-start.15
  590.9 11.8 %collective-permute-done.12.refs_1_ = bf16[960,4,128]{2,1,0:T(4,128)(2,1)S(1)} collective-permute-done((bf16[960,4,128]{2,1,0:T(4,128)(2,1)S(1)}, bf16[960,4,128]{2,1,0:T(4,128)(2,1)S(1)}, u32[]{:S(2)}, u32[]{:S(2)}) %collective-permute-start.12) | collective-permute-done | bytes 983072 | tf_op jit(solution)/shard_map/ppermute | solution.py:367
  602.8 7.2 collective-permute-done.50.refs_2_
  611.3 11.2 %collective-permute-done.46.refs_1_ = bf16[960,4,128]{2,1,0:T(4,128)(2,1)S(1)} collective-permute-done((bf16[960,4,128]{2,1,0:T(4,128)(2,1)S(1)}, bf16[960,4,128]{2,1,0:T(4,128)(2,1)S(1)}, u32[]{:S(2)}, u32[]{:S(2)}) %collective-permute-start.46) | collective-permute-done | bytes 983072 | tf_op jit(solution)/shard_map/ppermute | solution.py:367
  622.5 6.9 collective-permute-done.15.refs_2_
  631.9 1.2 collective-permute-start.10
  634.9 8.5 %collective-permute-done.28.refs_2_ = bf16[480,4,128]{2,1,0:T(4,128)(2,1)S(1)} collective-permute-done((bf16[480,4,128]{2,1,0:T(4,128)(2,1)S(1)}, bf16[480,4,128]{2,1,0:T(4,128)(2,1)S(1)}, u32[]{:S(2)}, u32[]{:S(2)}) %collective-permute-start.28) | collective-permute-done | bytes 491552 | tf_op jit(solution)/shard_map/ppermute | solution.py:367
  645.1 6.5 collective-permute-done.10.refs_2_
  656.0 1.1 collective-permute-done.7.refs_0_
  658.7 1.0 collective-permute-start.19
  663.1 19.3 %collective-permute-done.22.refs_2_ = bf16[960,4,128]{2,1,0:T(4,128)(2,1)S(1)} collective-permute-done((bf16[960,4,128]{2,1,0:T(4,128)(2,1)S(1)}, bf16[960,4,128]{2,1,0:T(4,128)(2,1)S(1)}, u32[]{:S(2)}, u32[]{:S(2)}) %collective-permute-start.22) | collective-permute-done | bytes 983072 | tf_op jit(solution)/shard_map/ppermute | solution.py:367
  682.3 1.0 collective-permute-done.19.refs_0_
  683.3 19.6 %collective-permute-done.16.refs_2_ = bf16[960,4,128]{2,1,0:T(4,128)(2,1)S(1)} collective-permute-done((bf16[960,4,128]{2,1,0:T(4,128)(2,1)S(1)}, bf16[960,4,128]{2,1,0:T(4,128)(2,1)S(1)}, u32[]{:S(2)}, u32[]{:S(2)}) %collective-permute-start.16) | collective-permute-done | bytes 983072 | tf_op jit(solution)/shard_map/ppermute | solution.py:367
  705.6 2.4 shard_map.112.refs_6_
  708.1 3.6 shard_map.113.refs_6_
  711.7 4.5 shard_map.114.refs_6_
  716.2 4.5 shard_map.115.refs_6_
  720.7 4.5 shard_map.116.refs_6_
  725.3 4.5 shard_map.117.refs_6_
  730.0 4.1 shard_map.118.refs_6_
  734.1 3.6 shard_map.119.refs_6_
  737.8 3.1 shard_map.120.refs_6_
  741.0 3.0 shard_map.121.refs_4_
  744.1 2.5 shard_map.122.refs_4_
  746.6 3.2 shard_map.123.refs_4_
  749.8 3.2 shard_map.124.refs_4_
  753.0 2.6 shard_map.125.refs_4_
  755.7 2.3 shard_map.126
  (202 shorter events, 35.4 us)
Async XLA Ops:
  429.2 49.1 %collective-permute-start.24 = (bf16[240,4,128]{2,1,0:T(4,128)(2,1)}, bf16[240,4,128]{2,1,0:T(4,128)(2,1)}, u32[]{:S(2)}, u32[]{:S(2)}) collective-permute-start(bf16[240,4,128]{2,1,0:T(4,128)(2,1)} %get-tuple-element.89.refs_0_), channel_id=1, source_target_pairs={{0,2},{1,3},{2,0},{3,1},{4,6},{5,7},{6,4},{7,5}} | collective-permute-start | bytes 737288 | tf_op jit(solution)/shard_map/ppermute | solution.py:367
  430.6 47.7 %collective-permute-start.66 = (bf16[240,4,128]{2,1,0:T(4,128)(2,1)}, bf16[240,4,128]{2,1,0:T(4,128)(2,1)}, u32[]{:S(2)}, u32[]{:S(2)}) collective-permute-start(bf16[240,4,128]{2,1,0:T(4,128)(2,1)} %get-tuple-element.89.refs_0_), channel_id=1, source_target_pairs={{0,4},{1,5},{2,6},{3,7},{4,0},{5,1},{6,2},{7,3}} | collective-permute-start | bytes 737288 | tf_op jit(solution)/shard_map/ppermute | solution.py:367
  431.3 48.4 %collective-permute-start.67 = (bf16[240,4,128]{2,1,0:T(4,128)(2,1)}, bf16[240,4,128]{2,1,0:T(4,128)(2,1)}, u32[]{:S(2)}, u32[]{:S(2)}) collective-permute-start(bf16[240,4,128]{2,1,0:T(4,128)(2,1)} %get-tuple-element.89.refs_0_), channel_id=1, source_target_pairs={{0,1},{1,0},{2,3},{3,2},{4,5},{5,4},{6,7},{7,6}} | collective-permute-start | bytes 737288 | tf_op jit(solution)/shard_map/ppermute | solution.py:367
  473.1 8.6 %collective-permute-start = (bf16[240,4,128]{2,1,0:T(4,128)(2,1)}, bf16[240,4,128]{2,1,0:T(4,128)(2,1)S(1)}, u32[]{:S(2)}, u32[]{:S(2)}) collective-permute-start(bf16[240,4,128]{2,1,0:T(4,128)(2,1)} %get-tuple-element.78.refs_0_), channel_id=1, source_target_pairs={{0,2},{1,3},{2,0},{3,1},{4,6},{5,7},{6,4},{7,5}} | collective-permute-start | bytes 737288 | tf_op jit(solution)/shard_map/ppermute | solution.py:367
  474.3 8.7 %collective-permute-start.34 = (bf16[240,4,128]{2,1,0:T(4,128)(2,1)}, bf16[240,4,128]{2,1,0:T(4,128)(2,1)S(1)}, u32[]{:S(2)}, u32[]{:S(2)}) collective-permute-start(bf16[240,4,128]{2,1,0:T(4,128)(2,1)} %get-tuple-element.78.refs_0_), channel_id=1, source_target_pairs={{0,4},{1,5},{2,6},{3,7},{4,0},{5,1},{6,2},{7,3}} | collective-permute-start | bytes 737288 | tf_op jit(solution)/shard_map/ppermute | solution.py:367
  478.3 4.8 collective-permute-start.35
  478.3 9.1 %collective-permute-start.30 = (bf16[240,4,128]{2,1,0:T(4,128)(2,1)}, bf16[240,4,128]{2,1,0:T(4,128)(2,1)S(1)}, u32[]{:S(2)}, u32[]{:S(2)}) collective-permute-start(bf16[240,4,128]{2,1,0:T(4,128)(2,1)} %get-tuple-element.82.refs_0_), channel_id=1, source_target_pairs={{0,2},{1,3},{2,0},{3,1},{4,6},{5,7},{6,4},{7,5}} | collective-permute-start | bytes 737288 | tf_op jit(solution)/shard_map/ppermute | solution.py:367
  479.7 18.2 %collective-permute-start.62 = (bf16[480,4,128]{2,1,0:T(4,128)(2,1)S(1)}, bf16[480,4,128]{2,1,0:T(4,128)(2,1)S(1)}, u32[]{:S(2)}, u32[]{:S(2)}) collective-permute-start(bf16[480,4,128]{2,1,0:T(4,128)(2,1)S(1)} %copy-done.19), channel_id=1, source_target_pairs={{0,2},{1,3},{2,0},{3,1},{4,6},{5,7},{6,4},{7,5}} | collective-permute-start | bytes 1474568 | tf_op jit(solution)/shard_map/ppermute | solution.py:367
  481.7 7.6 %collective-permute-start.3 = (bf16[240,4,128]{2,1,0:T(4,128)(2,1)}, bf16[240,4,128]{2,1,0:T(4,128)(2,1)S(1)}, u32[]{:S(2)}, u32[]{:S(2)}) collective-permute-start(bf16[240,4,128]{2,1,0:T(4,128)(2,1)} %get-tuple-element.82.refs_0_), channel_id=1, source_target_pairs={{0,4},{1,5},{2,6},{3,7},{4,0},{5,1},{6,2},{7,3}} | collective-permute-start | bytes 737288 | tf_op jit(solution)/shard_map/ppermute | solution.py:367
  483.0 7.6 %collective-permute-start.31 = (bf16[240,4,128]{2,1,0:T(4,128)(2,1)}, bf16[240,4,128]{2,1,0:T(4,128)(2,1)S(1)}, u32[]{:S(2)}, u32[]{:S(2)}) collective-permute-start(bf16[240,4,128]{2,1,0:T(4,128)(2,1)} %get-tuple-element.82.refs_0_), channel_id=1, source_target_pairs={{0,1},{1,0},{2,3},{3,2},{4,5},{5,4},{6,7},{7,6}} | collective-permute-start | bytes 737288 | tf_op jit(solution)/shard_map/ppermute | solution.py:367
  483.7 7.6 %collective-permute-start.68 = (bf16[240,4,128]{2,1,0:T(4,128)(2,1)}, bf16[240,4,128]{2,1,0:T(4,128)(2,1)S(1)}, u32[]{:S(2)}, u32[]{:S(2)}) collective-permute-start(bf16[240,4,128]{2,1,0:T(4,128)(2,1)} %collective-permute-done.24.refs_1_), channel_id=1, source_target_pairs={{0,1},{1,0},{2,3},{3,2},{4,5},{5,4},{6,7},{7,6}} | collective-permute-start | bytes 737288 | tf_op jit(solution)/shard_map/ppermute | solution.py:367
  487.4 4.7 collective-permute-start.69
  489.4 14.1 %collective-permute-start.27 = (bf16[480,4,128]{2,1,0:T(4,128)(2,1)S(1)}, bf16[480,4,128]{2,1,0:T(4,128)(2,1)S(1)}, u32[]{:S(2)}, u32[]{:S(2)}) collective-permute-start(bf16[480,4,128]{2,1,0:T(4,128)(2,1)S(1)} %copy-done.19), channel_id=1, source_target_pairs={{0,4},{1,5},{2,6},{3,7},{4,0},{5,1},{6,2},{7,3}} | collective-permute-start | bytes 1474568 | tf_op jit(solution)/shard_map/ppermute | solution.py:367
  491.3 12.1 %collective-permute-start.63 = (bf16[480,4,128]{2,1,0:T(4,128)(2,1)S(1)}, bf16[480,4,128]{2,1,0:T(4,128)(2,1)S(1)}, u32[]{:S(2)}, u32[]{:S(2)}) collective-permute-start(bf16[480,4,128]{2,1,0:T(4,128)(2,1)S(1)} %copy-done.19), channel_id=1, source_target_pairs={{0,1},{1,0},{2,3},{3,2},{4,5},{5,4},{6,7},{7,6}} | collective-permute-start | bytes 1474568 | tf_op jit(solution)/shard_map/ppermute | solution.py:367
  491.4 16.6 %collective-permute-start.38 = (bf16[480,4,128]{2,1,0:T(4,128)(2,1)S(1)}, bf16[480,4,128]{2,1,0:T(4,128)(2,1)S(1)}, u32[]{:S(2)}, u32[]{:S(2)}) collective-permute-start(bf16[480,4,128]{2,1,0:T(4,128)(2,1)S(1)} %copy-done.20), channel_id=1, source_target_pairs={{0,2},{1,3},{2,0},{3,1},{4,6},{5,7},{6,4},{7,5}} | collective-permute-start | bytes 1474568 | tf_op jit(solution)/shard_map/ppermute | solution.py:367
  492.0 19.7 %collective-permute-start.9 = (bf16[480,4,128]{2,1,0:T(4,128)(2,1)S(1)}, bf16[480,4,128]{2,1,0:T(4,128)(2,1)S(1)}, u32[]{:S(2)}, u32[]{:S(2)}) collective-permute-start(bf16[480,4,128]{2,1,0:T(4,128)(2,1)S(1)} %copy-done.20), channel_id=1, source_target_pairs={{0,4},{1,5},{2,6},{3,7},{4,0},{5,1},{6,2},{7,3}} | collective-permute-start | bytes 1474568 | tf_op jit(solution)/shard_map/ppermute | solution.py:367
  497.9 13.8 %collective-permute-start.39 = (bf16[480,4,128]{2,1,0:T(4,128)(2,1)S(1)}, bf16[480,4,128]{2,1,0:T(4,128)(2,1)S(1)}, u32[]{:S(2)}, u32[]{:S(2)}) collective-permute-start(bf16[480,4,128]{2,1,0:T(4,128)(2,1)S(1)} %copy-done.20), channel_id=1, source_target_pairs={{0,1},{1,0},{2,3},{3,2},{4,5},{5,4},{6,7},{7,6}} | collective-permute-start | bytes 1474568 | tf_op jit(solution)/shard_map/ppermute | solution.py:367
  503.4 9.6 %collective-permute-start.36 = (bf16[240,4,128]{2,1,0:T(4,128)(2,1)S(1)}, bf16[240,4,128]{2,1,0:T(4,128)(2,1)S(1)}, u32[]{:S(2)}, u32[]{:S(2)}) collective-permute-start(bf16[240,4,128]{2,1,0:T(4,128)(2,1)S(1)} %collective-permute-done.refs_1_), channel_id=1, source_target_pairs={{0,1},{1,0},{2,3},{3,2},{4,5},{5,4},{6,7},{7,6}} | collective-permute-start | bytes 737288 | tf_op jit(solution)/shard_map/ppermute | solution.py:367
  503.5 11.0 %collective-permute-start.37 = (bf16[240,4,128]{2,1,0:T(4,128)(2,1)S(1)}, bf16[240,4,128]{2,1,0:T(4,128)(2,1)S(1)}, u32[]{:S(2)}, u32[]{:S(2)}) collective-permute-start(bf16[240,4,128]{2,1,0:T(4,128)(2,1)S(1)} %collective-permute-done.34.refs_2_), channel_id=1, source_target_pairs={{0,1},{1,0},{2,3},{3,2},{4,5},{5,4},{6,7},{7,6}} | collective-permute-start | bytes 737288 | tf_op jit(solution)/shard_map/ppermute | solution.py:367
  508.0 8.5 %collective-permute-start.32 = (bf16[240,4,128]{2,1,0:T(4,128)(2,1)S(1)}, bf16[240,4,128]{2,1,0:T(4,128)(2,1)S(1)}, u32[]{:S(2)}, u32[]{:S(2)}) collective-permute-start(bf16[240,4,128]{2,1,0:T(4,128)(2,1)S(1)} %collective-permute-done.30.refs_1_), channel_id=1, source_target_pairs={{0,1},{1,0},{2,3},{3,2},{4,5},{5,4},{6,7},{7,6}} | collective-permute-start | bytes 737288 | tf_op jit(solution)/shard_map/ppermute | solution.py:367
  511.7 4.8 collective-permute-start.33
  511.7 32.2 %collective-permute-start.6 = (bf16[720,4,128]{2,1,0:T(4,128)(2,1)S(1)}, bf16[720,4,128]{2,1,0:T(4,128)(2,1)S(1)}, u32[]{:S(2)}, u32[]{:S(2)}) collective-permute-start(bf16[720,4,128]{2,1,0:T(4,128)(2,1)S(1)} %copy-done.8), channel_id=1, source_target_pairs={{0,2},{1,3},{2,0},{3,1},{4,6},{5,7},{6,4},{7,5}} | collective-permute-start | bytes 2211848 | tf_op jit(solution)/shard_map/ppermute | solution.py:367
  513.7 9.0 %collective-permute-start.25 = (bf16[240,4,128]{2,1,0:T(4,128)(2,1)}, bf16[240,4,128]{2,1,0:T(4,128)(2,1)S(1)}, u32[]{:S(2)}, u32[]{:S(2)}) collective-permute-start(bf16[240,4,128]{2,1,0:T(4,128)(2,1)} %collective-permute-done.24.refs_1_), channel_id=1, source_target_pairs={{0,4},{1,5},{2,6},{3,7},{4,0},{5,1},{6,2},{7,3}} | collective-permute-start | bytes 737288 | tf_op jit(solution)/shard_map/ppermute | solution.py:367
  515.2 28.7 %collective-permute-start.42 = (bf16[720,4,128]{2,1,0:T(4,128)(2,1)S(1)}, bf16[720,4,128]{2,1,0:T(4,128)(2,1)S(1)}, u32[]{:S(2)}, u32[]{:S(2)}) collective-permute-start(bf16[720,4,128]{2,1,0:T(4,128)(2,1)S(1)} %copy-done.8), channel_id=1, source_target_pairs={{0,4},{1,5},{2,6},{3,7},{4,0},{5,1},{6,2},{7,3}} | collective-permute-start | bytes 2211848 | tf_op jit(solution)/shard_map/ppermute | solution.py:367
  516.5 28.7 %collective-permute-start.43 = (bf16[720,4,128]{2,1,0:T(4,128)(2,1)S(1)}, bf16[720,4,128]{2,1,0:T(4,128)(2,1)S(1)}, u32[]{:S(2)}, u32[]{:S(2)}) collective-permute-start(bf16[720,4,128]{2,1,0:T(4,128)(2,1)S(1)} %copy-done.8), channel_id=1, source_target_pairs={{0,1},{1,0},{2,3},{3,2},{4,5},{5,4},{6,7},{7,6}} | collective-permute-start | bytes 2211848 | tf_op jit(solution)/shard_map/ppermute | solution.py:367
  516.5 19.5 %collective-permute-start.4 = (bf16[240,4,128]{2,1,0:T(4,128)(2,1)S(1)}, bf16[240,4,128]{2,1,0:T(4,128)(2,1)}, u32[]{:S(2)}, u32[]{:S(2)}) collective-permute-start(bf16[240,4,128]{2,1,0:T(4,128)(2,1)S(1)} %collective-permute-done.3.refs_2_), channel_id=1, source_target_pairs={{0,2},{1,3},{2,0},{3,1},{4,6},{5,7},{6,4},{7,5}} | collective-permute-start | bytes 737288 | tf_op jit(solution)/shard_map/ppermute | solution.py:367
  522.8 20.4 %collective-permute-start.1 = (bf16[240,4,128]{2,1,0:T(4,128)(2,1)S(1)}, bf16[240,4,128]{2,1,0:T(4,128)(2,1)}, u32[]{:S(2)}, u32[]{:S(2)}) collective-permute-start(bf16[240,4,128]{2,1,0:T(4,128)(2,1)S(1)} %collective-permute-done.refs_1_), channel_id=1, source_target_pairs={{0,4},{1,5},{2,6},{3,7},{4,0},{5,1},{6,2},{7,3}} | collective-permute-start | bytes 737288 | tf_op jit(solution)/shard_map/ppermute | solution.py:367
  536.0 24.6 %collective-permute-start.18 = (bf16[960,4,128]{2,1,0:T(4,128)(2,1)S(1)}, bf16[960,4,128]{2,1,0:T(4,128)(2,1)S(1)}, u32[]{:S(2)}, u32[]{:S(2)}) collective-permute-start(bf16[960,4,128]{2,1,0:T(4,128)(2,1)S(1)} %copy-done), channel_id=1, source_target_pairs={{0,2},{1,3},{2,0},{3,1},{4,6},{5,7},{6,4},{7,5}} | collective-permute-start | bytes 2949128 | tf_op jit(solution)/shard_map/ppermute | solution.py:367
  543.2 24.6 %collective-permute-start.58 = (bf16[960,4,128]{2,1,0:T(4,128)(2,1)S(1)}, bf16[960,4,128]{2,1,0:T(4,128)(2,1)S(1)}, u32[]{:S(2)}, u32[]{:S(2)}) collective-permute-start(bf16[960,4,128]{2,1,0:T(4,128)(2,1)S(1)} %copy-done), channel_id=1, source_target_pairs={{0,4},{1,5},{2,6},{3,7},{4,0},{5,1},{6,2},{7,3}} | collective-permute-start | bytes 2949128 | tf_op jit(solution)/shard_map/ppermute | solution.py:367
  543.9 3.3 collective-permute-start.64
  546.8 21.7 %collective-permute-start.59 = (bf16[960,4,128]{2,1,0:T(4,128)(2,1)S(1)}, bf16[960,4,128]{2,1,0:T(4,128)(2,1)S(1)}, u32[]{:S(2)}, u32[]{:S(2)}) collective-permute-start(bf16[960,4,128]{2,1,0:T(4,128)(2,1)S(1)} %copy-done), channel_id=1, source_target_pairs={{0,1},{1,0},{2,3},{3,2},{4,5},{5,4},{6,7},{7,6}} | collective-permute-start | bytes 2949128 | tf_op jit(solution)/shard_map/ppermute | solution.py:367
  547.2 34.5 %collective-permute-start.54 = (bf16[960,4,128]{2,1,0:T(4,128)(2,1)S(1)}, bf16[960,4,128]{2,1,0:T(4,128)(2,1)S(1)}, u32[]{:S(2)}, u32[]{:S(2)}) collective-permute-start(bf16[960,4,128]{2,1,0:T(4,128)(2,1)S(1)} %copy-done.1), channel_id=1, source_target_pairs={{0,2},{1,3},{2,0},{3,1},{4,6},{5,7},{6,4},{7,5}} | collective-permute-start | bytes 2949128 | tf_op jit(solution)/shard_map/ppermute | solution.py:367
  548.5 40.3 %collective-permute-start.21 = (bf16[960,4,128]{2,1,0:T(4,128)(2,1)S(1)}, bf16[960,4,128]{2,1,0:T(4,128)(2,1)S(1)}, u32[]{:S(2)}, u32[]{:S(2)}) collective-permute-start(bf16[960,4,128]{2,1,0:T(4,128)(2,1)S(1)} %copy-done.1), channel_id=1, source_target_pairs={{0,4},{1,5},{2,6},{3,7},{4,0},{5,1},{6,2},{7,3}} | collective-permute-start | bytes 2949128 | tf_op jit(solution)/shard_map/ppermute | solution.py:367
  560.6 29.0 %collective-permute-start.55 = (bf16[960,4,128]{2,1,0:T(4,128)(2,1)S(1)}, bf16[960,4,128]{2,1,0:T(4,128)(2,1)S(1)}, u32[]{:S(2)}, u32[]{:S(2)}) collective-permute-start(bf16[960,4,128]{2,1,0:T(4,128)(2,1)S(1)} %copy-done.1), channel_id=1, source_target_pairs={{0,1},{1,0},{2,3},{3,2},{4,5},{5,4},{6,7},{7,6}} | collective-permute-start | bytes 2949128 | tf_op jit(solution)/shard_map/ppermute | solution.py:367
  567.8 35.0 %collective-permute-start.12 = (bf16[960,4,128]{2,1,0:T(4,128)(2,1)S(1)}, bf16[960,4,128]{2,1,0:T(4,128)(2,1)S(1)}, u32[]{:S(2)}, u32[]{:S(2)}) collective-permute-start(bf16[960,4,128]{2,1,0:T(4,128)(2,1)S(1)} %copy-done.2), channel_id=1, source_target_pairs={{0,2},{1,3},{2,0},{3,1},{4,6},{5,7},{6,4},{7,5}} | collective-permute-start | bytes 2949128 | tf_op jit(solution)/shard_map/ppermute | solution.py:367
  568.6 41.3 %collective-permute-start.50 = (bf16[960,4,128]{2,1,0:T(4,128)(2,1)S(1)}, bf16[960,4,128]{2,1,0:T(4,128)(2,1)S(1)}, u32[]{:S(2)}, u32[]{:S(2)}) collective-permute-start(bf16[960,4,128]{2,1,0:T(4,128)(2,1)S(1)} %copy-done.2), channel_id=1, source_target_pairs={{0,4},{1,5},{2,6},{3,7},{4,0},{5,1},{6,2},{7,3}} | collective-permute-start | bytes 2949128 | tf_op jit(solution)/shard_map/ppermute | solution.py:367
  581.7 29.0 %collective-permute-start.51 = (bf16[960,4,128]{2,1,0:T(4,128)(2,1)S(1)}, bf16[960,4,128]{2,1,0:T(4,128)(2,1)S(1)}, u32[]{:S(2)}, u32[]{:S(2)}) collective-permute-start(bf16[960,4,128]{2,1,0:T(4,128)(2,1)S(1)} %copy-done.2), channel_id=1, source_target_pairs={{0,1},{1,0},{2,3},{3,2},{4,5},{5,4},{6,7},{7,6}} | collective-permute-start | bytes 2949128 | tf_op jit(solution)/shard_map/ppermute | solution.py:367
  588.9 33.6 %collective-permute-start.46 = (bf16[960,4,128]{2,1,0:T(4,128)(2,1)S(1)}, bf16[960,4,128]{2,1,0:T(4,128)(2,1)S(1)}, u32[]{:S(2)}, u32[]{:S(2)}) collective-permute-start(bf16[960,4,128]{2,1,0:T(4,128)(2,1)S(1)} %copy-done.3), channel_id=1, source_target_pairs={{0,2},{1,3},{2,0},{3,1},{4,6},{5,7},{6,4},{7,5}} | collective-permute-start | bytes 2949128 | tf_op jit(solution)/shard_map/ppermute | solution.py:367
  589.7 39.7 %collective-permute-start.15 = (bf16[960,4,128]{2,1,0:T(4,128)(2,1)S(1)}, bf16[960,4,128]{2,1,0:T(4,128)(2,1)S(1)}, u32[]{:S(2)}, u32[]{:S(2)}) collective-permute-start(bf16[960,4,128]{2,1,0:T(4,128)(2,1)S(1)} %copy-done.3), channel_id=1, source_target_pairs={{0,4},{1,5},{2,6},{3,7},{4,0},{5,1},{6,2},{7,3}} | collective-permute-start | bytes 2949128 | tf_op jit(solution)/shard_map/ppermute | solution.py:367
  602.8 27.4 %collective-permute-start.47 = (bf16[960,4,128]{2,1,0:T(4,128)(2,1)S(1)}, bf16[960,4,128]{2,1,0:T(4,128)(2,1)S(1)}, u32[]{:S(2)}, u32[]{:S(2)}) collective-permute-start(bf16[960,4,128]{2,1,0:T(4,128)(2,1)S(1)} %copy-done.3), channel_id=1, source_target_pairs={{0,1},{1,0},{2,3},{3,2},{4,5},{5,4},{6,7},{7,6}} | collective-permute-start | bytes 2949128 | tf_op jit(solution)/shard_map/ppermute | solution.py:367
  609.9 21.2 %collective-permute-start.40 = (bf16[480,4,128]{2,1,0:T(4,128)(2,1)S(1)}, bf16[480,4,128]{2,1,0:T(4,128)(2,1)S(1)}, u32[]{:S(2)}, u32[]{:S(2)}) collective-permute-start(bf16[480,4,128]{2,1,0:T(4,128)(2,1)S(1)} %collective-permute-done.38.refs_1_), channel_id=1, source_target_pairs={{0,1},{1,0},{2,3},{3,2},{4,5},{5,4},{6,7},{7,6}} | collective-permute-start | bytes 1474568 | tf_op jit(solution)/shard_map/ppermute | solution.py:367
  610.8 23.2 %collective-permute-start.41 = (bf16[480,4,128]{2,1,0:T(4,128)(2,1)S(1)}, bf16[480,4,128]{2,1,0:T(4,128)(2,1)S(1)}, u32[]{:S(2)}, u32[]{:S(2)}) collective-permute-start(bf16[480,4,128]{2,1,0:T(4,128)(2,1)S(1)} %collective-permute-done.9.refs_2_), channel_id=1, source_target_pairs={{0,1},{1,0},{2,3},{3,2},{4,5},{5,4},{6,7},{7,6}} | collective-permute-start | bytes 1474568 | tf_op jit(solution)/shard_map/ppermute | solution.py:367
  622.5 29.1 %collective-permute-start.44 = (bf16[720,4,128]{2,1,0:T(4,128)(2,1)S(1)}, bf16[720,4,128]{2,1,0:T(4,128)(2,1)S(1)}, u32[]{:S(2)}, u32[]{:S(2)}) collective-permute-start(bf16[720,4,128]{2,1,0:T(4,128)(2,1)S(1)} %collective-permute-done.6.refs_1_), channel_id=1, source_target_pairs={{0,1},{1,0},{2,3},{3,2},{4,5},{5,4},{6,7},{7,6}} | collective-permute-start | bytes 2211848 | tf_op jit(solution)/shard_map/ppermute | solution.py:367
  629.4 14.1 %collective-permute-start.28 = (bf16[480,4,128]{2,1,0:T(4,128)(2,1)S(1)}, bf16[480,4,128]{2,1,0:T(4,128)(2,1)S(1)}, u32[]{:S(2)}, u32[]{:S(2)}) collective-permute-start(bf16[480,4,128]{2,1,0:T(4,128)(2,1)S(1)} %collective-permute-done.27.refs_2_), channel_id=1, source_target_pairs={{0,2},{1,3},{2,0},{3,1},{4,6},{5,7},{6,4},{7,5}} | collective-permute-start | bytes 1474568 | tf_op jit(solution)/shard_map/ppermute | solution.py:367
  630.2 23.7 %collective-permute-start.45 = (bf16[720,4,128]{2,1,0:T(4,128)(2,1)S(1)}, bf16[720,4,128]{2,1,0:T(4,128)(2,1)S(1)}, u32[]{:S(2)}, u32[]{:S(2)}) collective-permute-start(bf16[720,4,128]{2,1,0:T(4,128)(2,1)S(1)} %collective-permute-done.42.refs_2_), channel_id=1, source_target_pairs={{0,1},{1,0},{2,3},{3,2},{4,5},{5,4},{6,7},{7,6}} | collective-permute-start | bytes 2211848 | tf_op jit(solution)/shard_map/ppermute | solution.py:367
  631.9 19.8 %collective-permute-start.10 = (bf16[480,4,128]{2,1,0:T(4,128)(2,1)S(1)}, bf16[480,4,128]{2,1,0:T(4,128)(2,1)}, u32[]{:S(2)}, u32[]{:S(2)}) collective-permute-start(bf16[480,4,128]{2,1,0:T(4,128)(2,1)S(1)} %collective-permute-done.9.refs_2_), channel_id=1, source_target_pairs={{0,2},{1,3},{2,0},{3,1},{4,6},{5,7},{6,4},{7,5}} | collective-permute-start | bytes 1474568 | tf_op jit(solution)/shard_map/ppermute | solution.py:367
  634.7 22.4 %collective-permute-start.60 = (bf16[960,4,128]{2,1,0:T(4,128)(2,1)S(1)}, bf16[960,4,128]{2,1,0:T(4,128)(2,1)S(1)}, u32[]{:S(2)}, u32[]{:S(2)}) collective-permute-start(bf16[960,4,128]{2,1,0:T(4,128)(2,1)S(1)} %collective-permute-done.18.refs_1_), channel_id=1, source_target_pairs={{0,1},{1,0},{2,3},{3,2},{4,5},{5,4},{6,7},{7,6}} | collective-permute-start | bytes 2949128 | tf_op jit(solution)/shard_map/ppermute | solution.py:367
  643.5 13.7 %collective-permute-start.7 = (bf16[720,4,128]{2,1,0:T(4,128)(2,1)S(1)}, bf16[720,4,128]{2,1,0:T(4,128)(2,1)}, u32[]{:S(2)}, u32[]{:S(2)}) collective-permute-start(bf16[720,4,128]{2,1,0:T(4,128)(2,1)S(1)} %collective-permute-done.6.refs_1_), channel_id=1, source_target_pairs={{0,4},{1,5},{2,6},{3,7},{4,0},{5,1},{6,2},{7,3}} | collective-permute-start | bytes 2211848 | tf_op jit(solution)/shard_map/ppermute | solution.py:367
  651.6 6.0 collective-permute-start.61
  655.7 3.0 collective-permute-start.57
  657.1 4.4 collective-permute-start.53
  657.6 5.3 collective-permute-start.48
  657.7 24.6 %collective-permute-start.22 = (bf16[960,4,128]{2,1,0:T(4,128)(2,1)S(1)}, bf16[960,4,128]{2,1,0:T(4,128)(2,1)S(1)}, u32[]{:S(2)}, u32[]{:S(2)}) collective-permute-start(bf16[960,4,128]{2,1,0:T(4,128)(2,1)S(1)} %collective-permute-done.21.refs_2_), channel_id=1, source_target_pairs={{0,2},{1,3},{2,0},{3,1},{4,6},{5,7},{6,4},{7,5}} | collective-permute-start | bytes 2949128 | tf_op jit(solution)/shard_map/ppermute | solution.py:367
  658.7 24.6 %collective-permute-start.19 = (bf16[960,4,128]{2,1,0:T(4,128)(2,1)S(1)}, bf16[960,4,128]{2,1,0:T(4,128)(2,1)S(1)}, u32[]{:S(2)}, u32[]{:S(2)}) collective-permute-start(bf16[960,4,128]{2,1,0:T(4,128)(2,1)S(1)} %collective-permute-done.18.refs_1_), channel_id=1, source_target_pairs={{0,4},{1,5},{2,6},{3,7},{4,0},{5,1},{6,2},{7,3}} | collective-permute-start | bytes 2949128 | tf_op jit(solution)/shard_map/ppermute | solution.py:367
  660.1 42.8 %collective-permute-start.16 = (bf16[960,4,128]{2,1,0:T(4,128)(2,1)S(1)}, bf16[960,4,128]{2,1,0:T(4,128)(2,1)S(1)}, u32[]{:S(2)}, u32[]{:S(2)}) collective-permute-start(bf16[960,4,128]{2,1,0:T(4,128)(2,1)S(1)} %collective-permute-done.15.refs_2_), channel_id=1, source_target_pairs={{0,2},{1,3},{2,0},{3,1},{4,6},{5,7},{6,4},{7,5}} | collective-permute-start | bytes 2949128 | tf_op jit(solution)/shard_map/ppermute | solution.py:367
  661.5 42.2 %collective-permute-start.13 = (bf16[960,4,128]{2,1,0:T(4,128)(2,1)S(1)}, bf16[960,4,128]{2,1,0:T(4,128)(2,1)}, u32[]{:S(2)}, u32[]{:S(2)}) collective-permute-start(bf16[960,4,128]{2,1,0:T(4,128)(2,1)S(1)} %collective-permute-done.12.refs_1_), channel_id=1, source_target_pairs={{0,4},{1,5},{2,6},{3,7},{4,0},{5,1},{6,2},{7,3}} | collective-permute-start | bytes 2949128 | tf_op jit(solution)/shard_map/ppermute | solution.py:367
  662.9 40.8 %collective-permute-start.49 = (bf16[960,4,128]{2,1,0:T(4,128)(2,1)S(1)}, bf16[960,4,128]{2,1,0:T(4,128)(2,1)S(1)}, u32[]{:S(2)}, u32[]{:S(2)}) collective-permute-start(bf16[960,4,128]{2,1,0:T(4,128)(2,1)S(1)} %collective-permute-done.15.refs_2_), channel_id=1, source_target_pairs={{0,1},{1,0},{2,3},{3,2},{4,5},{5,4},{6,7},{7,6}} | collective-permute-start | bytes 2949128 | tf_op jit(solution)/shard_map/ppermute | solution.py:367
  682.3 21.9 %collective-permute-start.23 = (bf16[960,4,128]{2,1,0:T(4,128)(2,1)S(1)}, bf16[960,4,128]{2,1,0:T(4,128)(2,1)S(1)}, u32[]{:S(2)}, u32[]{:S(2)}) collective-permute-start(bf16[960,4,128]{2,1,0:T(4,128)(2,1)S(1)} %collective-permute-done.22.refs_2_), channel_id=1, source_target_pairs={{0,1},{1,0},{2,3},{3,2},{4,5},{5,4},{6,7},{7,6}} | collective-permute-start | bytes 2949128 | tf_op jit(solution)/shard_map/ppermute | solution.py:367
  683.3 20.9 %collective-permute-start.20 = (bf16[960,4,128]{2,1,0:T(4,128)(2,1)S(1)}, bf16[960,4,128]{2,1,0:T(4,128)(2,1)S(1)}, u32[]{:S(2)}, u32[]{:S(2)}) collective-permute-start(bf16[960,4,128]{2,1,0:T(4,128)(2,1)S(1)} %collective-permute-done.19.refs_0_), channel_id=1, source_target_pairs={{0,1},{1,0},{2,3},{3,2},{4,5},{5,4},{6,7},{7,6}} | collective-permute-start | bytes 2949128 | tf_op jit(solution)/shard_map/ppermute | solution.py:367
  703.7 46.1 %collective-permute-start.14 = (bf16[960,4,128]{2,1,0:T(4,128)(2,1)}, bf16[960,4,128]{2,1,0:T(4,128)(2,1)}, u32[]{:S(2)}, u32[]{:S(2)}) collective-permute-start(bf16[960,4,128]{2,1,0:T(4,128)(2,1)} %collective-permute-done.13.refs_0_), channel_id=1, source_target_pairs={{0,1},{1,0},{2,3},{3,2},{4,5},{5,4},{6,7},{7,6}} | collective-permute-start | bytes 2949128 | tf_op jit(solution)/shard_map/ppermute | solution.py:367
  703.7 49.4 %collective-permute-start.8 = (bf16[720,4,128]{2,1,0:T(4,128)(2,1)}, bf16[720,4,128]{2,1,0:T(4,128)(2,1)}, u32[]{:S(2)}, u32[]{:S(2)}) collective-permute-start(bf16[720,4,128]{2,1,0:T(4,128)(2,1)} %collective-permute-done.7.refs_0_), channel_id=1, source_target_pairs={{0,1},{1,0},{2,3},{3,2},{4,5},{5,4},{6,7},{7,6}} | collective-permute-start | bytes 2211848 | tf_op jit(solution)/shard_map/ppermute | solution.py:367
  704.2 48.8 %collective-permute-start.11 = (bf16[480,4,128]{2,1,0:T(4,128)(2,1)}, bf16[480,4,128]{2,1,0:T(4,128)(2,1)}, u32[]{:S(2)}, u32[]{:S(2)}) collective-permute-start(bf16[480,4,128]{2,1,0:T(4,128)(2,1)} %collective-permute-done.10.refs_2_), channel_id=1, source_target_pairs={{0,1},{1,0},{2,3},{3,2},{4,5},{5,4},{6,7},{7,6}} | collective-permute-start | bytes 1474568 | tf_op jit(solution)/shard_map/ppermute | solution.py:367
  704.2 51.5 %collective-permute-start.5 = (bf16[240,4,128]{2,1,0:T(4,128)(2,1)}, bf16[240,4,128]{2,1,0:T(4,128)(2,1)}, u32[]{:S(2)}, u32[]{:S(2)}) collective-permute-start(bf16[240,4,128]{2,1,0:T(4,128)(2,1)} %collective-permute-done.4.refs_2_), channel_id=1, source_target_pairs={{0,1},{1,0},{2,3},{3,2},{4,5},{5,4},{6,7},{7,6}} | collective-permute-start | bytes 737288 | tf_op jit(solution)/shard_map/ppermute | solution.py:367
  705.5 50.2 %collective-permute-start.2 = (bf16[240,4,128]{2,1,0:T(4,128)(2,1)}, bf16[240,4,128]{2,1,0:T(4,128)(2,1)}, u32[]{:S(2)}, u32[]{:S(2)}) collective-permute-start(bf16[240,4,128]{2,1,0:T(4,128)(2,1)} %collective-permute-done.1.refs_0_), channel_id=1, source_target_pairs={{0,1},{1,0},{2,3},{3,2},{4,5},{5,4},{6,7},{7,6}} | collective-permute-start | bytes 737288 | tf_op jit(solution)/shard_map/ppermute | solution.py:367
  (56 other events, 768.7 us)

commit v3 on v2

--- a/solution.py
+++ b/solution.py
@@ -22,7 +22,7 @@
 SLOTS = 4
 VMEM_LIMIT = 20 << 20
 ADAM_ROWS = 960
-PARTS = (1, 2, 4, 4, 4, 4, 3, 2, 1, 1)
+PARTS = (2, 3, 4, 4, 4, 4, 2, 1, 1, 1)
 TILE_ROWS = 120
 
 
@@ -52,11 +52,25 @@
         device_id=(device,), device_id_type=MESH)
 
 
-def reduce_kernel(shard_rows, grad, w, m, g_out, w_out, m_out, norm_out,
-                  own, other, x_send, y_send, x_keep, y_keep, mine, x_recv, y_recv,
-                  x_fin, y_fin, x_last, y_last, acc, norm_recv,
-                  own_sem, part_ssem, part_rsem, x_ssem, x_rsem, y_ssem, y_rsem,
-                  xf_ssem, xf_rsem, yf_ssem, yf_rsem, n_ssem, n_rsem, w_sem, m_sem):
+def adamw_tile(g, w, m, v, mask, coef, rate):
+    h = g * coef
+    first = BETA_FIRST * m + (1.0 - BETA_FIRST) * h
+    second = BETA_SECOND * v + (1.0 - BETA_SECOND) * h * h
+    step_dir = (first * (1.0 / (1.0 - BETA_FIRST ** ADAM_STEP))) / (
+        jnp.sqrt(second * (1.0 / (1.0 - BETA_SECOND ** ADAM_STEP))) + ADAM_EPS)
+    new = w - rate * (step_dir + WEIGHT_DECAY * mask.astype(jnp.float32) * w)
+    return new, first, second
+
+
+def pack_tile(packed, t, new):
+    grains = TILE_ROWS // 4
+    packed[pl.ds(pl.multiple_of(t * grains, 2), grains)] = new.reshape(grains, 4, LANES).astype(packed.dtype)
+
+
+def reduce_kernel(shard_rows, lr, grad, w, m, v, mask, g_out, w_out, m_out, packed, norm_out,
+                  own, other, x_send, y_send, x_keep, y_keep, mine, x_recv, y_recv, acc, norm_recv,
+                  own_sem, part_ssem, part_rsem, x_ssem, x_rsem, y_ssem, y_rsem, n_ssem, n_rsem,
+                  v_part, mask_part, fetch_sem):
     me, part, along_x, along_y = places()
     diag = along_x + along_y - me
     shift = part - me
@@ -64,13 +78,13 @@
     shard_len = shard_rows * LANES
     full = CHUNK_ROWS * LANES
     chunks = -(-shard_rows // CHUNK_ROWS)
-    tail_rows = shard_rows - (chunks - 1) * CHUNK_ROWS
-    tail = tail_rows * LANES
-
+    tail = (shard_rows - (chunks - 1) * CHUNK_ROWS) * LANES
     num_dev = grad.shape[1] // shard_len
     others = [(me + k) % num_dev for k in range(1, num_dev)]
-    fetches = (pltpu.make_async_copy(w, w_out.at[pl.ds(0, shard_rows)], w_sem),
-               pltpu.make_async_copy(m, m_out.at[pl.ds(0, shard_rows)], m_sem))
+    ahead = v_part.shape[0]
+    fetches = [pltpu.make_async_copy(src, dst, fetch_sem.at[k]) for k, (src, dst) in enumerate((
+        (w, w_out.at[pl.ds(0, shard_rows)]), (m, m_out.at[pl.ds(0, shard_rows)]),
+        (v.at[pl.ds(0, ahead)], v_part), (mask.at[pl.ds(0, ahead)], mask_part)))]
 
     acc[...] = jnp.zeros_like(acc)
 
@@ -93,16 +107,6 @@
                 part_ssem.at[slot, b], part_rsem.at[slot, b], part))
         return out
 
-    def first_hops(j):
-        slot = j % SLOTS
-        return (remote(x_send.at[slot], x_recv.at[slot], x_ssem.at[slot], x_rsem.at[slot], along_x),
-                remote(y_send.at[slot], y_recv.at[slot], y_ssem.at[slot], y_rsem.at[slot], along_y))
-
-    def last_hops(j):
-        slot = j % SLOTS
-        return (remote(x_fin.at[slot], x_last.at[slot], xf_ssem.at[slot], xf_rsem.at[slot], along_x),
-                remote(y_fin.at[slot], y_last.at[slot], yf_ssem.at[slot], yf_rsem.at[slot], along_y))
-
     def for_size(i, do):
         @pl.when(i < chunks - 1)
         def _():
@@ -111,6 +115,24 @@
         @pl.when(i == chunks - 1)
         def _():
             do(tail)
+
+    def hops(q, planes):
+        slot = q % SLOTS
+        return (remote(x_send.at[slot, planes], x_recv.at[slot, planes], x_ssem.at[slot], x_rsem.at[slot], along_x),
+                remote(y_send.at[slot, planes], y_recv.at[slot, planes], y_ssem.at[slot], y_rsem.at[slot], along_y))
+
+    def for_planes(q, do):
+        @pl.when((q >= 1) & (q < 3))
+        def _():
+            do(pl.ds(0, 2))
+
+        @pl.when((q >= 3) & (q <= chunks))
+        def _():
+            do(pl.ds(0, 3))
+
+        @pl.when((q > chunks) & (q <= chunks + 2))
+        def _():
+            do(pl.ds(2, 1))
 
     for cp in loads(0, full):
         cp.start()
@@ -132,6 +154,8 @@
 
         for_size(j, do)
         slot = j % SLOTS
+        out = (j + 1) % SLOTS
+        kept = j % (SLOTS + 1)
 
         def tile(t, carry):
             for half in range(2):
@@ -143,44 +167,47 @@
                     o = other[slot, b, :, pl.ds(col, 8 * LANES)].astype(jnp.float32)
                     return (a + o).reshape(8, LANES)
 
-                mine[slot, half, pl.ds(row, 8)] = pair(0)
+                mine[kept, half, pl.ds(row, 8)] = pair(0)
                 if half == 0:
-                    x_send[slot, 0, pl.ds(row, 8)] = pair(1)
+                    x_send[out, 0, pl.ds(row, 8)] = pair(1)
                     y_keep[slot, pl.ds(row, 8)] = pair(2)
-                    x_send[slot, 1, pl.ds(row, 8)] = pair(3)
+                    x_send[out, 1, pl.ds(row, 8)] = pair(3)
                 else:
                     x_keep[slot, pl.ds(row, 8)] = pair(1)
-                    y_send[slot, 0, pl.ds(row, 8)] = pair(2)
-                    y_send[slot, 1, pl.ds(row, 8)] = pair(3)
+                    y_send[out, 0, pl.ds(row, 8)] = pair(2)
+                    y_send[out, 1, pl.ds(row, 8)] = pair(3)
             return carry
 
         lax.fori_loop(0, HALF_ROWS // 8, tile, 0)
-        for cp in first_hops(j):
-            cp.start()
+
+    def wait_for(q):
+        def do(planes):
+            for cp in hops(q, planes):
+                cp.wait()
+
+        for_planes(q, do)
 
     def relay(j):
-        for cp in first_hops(j):
-            cp.wait()
         slot = j % SLOTS
-        x_fin[slot] = x_keep[slot] + y_recv[slot, 1]
-        y_fin[slot] = y_keep[slot] + x_recv[slot, 1]
-        for cp in last_hops(j):
-            cp.start()
-        mine[slot, 0] = mine[slot, 0] + x_recv[slot, 0]
-        mine[slot, 1] = mine[slot, 1] + y_recv[slot, 0]
+        got = (j + 1) % SLOTS
+        out = (j + 3) % SLOTS
+        kept = j % (SLOTS + 1)
+        x_send[out, 2] = x_keep[slot] + y_recv[got, 1]
+        y_send[out, 2] = y_keep[slot] + x_recv[got, 1]
+        mine[kept, 0] = mine[kept, 0] + x_recv[got, 0]
+        mine[kept, 1] = mine[kept, 1] + y_recv[got, 0]
 
     def finish(j):
-        for cp in last_hops(j):
-            cp.wait()
-        slot = j % SLOTS
+        got = (j + 3) % SLOTS
+        kept = j % (SLOTS + 1)
         base = j * CHUNK_ROWS
         left = shard_rows - j * CHUNK_ROWS
         rows = lax.broadcasted_iota(jnp.int32, (8, LANES), 0)
 
         def tile(t, total):
             row = pl.multiple_of(t * 8, 8)
-            top = (mine[slot, 0, pl.ds(row, 8)] + y_last[slot, pl.ds(row, 8)]) * 0.125
-            low = (mine[slot, 1, pl.ds(row, 8)] + x_last[slot, pl.ds(row, 8)]) * 0.125
+            top = (mine[kept, 0, pl.ds(row, 8)] + y_recv[got, 2, pl.ds(row, 8)]) * 0.125
+            low = (mine[kept, 1, pl.ds(row, 8)] + x_recv[got, 2, pl.ds(row, 8)]) * 0.125
             g_out[pl.ds(pl.multiple_of(base + t * 8, 8), 8)] = top
             g_out[pl.ds(pl.multiple_of(base + HALF_ROWS + t * 8, 8), 8)] = low
             total = total + jnp.where(rows + t * 8 < left, top * top, 0.0)
@@ -193,26 +220,34 @@
         def _():
             begin(i)
 
-        @pl.when((i >= 1) & (i < chunks + 1))
+        @pl.when((i >= 1) & (i <= chunks))
         def _():
             pair_sums(i - 1)
 
-        @pl.when((i >= 2) & (i < chunks + 2))
-        def _():
-            relay(i - 2)
+        wait_for(i - 2)
+
+        @pl.when((i >= 3) & (i <= chunks + 2))
+        def _():
+            relay(i - 3)
+
+        @pl.when(i >= 5)
+        def _():
+            finish(i - 5)
+
+        def go(planes):
+            for cp in hops(i, planes):
+                cp.start()
+
+        for_planes(i, go)
 
         @pl.when(i == 4)
         def _():
             for cp in fetches:
                 cp.start()
 
-        @pl.when(i >= 4)
-        def _():
-            finish(i - 4)
-
         return carry
 
-    lax.fori_loop(0, chunks + 4, step, 0)
+    lax.fori_loop(0, chunks + 5, step, 0)
     norm_recv[me] = acc[...]
 
     def shares(peer, k):
@@ -220,42 +255,54 @@
 
     for k, peer in enumerate(others):
         shares(peer, k).start()
+    for cp in fetches:
+        cp.wait()
     for k, peer in enumerate(others):
         shares(peer, k).wait_send()
         remote(acc, norm_recv.at[peer], n_ssem.at[k], n_rsem.at[peer], peer).wait_recv()
     total = norm_recv[0]
     for k in range(1, num_dev):
         total = total + norm_recv[k]
-    for cp in fetches:
-        cp.wait()
-    norm_out[...] = jnp.broadcast_to(jnp.sqrt(jnp.sum(total, keepdims=True)), norm_out.shape)
-
-
-def reduce_scatter(grad_row, w, m, shard_rows, num_dev):
+    norm = jnp.broadcast_to(jnp.sqrt(jnp.sum(total, keepdims=True)), norm_out.shape)
+    norm_out[...] = norm
+    coef = jnp.minimum(1.0, 1.0 / (norm[0:1] + CLIP_EPS))
+    rate = lr[0]
+
+    def part_tile(t, carry):
+        at = pl.ds(pl.multiple_of(t * TILE_ROWS, 8), TILE_ROWS)
+        new, _, _ = adamw_tile(g_out[at], w_out[at], m_out[at], v_part[at], mask_part[at], coef, rate)
+        pack_tile(packed, t, new)
+        return carry
+
+    lax.fori_loop(0, ahead // TILE_ROWS, part_tile, 0)
+
+
+def reduce_scatter(lr, grad_row, w, m, v, mask, num_dev):
     f32, bf16 = jnp.float32, jnp.bfloat16
+    shard_rows = w.shape[0]
     chunks = -(-shard_rows // CHUNK_ROWS)
+    ahead = PARTS[0] * ADAM_ROWS
     vm, dma = pltpu.VMEM, pltpu.SemaphoreType.DMA
-    pair = (SLOTS, 2, HALF_ROWS, LANES)
+    three = (SLOTS, 3, HALF_ROWS, LANES)
     one = (SLOTS, HALF_ROWS, LANES)
     raw = (SLOTS, 4, 1, CHUNK_ROWS * LANES)
     state = vm((chunks * CHUNK_ROWS, LANES), f32)
     return pl.pallas_call(
         functools.partial(reduce_kernel, shard_rows),
-        out_shape=(state, state, state, jax.ShapeDtypeStruct((8, LANES), f32)),
-        in_specs=[pl.BlockSpec(memory_space=pltpu.HBM)] * 3,
-        out_specs=(pl.BlockSpec(memory_space=vm),) * 4,
+        out_shape=(state, state, state, vm((ahead // 4, 4, LANES), bf16), jax.ShapeDtypeStruct((8, LANES), f32)),
+        in_specs=[pl.BlockSpec(memory_space=pltpu.SMEM)] + [pl.BlockSpec(memory_space=pltpu.HBM)] * 5,
+        out_specs=(pl.BlockSpec(memory_space=vm),) * 5,
         scratch_shapes=[
-            vm(raw, bf16), vm(raw, bf16), vm(pair, f32), vm(pair, f32), vm(one, f32), vm(one, f32),
-            vm(pair, f32), vm(pair, f32), vm(pair, f32), vm(one, f32), vm(one, f32), vm(one, f32),
-            vm(one, f32), vm((8, LANES), f32),
+            vm(raw, bf16), vm(raw, bf16), vm(three, f32), vm(three, f32), vm(one, f32), vm(one, f32),
+            vm((SLOTS + 1, 2, HALF_ROWS, LANES), f32), vm(three, f32), vm(three, f32), vm((8, LANES), f32),
             vm((num_dev, 8, LANES), f32),
             dma((SLOTS, 4)), dma((SLOTS, 4)), dma((SLOTS, 4)),
             dma((SLOTS,)), dma((SLOTS,)), dma((SLOTS,)), dma((SLOTS,)),
-            dma((SLOTS,)), dma((SLOTS,)), dma((SLOTS,)), dma((SLOTS,)),
-            dma((num_dev - 1,)), dma((num_dev,)), dma, dma],
+            dma((num_dev - 1,)), dma((num_dev,)),
+            vm((ahead, LANES), f32), vm((ahead, LANES), jnp.int32), dma((4,))],
         compiler_params=pltpu.CompilerParams(collective_id=0, has_side_effects=True,
                                              vmem_limit_bytes=VMEM_LIMIT),
-    )(grad_row, w, m)
+    )(lr, grad_row, w, m, v, mask)
 
 
 def adamw_kernel(lr, norm, g, w, m, v, mask, *rest):
@@ -266,18 +313,9 @@
 
     def tile(t, carry):
         at = pl.ds(pl.multiple_of(t * TILE_ROWS, 8), TILE_ROWS)
-        h = g[at] * coef
-        first = BETA_FIRST * m[at] + (1.0 - BETA_FIRST) * h
-        second = BETA_SECOND * v[at] + (1.0 - BETA_SECOND) * h * h
-        step_dir = (first * (1.0 / (1.0 - BETA_FIRST ** ADAM_STEP))) / (
-            jnp.sqrt(second * (1.0 / (1.0 - BETA_SECOND ** ADAM_STEP))) + ADAM_EPS)
-        old = w[at]
-        new = old - rate * (step_dir + WEIGHT_DECAY * mask[at].astype(jnp.float32) * old)
-        w_out[at] = new
-        m_out[at] = first
-        v_out[at] = second
-        grains = TILE_ROWS // 4
-        packed[pl.ds(pl.multiple_of(t * grains, 2), grains)] = new.reshape(grains, 4, LANES).astype(packed.dtype)
+        w_out[at], m_out[at], v_out[at] = new, first, second = adamw_tile(
+            g[at], w[at], m[at], v[at], mask[at], coef, rate)
+        pack_tile(packed, t, new)
         return carry
 
     lax.fori_loop(0, ADAM_ROWS // TILE_ROWS, tile, 0)
@@ -369,16 +407,18 @@
         def put(pieces, spots, whole, direct=False):
             return (store(pieces, spots, whole, num_dev, grains, direct),)
 
-        g, w, m, norm = reduce_scatter(grad_row, flat(master), flat(mom_first), rows, num_dev)
+        v, mask = flat(mom_second), flat(decay_mask)
+        g, w, m, packed, norm = reduce_scatter(
+            learn_rate, grad_row, flat(master), flat(mom_first), v, mask, num_dev)
+        packs = {0: packed}
         state = ()
         whole = ()
-        arrived = []
         firsts = [sum(PARTS[:p]) for p in range(len(PARTS))]
-        for p, steps in enumerate(PARTS):
-            *state, packed, grad_norm = adamw(
-                firsts[p], steps, learn_rate, norm, g, w, m, flat(mom_second), flat(decay_mask), state)
-            arrived.append((packed, send(packed, "x"), send(packed, "y"),
-                            send(packed, "core")))
+        for p in (*range(1, len(PARTS)), 0):
+            *state, packed, grad_norm = adamw(firsts[p], PARTS[p], learn_rate, norm, g, w, m, v, mask, state)
+            packs.setdefault(p, packed)
+        arrived = [(packs[p], send(packs[p], "x"), send(packs[p], "y"),
+                    send(packs[p], "core")) for p in range(len(PARTS))]
         starts = [first * ADAM_ROWS // 4 for first in firsts]
         far = []
         for p, (packed, from_x, from_y, from_core) in enumerate(arrived):

time: 759 us -> 794 us (1.046)
  local copies, waits for them, and re-layouts: 14.2 us -> 51.6 us
    unnamed x100 -> x248, local copies, waits for them, and re-layouts: 14.2 us -> 51.6 us
  transfers between devices with their start and end apart: 70 -> 70, of which waited for: 32 -> 23; matrix products, arithmetic and copies ran while one was open for 0% -> 0% of each run, Pallas kernels for 12% -> 8%
where the time goes in v3:
time: 794 us; the launch traced here: 793 us
  Pallas kernels  526 us (66%)
  waiting for transfers between devices  176 us (22%)
  local copies, waits for them, and re-layouts  51.6 us (6%)
  starting transfers between devices  36.7 us (5%)
    pallas_call x1, Pallas kernels, reduce_scatter(): pl.pallas_call(functools.partial(reduce_kernel, shard_rows), out_shape=(s...  426 us
    ppermute x70, waiting for transfers between devices, send(): return lax.ppermute(a, 'dp', hop[along])  176 us
    pallas_call x15, Pallas kernels, store(): pl.pallas_call(functools.partial(store_kernel, [(which, start, min(p.shap...  52.1 us
    unnamed x248, local copies, waits for them, and re-layouts  51.6 us
    pallas_call x10, Pallas kernels, adamw(): pl.pallas_call(adamw_kernel, grid=(steps,), out_shape=(state, state, stat...  48.1 us
    ppermute x70, starting transfers between devices, send(): return lax.ppermute(a, 'dp', hop[along])  36.7 us
  transfers between devices with their start and end apart: 70, of which 23 were waited for; matrix products, arithmetic and copies ran while one was open for 0% of the time, Pallas kernels for 8%

profile of v3, /device:TPU:0, one launch (start us, length us, event | category | flops | bytes accessed | tf_op | source)
XLA Modules:
  0.0 793.0 jit_solution(2701839875228451193)
XLA Ops:
  1.3 426.3 %shard_map.101 = (f32[24960,128]{1,0:T(8,128)S(1)}, f32[24960,128]{1,0:T(8,128)S(1)}, f32[24960,128]{1,0:T(8,128)S(1)}, bf16[480,4,128]{2,1,0:T(4,128)(2,1)S(1)}, f32[8,128]{1,0:T(8,128)}) custom-call(f32[1]{0:T(128)S(6)} %copy.93.lr, bf16[1,25530368]{1,0:T(2,128)(2,1)} %grad.1, f32[24932,128]{1,0:T(8,128)} %bitcast.34, f32[24932,128]{1,0:T(8,128)} %bitcast.35, ...), custom_call_target="tpu_custom_call" | custom-call | tf_op jit(solution)/shard_map/pallas_call | solution.py:290
  427.6 5.8 shard_map.102
  433.4 6.4 shard_map.103
  439.8 6.5 shard_map.104
  446.3 6.4 shard_map.105
  452.7 6.5 shard_map.106
  459.2 3.7 shard_map.107
  462.9 3.0 shard_map.108
  465.9 1.1 collective-permute-start.38
  468.0 3.0 shard_map.109
  471.9 1.0 collective-permute-start.34
  472.9 1.1 collective-permute-done.38.refs_1_
  474.1 1.1 collective-permute-start.24
  475.3 3.1 shard_map.110
  482.8 12.6 %collective-permute-done.30.refs_1_ = bf16[240,4,128]{2,1,0:T(4,128)(2,1)S(1)} collective-permute-done((bf16[240,4,128]{2,1,0:T(4,128)(2,1)}, bf16[240,4,128]{2,1,0:T(4,128)(2,1)S(1)}, u32[]{:S(2)}, u32[]{:S(2)}) %collective-permute-start.30) | collective-permute-done | bytes 245792 | tf_op jit(solution)/shard_map/ppermute | solution.py:405
  497.0 1.0 collective-permute-start.42
  500.1 8.9 %collective-permute-done.6.refs_1_ = bf16[480,4,128]{2,1,0:T(4,128)(2,1)S(1)} collective-permute-done((bf16[480,4,128]{2,1,0:T(4,128)(2,1)S(1)}, bf16[480,4,128]{2,1,0:T(4,128)(2,1)S(1)}, u32[]{:S(2)}, u32[]{:S(2)}) %collective-permute-start.6) | collective-permute-done | bytes 491552 | tf_op jit(solution)/shard_map/ppermute | solution.py:405
  509.0 1.3 collective-permute-done.42.refs_2_
  516.2 1.1 collective-permute-start.62
  519.7 1.1 collective-permute-start.4
  523.9 17.1 %collective-permute-done.10.refs_2_ = bf16[240,4,128]{2,1,0:T(4,128)(2,1)} collective-permute-done((bf16[240,4,128]{2,1,0:T(4,128)(2,1)S(1)}, bf16[240,4,128]{2,1,0:T(4,128)(2,1)}, u32[]{:S(2)}, u32[]{:S(2)}) %collective-permute-start.10) | collective-permute-done | bytes 245792 | tf_op jit(solution)/shard_map/ppermute | solution.py:405
  541.0 1.1 collective-permute-start.18
  542.1 4.2 collective-permute-done.4.refs_2_
  551.3 1.1 collective-permute-start.54
  554.2 13.0 %collective-permute-done.18.refs_1_ = bf16[960,4,128]{2,1,0:T(4,128)(2,1)S(1)} collective-permute-done((bf16[960,4,128]{2,1,0:T(4,128)(2,1)S(1)}, bf16[960,4,128]{2,1,0:T(4,128)(2,1)S(1)}, u32[]{:S(2)}, u32[]{:S(2)}) %collective-permute-start.18) | collective-permute-done | bytes 983072 | tf_op jit(solution)/shard_map/ppermute | solution.py:405
  567.2 3.7 collective-permute-done.58.refs_2_
  570.9 1.1 collective-permute-start.12
  573.0 15.3 %collective-permute-done.54.refs_1_ = bf16[960,4,128]{2,1,0:T(4,128)(2,1)S(1)} collective-permute-done((bf16[960,4,128]{2,1,0:T(4,128)(2,1)S(1)}, bf16[960,4,128]{2,1,0:T(4,128)(2,1)S(1)}, u32[]{:S(2)}, u32[]{:S(2)}) %collective-permute-start.54) | collective-permute-done | bytes 983072 | tf_op jit(solution)/shard_map/ppermute | solution.py:405
  588.3 3.7 collective-permute-done.21.refs_2_
  591.9 1.1 collective-permute-start.46
  595.0 14.3 %collective-permute-done.12.refs_1_ = bf16[960,4,128]{2,1,0:T(4,128)(2,1)S(1)} collective-permute-done((bf16[960,4,128]{2,1,0:T(4,128)(2,1)S(1)}, bf16[960,4,128]{2,1,0:T(4,128)(2,1)S(1)}, u32[]{:S(2)}, u32[]{:S(2)}) %collective-permute-start.12) | collective-permute-done | bytes 983072 | tf_op jit(solution)/shard_map/ppermute | solution.py:405
  609.3 3.7 collective-permute-done.50.refs_2_
  615.3 14.4 %collective-permute-done.46.refs_1_ = bf16[960,4,128]{2,1,0:T(4,128)(2,1)S(1)} collective-permute-done((bf16[960,4,128]{2,1,0:T(4,128)(2,1)S(1)}, bf16[960,4,128]{2,1,0:T(4,128)(2,1)S(1)}, u32[]{:S(2)}, u32[]{:S(2)}) %collective-permute-start.46) | collective-permute-done | bytes 983072 | tf_op jit(solution)/shard_map/ppermute | solution.py:405
  630.7 1.1 collective-permute-done.15.refs_2_
  636.6 7.4 collective-permute-done.25.refs_0_
  644.9 8.2 %collective-permute-done.7.refs_0_ = bf16[480,4,128]{2,1,0:T(4,128)(2,1)} collective-permute-done((bf16[480,4,128]{2,1,0:T(4,128)(2,1)S(1)}, bf16[480,4,128]{2,1,0:T(4,128)(2,1)}, u32[]{:S(2)}, u32[]{:S(2)}) %collective-permute-start.7) | collective-permute-done | bytes 491552 | tf_op jit(solution)/shard_map/ppermute | solution.py:405
  653.0 1.1 collective-permute-start.28
  659.0 10.9 %collective-permute-done.28.refs_2_ = bf16[720,4,128]{2,1,0:T(4,128)(2,1)S(1)} collective-permute-done((bf16[720,4,128]{2,1,0:T(4,128)(2,1)S(1)}, bf16[720,4,128]{2,1,0:T(4,128)(2,1)S(1)}, u32[]{:S(2)}, u32[]{:S(2)}) %collective-permute-start.28) | collective-permute-done | bytes 737312 | tf_op jit(solution)/shard_map/ppermute | solution.py:405
  676.6 1.1 collective-permute-start.22
  685.5 1.0 collective-permute-start.13
  687.4 13.8 %collective-permute-done.22.refs_2_ = bf16[960,4,128]{2,1,0:T(4,128)(2,1)S(1)} collective-permute-done((bf16[960,4,128]{2,1,0:T(4,128)(2,1)S(1)}, bf16[960,4,128]{2,1,0:T(4,128)(2,1)S(1)}, u32[]{:S(2)}, u32[]{:S(2)}) %collective-permute-start.22) | collective-permute-done | bytes 983072 | tf_op jit(solution)/shard_map/ppermute | solution.py:405
  706.2 15.1 %collective-permute-done.16.refs_2_ = bf16[960,4,128]{2,1,0:T(4,128)(2,1)S(1)} collective-permute-done((bf16[960,4,128]{2,1,0:T(4,128)(2,1)S(1)}, bf16[960,4,128]{2,1,0:T(4,128)(2,1)S(1)}, u32[]{:S(2)}, u32[]{:S(2)}) %collective-permute-start.16) | collective-permute-done | bytes 983072 | tf_op jit(solution)/shard_map/ppermute | solution.py:405
  722.4 3.6 collective-permute-done.13.refs_0_
  730.8 3.7 shard_map.126
  734.5 1.0 copy-done.82
  735.6 1.0 copy-done.84
  736.6 1.0 copy-done.86
  737.6 1.0 copy-done.88
  738.7 1.0 copy-done.90
  739.7 3.3 shard_map.111.refs_6_
  743.1 4.1 shard_map.112.refs_6_
  747.2 4.5 shard_map.113.refs_6_
  751.9 4.5 shard_map.114.refs_6_
  756.5 4.5 shard_map.115.refs_6_
  761.1 4.5 shard_map.116.refs_6_
  765.8 3.6 shard_map.117.refs_6_
  769.5 3.1 shard_map.118.refs_6_
  772.8 3.1 shard_map.119.refs_6_
  776.0 3.0 shard_map.120.refs_4_
  779.2 2.8 shard_map.121.refs_4_
  782.0 3.2 shard_map.122.refs_4_
  785.3 3.2 shard_map.123.refs_4_
  788.5 2.2 shard_map.124.refs_4_
  790.7 2.3 shard_map.125
  (350 shorter events, 71.5 us)
Async XLA Ops:
  465.9 8.2 %collective-permute-start.38 = (bf16[240,4,128]{2,1,0:T(4,128)(2,1)}, bf16[240,4,128]{2,1,0:T(4,128)(2,1)S(1)}, u32[]{:S(2)}, u32[]{:S(2)}) collective-permute-start(bf16[240,4,128]{2,1,0:T(4,128)(2,1)} %get-tuple-element.81.refs_0_), channel_id=1, source_target_pairs={{0,2},{1,3},{2,0},{3,1},{4,6},{5,7},{6,4},{7,5}} | collective-permute-start | bytes 737288 | tf_op jit(solution)/shard_map/ppermute | solution.py:405
  467.0 8.2 %collective-permute-start.9 = (bf16[240,4,128]{2,1,0:T(4,128)(2,1)}, bf16[240,4,128]{2,1,0:T(4,128)(2,1)S(1)}, u32[]{:S(2)}, u32[]{:S(2)}) collective-permute-start(bf16[240,4,128]{2,1,0:T(4,128)(2,1)} %get-tuple-element.81.refs_0_), channel_id=1, source_target_pairs={{0,4},{1,5},{2,6},{3,7},{4,0},{5,1},{6,2},{7,3}} | collective-permute-start | bytes 737288 | tf_op jit(solution)/shard_map/ppermute | solution.py:405
  468.0 10.4 %collective-permute-start.39 = (bf16[240,4,128]{2,1,0:T(4,128)(2,1)}, bf16[240,4,128]{2,1,0:T(4,128)(2,1)S(1)}, u32[]{:S(2)}, u32[]{:S(2)}) collective-permute-start(bf16[240,4,128]{2,1,0:T(4,128)(2,1)} %get-tuple-element.81.refs_0_), channel_id=1, source_target_pairs={{0,1},{1,0},{2,3},{3,2},{4,5},{5,4},{6,7},{7,6}} | collective-permute-start | bytes 737288 | tf_op jit(solution)/shard_map/ppermute | solution.py:405
  471.0 9.1 %collective-permute-start = (bf16[240,4,128]{2,1,0:T(4,128)(2,1)}, bf16[240,4,128]{2,1,0:T(4,128)(2,1)S(1)}, u32[]{:S(2)}, u32[]{:S(2)}) collective-permute-start(bf16[240,4,128]{2,1,0:T(4,128)(2,1)} %get-tuple-element.75.refs_0_), channel_id=1, source_target_pairs={{0,2},{1,3},{2,0},{3,1},{4,6},{5,7},{6,4},{7,5}} | collective-permute-start | bytes 737288 | tf_op jit(solution)/shard_map/ppermute | solution.py:405
  471.9 9.1 %collective-permute-start.34 = (bf16[240,4,128]{2,1,0:T(4,128)(2,1)}, bf16[240,4,128]{2,1,0:T(4,128)(2,1)S(1)}, u32[]{:S(2)}, u32[]{:S(2)}) collective-permute-start(bf16[240,4,128]{2,1,0:T(4,128)(2,1)} %get-tuple-element.75.refs_0_), channel_id=1, source_target_pairs={{0,4},{1,5},{2,6},{3,7},{4,0},{5,1},{6,2},{7,3}} | collective-permute-start | bytes 737288 | tf_op jit(solution)/shard_map/ppermute | solution.py:405
  474.1 24.0 %collective-permute-start.24 = (bf16[480,4,128]{2,1,0:T(4,128)(2,1)S(1)}, bf16[480,4,128]{2,1,0:T(4,128)(2,1)}, u32[]{:S(2)}, u32[]{:S(2)}) collective-permute-start(bf16[480,4,128]{2,1,0:T(4,128)(2,1)S(1)} %get-tuple-element.86.refs_0_), channel_id=1, source_target_pairs={{0,2},{1,3},{2,0},{3,1},{4,6},{5,7},{6,4},{7,5}} | collective-permute-start | bytes 1474568 | tf_op jit(solution)/shard_map/ppermute | solution.py:405
  479.1 16.3 %collective-permute-start.30 = (bf16[240,4,128]{2,1,0:T(4,128)(2,1)}, bf16[240,4,128]{2,1,0:T(4,128)(2,1)S(1)}, u32[]{:S(2)}, u32[]{:S(2)}) collective-permute-start(bf16[240,4,128]{2,1,0:T(4,128)(2,1)} %get-tuple-element.79.refs_0_), channel_id=1, source_target_pairs={{0,2},{1,3},{2,0},{3,1},{4,6},{5,7},{6,4},{7,5}} | collective-permute-start | bytes 737288 | tf_op jit(solution)/shard_map/ppermute | solution.py:405
  480.1 15.3 %collective-permute-start.3 = (bf16[240,4,128]{2,1,0:T(4,128)(2,1)}, bf16[240,4,128]{2,1,0:T(4,128)(2,1)S(1)}, u32[]{:S(2)}, u32[]{:S(2)}) collective-permute-start(bf16[240,4,128]{2,1,0:T(4,128)(2,1)} %get-tuple-element.79.refs_0_), channel_id=1, source_target_pairs={{0,4},{1,5},{2,6},{3,7},{4,0},{5,1},{6,2},{7,3}} | collective-permute-start | bytes 737288 | tf_op jit(solution)/shard_map/ppermute | solution.py:405
  481.1 15.3 %collective-permute-start.31 = (bf16[240,4,128]{2,1,0:T(4,128)(2,1)}, bf16[240,4,128]{2,1,0:T(4,128)(2,1)S(1)}, u32[]{:S(2)}, u32[]{:S(2)}) collective-permute-start(bf16[240,4,128]{2,1,0:T(4,128)(2,1)} %get-tuple-element.79.refs_0_), channel_id=1, source_target_pairs={{0,1},{1,0},{2,3},{3,2},{4,5},{5,4},{6,7},{7,6}} | collective-permute-start | bytes 737288 | tf_op jit(solution)/shard_map/ppermute | solution.py:405
  481.8 17.0 %collective-permute-start.66 = (bf16[480,4,128]{2,1,0:T(4,128)(2,1)S(1)}, bf16[480,4,128]{2,1,0:T(4,128)(2,1)S(1)}, u32[]{:S(2)}, u32[]{:S(2)}) collective-permute-start(bf16[480,4,128]{2,1,0:T(4,128)(2,1)S(1)} %get-tuple-element.86.refs_0_), channel_id=1, source_target_pairs={{0,4},{1,5},{2,6},{3,7},{4,0},{5,1},{6,2},{7,3}} | collective-permute-start | bytes 1474568 | tf_op jit(solution)/shard_map/ppermute | solution.py:405
  495.4 13.6 %collective-permute-start.6 = (bf16[480,4,128]{2,1,0:T(4,128)(2,1)S(1)}, bf16[480,4,128]{2,1,0:T(4,128)(2,1)S(1)}, u32[]{:S(2)}, u32[]{:S(2)}) collective-permute-start(bf16[480,4,128]{2,1,0:T(4,128)(2,1)S(1)} %copy-done.65), channel_id=1, source_target_pairs={{0,2},{1,3},{2,0},{3,1},{4,6},{5,7},{6,4},{7,5}} | collective-permute-start | bytes 1474568 | tf_op jit(solution)/shard_map/ppermute | solution.py:405
  497.0 13.3 %collective-permute-start.42 = (bf16[480,4,128]{2,1,0:T(4,128)(2,1)S(1)}, bf16[480,4,128]{2,1,0:T(4,128)(2,1)S(1)}, u32[]{:S(2)}, u32[]{:S(2)}) collective-permute-start(bf16[480,4,128]{2,1,0:T(4,128)(2,1)S(1)} %copy-done.65), channel_id=1, source_target_pairs={{0,4},{1,5},{2,6},{3,7},{4,0},{5,1},{6,2},{7,3}} | collective-permute-start | bytes 1474568 | tf_op jit(solution)/shard_map/ppermute | solution.py:405
  498.1 13.0 %collective-permute-start.43 = (bf16[480,4,128]{2,1,0:T(4,128)(2,1)S(1)}, bf16[480,4,128]{2,1,0:T(4,128)(2,1)S(1)}, u32[]{:S(2)}, u32[]{:S(2)}) collective-permute-start(bf16[480,4,128]{2,1,0:T(4,128)(2,1)S(1)} %copy-done.65), channel_id=1, source_target_pairs={{0,1},{1,0},{2,3},{3,2},{4,5},{5,4},{6,7},{7,6}} | collective-permute-start | bytes 1474568 | tf_op jit(solution)/shard_map/ppermute | solution.py:405
  498.8 14.3 %collective-permute-start.40 = (bf16[240,4,128]{2,1,0:T(4,128)(2,1)S(1)}, bf16[240,4,128]{2,1,0:T(4,128)(2,1)S(1)}, u32[]{:S(2)}, u32[]{:S(2)}) collective-permute-start(bf16[240,4,128]{2,1,0:T(4,128)(2,1)S(1)} %collective-permute-done.38.refs_1_), channel_id=1, source_target_pairs={{0,1},{1,0},{2,3},{3,2},{4,5},{5,4},{6,7},{7,6}} | collective-permute-start | bytes 737288 | tf_op jit(solution)/shard_map/ppermute | solution.py:405
  499.6 14.2 %collective-permute-start.41 = (bf16[240,4,128]{2,1,0:T(4,128)(2,1)S(1)}, bf16[240,4,128]{2,1,0:T(4,128)(2,1)S(1)}, u32[]{:S(2)}, u32[]{:S(2)}) collective-permute-start(bf16[240,4,128]{2,1,0:T(4,128)(2,1)S(1)} %collective-permute-done.9.refs_2_), channel_id=1, source_target_pairs={{0,1},{1,0},{2,3},{3,2},{4,5},{5,4},{6,7},{7,6}} | collective-permute-start | bytes 737288 | tf_op jit(solution)/shard_map/ppermute | solution.py:405
  510.4 7.0 collective-permute-start.37
  511.9 7.1 collective-permute-start.32
  513.8 7.7 collective-permute-start.33
  514.5 32.8 %collective-permute-start.27 = (bf16[720,4,128]{2,1,0:T(4,128)(2,1)S(1)}, bf16[720,4,128]{2,1,0:T(4,128)(2,1)S(1)}, u32[]{:S(2)}, u32[]{:S(2)}) collective-permute-start(bf16[720,4,128]{2,1,0:T(4,128)(2,1)S(1)} %copy-done.50), channel_id=1, source_target_pairs={{0,4},{1,5},{2,6},{3,7},{4,0},{5,1},{6,2},{7,3}} | collective-permute-start | bytes 2211848 | tf_op jit(solution)/shard_map/ppermute | solution.py:405
  516.2 31.5 %collective-permute-start.62 = (bf16[720,4,128]{2,1,0:T(4,128)(2,1)S(1)}, bf16[720,4,128]{2,1,0:T(4,128)(2,1)S(1)}, u32[]{:S(2)}, u32[]{:S(2)}) collective-permute-start(bf16[720,4,128]{2,1,0:T(4,128)(2,1)S(1)} %copy-done.50), channel_id=1, source_target_pairs={{0,2},{1,3},{2,0},{3,1},{4,6},{5,7},{6,4},{7,5}} | collective-permute-start | bytes 2211848 | tf_op jit(solution)/shard_map/ppermute | solution.py:405
  518.1 22.9 %collective-permute-start.10 = (bf16[240,4,128]{2,1,0:T(4,128)(2,1)S(1)}, bf16[240,4,128]{2,1,0:T(4,128)(2,1)}, u32[]{:S(2)}, u32[]{:S(2)}) collective-permute-start(bf16[240,4,128]{2,1,0:T(4,128)(2,1)S(1)} %collective-permute-done.9.refs_2_), channel_id=1, source_target_pairs={{0,2},{1,3},{2,0},{3,1},{4,6},{5,7},{6,4},{7,5}} | collective-permute-start | bytes 737288 | tf_op jit(solution)/shard_map/ppermute | solution.py:405
  519.7 26.5 %collective-permute-start.4 = (bf16[240,4,128]{2,1,0:T(4,128)(2,1)S(1)}, bf16[240,4,128]{2,1,0:T(4,128)(2,1)}, u32[]{:S(2)}, u32[]{:S(2)}) collective-permute-start(bf16[240,4,128]{2,1,0:T(4,128)(2,1)S(1)} %collective-permute-done.3.refs_2_), channel_id=1, source_target_pairs={{0,2},{1,3},{2,0},{3,1},{4,6},{5,7},{6,4},{7,5}} | collective-permute-start | bytes 737288 | tf_op jit(solution)/shard_map/ppermute | solution.py:405
  522.2 25.1 %collective-permute-start.1 = (bf16[240,4,128]{2,1,0:T(4,128)(2,1)S(1)}, bf16[240,4,128]{2,1,0:T(4,128)(2,1)}, u32[]{:S(2)}, u32[]{:S(2)}) collective-permute-start(bf16[240,4,128]{2,1,0:T(4,128)(2,1)S(1)} %collective-permute-done.refs_1_), channel_id=1, source_target_pairs={{0,4},{1,5},{2,6},{3,7},{4,0},{5,1},{6,2},{7,3}} | collective-permute-start | bytes 737288 | tf_op jit(solution)/shard_map/ppermute | solution.py:405
  541.0 26.2 %collective-permute-start.18 = (bf16[960,4,128]{2,1,0:T(4,128)(2,1)S(1)}, bf16[960,4,128]{2,1,0:T(4,128)(2,1)S(1)}, u32[]{:S(2)}, u32[]{:S(2)}) collective-permute-start(bf16[960,4,128]{2,1,0:T(4,128)(2,1)S(1)} %copy-done), channel_id=1, source_target_pairs={{0,2},{1,3},{2,0},{3,1},{4,6},{5,7},{6,4},{7,5}} | collective-permute-start | bytes 2949128 | tf_op jit(solution)/shard_map/ppermute | solution.py:405
  546.2 24.6 %collective-permute-start.58 = (bf16[960,4,128]{2,1,0:T(4,128)(2,1)S(1)}, bf16[960,4,128]{2,1,0:T(4,128)(2,1)S(1)}, u32[]{:S(2)}, u32[]{:S(2)}) collective-permute-start(bf16[960,4,128]{2,1,0:T(4,128)(2,1)S(1)} %copy-done), channel_id=1, source_target_pairs={{0,4},{1,5},{2,6},{3,7},{4,0},{5,1},{6,2},{7,3}} | collective-permute-start | bytes 2949128 | tf_op jit(solution)/shard_map/ppermute | solution.py:405
  550.4 21.6 %collective-permute-start.59 = (bf16[960,4,128]{2,1,0:T(4,128)(2,1)S(1)}, bf16[960,4,128]{2,1,0:T(4,128)(2,1)S(1)}, u32[]{:S(2)}, u32[]{:S(2)}) collective-permute-start(bf16[960,4,128]{2,1,0:T(4,128)(2,1)S(1)} %copy-done), channel_id=1, source_target_pairs={{0,1},{1,0},{2,3},{3,2},{4,5},{5,4},{6,7},{7,6}} | collective-permute-start | bytes 2949128 | tf_op jit(solution)/shard_map/ppermute | solution.py:405
  551.3 37.0 %collective-permute-start.54 = (bf16[960,4,128]{2,1,0:T(4,128)(2,1)S(1)}, bf16[960,4,128]{2,1,0:T(4,128)(2,1)S(1)}, u32[]{:S(2)}, u32[]{:S(2)}) collective-permute-start(bf16[960,4,128]{2,1,0:T(4,128)(2,1)S(1)} %copy-done.1), channel_id=1, source_target_pairs={{0,2},{1,3},{2,0},{3,1},{4,6},{5,7},{6,4},{7,5}} | collective-permute-start | bytes 2949128 | tf_op jit(solution)/shard_map/ppermute | solution.py:405
  553.2 38.7 %collective-permute-start.21 = (bf16[960,4,128]{2,1,0:T(4,128)(2,1)S(1)}, bf16[960,4,128]{2,1,0:T(4,128)(2,1)S(1)}, u32[]{:S(2)}, u32[]{:S(2)}) collective-permute-start(bf16[960,4,128]{2,1,0:T(4,128)(2,1)S(1)} %copy-done.1), channel_id=1, source_target_pairs={{0,4},{1,5},{2,6},{3,7},{4,0},{5,1},{6,2},{7,3}} | collective-permute-start | bytes 2949128 | tf_op jit(solution)/shard_map/ppermute | solution.py:405
  567.2 25.8 %collective-permute-start.55 = (bf16[960,4,128]{2,1,0:T(4,128)(2,1)S(1)}, bf16[960,4,128]{2,1,0:T(4,128)(2,1)S(1)}, u32[]{:S(2)}, u32[]{:S(2)}) collective-permute-start(bf16[960,4,128]{2,1,0:T(4,128)(2,1)S(1)} %copy-done.1), channel_id=1, source_target_pairs={{0,1},{1,0},{2,3},{3,2},{4,5},{5,4},{6,7},{7,6}} | collective-permute-start | bytes 2949128 | tf_op jit(solution)/shard_map/ppermute | solution.py:405
  570.9 38.5 %collective-permute-start.12 = (bf16[960,4,128]{2,1,0:T(4,128)(2,1)S(1)}, bf16[960,4,128]{2,1,0:T(4,128)(2,1)S(1)}, u32[]{:S(2)}, u32[]{:S(2)}) collective-permute-start(bf16[960,4,128]{2,1,0:T(4,128)(2,1)S(1)} %copy-done.2), channel_id=1, source_target_pairs={{0,2},{1,3},{2,0},{3,1},{4,6},{5,7},{6,4},{7,5}} | collective-permute-start | bytes 2949128 | tf_op jit(solution)/shard_map/ppermute | solution.py:405
  572.0 41.0 %collective-permute-start.50 = (bf16[960,4,128]{2,1,0:T(4,128)(2,1)S(1)}, bf16[960,4,128]{2,1,0:T(4,128)(2,1)S(1)}, u32[]{:S(2)}, u32[]{:S(2)}) collective-permute-start(bf16[960,4,128]{2,1,0:T(4,128)(2,1)S(1)} %copy-done.2), channel_id=1, source_target_pairs={{0,4},{1,5},{2,6},{3,7},{4,0},{5,1},{6,2},{7,3}} | collective-permute-start | bytes 2949128 | tf_op jit(solution)/shard_map/ppermute | solution.py:405
  588.3 24.7 %collective-permute-start.51 = (bf16[960,4,128]{2,1,0:T(4,128)(2,1)S(1)}, bf16[960,4,128]{2,1,0:T(4,128)(2,1)S(1)}, u32[]{:S(2)}, u32[]{:S(2)}) collective-permute-start(bf16[960,4,128]{2,1,0:T(4,128)(2,1)S(1)} %copy-done.2), channel_id=1, source_target_pairs={{0,1},{1,0},{2,3},{3,2},{4,5},{5,4},{6,7},{7,6}} | collective-permute-start | bytes 2949128 | tf_op jit(solution)/shard_map/ppermute | solution.py:405
  591.9 37.7 %collective-permute-start.46 = (bf16[960,4,128]{2,1,0:T(4,128)(2,1)S(1)}, bf16[960,4,128]{2,1,0:T(4,128)(2,1)S(1)}, u32[]{:S(2)}, u32[]{:S(2)}) collective-permute-start(bf16[960,4,128]{2,1,0:T(4,128)(2,1)S(1)} %copy-done.3), channel_id=1, source_target_pairs={{0,2},{1,3},{2,0},{3,1},{4,6},{5,7},{6,4},{7,5}} | collective-permute-start | bytes 2949128 | tf_op jit(solution)/shard_map/ppermute | solution.py:405
  594.0 37.7 %collective-permute-start.15 = (bf16[960,4,128]{2,1,0:T(4,128)(2,1)S(1)}, bf16[960,4,128]{2,1,0:T(4,128)(2,1)S(1)}, u32[]{:S(2)}, u32[]{:S(2)}) collective-permute-start(bf16[960,4,128]{2,1,0:T(4,128)(2,1)S(1)} %copy-done.3), channel_id=1, source_target_pairs={{0,4},{1,5},{2,6},{3,7},{4,0},{5,1},{6,2},{7,3}} | collective-permute-start | bytes 2949128 | tf_op jit(solution)/shard_map/ppermute | solution.py:405
  609.3 24.2 %collective-permute-start.47 = (bf16[960,4,128]{2,1,0:T(4,128)(2,1)S(1)}, bf16[960,4,128]{2,1,0:T(4,128)(2,1)S(1)}, u32[]{:S(2)}, u32[]{:S(2)}) collective-permute-start(bf16[960,4,128]{2,1,0:T(4,128)(2,1)S(1)} %copy-done.3), channel_id=1, source_target_pairs={{0,1},{1,0},{2,3},{3,2},{4,5},{5,4},{6,7},{7,6}} | collective-permute-start | bytes 2949128 | tf_op jit(solution)/shard_map/ppermute | solution.py:405
  613.0 21.5 %collective-permute-start.44 = (bf16[480,4,128]{2,1,0:T(4,128)(2,1)S(1)}, bf16[480,4,128]{2,1,0:T(4,128)(2,1)S(1)}, u32[]{:S(2)}, u32[]{:S(2)}) collective-permute-start(bf16[480,4,128]{2,1,0:T(4,128)(2,1)S(1)} %collective-permute-done.6.refs_1_), channel_id=1, source_target_pairs={{0,1},{1,0},{2,3},{3,2},{4,5},{5,4},{6,7},{7,6}} | collective-permute-start | bytes 1474568 | tf_op jit(solution)/shard_map/ppermute | solution.py:405
  614.0 21.8 %collective-permute-start.45 = (bf16[480,4,128]{2,1,0:T(4,128)(2,1)S(1)}, bf16[480,4,128]{2,1,0:T(4,128)(2,1)S(1)}, u32[]{:S(2)}, u32[]{:S(2)}) collective-permute-start(bf16[480,4,128]{2,1,0:T(4,128)(2,1)S(1)} %collective-permute-done.42.refs_2_), channel_id=1, source_target_pairs={{0,1},{1,0},{2,3},{3,2},{4,5},{5,4},{6,7},{7,6}} | collective-permute-start | bytes 1474568 | tf_op jit(solution)/shard_map/ppermute | solution.py:405
  629.7 14.3 %collective-permute-start.25 = (bf16[480,4,128]{2,1,0:T(4,128)(2,1)}, bf16[480,4,128]{2,1,0:T(4,128)(2,1)S(1)}, u32[]{:S(2)}, u32[]{:S(2)}) collective-permute-start(bf16[480,4,128]{2,1,0:T(4,128)(2,1)} %collective-permute-done.24.refs_1_), channel_id=1, source_target_pairs={{0,4},{1,5},{2,6},{3,7},{4,0},{5,1},{6,2},{7,3}} | collective-permute-start | bytes 1474568 | tf_op jit(solution)/shard_map/ppermute | solution.py:405
  631.7 21.3 %collective-permute-start.7 = (bf16[480,4,128]{2,1,0:T(4,128)(2,1)S(1)}, bf16[480,4,128]{2,1,0:T(4,128)(2,1)}, u32[]{:S(2)}, u32[]{:S(2)}) collective-permute-start(bf16[480,4,128]{2,1,0:T(4,128)(2,1)S(1)} %collective-permute-done.6.refs_1_), channel_id=1, source_target_pairs={{0,4},{1,5},{2,6},{3,7},{4,0},{5,1},{6,2},{7,3}} | collective-permute-start | bytes 1474568 | tf_op jit(solution)/shard_map/ppermute | solution.py:405
  634.5 20.5 %collective-permute-start.65 = (bf16[720,4,128]{2,1,0:T(4,128)(2,1)S(1)}, bf16[720,4,128]{2,1,0:T(4,128)(2,1)S(1)}, u32[]{:S(2)}, u32[]{:S(2)}) collective-permute-start(bf16[720,4,128]{2,1,0:T(4,128)(2,1)S(1)} %collective-permute-done.27.refs_2_), channel_id=1, source_target_pairs={{0,1},{1,0},{2,3},{3,2},{4,5},{5,4},{6,7},{7,6}} | collective-permute-start | bytes 2211848 | tf_op jit(solution)/shard_map/ppermute | solution.py:405
  635.3 35.9 %collective-permute-start.60 = (bf16[960,4,128]{2,1,0:T(4,128)(2,1)S(1)}, bf16[960,4,128]{2,1,0:T(4,128)(2,1)S(1)}, u32[]{:S(2)}, u32[]{:S(2)}) collective-permute-start(bf16[960,4,128]{2,1,0:T(4,128)(2,1)S(1)} %collective-permute-done.18.refs_1_), channel_id=1, source_target_pairs={{0,1},{1,0},{2,3},{3,2},{4,5},{5,4},{6,7},{7,6}} | collective-permute-start | bytes 2949128 | tf_op jit(solution)/shard_map/ppermute | solution.py:405
  636.6 36.6 %collective-permute-start.61 = (bf16[960,4,128]{2,1,0:T(4,128)(2,1)S(1)}, bf16[960,4,128]{2,1,0:T(4,128)(2,1)S(1)}, u32[]{:S(2)}, u32[]{:S(2)}) collective-permute-start(bf16[960,4,128]{2,1,0:T(4,128)(2,1)S(1)} %collective-permute-done.58.refs_2_), channel_id=1, source_target_pairs={{0,1},{1,0},{2,3},{3,2},{4,5},{5,4},{6,7},{7,6}} | collective-permute-start | bytes 2949128 | tf_op jit(solution)/shard_map/ppermute | solution.py:405
  644.0 12.7 %collective-permute-start.64 = (bf16[720,4,128]{2,1,0:T(4,128)(2,1)S(1)}, bf16[720,4,128]{2,1,0:T(4,128)(2,1)S(1)}, u32[]{:S(2)}, u32[]{:S(2)}) collective-permute-start(bf16[720,4,128]{2,1,0:T(4,128)(2,1)S(1)} %collective-permute-done.62.refs_1_), channel_id=1, source_target_pairs={{0,1},{1,0},{2,3},{3,2},{4,5},{5,4},{6,7},{7,6}} | collective-permute-start | bytes 2211848 | tf_op jit(solution)/shard_map/ppermute | solution.py:405
  653.0 16.9 %collective-permute-start.28 = (bf16[720,4,128]{2,1,0:T(4,128)(2,1)S(1)}, bf16[720,4,128]{2,1,0:T(4,128)(2,1)S(1)}, u32[]{:S(2)}, u32[]{:S(2)}) collective-permute-start(bf16[720,4,128]{2,1,0:T(4,128)(2,1)S(1)} %collective-permute-done.27.refs_2_), channel_id=1, source_target_pairs={{0,2},{1,3},{2,0},{3,1},{4,6},{5,7},{6,4},{7,5}} | collective-permute-start | bytes 2211848 | tf_op jit(solution)/shard_map/ppermute | solution.py:405
  655.9 14.1 %collective-permute-start.26 = (bf16[480,4,128]{2,1,0:T(4,128)(2,1)S(1)}, bf16[480,4,128]{2,1,0:T(4,128)(2,1)S(1)}, u32[]{:S(2)}, u32[]{:S(2)}) collective-permute-start(bf16[480,4,128]{2,1,0:T(4,128)(2,1)S(1)} %collective-permute-done.25.refs_0_), channel_id=1, source_target_pairs={{0,1},{1,0},{2,3},{3,2},{4,5},{5,4},{6,7},{7,6}} | collective-permute-start | bytes 1474568 | tf_op jit(solution)/shard_map/ppermute | solution.py:405
  657.5 18.1 %collective-permute-start.56 = (bf16[960,4,128]{2,1,0:T(4,128)(2,1)S(1)}, bf16[960,4,128]{2,1,0:T(4,128)(2,1)S(1)}, u32[]{:S(2)}, u32[]{:S(2)}) collective-permute-start(bf16[960,4,128]{2,1,0:T(4,128)(2,1)S(1)} %collective-permute-done.54.refs_1_), channel_id=1, source_target_pairs={{0,1},{1,0},{2,3},{3,2},{4,5},{5,4},{6,7},{7,6}} | collective-permute-start | bytes 2949128 | tf_op jit(solution)/shard_map/ppermute | solution.py:405
  669.9 8.8 %collective-permute-start.57 = (bf16[960,4,128]{2,1,0:T(4,128)(2,1)S(1)}, bf16[960,4,128]{2,1,0:T(4,128)(2,1)S(1)}, u32[]{:S(2)}, u32[]{:S(2)}) collective-permute-start(bf16[960,4,128]{2,1,0:T(4,128)(2,1)S(1)} %collective-permute-done.21.refs_2_), channel_id=1, source_target_pairs={{0,1},{1,0},{2,3},{3,2},{4,5},{5,4},{6,7},{7,6}} | collective-permute-start | bytes 2949128 | tf_op jit(solution)/shard_map/ppermute | solution.py:405
  670.7 9.0 %collective-permute-start.52 = (bf16[960,4,128]{2,1,0:T(4,128)(2,1)S(1)}, bf16[960,4,128]{2,1,0:T(4,128)(2,1)S(1)}, u32[]{:S(2)}, u32[]{:S(2)}) collective-permute-start(bf16[960,4,128]{2,1,0:T(4,128)(2,1)S(1)} %collective-permute-done.12.refs_1_), channel_id=1, source_target_pairs={{0,1},{1,0},{2,3},{3,2},{4,5},{5,4},{6,7},{7,6}} | collective-permute-start | bytes 2949128 | tf_op jit(solution)/shard_map/ppermute | solution.py:405
  672.2 9.5 %collective-permute-start.53 = (bf16[960,4,128]{2,1,0:T(4,128)(2,1)S(1)}, bf16[960,4,128]{2,1,0:T(4,128)(2,1)S(1)}, u32[]{:S(2)}, u32[]{:S(2)}) collective-permute-start(bf16[960,4,128]{2,1,0:T(4,128)(2,1)S(1)} %collective-permute-done.50.refs_2_), channel_id=1, source_target_pairs={{0,1},{1,0},{2,3},{3,2},{4,5},{5,4},{6,7},{7,6}} | collective-permute-start | bytes 2949128 | tf_op jit(solution)/shard_map/ppermute | solution.py:405
  674.2 10.3 %collective-permute-start.48 = (bf16[960,4,128]{2,1,0:T(4,128)(2,1)S(1)}, bf16[960,4,128]{2,1,0:T(4,128)(2,1)S(1)}, u32[]{:S(2)}, u32[]{:S(2)}) collective-permute-start(bf16[960,4,128]{2,1,0:T(4,128)(2,1)S(1)} %collective-permute-done.46.refs_1_), channel_id=1, source_target_pairs={{0,1},{1,0},{2,3},{3,2},{4,5},{5,4},{6,7},{7,6}} | collective-permute-start | bytes 2949128 | tf_op jit(solution)/shard_map/ppermute | solution.py:405
  676.6 24.6 %collective-permute-start.22 = (bf16[960,4,128]{2,1,0:T(4,128)(2,1)S(1)}, bf16[960,4,128]{2,1,0:T(4,128)(2,1)S(1)}, u32[]{:S(2)}, u32[]{:S(2)}) collective-permute-start(bf16[960,4,128]{2,1,0:T(4,128)(2,1)S(1)} %collective-permute-done.21.refs_2_), channel_id=1, source_target_pairs={{0,2},{1,3},{2,0},{3,1},{4,6},{5,7},{6,4},{7,5}} | collective-permute-start | bytes 2949128 | tf_op jit(solution)/shard_map/ppermute | solution.py:405
  679.7 22.6 %collective-permute-start.49 = (bf16[960,4,128]{2,1,0:T(4,128)(2,1)S(1)}, bf16[960,4,128]{2,1,0:T(4,128)(2,1)S(1)}, u32[]{:S(2)}, u32[]{:S(2)}) collective-permute-start(bf16[960,4,128]{2,1,0:T(4,128)(2,1)S(1)} %collective-permute-done.15.refs_2_), channel_id=1, source_target_pairs={{0,1},{1,0},{2,3},{3,2},{4,5},{5,4},{6,7},{7,6}} | collective-permute-start | bytes 2949128 | tf_op jit(solution)/shard_map/ppermute | solution.py:405
  680.6 24.6 %collective-permute-start.19 = (bf16[960,4,128]{2,1,0:T(4,128)(2,1)S(1)}, bf16[960,4,128]{2,1,0:T(4,128)(2,1)S(1)}, u32[]{:S(2)}, u32[]{:S(2)}) collective-permute-start(bf16[960,4,128]{2,1,0:T(4,128)(2,1)S(1)} %collective-permute-done.18.refs_1_), channel_id=1, source_target_pairs={{0,4},{1,5},{2,6},{3,7},{4,0},{5,1},{6,2},{7,3}} | collective-permute-start | bytes 2949128 | tf_op jit(solution)/shard_map/ppermute | solution.py:405
  682.6 38.7 %collective-permute-start.16 = (bf16[960,4,128]{2,1,0:T(4,128)(2,1)S(1)}, bf16[960,4,128]{2,1,0:T(4,128)(2,1)S(1)}, u32[]{:S(2)}, u32[]{:S(2)}) collective-permute-start(bf16[960,4,128]{2,1,0:T(4,128)(2,1)S(1)} %collective-permute-done.15.refs_2_), channel_id=1, source_target_pairs={{0,2},{1,3},{2,0},{3,1},{4,6},{5,7},{6,4},{7,5}} | collective-permute-start | bytes 2949128 | tf_op jit(solution)/shard_map/ppermute | solution.py:405
  685.5 40.5 %collective-permute-start.13 = (bf16[960,4,128]{2,1,0:T(4,128)(2,1)S(1)}, bf16[960,4,128]{2,1,0:T(4,128)(2,1)}, u32[]{:S(2)}, u32[]{:S(2)}) collective-permute-start(bf16[960,4,128]{2,1,0:T(4,128)(2,1)S(1)} %collective-permute-done.12.refs_1_), channel_id=1, source_target_pairs={{0,4},{1,5},{2,6},{3,7},{4,0},{5,1},{6,2},{7,3}} | collective-permute-start | bytes 2949128 | tf_op jit(solution)/shard_map/ppermute | solution.py:405
  701.3 26.1 %collective-permute-start.23 = (bf16[960,4,128]{2,1,0:T(4,128)(2,1)S(1)}, bf16[960,4,128]{2,1,0:T(4,128)(2,1)S(1)}, u32[]{:S(2)}, u32[]{:S(2)}) collective-permute-start(bf16[960,4,128]{2,1,0:T(4,128)(2,1)S(1)} %collective-permute-done.22.refs_2_), channel_id=1, source_target_pairs={{0,1},{1,0},{2,3},{3,2},{4,5},{5,4},{6,7},{7,6}} | collective-permute-start | bytes 2949128 | tf_op jit(solution)/shard_map/ppermute | solution.py:405
  703.2 22.8 %collective-permute-start.29 = (bf16[720,4,128]{2,1,0:T(4,128)(2,1)S(1)}, bf16[720,4,128]{2,1,0:T(4,128)(2,1)S(1)}, u32[]{:S(2)}, u32[]{:S(2)}) collective-permute-start(bf16[720,4,128]{2,1,0:T(4,128)(2,1)S(1)} %collective-permute-done.28.refs_2_), channel_id=1, source_target_pairs={{0,1},{1,0},{2,3},{3,2},{4,5},{5,4},{6,7},{7,6}} | collective-permute-start | bytes 2211848 | tf_op jit(solution)/shard_map/ppermute | solution.py:405
  705.3 23.1 %collective-permute-start.20 = (bf16[960,4,128]{2,1,0:T(4,128)(2,1)S(1)}, bf16[960,4,128]{2,1,0:T(4,128)(2,1)S(1)}, u32[]{:S(2)}, u32[]{:S(2)}) collective-permute-start(bf16[960,4,128]{2,1,0:T(4,128)(2,1)S(1)} %collective-permute-done.19.refs_0_), channel_id=1, source_target_pairs={{0,1},{1,0},{2,3},{3,2},{4,5},{5,4},{6,7},{7,6}} | collective-permute-start | bytes 2949128 | tf_op jit(solution)/shard_map/ppermute | solution.py:405
  721.4 8.5 %collective-permute-start.17 = (bf16[960,4,128]{2,1,0:T(4,128)(2,1)S(1)}, bf16[960,4,128]{2,1,0:T(4,128)(2,1)S(1)}, u32[]{:S(2)}, u32[]{:S(2)}) collective-permute-start(bf16[960,4,128]{2,1,0:T(4,128)(2,1)S(1)} %collective-permute-done.16.refs_2_), channel_id=1, source_target_pairs={{0,1},{1,0},{2,3},{3,2},{4,5},{5,4},{6,7},{7,6}} | collective-permute-start | bytes 2949128 | tf_op jit(solution)/shard_map/ppermute | solution.py:405
  726.0 59.3 %collective-permute-start.14 = (bf16[960,4,128]{2,1,0:T(4,128)(2,1)}, bf16[960,4,128]{2,1,0:T(4,128)(2,1)}, u32[]{:S(2)}, u32[]{:S(2)}) collective-permute-start(bf16[960,4,128]{2,1,0:T(4,128)(2,1)} %collective-permute-done.13.refs_0_), channel_id=1, source_target_pairs={{0,1},{1,0},{2,3},{3,2},{4,5},{5,4},{6,7},{7,6}} | collective-permute-start | bytes 2949128 | tf_op jit(solution)/shard_map/ppermute | solution.py:405
  726.9 61.6 %collective-permute-start.8 = (bf16[480,4,128]{2,1,0:T(4,128)(2,1)}, bf16[480,4,128]{2,1,0:T(4,128)(2,1)}, u32[]{:S(2)}, u32[]{:S(2)}) collective-permute-start(bf16[480,4,128]{2,1,0:T(4,128)(2,1)} %collective-permute-done.7.refs_0_), channel_id=1, source_target_pairs={{0,1},{1,0},{2,3},{3,2},{4,5},{5,4},{6,7},{7,6}} | collective-permute-start | bytes 1474568 | tf_op jit(solution)/shard_map/ppermute | solution.py:405
  728.4 60.1 %collective-permute-start.11 = (bf16[240,4,128]{2,1,0:T(4,128)(2,1)}, bf16[240,4,128]{2,1,0:T(4,128)(2,1)}, u32[]{:S(2)}, u32[]{:S(2)}) collective-permute-start(bf16[240,4,128]{2,1,0:T(4,128)(2,1)} %collective-permute-done.10.refs_2_), channel_id=1, source_target_pairs={{0,1},{1,0},{2,3},{3,2},{4,5},{5,4},{6,7},{7,6}} | collective-permute-start | bytes 737288 | tf_op jit(solution)/shard_map/ppermute | solution.py:405
  729.4 61.3 %collective-permute-start.5 = (bf16[240,4,128]{2,1,0:T(4,128)(2,1)}, bf16[240,4,128]{2,1,0:T(4,128)(2,1)}, u32[]{:S(2)}, u32[]{:S(2)}) collective-permute-start(bf16[240,4,128]{2,1,0:T(4,128)(2,1)} %collective-permute-done.4.refs_2_), channel_id=1, source_target_pairs={{0,1},{1,0},{2,3},{3,2},{4,5},{5,4},{6,7},{7,6}} | collective-permute-start | bytes 737288 | tf_op jit(solution)/shard_map/ppermute | solution.py:405
  730.8 59.9 %collective-permute-start.2 = (bf16[240,4,128]{2,1,0:T(4,128)(2,1)}, bf16[240,4,128]{2,1,0:T(4,128)(2,1)}, u32[]{:S(2)}, u32[]{:S(2)}) collective-permute-start(bf16[240,4,128]{2,1,0:T(4,128)(2,1)} %collective-permute-done.1.refs_0_), channel_id=1, source_target_pairs={{0,1},{1,0},{2,3},{3,2},{4,5},{5,4},{6,7},{7,6}} | collective-permute-start | bytes 737288 | tf_op jit(solution)/shard_map/ppermute | solution.py:405
  (130 other events, 837.4 us)

commit v4 on v3

--- a/solution.py
+++ b/solution.py
@@ -35,13 +35,6 @@
     return me, part, along_x, along_y
 
 
-def meet(peers):
-    barrier = pltpu.get_barrier_semaphore()
-    for peer in peers:
-        pl.semaphore_signal(barrier, inc=1, device_id=(peer,), device_id_type=MESH)
-    pl.semaphore_wait(barrier, len(peers))
-
-
 def stay(array):
     return pltpu.with_memory_space_constraint(array, pltpu.VMEM)
 
@@ -70,7 +63,7 @@
 def reduce_kernel(shard_rows, lr, grad, w, m, v, mask, g_out, w_out, m_out, packed, norm_out,
                   own, other, x_send, y_send, x_keep, y_keep, mine, x_recv, y_recv, acc, norm_recv,
                   own_sem, part_ssem, part_rsem, x_ssem, x_rsem, y_ssem, y_rsem, n_ssem, n_rsem,
-                  v_part, mask_part, fetch_sem):
+                  v_part, mask_part, fetch_sem, head, head_sem):
     me, part, along_x, along_y = places()
     diag = along_x + along_y - me
     shift = part - me
@@ -86,6 +79,7 @@
         (w, w_out.at[pl.ds(0, shard_rows)]), (m, m_out.at[pl.ds(0, shard_rows)]),
         (v.at[pl.ds(0, ahead)], v_part), (mask.at[pl.ds(0, ahead)], mask_part)))]
 
+    barrier = pltpu.get_barrier_semaphore()
     acc[...] = jnp.zeros_like(acc)
 
     def loads(i, size):
@@ -134,11 +128,19 @@
         def _():
             do(pl.ds(2, 1))
 
-    for cp in loads(0, full):
+    staged = []
+    for b, block in enumerate(blocks):
+        src = pl.multiple_of((block + shift) * shard_len, LANES)
+        staged.append(pltpu.make_async_copy(grad.at[:, pl.ds(src, full)], head.at[b], head_sem.at[b]))
+    for cp in staged + loads(0, full):
         cp.start()
-    meet(others)
-    for cp in swaps(0, full):
-        cp.start()
+    for peer in (part, along_x, along_y):
+        pl.semaphore_signal(barrier, inc=1, device_id=(peer,), device_id_type=MESH)
+    for cp in staged:
+        cp.wait()
+    pl.semaphore_wait(barrier, 3)
+    for b in range(len(blocks)):
+        remote(head.at[b], other.at[0, b], part_ssem.at[0, b], part_rsem.at[0, b], part).start()
 
     def begin(i):
         def do(size):
@@ -299,7 +301,8 @@
             dma((SLOTS, 4)), dma((SLOTS, 4)), dma((SLOTS, 4)),
             dma((SLOTS,)), dma((SLOTS,)), dma((SLOTS,)), dma((SLOTS,)),
             dma((num_dev - 1,)), dma((num_dev,)),
-            vm((ahead, LANES), f32), vm((ahead, LANES), jnp.int32), dma((4,))],
+            vm((ahead, LANES), f32), vm((ahead, LANES), jnp.int32), dma((4,)),
+            vm(raw[1:], bf16), dma((4,))],
         compiler_params=pltpu.CompilerParams(collective_id=0, has_side_effects=True,
                                              vmem_limit_bytes=VMEM_LIMIT),
     )(lr, grad_row, w, m, v, mask)

time: 794 us -> 794 us (level)
  no operation moved by 1% of the time
where the time goes in v4:
time: 794 us; the launch traced here: 793 us
  Pallas kernels  526 us (66%)
  waiting for transfers between devices  176 us (22%)
  local copies, waits for them, and re-layouts  51.6 us (6%)
  starting transfers between devices  36.8 us (5%)
    pallas_call x1, Pallas kernels, reduce_scatter(): pl.pallas_call(functools.partial(reduce_kernel, shard_rows), out_shape=(s...  426 us
    ppermute x70, waiting for transfers between devices, send(): return lax.ppermute(a, 'dp', hop[along])  176 us
    pallas_call x15, Pallas kernels, store(): pl.pallas_call(functools.partial(store_kernel, [(which, start, min(p.shap...  52.1 us
    unnamed x248, local copies, waits for them, and re-layouts  51.6 us
    pallas_call x10, Pallas kernels, adamw(): pl.pallas_call(adamw_kernel, grid=(steps,), out_shape=(state, state, stat...  48.1 us
    ppermute x70, starting transfers between devices, send(): return lax.ppermute(a, 'dp', hop[along])  36.8 us
  transfers between devices with their start and end apart: 70, of which 23 were waited for; matrix products, arithmetic and copies ran while one was open for 0% of the time, Pallas kernels for 8%

profile of v4, /device:TPU:0, one launch (start us, length us, event | category | flops | bytes accessed | tf_op | source)
XLA Modules:
  0.0 792.8 jit_solution(15150627752325474695)
XLA Ops:
  1.3 426.0 %shard_map.101 = (f32[24960,128]{1,0:T(8,128)S(1)}, f32[24960,128]{1,0:T(8,128)S(1)}, f32[24960,128]{1,0:T(8,128)S(1)}, bf16[480,4,128]{2,1,0:T(4,128)(2,1)S(1)}, f32[8,128]{1,0:T(8,128)}) custom-call(f32[1]{0:T(128)S(6)} %copy.93.lr, bf16[1,25530368]{1,0:T(2,128)(2,1)} %grad.1, f32[24932,128]{1,0:T(8,128)} %bitcast.34, f32[24932,128]{1,0:T(8,128)} %bitcast.35, ...), custom_call_target="tpu_custom_call" | custom-call | tf_op jit(solution)/shard_map/pallas_call | solution.py:292
  427.3 5.8 shard_map.102
  433.1 6.4 shard_map.103
  439.6 6.5 shard_map.104
  446.0 6.4 shard_map.105
  452.5 6.5 shard_map.106
  458.9 3.7 shard_map.107
  462.6 3.0 shard_map.108
  465.6 1.1 collective-permute-start.38
  466.7 1.0 collective-permute-start.9
  467.8 3.0 shard_map.109
  472.7 1.1 collective-permute-done.38.refs_1_
  473.8 1.1 collective-permute-start.24
  475.0 3.1 shard_map.110
  481.5 1.0 collective-permute-start.66
  482.5 12.6 %collective-permute-done.30.refs_1_ = bf16[240,4,128]{2,1,0:T(4,128)(2,1)S(1)} collective-permute-done((bf16[240,4,128]{2,1,0:T(4,128)(2,1)}, bf16[240,4,128]{2,1,0:T(4,128)(2,1)S(1)}, u32[]{:S(2)}, u32[]{:S(2)}) %collective-permute-start.30) | collective-permute-done | bytes 245792 | tf_op jit(solution)/shard_map/ppermute | solution.py:408
  499.8 8.9 %collective-permute-done.6.refs_1_ = bf16[480,4,128]{2,1,0:T(4,128)(2,1)S(1)} collective-permute-done((bf16[480,4,128]{2,1,0:T(4,128)(2,1)S(1)}, bf16[480,4,128]{2,1,0:T(4,128)(2,1)S(1)}, u32[]{:S(2)}, u32[]{:S(2)}) %collective-permute-start.6) | collective-permute-done | bytes 491552 | tf_op jit(solution)/shard_map/ppermute | solution.py:408
  508.8 1.3 collective-permute-done.42.refs_2_
  516.0 1.1 collective-permute-start.62
  519.4 1.1 collective-permute-start.4
  523.6 17.1 %collective-permute-done.10.refs_2_ = bf16[240,4,128]{2,1,0:T(4,128)(2,1)} collective-permute-done((bf16[240,4,128]{2,1,0:T(4,128)(2,1)S(1)}, bf16[240,4,128]{2,1,0:T(4,128)(2,1)}, u32[]{:S(2)}, u32[]{:S(2)}) %collective-permute-start.10) | collective-permute-done | bytes 245792 | tf_op jit(solution)/shard_map/ppermute | solution.py:408
  540.7 1.1 collective-permute-start.18
  541.8 4.2 collective-permute-done.4.refs_2_
  551.0 1.1 collective-permute-start.54
  554.0 13.0 %collective-permute-done.18.refs_1_ = bf16[960,4,128]{2,1,0:T(4,128)(2,1)S(1)} collective-permute-done((bf16[960,4,128]{2,1,0:T(4,128)(2,1)S(1)}, bf16[960,4,128]{2,1,0:T(4,128)(2,1)S(1)}, u32[]{:S(2)}, u32[]{:S(2)}) %collective-permute-start.18) | collective-permute-done | bytes 983072 | tf_op jit(solution)/shard_map/ppermute | solution.py:408
  566.9 3.7 collective-permute-done.58.refs_2_
  570.6 1.1 collective-permute-start.12
  571.7 1.0 collective-permute-start.50
  572.7 15.3 %collective-permute-done.54.refs_1_ = bf16[960,4,128]{2,1,0:T(4,128)(2,1)S(1)} collective-permute-done((bf16[960,4,128]{2,1,0:T(4,128)(2,1)S(1)}, bf16[960,4,128]{2,1,0:T(4,128)(2,1)S(1)}, u32[]{:S(2)}, u32[]{:S(2)}) %collective-permute-start.54) | collective-permute-done | bytes 983072 | tf_op jit(solution)/shard_map/ppermute | solution.py:408
  588.0 3.7 collective-permute-done.21.refs_2_
  591.7 1.1 collective-permute-start.46
  594.8 14.3 %collective-permute-done.12.refs_1_ = bf16[960,4,128]{2,1,0:T(4,128)(2,1)S(1)} collective-permute-done((bf16[960,4,128]{2,1,0:T(4,128)(2,1)S(1)}, bf16[960,4,128]{2,1,0:T(4,128)(2,1)S(1)}, u32[]{:S(2)}, u32[]{:S(2)}) %collective-permute-start.12) | collective-permute-done | bytes 983072 | tf_op jit(solution)/shard_map/ppermute | solution.py:408
  609.1 3.7 collective-permute-done.50.refs_2_
  615.0 14.4 %collective-permute-done.46.refs_1_ = bf16[960,4,128]{2,1,0:T(4,128)(2,1)S(1)} collective-permute-done((bf16[960,4,128]{2,1,0:T(4,128)(2,1)S(1)}, bf16[960,4,128]{2,1,0:T(4,128)(2,1)S(1)}, u32[]{:S(2)}, u32[]{:S(2)}) %collective-permute-start.46) | collective-permute-done | bytes 983072 | tf_op jit(solution)/shard_map/ppermute | solution.py:408
  630.4 1.1 collective-permute-done.15.refs_2_
  636.3 7.4 collective-permute-done.25.refs_0_
  644.6 8.2 %collective-permute-done.7.refs_0_ = bf16[480,4,128]{2,1,0:T(4,128)(2,1)} collective-permute-done((bf16[480,4,128]{2,1,0:T(4,128)(2,1)S(1)}, bf16[480,4,128]{2,1,0:T(4,128)(2,1)}, u32[]{:S(2)}, u32[]{:S(2)}) %collective-permute-start.7) | collective-permute-done | bytes 491552 | tf_op jit(solution)/shard_map/ppermute | solution.py:408
  652.7 1.1 collective-permute-start.28
  658.7 10.9 %collective-permute-done.28.refs_2_ = bf16[720,4,128]{2,1,0:T(4,128)(2,1)S(1)} collective-permute-done((bf16[720,4,128]{2,1,0:T(4,128)(2,1)S(1)}, bf16[720,4,128]{2,1,0:T(4,128)(2,1)S(1)}, u32[]{:S(2)}, u32[]{:S(2)}) %collective-permute-start.28) | collective-permute-done | bytes 737312 | tf_op jit(solution)/shard_map/ppermute | solution.py:408
  676.4 1.1 collective-permute-start.22
  687.2 13.8 %collective-permute-done.22.refs_2_ = bf16[960,4,128]{2,1,0:T(4,128)(2,1)S(1)} collective-permute-done((bf16[960,4,128]{2,1,0:T(4,128)(2,1)S(1)}, bf16[960,4,128]{2,1,0:T(4,128)(2,1)S(1)}, u32[]{:S(2)}, u32[]{:S(2)}) %collective-permute-start.22) | collective-permute-done | bytes 983072 | tf_op jit(solution)/shard_map/ppermute | solution.py:408
  706.0 15.1 %collective-permute-done.16.refs_2_ = bf16[960,4,128]{2,1,0:T(4,128)(2,1)S(1)} collective-permute-done((bf16[960,4,128]{2,1,0:T(4,128)(2,1)S(1)}, bf16[960,4,128]{2,1,0:T(4,128)(2,1)S(1)}, u32[]{:S(2)}, u32[]{:S(2)}) %collective-permute-start.16) | collective-permute-done | bytes 983072 | tf_op jit(solution)/shard_map/ppermute | solution.py:408
  722.1 3.6 collective-permute-done.13.refs_0_
  730.6 3.7 shard_map.126
  734.3 1.0 copy-done.82
  735.3 1.0 copy-done.84
  736.3 1.0 copy-done.86
  737.4 1.0 copy-done.88
  738.4 1.0 copy-done.90
  739.5 3.3 shard_map.111.refs_6_
  742.8 4.1 shard_map.112.refs_6_
  747.0 4.5 shard_map.113.refs_6_
  751.6 4.5 shard_map.114.refs_6_
  756.2 4.5 shard_map.115.refs_6_
  760.9 4.5 shard_map.116.refs_6_
  765.5 3.6 shard_map.117.refs_6_
  769.3 3.1 shard_map.118.refs_6_
  772.5 3.1 shard_map.119.refs_6_
  775.7 3.0 shard_map.120.refs_4_
  778.9 2.8 shard_map.121.refs_4_
  781.7 3.2 shard_map.122.refs_4_
  785.0 3.2 shard_map.123.refs_4_
  788.2 2.2 shard_map.124.refs_4_
  790.4 2.3 shard_map.125
  (350 shorter events, 71.5 us)
Async XLA Ops:
  465.6 8.2 %collective-permute-start.38 = (bf16[240,4,128]{2,1,0:T(4,128)(2,1)}, bf16[240,4,128]{2,1,0:T(4,128)(2,1)S(1)}, u32[]{:S(2)}, u32[]{:S(2)}) collective-permute-start(bf16[240,4,128]{2,1,0:T(4,128)(2,1)} %get-tuple-element.81.refs_0_), channel_id=1, source_target_pairs={{0,2},{1,3},{2,0},{3,1},{4,6},{5,7},{6,4},{7,5}} | collective-permute-start | bytes 737288 | tf_op jit(solution)/shard_map/ppermute | solution.py:408
  466.7 8.2 %collective-permute-start.9 = (bf16[240,4,128]{2,1,0:T(4,128)(2,1)}, bf16[240,4,128]{2,1,0:T(4,128)(2,1)S(1)}, u32[]{:S(2)}, u32[]{:S(2)}) collective-permute-start(bf16[240,4,128]{2,1,0:T(4,128)(2,1)} %get-tuple-element.81.refs_0_), channel_id=1, source_target_pairs={{0,4},{1,5},{2,6},{3,7},{4,0},{5,1},{6,2},{7,3}} | collective-permute-start | bytes 737288 | tf_op jit(solution)/shard_map/ppermute | solution.py:408
  467.8 10.4 %collective-permute-start.39 = (bf16[240,4,128]{2,1,0:T(4,128)(2,1)}, bf16[240,4,128]{2,1,0:T(4,128)(2,1)S(1)}, u32[]{:S(2)}, u32[]{:S(2)}) collective-permute-start(bf16[240,4,128]{2,1,0:T(4,128)(2,1)} %get-tuple-element.81.refs_0_), channel_id=1, source_target_pairs={{0,1},{1,0},{2,3},{3,2},{4,5},{5,4},{6,7},{7,6}} | collective-permute-start | bytes 737288 | tf_op jit(solution)/shard_map/ppermute | solution.py:408
  470.7 9.1 %collective-permute-start = (bf16[240,4,128]{2,1,0:T(4,128)(2,1)}, bf16[240,4,128]{2,1,0:T(4,128)(2,1)S(1)}, u32[]{:S(2)}, u32[]{:S(2)}) collective-permute-start(bf16[240,4,128]{2,1,0:T(4,128)(2,1)} %get-tuple-element.75.refs_0_), channel_id=1, source_target_pairs={{0,2},{1,3},{2,0},{3,1},{4,6},{5,7},{6,4},{7,5}} | collective-permute-start | bytes 737288 | tf_op jit(solution)/shard_map/ppermute | solution.py:408
  471.7 9.1 %collective-permute-start.34 = (bf16[240,4,128]{2,1,0:T(4,128)(2,1)}, bf16[240,4,128]{2,1,0:T(4,128)(2,1)S(1)}, u32[]{:S(2)}, u32[]{:S(2)}) collective-permute-start(bf16[240,4,128]{2,1,0:T(4,128)(2,1)} %get-tuple-element.75.refs_0_), channel_id=1, source_target_pairs={{0,4},{1,5},{2,6},{3,7},{4,0},{5,1},{6,2},{7,3}} | collective-permute-start | bytes 737288 | tf_op jit(solution)/shard_map/ppermute | solution.py:408
  473.8 24.0 %collective-permute-start.24 = (bf16[480,4,128]{2,1,0:T(4,128)(2,1)S(1)}, bf16[480,4,128]{2,1,0:T(4,128)(2,1)}, u32[]{:S(2)}, u32[]{:S(2)}) collective-permute-start(bf16[480,4,128]{2,1,0:T(4,128)(2,1)S(1)} %get-tuple-element.86.refs_0_), channel_id=1, source_target_pairs={{0,2},{1,3},{2,0},{3,1},{4,6},{5,7},{6,4},{7,5}} | collective-permute-start | bytes 1474568 | tf_op jit(solution)/shard_map/ppermute | solution.py:408
  478.8 16.3 %collective-permute-start.30 = (bf16[240,4,128]{2,1,0:T(4,128)(2,1)}, bf16[240,4,128]{2,1,0:T(4,128)(2,1)S(1)}, u32[]{:S(2)}, u32[]{:S(2)}) collective-permute-start(bf16[240,4,128]{2,1,0:T(4,128)(2,1)} %get-tuple-element.79.refs_0_), channel_id=1, source_target_pairs={{0,2},{1,3},{2,0},{3,1},{4,6},{5,7},{6,4},{7,5}} | collective-permute-start | bytes 737288 | tf_op jit(solution)/shard_map/ppermute | solution.py:408
  479.8 15.3 %collective-permute-start.3 = (bf16[240,4,128]{2,1,0:T(4,128)(2,1)}, bf16[240,4,128]{2,1,0:T(4,128)(2,1)S(1)}, u32[]{:S(2)}, u32[]{:S(2)}) collective-permute-start(bf16[240,4,128]{2,1,0:T(4,128)(2,1)} %get-tuple-element.79.refs_0_), channel_id=1, source_target_pairs={{0,4},{1,5},{2,6},{3,7},{4,0},{5,1},{6,2},{7,3}} | collective-permute-start | bytes 737288 | tf_op jit(solution)/shard_map/ppermute | solution.py:408
  480.8 15.3 %collective-permute-start.31 = (bf16[240,4,128]{2,1,0:T(4,128)(2,1)}, bf16[240,4,128]{2,1,0:T(4,128)(2,1)S(1)}, u32[]{:S(2)}, u32[]{:S(2)}) collective-permute-start(bf16[240,4,128]{2,1,0:T(4,128)(2,1)} %get-tuple-element.79.refs_0_), channel_id=1, source_target_pairs={{0,1},{1,0},{2,3},{3,2},{4,5},{5,4},{6,7},{7,6}} | collective-permute-start | bytes 737288 | tf_op jit(solution)/shard_map/ppermute | solution.py:408
  481.5 17.0 %collective-permute-start.66 = (bf16[480,4,128]{2,1,0:T(4,128)(2,1)S(1)}, bf16[480,4,128]{2,1,0:T(4,128)(2,1)S(1)}, u32[]{:S(2)}, u32[]{:S(2)}) collective-permute-start(bf16[480,4,128]{2,1,0:T(4,128)(2,1)S(1)} %get-tuple-element.86.refs_0_), channel_id=1, source_target_pairs={{0,4},{1,5},{2,6},{3,7},{4,0},{5,1},{6,2},{7,3}} | collective-permute-start | bytes 1474568 | tf_op jit(solution)/shard_map/ppermute | solution.py:408
  495.2 13.6 %collective-permute-start.6 = (bf16[480,4,128]{2,1,0:T(4,128)(2,1)S(1)}, bf16[480,4,128]{2,1,0:T(4,128)(2,1)S(1)}, u32[]{:S(2)}, u32[]{:S(2)}) collective-permute-start(bf16[480,4,128]{2,1,0:T(4,128)(2,1)S(1)} %copy-done.65), channel_id=1, source_target_pairs={{0,2},{1,3},{2,0},{3,1},{4,6},{5,7},{6,4},{7,5}} | collective-permute-start | bytes 1474568 | tf_op jit(solution)/shard_map/ppermute | solution.py:408
  496.8 13.3 %collective-permute-start.42 = (bf16[480,4,128]{2,1,0:T(4,128)(2,1)S(1)}, bf16[480,4,128]{2,1,0:T(4,128)(2,1)S(1)}, u32[]{:S(2)}, u32[]{:S(2)}) collective-permute-start(bf16[480,4,128]{2,1,0:T(4,128)(2,1)S(1)} %copy-done.65), channel_id=1, source_target_pairs={{0,4},{1,5},{2,6},{3,7},{4,0},{5,1},{6,2},{7,3}} | collective-permute-start | bytes 1474568 | tf_op jit(solution)/shard_map/ppermute | solution.py:408
  497.8 13.0 %collective-permute-start.43 = (bf16[480,4,128]{2,1,0:T(4,128)(2,1)S(1)}, bf16[480,4,128]{2,1,0:T(4,128)(2,1)S(1)}, u32[]{:S(2)}, u32[]{:S(2)}) collective-permute-start(bf16[480,4,128]{2,1,0:T(4,128)(2,1)S(1)} %copy-done.65), channel_id=1, source_target_pairs={{0,1},{1,0},{2,3},{3,2},{4,5},{5,4},{6,7},{7,6}} | collective-permute-start | bytes 1474568 | tf_op jit(solution)/shard_map/ppermute | solution.py:408
  498.5 14.3 %collective-permute-start.40 = (bf16[240,4,128]{2,1,0:T(4,128)(2,1)S(1)}, bf16[240,4,128]{2,1,0:T(4,128)(2,1)S(1)}, u32[]{:S(2)}, u32[]{:S(2)}) collective-permute-start(bf16[240,4,128]{2,1,0:T(4,128)(2,1)S(1)} %collective-permute-done.38.refs_1_), channel_id=1, source_target_pairs={{0,1},{1,0},{2,3},{3,2},{4,5},{5,4},{6,7},{7,6}} | collective-permute-start | bytes 737288 | tf_op jit(solution)/shard_map/ppermute | solution.py:408
  499.3 14.2 %collective-permute-start.41 = (bf16[240,4,128]{2,1,0:T(4,128)(2,1)S(1)}, bf16[240,4,128]{2,1,0:T(4,128)(2,1)S(1)}, u32[]{:S(2)}, u32[]{:S(2)}) collective-permute-start(bf16[240,4,128]{2,1,0:T(4,128)(2,1)S(1)} %collective-permute-done.9.refs_2_), channel_id=1, source_target_pairs={{0,1},{1,0},{2,3},{3,2},{4,5},{5,4},{6,7},{7,6}} | collective-permute-start | bytes 737288 | tf_op jit(solution)/shard_map/ppermute | solution.py:408
  510.1 7.0 collective-permute-start.37
  511.6 7.1 collective-permute-start.32
  513.5 7.7 collective-permute-start.33
  514.2 32.8 %collective-permute-start.27 = (bf16[720,4,128]{2,1,0:T(4,128)(2,1)S(1)}, bf16[720,4,128]{2,1,0:T(4,128)(2,1)S(1)}, u32[]{:S(2)}, u32[]{:S(2)}) collective-permute-start(bf16[720,4,128]{2,1,0:T(4,128)(2,1)S(1)} %copy-done.50), channel_id=1, source_target_pairs={{0,4},{1,5},{2,6},{3,7},{4,0},{5,1},{6,2},{7,3}} | collective-permute-start | bytes 2211848 | tf_op jit(solution)/shard_map/ppermute | solution.py:408
  516.0 31.5 %collective-permute-start.62 = (bf16[720,4,128]{2,1,0:T(4,128)(2,1)S(1)}, bf16[720,4,128]{2,1,0:T(4,128)(2,1)S(1)}, u32[]{:S(2)}, u32[]{:S(2)}) collective-permute-start(bf16[720,4,128]{2,1,0:T(4,128)(2,1)S(1)} %copy-done.50), channel_id=1, source_target_pairs={{0,2},{1,3},{2,0},{3,1},{4,6},{5,7},{6,4},{7,5}} | collective-permute-start | bytes 2211848 | tf_op jit(solution)/shard_map/ppermute | solution.py:408
  517.8 22.9 %collective-permute-start.10 = (bf16[240,4,128]{2,1,0:T(4,128)(2,1)S(1)}, bf16[240,4,128]{2,1,0:T(4,128)(2,1)}, u32[]{:S(2)}, u32[]{:S(2)}) collective-permute-start(bf16[240,4,128]{2,1,0:T(4,128)(2,1)S(1)} %collective-permute-done.9.refs_2_), channel_id=1, source_target_pairs={{0,2},{1,3},{2,0},{3,1},{4,6},{5,7},{6,4},{7,5}} | collective-permute-start | bytes 737288 | tf_op jit(solution)/shard_map/ppermute | solution.py:408
  519.4 26.5 %collective-permute-start.4 = (bf16[240,4,128]{2,1,0:T(4,128)(2,1)S(1)}, bf16[240,4,128]{2,1,0:T(4,128)(2,1)}, u32[]{:S(2)}, u32[]{:S(2)}) collective-permute-start(bf16[240,4,128]{2,1,0:T(4,128)(2,1)S(1)} %collective-permute-done.3.refs_2_), channel_id=1, source_target_pairs={{0,2},{1,3},{2,0},{3,1},{4,6},{5,7},{6,4},{7,5}} | collective-permute-start | bytes 737288 | tf_op jit(solution)/shard_map/ppermute | solution.py:408
  521.9 25.1 %collective-permute-start.1 = (bf16[240,4,128]{2,1,0:T(4,128)(2,1)S(1)}, bf16[240,4,128]{2,1,0:T(4,128)(2,1)}, u32[]{:S(2)}, u32[]{:S(2)}) collective-permute-start(bf16[240,4,128]{2,1,0:T(4,128)(2,1)S(1)} %collective-permute-done.refs_1_), channel_id=1, source_target_pairs={{0,4},{1,5},{2,6},{3,7},{4,0},{5,1},{6,2},{7,3}} | collective-permute-start | bytes 737288 | tf_op jit(solution)/shard_map/ppermute | solution.py:408
  540.7 26.2 %collective-permute-start.18 = (bf16[960,4,128]{2,1,0:T(4,128)(2,1)S(1)}, bf16[960,4,128]{2,1,0:T(4,128)(2,1)S(1)}, u32[]{:S(2)}, u32[]{:S(2)}) collective-permute-start(bf16[960,4,128]{2,1,0:T(4,128)(2,1)S(1)} %copy-done), channel_id=1, source_target_pairs={{0,2},{1,3},{2,0},{3,1},{4,6},{5,7},{6,4},{7,5}} | collective-permute-start | bytes 2949128 | tf_op jit(solution)/shard_map/ppermute | solution.py:408
  546.0 24.6 %collective-permute-start.58 = (bf16[960,4,128]{2,1,0:T(4,128)(2,1)S(1)}, bf16[960,4,128]{2,1,0:T(4,128)(2,1)S(1)}, u32[]{:S(2)}, u32[]{:S(2)}) collective-permute-start(bf16[960,4,128]{2,1,0:T(4,128)(2,1)S(1)} %copy-done), channel_id=1, source_target_pairs={{0,4},{1,5},{2,6},{3,7},{4,0},{5,1},{6,2},{7,3}} | collective-permute-start | bytes 2949128 | tf_op jit(solution)/shard_map/ppermute | solution.py:408
  550.1 21.6 %collective-permute-start.59 = (bf16[960,4,128]{2,1,0:T(4,128)(2,1)S(1)}, bf16[960,4,128]{2,1,0:T(4,128)(2,1)S(1)}, u32[]{:S(2)}, u32[]{:S(2)}) collective-permute-start(bf16[960,4,128]{2,1,0:T(4,128)(2,1)S(1)} %copy-done), channel_id=1, source_target_pairs={{0,1},{1,0},{2,3},{3,2},{4,5},{5,4},{6,7},{7,6}} | collective-permute-start | bytes 2949128 | tf_op jit(solution)/shard_map/ppermute | solution.py:408
  551.0 37.0 %collective-permute-start.54 = (bf16[960,4,128]{2,1,0:T(4,128)(2,1)S(1)}, bf16[960,4,128]{2,1,0:T(4,128)(2,1)S(1)}, u32[]{:S(2)}, u32[]{:S(2)}) collective-permute-start(bf16[960,4,128]{2,1,0:T(4,128)(2,1)S(1)} %copy-done.1), channel_id=1, source_target_pairs={{0,2},{1,3},{2,0},{3,1},{4,6},{5,7},{6,4},{7,5}} | collective-permute-start | bytes 2949128 | tf_op jit(solution)/shard_map/ppermute | solution.py:408
  553.0 38.7 %collective-permute-start.21 = (bf16[960,4,128]{2,1,0:T(4,128)(2,1)S(1)}, bf16[960,4,128]{2,1,0:T(4,128)(2,1)S(1)}, u32[]{:S(2)}, u32[]{:S(2)}) collective-permute-start(bf16[960,4,128]{2,1,0:T(4,128)(2,1)S(1)} %copy-done.1), channel_id=1, source_target_pairs={{0,4},{1,5},{2,6},{3,7},{4,0},{5,1},{6,2},{7,3}} | collective-permute-start | bytes 2949128 | tf_op jit(solution)/shard_map/ppermute | solution.py:408
  566.9 25.8 %collective-permute-start.55 = (bf16[960,4,128]{2,1,0:T(4,128)(2,1)S(1)}, bf16[960,4,128]{2,1,0:T(4,128)(2,1)S(1)}, u32[]{:S(2)}, u32[]{:S(2)}) collective-permute-start(bf16[960,4,128]{2,1,0:T(4,128)(2,1)S(1)} %copy-done.1), channel_id=1, source_target_pairs={{0,1},{1,0},{2,3},{3,2},{4,5},{5,4},{6,7},{7,6}} | collective-permute-start | bytes 2949128 | tf_op jit(solution)/shard_map/ppermute | solution.py:408
  570.6 38.5 %collective-permute-start.12 = (bf16[960,4,128]{2,1,0:T(4,128)(2,1)S(1)}, bf16[960,4,128]{2,1,0:T(4,128)(2,1)S(1)}, u32[]{:S(2)}, u32[]{:S(2)}) collective-permute-start(bf16[960,4,128]{2,1,0:T(4,128)(2,1)S(1)} %copy-done.2), channel_id=1, source_target_pairs={{0,2},{1,3},{2,0},{3,1},{4,6},{5,7},{6,4},{7,5}} | collective-permute-start | bytes 2949128 | tf_op jit(solution)/shard_map/ppermute | solution.py:408
  571.7 41.0 %collective-permute-start.50 = (bf16[960,4,128]{2,1,0:T(4,128)(2,1)S(1)}, bf16[960,4,128]{2,1,0:T(4,128)(2,1)S(1)}, u32[]{:S(2)}, u32[]{:S(2)}) collective-permute-start(bf16[960,4,128]{2,1,0:T(4,128)(2,1)S(1)} %copy-done.2), channel_id=1, source_target_pairs={{0,4},{1,5},{2,6},{3,7},{4,0},{5,1},{6,2},{7,3}} | collective-permute-start | bytes 2949128 | tf_op jit(solution)/shard_map/ppermute | solution.py:408
  588.0 24.7 %collective-permute-start.51 = (bf16[960,4,128]{2,1,0:T(4,128)(2,1)S(1)}, bf16[960,4,128]{2,1,0:T(4,128)(2,1)S(1)}, u32[]{:S(2)}, u32[]{:S(2)}) collective-permute-start(bf16[960,4,128]{2,1,0:T(4,128)(2,1)S(1)} %copy-done.2), channel_id=1, source_target_pairs={{0,1},{1,0},{2,3},{3,2},{4,5},{5,4},{6,7},{7,6}} | collective-permute-start | bytes 2949128 | tf_op jit(solution)/shard_map/ppermute | solution.py:408
  591.7 37.7 %collective-permute-start.46 = (bf16[960,4,128]{2,1,0:T(4,128)(2,1)S(1)}, bf16[960,4,128]{2,1,0:T(4,128)(2,1)S(1)}, u32[]{:S(2)}, u32[]{:S(2)}) collective-permute-start(bf16[960,4,128]{2,1,0:T(4,128)(2,1)S(1)} %copy-done.3), channel_id=1, source_target_pairs={{0,2},{1,3},{2,0},{3,1},{4,6},{5,7},{6,4},{7,5}} | collective-permute-start | bytes 2949128 | tf_op jit(solution)/shard_map/ppermute | solution.py:408
  593.8 37.7 %collective-permute-start.15 = (bf16[960,4,128]{2,1,0:T(4,128)(2,1)S(1)}, bf16[960,4,128]{2,1,0:T(4,128)(2,1)S(1)}, u32[]{:S(2)}, u32[]{:S(2)}) collective-permute-start(bf16[960,4,128]{2,1,0:T(4,128)(2,1)S(1)} %copy-done.3), channel_id=1, source_target_pairs={{0,4},{1,5},{2,6},{3,7},{4,0},{5,1},{6,2},{7,3}} | collective-permute-start | bytes 2949128 | tf_op jit(solution)/shard_map/ppermute | solution.py:408
  609.1 24.2 %collective-permute-start.47 = (bf16[960,4,128]{2,1,0:T(4,128)(2,1)S(1)}, bf16[960,4,128]{2,1,0:T(4,128)(2,1)S(1)}, u32[]{:S(2)}, u32[]{:S(2)}) collective-permute-start(bf16[960,4,128]{2,1,0:T(4,128)(2,1)S(1)} %copy-done.3), channel_id=1, source_target_pairs={{0,1},{1,0},{2,3},{3,2},{4,5},{5,4},{6,7},{7,6}} | collective-permute-start | bytes 2949128 | tf_op jit(solution)/shard_map/ppermute | solution.py:408
  612.7 21.5 %collective-permute-start.44 = (bf16[480,4,128]{2,1,0:T(4,128)(2,1)S(1)}, bf16[480,4,128]{2,1,0:T(4,128)(2,1)S(1)}, u32[]{:S(2)}, u32[]{:S(2)}) collective-permute-start(bf16[480,4,128]{2,1,0:T(4,128)(2,1)S(1)} %collective-permute-done.6.refs_1_), channel_id=1, source_target_pairs={{0,1},{1,0},{2,3},{3,2},{4,5},{5,4},{6,7},{7,6}} | collective-permute-start | bytes 1474568 | tf_op jit(solution)/shard_map/ppermute | solution.py:408
  613.7 21.8 %collective-permute-start.45 = (bf16[480,4,128]{2,1,0:T(4,128)(2,1)S(1)}, bf16[480,4,128]{2,1,0:T(4,128)(2,1)S(1)}, u32[]{:S(2)}, u32[]{:S(2)}) collective-permute-start(bf16[480,4,128]{2,1,0:T(4,128)(2,1)S(1)} %collective-permute-done.42.refs_2_), channel_id=1, source_target_pairs={{0,1},{1,0},{2,3},{3,2},{4,5},{5,4},{6,7},{7,6}} | collective-permute-start | bytes 1474568 | tf_op jit(solution)/shard_map/ppermute | solution.py:408
  629.4 14.3 %collective-permute-start.25 = (bf16[480,4,128]{2,1,0:T(4,128)(2,1)}, bf16[480,4,128]{2,1,0:T(4,128)(2,1)S(1)}, u32[]{:S(2)}, u32[]{:S(2)}) collective-permute-start(bf16[480,4,128]{2,1,0:T(4,128)(2,1)} %collective-permute-done.24.refs_1_), channel_id=1, source_target_pairs={{0,4},{1,5},{2,6},{3,7},{4,0},{5,1},{6,2},{7,3}} | collective-permute-start | bytes 1474568 | tf_op jit(solution)/shard_map/ppermute | solution.py:408
  631.5 21.3 %collective-permute-start.7 = (bf16[480,4,128]{2,1,0:T(4,128)(2,1)S(1)}, bf16[480,4,128]{2,1,0:T(4,128)(2,1)}, u32[]{:S(2)}, u32[]{:S(2)}) collective-permute-start(bf16[480,4,128]{2,1,0:T(4,128)(2,1)S(1)} %collective-permute-done.6.refs_1_), channel_id=1, source_target_pairs={{0,4},{1,5},{2,6},{3,7},{4,0},{5,1},{6,2},{7,3}} | collective-permute-start | bytes 1474568 | tf_op jit(solution)/shard_map/ppermute | solution.py:408
  634.2 20.5 %collective-permute-start.65 = (bf16[720,4,128]{2,1,0:T(4,128)(2,1)S(1)}, bf16[720,4,128]{2,1,0:T(4,128)(2,1)S(1)}, u32[]{:S(2)}, u32[]{:S(2)}) collective-permute-start(bf16[720,4,128]{2,1,0:T(4,128)(2,1)S(1)} %collective-permute-done.27.refs_2_), channel_id=1, source_target_pairs={{0,1},{1,0},{2,3},{3,2},{4,5},{5,4},{6,7},{7,6}} | collective-permute-start | bytes 2211848 | tf_op jit(solution)/shard_map/ppermute | solution.py:408
  635.0 35.9 %collective-permute-start.60 = (bf16[960,4,128]{2,1,0:T(4,128)(2,1)S(1)}, bf16[960,4,128]{2,1,0:T(4,128)(2,1)S(1)}, u32[]{:S(2)}, u32[]{:S(2)}) collective-permute-start(bf16[960,4,128]{2,1,0:T(4,128)(2,1)S(1)} %collective-permute-done.18.refs_1_), channel_id=1, source_target_pairs={{0,1},{1,0},{2,3},{3,2},{4,5},{5,4},{6,7},{7,6}} | collective-permute-start | bytes 2949128 | tf_op jit(solution)/shard_map/ppermute | solution.py:408
  636.3 36.6 %collective-permute-start.61 = (bf16[960,4,128]{2,1,0:T(4,128)(2,1)S(1)}, bf16[960,4,128]{2,1,0:T(4,128)(2,1)S(1)}, u32[]{:S(2)}, u32[]{:S(2)}) collective-permute-start(bf16[960,4,128]{2,1,0:T(4,128)(2,1)S(1)} %collective-permute-done.58.refs_2_), channel_id=1, source_target_pairs={{0,1},{1,0},{2,3},{3,2},{4,5},{5,4},{6,7},{7,6}} | collective-permute-start | bytes 2949128 | tf_op jit(solution)/shard_map/ppermute | solution.py:408
  643.7 12.7 %collective-permute-start.64 = (bf16[720,4,128]{2,1,0:T(4,128)(2,1)S(1)}, bf16[720,4,128]{2,1,0:T(4,128)(2,1)S(1)}, u32[]{:S(2)}, u32[]{:S(2)}) collective-permute-start(bf16[720,4,128]{2,1,0:T(4,128)(2,1)S(1)} %collective-permute-done.62.refs_1_), channel_id=1, source_target_pairs={{0,1},{1,0},{2,3},{3,2},{4,5},{5,4},{6,7},{7,6}} | collective-permute-start | bytes 2211848 | tf_op jit(solution)/shard_map/ppermute | solution.py:408
  652.7 16.9 %collective-permute-start.28 = (bf16[720,4,128]{2,1,0:T(4,128)(2,1)S(1)}, bf16[720,4,128]{2,1,0:T(4,128)(2,1)S(1)}, u32[]{:S(2)}, u32[]{:S(2)}) collective-permute-start(bf16[720,4,128]{2,1,0:T(4,128)(2,1)S(1)} %collective-permute-done.27.refs_2_), channel_id=1, source_target_pairs={{0,2},{1,3},{2,0},{3,1},{4,6},{5,7},{6,4},{7,5}} | collective-permute-start | bytes 2211848 | tf_op jit(solution)/shard_map/ppermute | solution.py:408
  655.6 14.1 %collective-permute-start.26 = (bf16[480,4,128]{2,1,0:T(4,128)(2,1)S(1)}, bf16[480,4,128]{2,1,0:T(4,128)(2,1)S(1)}, u32[]{:S(2)}, u32[]{:S(2)}) collective-permute-start(bf16[480,4,128]{2,1,0:T(4,128)(2,1)S(1)} %collective-permute-done.25.refs_0_), channel_id=1, source_target_pairs={{0,1},{1,0},{2,3},{3,2},{4,5},{5,4},{6,7},{7,6}} | collective-permute-start | bytes 1474568 | tf_op jit(solution)/shard_map/ppermute | solution.py:408
  657.2 18.1 %collective-permute-start.56 = (bf16[960,4,128]{2,1,0:T(4,128)(2,1)S(1)}, bf16[960,4,128]{2,1,0:T(4,128)(2,1)S(1)}, u32[]{:S(2)}, u32[]{:S(2)}) collective-permute-start(bf16[960,4,128]{2,1,0:T(4,128)(2,1)S(1)} %collective-permute-done.54.refs_1_), channel_id=1, source_target_pairs={{0,1},{1,0},{2,3},{3,2},{4,5},{5,4},{6,7},{7,6}} | collective-permute-start | bytes 2949128 | tf_op jit(solution)/shard_map/ppermute | solution.py:408
  669.7 8.8 %collective-permute-start.57 = (bf16[960,4,128]{2,1,0:T(4,128)(2,1)S(1)}, bf16[960,4,128]{2,1,0:T(4,128)(2,1)S(1)}, u32[]{:S(2)}, u32[]{:S(2)}) collective-permute-start(bf16[960,4,128]{2,1,0:T(4,128)(2,1)S(1)} %collective-permute-done.21.refs_2_), channel_id=1, source_target_pairs={{0,1},{1,0},{2,3},{3,2},{4,5},{5,4},{6,7},{7,6}} | collective-permute-start | bytes 2949128 | tf_op jit(solution)/shard_map/ppermute | solution.py:408
  670.5 9.0 %collective-permute-start.52 = (bf16[960,4,128]{2,1,0:T(4,128)(2,1)S(1)}, bf16[960,4,128]{2,1,0:T(4,128)(2,1)S(1)}, u32[]{:S(2)}, u32[]{:S(2)}) collective-permute-start(bf16[960,4,128]{2,1,0:T(4,128)(2,1)S(1)} %collective-permute-done.12.refs_1_), channel_id=1, source_target_pairs={{0,1},{1,0},{2,3},{3,2},{4,5},{5,4},{6,7},{7,6}} | collective-permute-start | bytes 2949128 | tf_op jit(solution)/shard_map/ppermute | solution.py:408
  671.9 9.5 %collective-permute-start.53 = (bf16[960,4,128]{2,1,0:T(4,128)(2,1)S(1)}, bf16[960,4,128]{2,1,0:T(4,128)(2,1)S(1)}, u32[]{:S(2)}, u32[]{:S(2)}) collective-permute-start(bf16[960,4,128]{2,1,0:T(4,128)(2,1)S(1)} %collective-permute-done.50.refs_2_), channel_id=1, source_target_pairs={{0,1},{1,0},{2,3},{3,2},{4,5},{5,4},{6,7},{7,6}} | collective-permute-start | bytes 2949128 | tf_op jit(solution)/shard_map/ppermute | solution.py:408
  673.9 10.3 %collective-permute-start.48 = (bf16[960,4,128]{2,1,0:T(4,128)(2,1)S(1)}, bf16[960,4,128]{2,1,0:T(4,128)(2,1)S(1)}, u32[]{:S(2)}, u32[]{:S(2)}) collective-permute-start(bf16[960,4,128]{2,1,0:T(4,128)(2,1)S(1)} %collective-permute-done.46.refs_1_), channel_id=1, source_target_pairs={{0,1},{1,0},{2,3},{3,2},{4,5},{5,4},{6,7},{7,6}} | collective-permute-start | bytes 2949128 | tf_op jit(solution)/shard_map/ppermute | solution.py:408
  676.4 24.6 %collective-permute-start.22 = (bf16[960,4,128]{2,1,0:T(4,128)(2,1)S(1)}, bf16[960,4,128]{2,1,0:T(4,128)(2,1)S(1)}, u32[]{:S(2)}, u32[]{:S(2)}) collective-permute-start(bf16[960,4,128]{2,1,0:T(4,128)(2,1)S(1)} %collective-permute-done.21.refs_2_), channel_id=1, source_target_pairs={{0,2},{1,3},{2,0},{3,1},{4,6},{5,7},{6,4},{7,5}} | collective-permute-start | bytes 2949128 | tf_op jit(solution)/shard_map/ppermute | solution.py:408
  679.4 22.6 %collective-permute-start.49 = (bf16[960,4,128]{2,1,0:T(4,128)(2,1)S(1)}, bf16[960,4,128]{2,1,0:T(4,128)(2,1)S(1)}, u32[]{:S(2)}, u32[]{:S(2)}) collective-permute-start(bf16[960,4,128]{2,1,0:T(4,128)(2,1)S(1)} %collective-permute-done.15.refs_2_), channel_id=1, source_target_pairs={{0,1},{1,0},{2,3},{3,2},{4,5},{5,4},{6,7},{7,6}} | collective-permute-start | bytes 2949128 | tf_op jit(solution)/shard_map/ppermute | solution.py:408
  680.4 24.6 %collective-permute-start.19 = (bf16[960,4,128]{2,1,0:T(4,128)(2,1)S(1)}, bf16[960,4,128]{2,1,0:T(4,128)(2,1)S(1)}, u32[]{:S(2)}, u32[]{:S(2)}) collective-permute-start(bf16[960,4,128]{2,1,0:T(4,128)(2,1)S(1)} %collective-permute-done.18.refs_1_), channel_id=1, source_target_pairs={{0,4},{1,5},{2,6},{3,7},{4,0},{5,1},{6,2},{7,3}} | collective-permute-start | bytes 2949128 | tf_op jit(solution)/shard_map/ppermute | solution.py:408
  682.4 38.7 %collective-permute-start.16 = (bf16[960,4,128]{2,1,0:T(4,128)(2,1)S(1)}, bf16[960,4,128]{2,1,0:T(4,128)(2,1)S(1)}, u32[]{:S(2)}, u32[]{:S(2)}) collective-permute-start(bf16[960,4,128]{2,1,0:T(4,128)(2,1)S(1)} %collective-permute-done.15.refs_2_), channel_id=1, source_target_pairs={{0,2},{1,3},{2,0},{3,1},{4,6},{5,7},{6,4},{7,5}} | collective-permute-start | bytes 2949128 | tf_op jit(solution)/shard_map/ppermute | solution.py:408
  685.2 40.5 %collective-permute-start.13 = (bf16[960,4,128]{2,1,0:T(4,128)(2,1)S(1)}, bf16[960,4,128]{2,1,0:T(4,128)(2,1)}, u32[]{:S(2)}, u32[]{:S(2)}) collective-permute-start(bf16[960,4,128]{2,1,0:T(4,128)(2,1)S(1)} %collective-permute-done.12.refs_1_), channel_id=1, source_target_pairs={{0,4},{1,5},{2,6},{3,7},{4,0},{5,1},{6,2},{7,3}} | collective-permute-start | bytes 2949128 | tf_op jit(solution)/shard_map/ppermute | solution.py:408
  701.0 26.1 %collective-permute-start.23 = (bf16[960,4,128]{2,1,0:T(4,128)(2,1)S(1)}, bf16[960,4,128]{2,1,0:T(4,128)(2,1)S(1)}, u32[]{:S(2)}, u32[]{:S(2)}) collective-permute-start(bf16[960,4,128]{2,1,0:T(4,128)(2,1)S(1)} %collective-permute-done.22.refs_2_), channel_id=1, source_target_pairs={{0,1},{1,0},{2,3},{3,2},{4,5},{5,4},{6,7},{7,6}} | collective-permute-start | bytes 2949128 | tf_op jit(solution)/shard_map/ppermute | solution.py:408
  702.9 22.8 %collective-permute-start.29 = (bf16[720,4,128]{2,1,0:T(4,128)(2,1)S(1)}, bf16[720,4,128]{2,1,0:T(4,128)(2,1)S(1)}, u32[]{:S(2)}, u32[]{:S(2)}) collective-permute-start(bf16[720,4,128]{2,1,0:T(4,128)(2,1)S(1)} %collective-permute-done.28.refs_2_), channel_id=1, source_target_pairs={{0,1},{1,0},{2,3},{3,2},{4,5},{5,4},{6,7},{7,6}} | collective-permute-start | bytes 2211848 | tf_op jit(solution)/shard_map/ppermute | solution.py:408
  705.0 23.1 %collective-permute-start.20 = (bf16[960,4,128]{2,1,0:T(4,128)(2,1)S(1)}, bf16[960,4,128]{2,1,0:T(4,128)(2,1)S(1)}, u32[]{:S(2)}, u32[]{:S(2)}) collective-permute-start(bf16[960,4,128]{2,1,0:T(4,128)(2,1)S(1)} %collective-permute-done.19.refs_0_), channel_id=1, source_target_pairs={{0,1},{1,0},{2,3},{3,2},{4,5},{5,4},{6,7},{7,6}} | collective-permute-start | bytes 2949128 | tf_op jit(solution)/shard_map/ppermute | solution.py:408
  721.1 8.5 %collective-permute-start.17 = (bf16[960,4,128]{2,1,0:T(4,128)(2,1)S(1)}, bf16[960,4,128]{2,1,0:T(4,128)(2,1)S(1)}, u32[]{:S(2)}, u32[]{:S(2)}) collective-permute-start(bf16[960,4,128]{2,1,0:T(4,128)(2,1)S(1)} %collective-permute-done.16.refs_2_), channel_id=1, source_target_pairs={{0,1},{1,0},{2,3},{3,2},{4,5},{5,4},{6,7},{7,6}} | collective-permute-start | bytes 2949128 | tf_op jit(solution)/shard_map/ppermute | solution.py:408
  725.7 59.3 %collective-permute-start.14 = (bf16[960,4,128]{2,1,0:T(4,128)(2,1)}, bf16[960,4,128]{2,1,0:T(4,128)(2,1)}, u32[]{:S(2)}, u32[]{:S(2)}) collective-permute-start(bf16[960,4,128]{2,1,0:T(4,128)(2,1)} %collective-permute-done.13.refs_0_), channel_id=1, source_target_pairs={{0,1},{1,0},{2,3},{3,2},{4,5},{5,4},{6,7},{7,6}} | collective-permute-start | bytes 2949128 | tf_op jit(solution)/shard_map/ppermute | solution.py:408
  726.6 61.6 %collective-permute-start.8 = (bf16[480,4,128]{2,1,0:T(4,128)(2,1)}, bf16[480,4,128]{2,1,0:T(4,128)(2,1)}, u32[]{:S(2)}, u32[]{:S(2)}) collective-permute-start(bf16[480,4,128]{2,1,0:T(4,128)(2,1)} %collective-permute-done.7.refs_0_), channel_id=1, source_target_pairs={{0,1},{1,0},{2,3},{3,2},{4,5},{5,4},{6,7},{7,6}} | collective-permute-start | bytes 1474568 | tf_op jit(solution)/shard_map/ppermute | solution.py:408
  728.1 60.1 %collective-permute-start.11 = (bf16[240,4,128]{2,1,0:T(4,128)(2,1)}, bf16[240,4,128]{2,1,0:T(4,128)(2,1)}, u32[]{:S(2)}, u32[]{:S(2)}) collective-permute-start(bf16[240,4,128]{2,1,0:T(4,128)(2,1)} %collective-permute-done.10.refs_2_), channel_id=1, source_target_pairs={{0,1},{1,0},{2,3},{3,2},{4,5},{5,4},{6,7},{7,6}} | collective-permute-start | bytes 737288 | tf_op jit(solution)/shard_map/ppermute | solution.py:408
  729.1 61.3 %collective-permute-start.5 = (bf16[240,4,128]{2,1,0:T(4,128)(2,1)}, bf16[240,4,128]{2,1,0:T(4,128)(2,1)}, u32[]{:S(2)}, u32[]{:S(2)}) collective-permute-start(bf16[240,4,128]{2,1,0:T(4,128)(2,1)} %collective-permute-done.4.refs_2_), channel_id=1, source_target_pairs={{0,1},{1,0},{2,3},{3,2},{4,5},{5,4},{6,7},{7,6}} | collective-permute-start | bytes 737288 | tf_op jit(solution)/shard_map/ppermute | solution.py:408
  730.6 59.9 %collective-permute-start.2 = (bf16[240,4,128]{2,1,0:T(4,128)(2,1)}, bf16[240,4,128]{2,1,0:T(4,128)(2,1)}, u32[]{:S(2)}, u32[]{:S(2)}) collective-permute-start(bf16[240,4,128]{2,1,0:T(4,128)(2,1)} %collective-permute-done.1.refs_0_), channel_id=1, source_target_pairs={{0,1},{1,0},{2,3},{3,2},{4,5},{5,4},{6,7},{7,6}} | collective-permute-start | bytes 737288 | tf_op jit(solution)/shard_map/ppermute | solution.py:408
  (130 other events, 837.4 us)

commit v5 on v4

--- a/solution.py
+++ b/solution.py
@@ -79,6 +79,11 @@
         (w, w_out.at[pl.ds(0, shard_rows)]), (m, m_out.at[pl.ds(0, shard_rows)]),
         (v.at[pl.ds(0, ahead)], v_part), (mask.at[pl.ds(0, ahead)], mask_part)))]
 
+    def fetch(i, size):
+        at = pl.ds(pl.multiple_of(i * CHUNK_ROWS, 8), size // LANES)
+        return [pltpu.make_async_copy(src.at[at], dst.at[at], fetch_sem.at[k])
+                for k, (src, dst) in enumerate(((w, w_out), (m, m_out)))]
+
     barrier = pltpu.get_barrier_semaphore()
     acc[...] = jnp.zeros_like(acc)
 
@@ -144,7 +149,7 @@
 
     def begin(i):
         def do(size):
-            for cp in swaps(i, size) + loads(i, size):
+            for cp in swaps(i, size) + loads(i, size) + fetch(i, size):
                 cp.start()
 
         for_size(i, do)
@@ -244,7 +249,7 @@
 
         @pl.when(i == 4)
         def _():
-            for cp in fetches:
+            for cp in fetches[2:] + fetch(0, full):
                 cp.start()
 
         return carry

time: 794 us -> 794 us (level)
  no operation moved by 1% of the time
where the time goes in v5:
time: 794 us; the launch traced here: 793 us
  Pallas kernels  526 us (66%)
  waiting for transfers between devices  176 us (22%)
  local copies, waits for them, and re-layouts  51.6 us (6%)
  starting transfers between devices  36.7 us (5%)
    pallas_call x1, Pallas kernels, reduce_scatter(): pl.pallas_call(functools.partial(reduce_kernel, shard_rows), out_shape=(s...  426 us
    ppermute x70, waiting for transfers between devices, send(): return lax.ppermute(a, 'dp', hop[along])  176 us
    pallas_call x15, Pallas kernels, store(): pl.pallas_call(functools.partial(store_kernel, [(which, start, min(p.shap...  52.1 us
    unnamed x248, local copies, waits for them, and re-layouts  51.6 us
    pallas_call x10, Pallas kernels, adamw(): pl.pallas_call(adamw_kernel, grid=(steps,), out_shape=(state, state, stat...  48.1 us
    ppermute x70, starting transfers between devices, send(): return lax.ppermute(a, 'dp', hop[along])  36.7 us
  transfers between devices with their start and end apart: 70, of which 23 were waited for; matrix products, arithmetic and copies ran while one was open for 0% of the time, Pallas kernels for 8%

profile of v5, /device:TPU:0, one launch (start us, length us, event | category | flops | bytes accessed | tf_op | source)
XLA Modules:
  0.0 792.8 jit_solution(2661750583941492408)
XLA Ops:
  1.3 426.0 %shard_map.101 = (f32[24960,128]{1,0:T(8,128)S(1)}, f32[24960,128]{1,0:T(8,128)S(1)}, f32[24960,128]{1,0:T(8,128)S(1)}, bf16[480,4,128]{2,1,0:T(4,128)(2,1)S(1)}, f32[8,128]{1,0:T(8,128)}) custom-call(f32[1]{0:T(128)S(6)} %copy.93.lr, bf16[1,25530368]{1,0:T(2,128)(2,1)} %grad.1, f32[24932,128]{1,0:T(8,128)} %bitcast.34, f32[24932,128]{1,0:T(8,128)} %bitcast.35, ...), custom_call_target="tpu_custom_call" | custom-call | tf_op jit(solution)/shard_map/pallas_call | solution.py:297
  427.3 5.8 shard_map.102
  433.1 6.4 shard_map.103
  439.6 6.5 shard_map.104
  446.0 6.4 shard_map.105
  452.5 6.5 shard_map.106
  458.9 3.7 shard_map.107
  462.7 3.0 shard_map.108
  465.6 1.1 collective-permute-start.38
  466.7 1.0 collective-permute-start.9
  467.8 3.0 shard_map.109
  472.7 1.1 collective-permute-done.38.refs_1_
  473.8 1.1 collective-permute-start.24
  475.0 3.1 shard_map.110
  481.5 1.0 collective-permute-start.66
  482.5 12.6 %collective-permute-done.30.refs_1_ = bf16[240,4,128]{2,1,0:T(4,128)(2,1)S(1)} collective-permute-done((bf16[240,4,128]{2,1,0:T(4,128)(2,1)}, bf16[240,4,128]{2,1,0:T(4,128)(2,1)S(1)}, u32[]{:S(2)}, u32[]{:S(2)}) %collective-permute-start.30) | collective-permute-done | bytes 245792 | tf_op jit(solution)/shard_map/ppermute | solution.py:413
  499.9 8.9 %collective-permute-done.6.refs_1_ = bf16[480,4,128]{2,1,0:T(4,128)(2,1)S(1)} collective-permute-done((bf16[480,4,128]{2,1,0:T(4,128)(2,1)S(1)}, bf16[480,4,128]{2,1,0:T(4,128)(2,1)S(1)}, u32[]{:S(2)}, u32[]{:S(2)}) %collective-permute-start.6) | collective-permute-done | bytes 491552 | tf_op jit(solution)/shard_map/ppermute | solution.py:413
  508.8 1.3 collective-permute-done.42.refs_2_
  516.0 1.1 collective-permute-start.62
  519.5 1.1 collective-permute-start.4
  523.7 17.1 %collective-permute-done.10.refs_2_ = bf16[240,4,128]{2,1,0:T(4,128)(2,1)} collective-permute-done((bf16[240,4,128]{2,1,0:T(4,128)(2,1)S(1)}, bf16[240,4,128]{2,1,0:T(4,128)(2,1)}, u32[]{:S(2)}, u32[]{:S(2)}) %collective-permute-start.10) | collective-permute-done | bytes 245792 | tf_op jit(solution)/shard_map/ppermute | solution.py:413
  540.7 1.1 collective-permute-start.18
  541.8 4.2 collective-permute-done.4.refs_2_
  551.0 1.1 collective-permute-start.54
  554.0 13.0 %collective-permute-done.18.refs_1_ = bf16[960,4,128]{2,1,0:T(4,128)(2,1)S(1)} collective-permute-done((bf16[960,4,128]{2,1,0:T(4,128)(2,1)S(1)}, bf16[960,4,128]{2,1,0:T(4,128)(2,1)S(1)}, u32[]{:S(2)}, u32[]{:S(2)}) %collective-permute-start.18) | collective-permute-done | bytes 983072 | tf_op jit(solution)/shard_map/ppermute | solution.py:413
  567.0 3.7 collective-permute-done.58.refs_2_
  570.6 1.1 collective-permute-start.12
  571.7 1.0 collective-permute-start.50
  572.8 15.3 %collective-permute-done.54.refs_1_ = bf16[960,4,128]{2,1,0:T(4,128)(2,1)S(1)} collective-permute-done((bf16[960,4,128]{2,1,0:T(4,128)(2,1)S(1)}, bf16[960,4,128]{2,1,0:T(4,128)(2,1)S(1)}, u32[]{:S(2)}, u32[]{:S(2)}) %collective-permute-start.54) | collective-permute-done | bytes 983072 | tf_op jit(solution)/shard_map/ppermute | solution.py:413
  588.0 3.7 collective-permute-done.21.refs_2_
  591.7 1.1 collective-permute-start.46
  594.8 14.3 %collective-permute-done.12.refs_1_ = bf16[960,4,128]{2,1,0:T(4,128)(2,1)S(1)} collective-permute-done((bf16[960,4,128]{2,1,0:T(4,128)(2,1)S(1)}, bf16[960,4,128]{2,1,0:T(4,128)(2,1)S(1)}, u32[]{:S(2)}, u32[]{:S(2)}) %collective-permute-start.12) | collective-permute-done | bytes 983072 | tf_op jit(solution)/shard_map/ppermute | solution.py:413
  609.1 3.7 collective-permute-done.50.refs_2_
  615.1 14.4 %collective-permute-done.46.refs_1_ = bf16[960,4,128]{2,1,0:T(4,128)(2,1)S(1)} collective-permute-done((bf16[960,4,128]{2,1,0:T(4,128)(2,1)S(1)}, bf16[960,4,128]{2,1,0:T(4,128)(2,1)S(1)}, u32[]{:S(2)}, u32[]{:S(2)}) %collective-permute-start.46) | collective-permute-done | bytes 983072 | tf_op jit(solution)/shard_map/ppermute | solution.py:413
  630.4 1.1 collective-permute-done.15.refs_2_
  636.3 7.4 collective-permute-done.25.refs_0_
  644.6 8.2 %collective-permute-done.7.refs_0_ = bf16[480,4,128]{2,1,0:T(4,128)(2,1)} collective-permute-done((bf16[480,4,128]{2,1,0:T(4,128)(2,1)S(1)}, bf16[480,4,128]{2,1,0:T(4,128)(2,1)}, u32[]{:S(2)}, u32[]{:S(2)}) %collective-permute-start.7) | collective-permute-done | bytes 491552 | tf_op jit(solution)/shard_map/ppermute | solution.py:413
  652.8 1.1 collective-permute-start.28
  658.7 10.9 %collective-permute-done.28.refs_2_ = bf16[720,4,128]{2,1,0:T(4,128)(2,1)S(1)} collective-permute-done((bf16[720,4,128]{2,1,0:T(4,128)(2,1)S(1)}, bf16[720,4,128]{2,1,0:T(4,128)(2,1)S(1)}, u32[]{:S(2)}, u32[]{:S(2)}) %collective-permute-start.28) | collective-permute-done | bytes 737312 | tf_op jit(solution)/shard_map/ppermute | solution.py:413
  676.4 1.1 collective-permute-start.22
  687.2 13.8 %collective-permute-done.22.refs_2_ = bf16[960,4,128]{2,1,0:T(4,128)(2,1)S(1)} collective-permute-done((bf16[960,4,128]{2,1,0:T(4,128)(2,1)S(1)}, bf16[960,4,128]{2,1,0:T(4,128)(2,1)S(1)}, u32[]{:S(2)}, u32[]{:S(2)}) %collective-permute-start.22) | collective-permute-done | bytes 983072 | tf_op jit(solution)/shard_map/ppermute | solution.py:413
  706.0 15.1 %collective-permute-done.16.refs_2_ = bf16[960,4,128]{2,1,0:T(4,128)(2,1)S(1)} collective-permute-done((bf16[960,4,128]{2,1,0:T(4,128)(2,1)S(1)}, bf16[960,4,128]{2,1,0:T(4,128)(2,1)S(1)}, u32[]{:S(2)}, u32[]{:S(2)}) %collective-permute-start.16) | collective-permute-done | bytes 983072 | tf_op jit(solution)/shard_map/ppermute | solution.py:413
  722.1 3.6 collective-permute-done.13.refs_0_
  730.6 3.7 shard_map.126
  734.3 1.0 copy-done.82
  735.3 1.0 copy-done.84
  736.4 1.0 copy-done.86
  737.4 1.0 copy-done.88
  738.4 1.0 copy-done.90
  739.5 3.3 shard_map.111.refs_6_
  742.8 4.1 shard_map.112.refs_6_
  747.0 4.5 shard_map.113.refs_6_
  751.6 4.5 shard_map.114.refs_6_
  756.2 4.5 shard_map.115.refs_6_
  760.9 4.5 shard_map.116.refs_6_
  765.6 3.6 shard_map.117.refs_6_
  769.3 3.1 shard_map.118.refs_6_
  772.5 3.1 shard_map.119.refs_6_
  775.8 3.0 shard_map.120.refs_4_
  778.9 2.8 shard_map.121.refs_4_
  781.7 3.2 shard_map.122.refs_4_
  785.0 3.2 shard_map.123.refs_4_
  788.2 2.2 shard_map.124.refs_4_
  790.5 2.3 shard_map.125
  (350 shorter events, 71.5 us)
Async XLA Ops:
  465.6 8.2 %collective-permute-start.38 = (bf16[240,4,128]{2,1,0:T(4,128)(2,1)}, bf16[240,4,128]{2,1,0:T(4,128)(2,1)S(1)}, u32[]{:S(2)}, u32[]{:S(2)}) collective-permute-start(bf16[240,4,128]{2,1,0:T(4,128)(2,1)} %get-tuple-element.81.refs_0_), channel_id=1, source_target_pairs={{0,2},{1,3},{2,0},{3,1},{4,6},{5,7},{6,4},{7,5}} | collective-permute-start | bytes 737288 | tf_op jit(solution)/shard_map/ppermute | solution.py:413
  466.7 8.2 %collective-permute-start.9 = (bf16[240,4,128]{2,1,0:T(4,128)(2,1)}, bf16[240,4,128]{2,1,0:T(4,128)(2,1)S(1)}, u32[]{:S(2)}, u32[]{:S(2)}) collective-permute-start(bf16[240,4,128]{2,1,0:T(4,128)(2,1)} %get-tuple-element.81.refs_0_), channel_id=1, source_target_pairs={{0,4},{1,5},{2,6},{3,7},{4,0},{5,1},{6,2},{7,3}} | collective-permute-start | bytes 737288 | tf_op jit(solution)/shard_map/ppermute | solution.py:413
  467.8 10.4 %collective-permute-start.39 = (bf16[240,4,128]{2,1,0:T(4,128)(2,1)}, bf16[240,4,128]{2,1,0:T(4,128)(2,1)S(1)}, u32[]{:S(2)}, u32[]{:S(2)}) collective-permute-start(bf16[240,4,128]{2,1,0:T(4,128)(2,1)} %get-tuple-element.81.refs_0_), channel_id=1, source_target_pairs={{0,1},{1,0},{2,3},{3,2},{4,5},{5,4},{6,7},{7,6}} | collective-permute-start | bytes 737288 | tf_op jit(solution)/shard_map/ppermute | solution.py:413
  470.8 9.1 %collective-permute-start = (bf16[240,4,128]{2,1,0:T(4,128)(2,1)}, bf16[240,4,128]{2,1,0:T(4,128)(2,1)S(1)}, u32[]{:S(2)}, u32[]{:S(2)}) collective-permute-start(bf16[240,4,128]{2,1,0:T(4,128)(2,1)} %get-tuple-element.75.refs_0_), channel_id=1, source_target_pairs={{0,2},{1,3},{2,0},{3,1},{4,6},{5,7},{6,4},{7,5}} | collective-permute-start | bytes 737288 | tf_op jit(solution)/shard_map/ppermute | solution.py:413
  471.7 9.1 %collective-permute-start.34 = (bf16[240,4,128]{2,1,0:T(4,128)(2,1)}, bf16[240,4,128]{2,1,0:T(4,128)(2,1)S(1)}, u32[]{:S(2)}, u32[]{:S(2)}) collective-permute-start(bf16[240,4,128]{2,1,0:T(4,128)(2,1)} %get-tuple-element.75.refs_0_), channel_id=1, source_target_pairs={{0,4},{1,5},{2,6},{3,7},{4,0},{5,1},{6,2},{7,3}} | collective-permute-start | bytes 737288 | tf_op jit(solution)/shard_map/ppermute | solution.py:413
  473.8 24.0 %collective-permute-start.24 = (bf16[480,4,128]{2,1,0:T(4,128)(2,1)S(1)}, bf16[480,4,128]{2,1,0:T(4,128)(2,1)}, u32[]{:S(2)}, u32[]{:S(2)}) collective-permute-start(bf16[480,4,128]{2,1,0:T(4,128)(2,1)S(1)} %get-tuple-element.86.refs_0_), channel_id=1, source_target_pairs={{0,2},{1,3},{2,0},{3,1},{4,6},{5,7},{6,4},{7,5}} | collective-permute-start | bytes 1474568 | tf_op jit(solution)/shard_map/ppermute | solution.py:413
  478.8 16.3 %collective-permute-start.30 = (bf16[240,4,128]{2,1,0:T(4,128)(2,1)}, bf16[240,4,128]{2,1,0:T(4,128)(2,1)S(1)}, u32[]{:S(2)}, u32[]{:S(2)}) collective-permute-start(bf16[240,4,128]{2,1,0:T(4,128)(2,1)} %get-tuple-element.79.refs_0_), channel_id=1, source_target_pairs={{0,2},{1,3},{2,0},{3,1},{4,6},{5,7},{6,4},{7,5}} | collective-permute-start | bytes 737288 | tf_op jit(solution)/shard_map/ppermute | solution.py:413
  479.8 15.3 %collective-permute-start.3 = (bf16[240,4,128]{2,1,0:T(4,128)(2,1)}, bf16[240,4,128]{2,1,0:T(4,128)(2,1)S(1)}, u32[]{:S(2)}, u32[]{:S(2)}) collective-permute-start(bf16[240,4,128]{2,1,0:T(4,128)(2,1)} %get-tuple-element.79.refs_0_), channel_id=1, source_target_pairs={{0,4},{1,5},{2,6},{3,7},{4,0},{5,1},{6,2},{7,3}} | collective-permute-start | bytes 737288 | tf_op jit(solution)/shard_map/ppermute | solution.py:413
  480.8 15.3 %collective-permute-start.31 = (bf16[240,4,128]{2,1,0:T(4,128)(2,1)}, bf16[240,4,128]{2,1,0:T(4,128)(2,1)S(1)}, u32[]{:S(2)}, u32[]{:S(2)}) collective-permute-start(bf16[240,4,128]{2,1,0:T(4,128)(2,1)} %get-tuple-element.79.refs_0_), channel_id=1, source_target_pairs={{0,1},{1,0},{2,3},{3,2},{4,5},{5,4},{6,7},{7,6}} | collective-permute-start | bytes 737288 | tf_op jit(solution)/shard_map/ppermute | solution.py:413
  481.5 17.1 %collective-permute-start.66 = (bf16[480,4,128]{2,1,0:T(4,128)(2,1)S(1)}, bf16[480,4,128]{2,1,0:T(4,128)(2,1)S(1)}, u32[]{:S(2)}, u32[]{:S(2)}) collective-permute-start(bf16[480,4,128]{2,1,0:T(4,128)(2,1)S(1)} %get-tuple-element.86.refs_0_), channel_id=1, source_target_pairs={{0,4},{1,5},{2,6},{3,7},{4,0},{5,1},{6,2},{7,3}} | collective-permute-start | bytes 1474568 | tf_op jit(solution)/shard_map/ppermute | solution.py:413
  495.2 13.6 %collective-permute-start.6 = (bf16[480,4,128]{2,1,0:T(4,128)(2,1)S(1)}, bf16[480,4,128]{2,1,0:T(4,128)(2,1)S(1)}, u32[]{:S(2)}, u32[]{:S(2)}) collective-permute-start(bf16[480,4,128]{2,1,0:T(4,128)(2,1)S(1)} %copy-done.65), channel_id=1, source_target_pairs={{0,2},{1,3},{2,0},{3,1},{4,6},{5,7},{6,4},{7,5}} | collective-permute-start | bytes 1474568 | tf_op jit(solution)/shard_map/ppermute | solution.py:413
  496.8 13.3 %collective-permute-start.42 = (bf16[480,4,128]{2,1,0:T(4,128)(2,1)S(1)}, bf16[480,4,128]{2,1,0:T(4,128)(2,1)S(1)}, u32[]{:S(2)}, u32[]{:S(2)}) collective-permute-start(bf16[480,4,128]{2,1,0:T(4,128)(2,1)S(1)} %copy-done.65), channel_id=1, source_target_pairs={{0,4},{1,5},{2,6},{3,7},{4,0},{5,1},{6,2},{7,3}} | collective-permute-start | bytes 1474568 | tf_op jit(solution)/shard_map/ppermute | solution.py:413
  497.8 13.0 %collective-permute-start.43 = (bf16[480,4,128]{2,1,0:T(4,128)(2,1)S(1)}, bf16[480,4,128]{2,1,0:T(4,128)(2,1)S(1)}, u32[]{:S(2)}, u32[]{:S(2)}) collective-permute-start(bf16[480,4,128]{2,1,0:T(4,128)(2,1)S(1)} %copy-done.65), channel_id=1, source_target_pairs={{0,1},{1,0},{2,3},{3,2},{4,5},{5,4},{6,7},{7,6}} | collective-permute-start | bytes 1474568 | tf_op jit(solution)/shard_map/ppermute | solution.py:413
  498.6 14.3 %collective-permute-start.40 = (bf16[240,4,128]{2,1,0:T(4,128)(2,1)S(1)}, bf16[240,4,128]{2,1,0:T(4,128)(2,1)S(1)}, u32[]{:S(2)}, u32[]{:S(2)}) collective-permute-start(bf16[240,4,128]{2,1,0:T(4,128)(2,1)S(1)} %collective-permute-done.38.refs_1_), channel_id=1, source_target_pairs={{0,1},{1,0},{2,3},{3,2},{4,5},{5,4},{6,7},{7,6}} | collective-permute-start | bytes 737288 | tf_op jit(solution)/shard_map/ppermute | solution.py:413
  499.4 14.2 %collective-permute-start.41 = (bf16[240,4,128]{2,1,0:T(4,128)(2,1)S(1)}, bf16[240,4,128]{2,1,0:T(4,128)(2,1)S(1)}, u32[]{:S(2)}, u32[]{:S(2)}) collective-permute-start(bf16[240,4,128]{2,1,0:T(4,128)(2,1)S(1)} %collective-permute-done.9.refs_2_), channel_id=1, source_target_pairs={{0,1},{1,0},{2,3},{3,2},{4,5},{5,4},{6,7},{7,6}} | collective-permute-start | bytes 737288 | tf_op jit(solution)/shard_map/ppermute | solution.py:413
  510.1 7.0 collective-permute-start.37
  511.6 7.1 collective-permute-start.32
  513.5 7.7 collective-permute-start.33
  514.3 32.8 %collective-permute-start.27 = (bf16[720,4,128]{2,1,0:T(4,128)(2,1)S(1)}, bf16[720,4,128]{2,1,0:T(4,128)(2,1)S(1)}, u32[]{:S(2)}, u32[]{:S(2)}) collective-permute-start(bf16[720,4,128]{2,1,0:T(4,128)(2,1)S(1)} %copy-done.50), channel_id=1, source_target_pairs={{0,4},{1,5},{2,6},{3,7},{4,0},{5,1},{6,2},{7,3}} | collective-permute-start | bytes 2211848 | tf_op jit(solution)/shard_map/ppermute | solution.py:413
  516.0 31.5 %collective-permute-start.62 = (bf16[720,4,128]{2,1,0:T(4,128)(2,1)S(1)}, bf16[720,4,128]{2,1,0:T(4,128)(2,1)S(1)}, u32[]{:S(2)}, u32[]{:S(2)}) collective-permute-start(bf16[720,4,128]{2,1,0:T(4,128)(2,1)S(1)} %copy-done.50), channel_id=1, source_target_pairs={{0,2},{1,3},{2,0},{3,1},{4,6},{5,7},{6,4},{7,5}} | collective-permute-start | bytes 2211848 | tf_op jit(solution)/shard_map/ppermute | solution.py:413
  517.8 22.9 %collective-permute-start.10 = (bf16[240,4,128]{2,1,0:T(4,128)(2,1)S(1)}, bf16[240,4,128]{2,1,0:T(4,128)(2,1)}, u32[]{:S(2)}, u32[]{:S(2)}) collective-permute-start(bf16[240,4,128]{2,1,0:T(4,128)(2,1)S(1)} %collective-permute-done.9.refs_2_), channel_id=1, source_target_pairs={{0,2},{1,3},{2,0},{3,1},{4,6},{5,7},{6,4},{7,5}} | collective-permute-start | bytes 737288 | tf_op jit(solution)/shard_map/ppermute | solution.py:413
  519.5 26.5 %collective-permute-start.4 = (bf16[240,4,128]{2,1,0:T(4,128)(2,1)S(1)}, bf16[240,4,128]{2,1,0:T(4,128)(2,1)}, u32[]{:S(2)}, u32[]{:S(2)}) collective-permute-start(bf16[240,4,128]{2,1,0:T(4,128)(2,1)S(1)} %collective-permute-done.3.refs_2_), channel_id=1, source_target_pairs={{0,2},{1,3},{2,0},{3,1},{4,6},{5,7},{6,4},{7,5}} | collective-permute-start | bytes 737288 | tf_op jit(solution)/shard_map/ppermute | solution.py:413
  521.9 25.1 %collective-permute-start.1 = (bf16[240,4,128]{2,1,0:T(4,128)(2,1)S(1)}, bf16[240,4,128]{2,1,0:T(4,128)(2,1)}, u32[]{:S(2)}, u32[]{:S(2)}) collective-permute-start(bf16[240,4,128]{2,1,0:T(4,128)(2,1)S(1)} %collective-permute-done.refs_1_), channel_id=1, source_target_pairs={{0,4},{1,5},{2,6},{3,7},{4,0},{5,1},{6,2},{7,3}} | collective-permute-start | bytes 737288 | tf_op jit(solution)/shard_map/ppermute | solution.py:413
  540.7 26.2 %collective-permute-start.18 = (bf16[960,4,128]{2,1,0:T(4,128)(2,1)S(1)}, bf16[960,4,128]{2,1,0:T(4,128)(2,1)S(1)}, u32[]{:S(2)}, u32[]{:S(2)}) collective-permute-start(bf16[960,4,128]{2,1,0:T(4,128)(2,1)S(1)} %copy-done), channel_id=1, source_target_pairs={{0,2},{1,3},{2,0},{3,1},{4,6},{5,7},{6,4},{7,5}} | collective-permute-start | bytes 2949128 | tf_op jit(solution)/shard_map/ppermute | solution.py:413
  546.0 24.6 %collective-permute-start.58 = (bf16[960,4,128]{2,1,0:T(4,128)(2,1)S(1)}, bf16[960,4,128]{2,1,0:T(4,128)(2,1)S(1)}, u32[]{:S(2)}, u32[]{:S(2)}) collective-permute-start(bf16[960,4,128]{2,1,0:T(4,128)(2,1)S(1)} %copy-done), channel_id=1, source_target_pairs={{0,4},{1,5},{2,6},{3,7},{4,0},{5,1},{6,2},{7,3}} | collective-permute-start | bytes 2949128 | tf_op jit(solution)/shard_map/ppermute | solution.py:413
  550.1 21.6 %collective-permute-start.59 = (bf16[960,4,128]{2,1,0:T(4,128)(2,1)S(1)}, bf16[960,4,128]{2,1,0:T(4,128)(2,1)S(1)}, u32[]{:S(2)}, u32[]{:S(2)}) collective-permute-start(bf16[960,4,128]{2,1,0:T(4,128)(2,1)S(1)} %copy-done), channel_id=1, source_target_pairs={{0,1},{1,0},{2,3},{3,2},{4,5},{5,4},{6,7},{7,6}} | collective-permute-start | bytes 2949128 | tf_op jit(solution)/shard_map/ppermute | solution.py:413
  551.0 37.0 %collective-permute-start.54 = (bf16[960,4,128]{2,1,0:T(4,128)(2,1)S(1)}, bf16[960,4,128]{2,1,0:T(4,128)(2,1)S(1)}, u32[]{:S(2)}, u32[]{:S(2)}) collective-permute-start(bf16[960,4,128]{2,1,0:T(4,128)(2,1)S(1)} %copy-done.1), channel_id=1, source_target_pairs={{0,2},{1,3},{2,0},{3,1},{4,6},{5,7},{6,4},{7,5}} | collective-permute-start | bytes 2949128 | tf_op jit(solution)/shard_map/ppermute | solution.py:413
  553.0 38.7 %collective-permute-start.21 = (bf16[960,4,128]{2,1,0:T(4,128)(2,1)S(1)}, bf16[960,4,128]{2,1,0:T(4,128)(2,1)S(1)}, u32[]{:S(2)}, u32[]{:S(2)}) collective-permute-start(bf16[960,4,128]{2,1,0:T(4,128)(2,1)S(1)} %copy-done.1), channel_id=1, source_target_pairs={{0,4},{1,5},{2,6},{3,7},{4,0},{5,1},{6,2},{7,3}} | collective-permute-start | bytes 2949128 | tf_op jit(solution)/shard_map/ppermute | solution.py:413
  567.0 25.8 %collective-permute-start.55 = (bf16[960,4,128]{2,1,0:T(4,128)(2,1)S(1)}, bf16[960,4,128]{2,1,0:T(4,128)(2,1)S(1)}, u32[]{:S(2)}, u32[]{:S(2)}) collective-permute-start(bf16[960,4,128]{2,1,0:T(4,128)(2,1)S(1)} %copy-done.1), channel_id=1, source_target_pairs={{0,1},{1,0},{2,3},{3,2},{4,5},{5,4},{6,7},{7,6}} | collective-permute-start | bytes 2949128 | tf_op jit(solution)/shard_map/ppermute | solution.py:413
  570.6 38.5 %collective-permute-start.12 = (bf16[960,4,128]{2,1,0:T(4,128)(2,1)S(1)}, bf16[960,4,128]{2,1,0:T(4,128)(2,1)S(1)}, u32[]{:S(2)}, u32[]{:S(2)}) collective-permute-start(bf16[960,4,128]{2,1,0:T(4,128)(2,1)S(1)} %copy-done.2), channel_id=1, source_target_pairs={{0,2},{1,3},{2,0},{3,1},{4,6},{5,7},{6,4},{7,5}} | collective-permute-start | bytes 2949128 | tf_op jit(solution)/shard_map/ppermute | solution.py:413
  571.7 41.0 %collective-permute-start.50 = (bf16[960,4,128]{2,1,0:T(4,128)(2,1)S(1)}, bf16[960,4,128]{2,1,0:T(4,128)(2,1)S(1)}, u32[]{:S(2)}, u32[]{:S(2)}) collective-permute-start(bf16[960,4,128]{2,1,0:T(4,128)(2,1)S(1)} %copy-done.2), channel_id=1, source_target_pairs={{0,4},{1,5},{2,6},{3,7},{4,0},{5,1},{6,2},{7,3}} | collective-permute-start | bytes 2949128 | tf_op jit(solution)/shard_map/ppermute | solution.py:413
  588.0 24.7 %collective-permute-start.51 = (bf16[960,4,128]{2,1,0:T(4,128)(2,1)S(1)}, bf16[960,4,128]{2,1,0:T(4,128)(2,1)S(1)}, u32[]{:S(2)}, u32[]{:S(2)}) collective-permute-start(bf16[960,4,128]{2,1,0:T(4,128)(2,1)S(1)} %copy-done.2), channel_id=1, source_target_pairs={{0,1},{1,0},{2,3},{3,2},{4,5},{5,4},{6,7},{7,6}} | collective-permute-start | bytes 2949128 | tf_op jit(solution)/shard_map/ppermute | solution.py:413
  591.7 37.7 %collective-permute-start.46 = (bf16[960,4,128]{2,1,0:T(4,128)(2,1)S(1)}, bf16[960,4,128]{2,1,0:T(4,128)(2,1)S(1)}, u32[]{:S(2)}, u32[]{:S(2)}) collective-permute-start(bf16[960,4,128]{2,1,0:T(4,128)(2,1)S(1)} %copy-done.3), channel_id=1, source_target_pairs={{0,2},{1,3},{2,0},{3,1},{4,6},{5,7},{6,4},{7,5}} | collective-permute-start | bytes 2949128 | tf_op jit(solution)/shard_map/ppermute | solution.py:413
  593.8 37.7 %collective-permute-start.15 = (bf16[960,4,128]{2,1,0:T(4,128)(2,1)S(1)}, bf16[960,4,128]{2,1,0:T(4,128)(2,1)S(1)}, u32[]{:S(2)}, u32[]{:S(2)}) collective-permute-start(bf16[960,4,128]{2,1,0:T(4,128)(2,1)S(1)} %copy-done.3), channel_id=1, source_target_pairs={{0,4},{1,5},{2,6},{3,7},{4,0},{5,1},{6,2},{7,3}} | collective-permute-start | bytes 2949128 | tf_op jit(solution)/shard_map/ppermute | solution.py:413
  609.1 24.2 %collective-permute-start.47 = (bf16[960,4,128]{2,1,0:T(4,128)(2,1)S(1)}, bf16[960,4,128]{2,1,0:T(4,128)(2,1)S(1)}, u32[]{:S(2)}, u32[]{:S(2)}) collective-permute-start(bf16[960,4,128]{2,1,0:T(4,128)(2,1)S(1)} %copy-done.3), channel_id=1, source_target_pairs={{0,1},{1,0},{2,3},{3,2},{4,5},{5,4},{6,7},{7,6}} | collective-permute-start | bytes 2949128 | tf_op jit(solution)/shard_map/ppermute | solution.py:413
  612.8 21.5 %collective-permute-start.44 = (bf16[480,4,128]{2,1,0:T(4,128)(2,1)S(1)}, bf16[480,4,128]{2,1,0:T(4,128)(2,1)S(1)}, u32[]{:S(2)}, u32[]{:S(2)}) collective-permute-start(bf16[480,4,128]{2,1,0:T(4,128)(2,1)S(1)} %collective-permute-done.6.refs_1_), channel_id=1, source_target_pairs={{0,1},{1,0},{2,3},{3,2},{4,5},{5,4},{6,7},{7,6}} | collective-permute-start | bytes 1474568 | tf_op jit(solution)/shard_map/ppermute | solution.py:413
  613.7 21.8 %collective-permute-start.45 = (bf16[480,4,128]{2,1,0:T(4,128)(2,1)S(1)}, bf16[480,4,128]{2,1,0:T(4,128)(2,1)S(1)}, u32[]{:S(2)}, u32[]{:S(2)}) collective-permute-start(bf16[480,4,128]{2,1,0:T(4,128)(2,1)S(1)} %collective-permute-done.42.refs_2_), channel_id=1, source_target_pairs={{0,1},{1,0},{2,3},{3,2},{4,5},{5,4},{6,7},{7,6}} | collective-permute-start | bytes 1474568 | tf_op jit(solution)/shard_map/ppermute | solution.py:413
  629.4 14.3 %collective-permute-start.25 = (bf16[480,4,128]{2,1,0:T(4,128)(2,1)}, bf16[480,4,128]{2,1,0:T(4,128)(2,1)S(1)}, u32[]{:S(2)}, u32[]{:S(2)}) collective-permute-start(bf16[480,4,128]{2,1,0:T(4,128)(2,1)} %collective-permute-done.24.refs_1_), channel_id=1, source_target_pairs={{0,4},{1,5},{2,6},{3,7},{4,0},{5,1},{6,2},{7,3}} | collective-permute-start | bytes 1474568 | tf_op jit(solution)/shard_map/ppermute | solution.py:413
  631.5 21.3 %collective-permute-start.7 = (bf16[480,4,128]{2,1,0:T(4,128)(2,1)S(1)}, bf16[480,4,128]{2,1,0:T(4,128)(2,1)}, u32[]{:S(2)}, u32[]{:S(2)}) collective-permute-start(bf16[480,4,128]{2,1,0:T(4,128)(2,1)S(1)} %collective-permute-done.6.refs_1_), channel_id=1, source_target_pairs={{0,4},{1,5},{2,6},{3,7},{4,0},{5,1},{6,2},{7,3}} | collective-permute-start | bytes 1474568 | tf_op jit(solution)/shard_map/ppermute | solution.py:413
  634.2 20.5 %collective-permute-start.65 = (bf16[720,4,128]{2,1,0:T(4,128)(2,1)S(1)}, bf16[720,4,128]{2,1,0:T(4,128)(2,1)S(1)}, u32[]{:S(2)}, u32[]{:S(2)}) collective-permute-start(bf16[720,4,128]{2,1,0:T(4,128)(2,1)S(1)} %collective-permute-done.27.refs_2_), channel_id=1, source_target_pairs={{0,1},{1,0},{2,3},{3,2},{4,5},{5,4},{6,7},{7,6}} | collective-permute-start | bytes 2211848 | tf_op jit(solution)/shard_map/ppermute | solution.py:413
  635.0 35.9 %collective-permute-start.60 = (bf16[960,4,128]{2,1,0:T(4,128)(2,1)S(1)}, bf16[960,4,128]{2,1,0:T(4,128)(2,1)S(1)}, u32[]{:S(2)}, u32[]{:S(2)}) collective-permute-start(bf16[960,4,128]{2,1,0:T(4,128)(2,1)S(1)} %collective-permute-done.18.refs_1_), channel_id=1, source_target_pairs={{0,1},{1,0},{2,3},{3,2},{4,5},{5,4},{6,7},{7,6}} | collective-permute-start | bytes 2949128 | tf_op jit(solution)/shard_map/ppermute | solution.py:413
  636.3 36.6 %collective-permute-start.61 = (bf16[960,4,128]{2,1,0:T(4,128)(2,1)S(1)}, bf16[960,4,128]{2,1,0:T(4,128)(2,1)S(1)}, u32[]{:S(2)}, u32[]{:S(2)}) collective-permute-start(bf16[960,4,128]{2,1,0:T(4,128)(2,1)S(1)} %collective-permute-done.58.refs_2_), channel_id=1, source_target_pairs={{0,1},{1,0},{2,3},{3,2},{4,5},{5,4},{6,7},{7,6}} | collective-permute-start | bytes 2949128 | tf_op jit(solution)/shard_map/ppermute | solution.py:413
  643.7 12.7 %collective-permute-start.64 = (bf16[720,4,128]{2,1,0:T(4,128)(2,1)S(1)}, bf16[720,4,128]{2,1,0:T(4,128)(2,1)S(1)}, u32[]{:S(2)}, u32[]{:S(2)}) collective-permute-start(bf16[720,4,128]{2,1,0:T(4,128)(2,1)S(1)} %collective-permute-done.62.refs_1_), channel_id=1, source_target_pairs={{0,1},{1,0},{2,3},{3,2},{4,5},{5,4},{6,7},{7,6}} | collective-permute-start | bytes 2211848 | tf_op jit(solution)/shard_map/ppermute | solution.py:413
  652.8 16.9 %collective-permute-start.28 = (bf16[720,4,128]{2,1,0:T(4,128)(2,1)S(1)}, bf16[720,4,128]{2,1,0:T(4,128)(2,1)S(1)}, u32[]{:S(2)}, u32[]{:S(2)}) collective-permute-start(bf16[720,4,128]{2,1,0:T(4,128)(2,1)S(1)} %collective-permute-done.27.refs_2_), channel_id=1, source_target_pairs={{0,2},{1,3},{2,0},{3,1},{4,6},{5,7},{6,4},{7,5}} | collective-permute-start | bytes 2211848 | tf_op jit(solution)/shard_map/ppermute | solution.py:413
  655.6 14.1 %collective-permute-start.26 = (bf16[480,4,128]{2,1,0:T(4,128)(2,1)S(1)}, bf16[480,4,128]{2,1,0:T(4,128)(2,1)S(1)}, u32[]{:S(2)}, u32[]{:S(2)}) collective-permute-start(bf16[480,4,128]{2,1,0:T(4,128)(2,1)S(1)} %collective-permute-done.25.refs_0_), channel_id=1, source_target_pairs={{0,1},{1,0},{2,3},{3,2},{4,5},{5,4},{6,7},{7,6}} | collective-permute-start | bytes 1474568 | tf_op jit(solution)/shard_map/ppermute | solution.py:413
  657.2 18.2 %collective-permute-start.56 = (bf16[960,4,128]{2,1,0:T(4,128)(2,1)S(1)}, bf16[960,4,128]{2,1,0:T(4,128)(2,1)S(1)}, u32[]{:S(2)}, u32[]{:S(2)}) collective-permute-start(bf16[960,4,128]{2,1,0:T(4,128)(2,1)S(1)} %collective-permute-done.54.refs_1_), channel_id=1, source_target_pairs={{0,1},{1,0},{2,3},{3,2},{4,5},{5,4},{6,7},{7,6}} | collective-permute-start | bytes 2949128 | tf_op jit(solution)/shard_map/ppermute | solution.py:413
  669.7 8.8 %collective-permute-start.57 = (bf16[960,4,128]{2,1,0:T(4,128)(2,1)S(1)}, bf16[960,4,128]{2,1,0:T(4,128)(2,1)S(1)}, u32[]{:S(2)}, u32[]{:S(2)}) collective-permute-start(bf16[960,4,128]{2,1,0:T(4,128)(2,1)S(1)} %collective-permute-done.21.refs_2_), channel_id=1, source_target_pairs={{0,1},{1,0},{2,3},{3,2},{4,5},{5,4},{6,7},{7,6}} | collective-permute-start | bytes 2949128 | tf_op jit(solution)/shard_map/ppermute | solution.py:413
  670.5 9.0 %collective-permute-start.52 = (bf16[960,4,128]{2,1,0:T(4,128)(2,1)S(1)}, bf16[960,4,128]{2,1,0:T(4,128)(2,1)S(1)}, u32[]{:S(2)}, u32[]{:S(2)}) collective-permute-start(bf16[960,4,128]{2,1,0:T(4,128)(2,1)S(1)} %collective-permute-done.12.refs_1_), channel_id=1, source_target_pairs={{0,1},{1,0},{2,3},{3,2},{4,5},{5,4},{6,7},{7,6}} | collective-permute-start | bytes 2949128 | tf_op jit(solution)/shard_map/ppermute | solution.py:413
  671.9 9.5 %collective-permute-start.53 = (bf16[960,4,128]{2,1,0:T(4,128)(2,1)S(1)}, bf16[960,4,128]{2,1,0:T(4,128)(2,1)S(1)}, u32[]{:S(2)}, u32[]{:S(2)}) collective-permute-start(bf16[960,4,128]{2,1,0:T(4,128)(2,1)S(1)} %collective-permute-done.50.refs_2_), channel_id=1, source_target_pairs={{0,1},{1,0},{2,3},{3,2},{4,5},{5,4},{6,7},{7,6}} | collective-permute-start | bytes 2949128 | tf_op jit(solution)/shard_map/ppermute | solution.py:413
  673.9 10.3 %collective-permute-start.48 = (bf16[960,4,128]{2,1,0:T(4,128)(2,1)S(1)}, bf16[960,4,128]{2,1,0:T(4,128)(2,1)S(1)}, u32[]{:S(2)}, u32[]{:S(2)}) collective-permute-start(bf16[960,4,128]{2,1,0:T(4,128)(2,1)S(1)} %collective-permute-done.46.refs_1_), channel_id=1, source_target_pairs={{0,1},{1,0},{2,3},{3,2},{4,5},{5,4},{6,7},{7,6}} | collective-permute-start | bytes 2949128 | tf_op jit(solution)/shard_map/ppermute | solution.py:413
  676.4 24.6 %collective-permute-start.22 = (bf16[960,4,128]{2,1,0:T(4,128)(2,1)S(1)}, bf16[960,4,128]{2,1,0:T(4,128)(2,1)S(1)}, u32[]{:S(2)}, u32[]{:S(2)}) collective-permute-start(bf16[960,4,128]{2,1,0:T(4,128)(2,1)S(1)} %collective-permute-done.21.refs_2_), channel_id=1, source_target_pairs={{0,2},{1,3},{2,0},{3,1},{4,6},{5,7},{6,4},{7,5}} | collective-permute-start | bytes 2949128 | tf_op jit(solution)/shard_map/ppermute | solution.py:413
  679.4 22.6 %collective-permute-start.49 = (bf16[960,4,128]{2,1,0:T(4,128)(2,1)S(1)}, bf16[960,4,128]{2,1,0:T(4,128)(2,1)S(1)}, u32[]{:S(2)}, u32[]{:S(2)}) collective-permute-start(bf16[960,4,128]{2,1,0:T(4,128)(2,1)S(1)} %collective-permute-done.15.refs_2_), channel_id=1, source_target_pairs={{0,1},{1,0},{2,3},{3,2},{4,5},{5,4},{6,7},{7,6}} | collective-permute-start | bytes 2949128 | tf_op jit(solution)/shard_map/ppermute | solution.py:413
  680.4 24.6 %collective-permute-start.19 = (bf16[960,4,128]{2,1,0:T(4,128)(2,1)S(1)}, bf16[960,4,128]{2,1,0:T(4,128)(2,1)S(1)}, u32[]{:S(2)}, u32[]{:S(2)}) collective-permute-start(bf16[960,4,128]{2,1,0:T(4,128)(2,1)S(1)} %collective-permute-done.18.refs_1_), channel_id=1, source_target_pairs={{0,4},{1,5},{2,6},{3,7},{4,0},{5,1},{6,2},{7,3}} | collective-permute-start | bytes 2949128 | tf_op jit(solution)/shard_map/ppermute | solution.py:413
  682.4 38.7 %collective-permute-start.16 = (bf16[960,4,128]{2,1,0:T(4,128)(2,1)S(1)}, bf16[960,4,128]{2,1,0:T(4,128)(2,1)S(1)}, u32[]{:S(2)}, u32[]{:S(2)}) collective-permute-start(bf16[960,4,128]{2,1,0:T(4,128)(2,1)S(1)} %collective-permute-done.15.refs_2_), channel_id=1, source_target_pairs={{0,2},{1,3},{2,0},{3,1},{4,6},{5,7},{6,4},{7,5}} | collective-permute-start | bytes 2949128 | tf_op jit(solution)/shard_map/ppermute | solution.py:413
  685.2 40.5 %collective-permute-start.13 = (bf16[960,4,128]{2,1,0:T(4,128)(2,1)S(1)}, bf16[960,4,128]{2,1,0:T(4,128)(2,1)}, u32[]{:S(2)}, u32[]{:S(2)}) collective-permute-start(bf16[960,4,128]{2,1,0:T(4,128)(2,1)S(1)} %collective-permute-done.12.refs_1_), channel_id=1, source_target_pairs={{0,4},{1,5},{2,6},{3,7},{4,0},{5,1},{6,2},{7,3}} | collective-permute-start | bytes 2949128 | tf_op jit(solution)/shard_map/ppermute | solution.py:413
  701.0 26.1 %collective-permute-start.23 = (bf16[960,4,128]{2,1,0:T(4,128)(2,1)S(1)}, bf16[960,4,128]{2,1,0:T(4,128)(2,1)S(1)}, u32[]{:S(2)}, u32[]{:S(2)}) collective-permute-start(bf16[960,4,128]{2,1,0:T(4,128)(2,1)S(1)} %collective-permute-done.22.refs_2_), channel_id=1, source_target_pairs={{0,1},{1,0},{2,3},{3,2},{4,5},{5,4},{6,7},{7,6}} | collective-permute-start | bytes 2949128 | tf_op jit(solution)/shard_map/ppermute | solution.py:413
  703.0 22.8 %collective-permute-start.29 = (bf16[720,4,128]{2,1,0:T(4,128)(2,1)S(1)}, bf16[720,4,128]{2,1,0:T(4,128)(2,1)S(1)}, u32[]{:S(2)}, u32[]{:S(2)}) collective-permute-start(bf16[720,4,128]{2,1,0:T(4,128)(2,1)S(1)} %collective-permute-done.28.refs_2_), channel_id=1, source_target_pairs={{0,1},{1,0},{2,3},{3,2},{4,5},{5,4},{6,7},{7,6}} | collective-permute-start | bytes 2211848 | tf_op jit(solution)/shard_map/ppermute | solution.py:413
  705.0 23.1 %collective-permute-start.20 = (bf16[960,4,128]{2,1,0:T(4,128)(2,1)S(1)}, bf16[960,4,128]{2,1,0:T(4,128)(2,1)S(1)}, u32[]{:S(2)}, u32[]{:S(2)}) collective-permute-start(bf16[960,4,128]{2,1,0:T(4,128)(2,1)S(1)} %collective-permute-done.19.refs_0_), channel_id=1, source_target_pairs={{0,1},{1,0},{2,3},{3,2},{4,5},{5,4},{6,7},{7,6}} | collective-permute-start | bytes 2949128 | tf_op jit(solution)/shard_map/ppermute | solution.py:413
  721.1 8.5 %collective-permute-start.17 = (bf16[960,4,128]{2,1,0:T(4,128)(2,1)S(1)}, bf16[960,4,128]{2,1,0:T(4,128)(2,1)S(1)}, u32[]{:S(2)}, u32[]{:S(2)}) collective-permute-start(bf16[960,4,128]{2,1,0:T(4,128)(2,1)S(1)} %collective-permute-done.16.refs_2_), channel_id=1, source_target_pairs={{0,1},{1,0},{2,3},{3,2},{4,5},{5,4},{6,7},{7,6}} | collective-permute-start | bytes 2949128 | tf_op jit(solution)/shard_map/ppermute | solution.py:413
  725.7 59.3 %collective-permute-start.14 = (bf16[960,4,128]{2,1,0:T(4,128)(2,1)}, bf16[960,4,128]{2,1,0:T(4,128)(2,1)}, u32[]{:S(2)}, u32[]{:S(2)}) collective-permute-start(bf16[960,4,128]{2,1,0:T(4,128)(2,1)} %collective-permute-done.13.refs_0_), channel_id=1, source_target_pairs={{0,1},{1,0},{2,3},{3,2},{4,5},{5,4},{6,7},{7,6}} | collective-permute-start | bytes 2949128 | tf_op jit(solution)/shard_map/ppermute | solution.py:413
  726.6 61.6 %collective-permute-start.8 = (bf16[480,4,128]{2,1,0:T(4,128)(2,1)}, bf16[480,4,128]{2,1,0:T(4,128)(2,1)}, u32[]{:S(2)}, u32[]{:S(2)}) collective-permute-start(bf16[480,4,128]{2,1,0:T(4,128)(2,1)} %collective-permute-done.7.refs_0_), channel_id=1, source_target_pairs={{0,1},{1,0},{2,3},{3,2},{4,5},{5,4},{6,7},{7,6}} | collective-permute-start | bytes 1474568 | tf_op jit(solution)/shard_map/ppermute | solution.py:413
  728.1 60.1 %collective-permute-start.11 = (bf16[240,4,128]{2,1,0:T(4,128)(2,1)}, bf16[240,4,128]{2,1,0:T(4,128)(2,1)}, u32[]{:S(2)}, u32[]{:S(2)}) collective-permute-start(bf16[240,4,128]{2,1,0:T(4,128)(2,1)} %collective-permute-done.10.refs_2_), channel_id=1, source_target_pairs={{0,1},{1,0},{2,3},{3,2},{4,5},{5,4},{6,7},{7,6}} | collective-permute-start | bytes 737288 | tf_op jit(solution)/shard_map/ppermute | solution.py:413
  729.1 61.3 %collective-permute-start.5 = (bf16[240,4,128]{2,1,0:T(4,128)(2,1)}, bf16[240,4,128]{2,1,0:T(4,128)(2,1)}, u32[]{:S(2)}, u32[]{:S(2)}) collective-permute-start(bf16[240,4,128]{2,1,0:T(4,128)(2,1)} %collective-permute-done.4.refs_2_), channel_id=1, source_target_pairs={{0,1},{1,0},{2,3},{3,2},{4,5},{5,4},{6,7},{7,6}} | collective-permute-start | bytes 737288 | tf_op jit(solution)/shard_map/ppermute | solution.py:413
  730.6 59.9 %collective-permute-start.2 = (bf16[240,4,128]{2,1,0:T(4,128)(2,1)}, bf16[240,4,128]{2,1,0:T(4,128)(2,1)}, u32[]{:S(2)}, u32[]{:S(2)}) collective-permute-start(bf16[240,4,128]{2,1,0:T(4,128)(2,1)} %collective-permute-done.1.refs_0_), channel_id=1, source_target_pairs={{0,1},{1,0},{2,3},{3,2},{4,5},{5,4},{6,7},{7,6}} | collective-permute-start | bytes 737288 | tf_op jit(solution)/shard_map/ppermute | solution.py:413
  (130 other events, 837.4 us)

commit v6 on v3

--- a/solution.py
+++ b/solution.py
@@ -35,13 +35,6 @@
     return me, part, along_x, along_y
 
 
-def meet(peers):
-    barrier = pltpu.get_barrier_semaphore()
-    for peer in peers:
-        pl.semaphore_signal(barrier, inc=1, device_id=(peer,), device_id_type=MESH)
-    pl.semaphore_wait(barrier, len(peers))
-
-
 def stay(array):
     return pltpu.with_memory_space_constraint(array, pltpu.VMEM)
 
@@ -60,6 +53,10 @@
         jnp.sqrt(second * (1.0 / (1.0 - BETA_SECOND ** ADAM_STEP))) + ADAM_EPS)
     new = w - rate * (step_dir + WEIGHT_DECAY * mask.astype(jnp.float32) * w)
     return new, first, second
+
+
+def chunk_count(shard_rows):
+    return 1 + -(-shard_rows // CHUNK_ROWS)
 
 
 def pack_tile(packed, t, new):
@@ -77,8 +74,9 @@
     blocks = (me, along_x, along_y, diag)
     shard_len = shard_rows * LANES
     full = CHUNK_ROWS * LANES
-    chunks = -(-shard_rows // CHUNK_ROWS)
-    tail = (shard_rows - (chunks - 1) * CHUNK_ROWS) * LANES
+    edge = full // 2
+    chunks = chunk_count(shard_rows)
+    tail = shard_rows * LANES - edge - (chunks - 2) * full
     num_dev = grad.shape[1] // shard_len
     others = [(me + k) % num_dev for k in range(1, num_dev)]
     ahead = v_part.shape[0]
@@ -86,13 +84,20 @@
         (w, w_out.at[pl.ds(0, shard_rows)]), (m, m_out.at[pl.ds(0, shard_rows)]),
         (v.at[pl.ds(0, ahead)], v_part), (mask.at[pl.ds(0, ahead)], mask_part)))]
 
+    barrier = pltpu.get_barrier_semaphore()
     acc[...] = jnp.zeros_like(acc)
+
+    def row_of(i):
+        return jnp.maximum(i * CHUNK_ROWS - HALF_ROWS, 0)
+
+    def half_of(i):
+        return jnp.where((i == 0) | (i == chunks - 1), HALF_ROWS // 2, HALF_ROWS)
 
     def loads(i, size):
         slot = i % SLOTS
         out = []
         for b, block in enumerate(blocks):
-            src = pl.multiple_of(block * shard_len + i * full, LANES)
+            src = pl.multiple_of(block * shard_len + row_of(i) * LANES, LANES)
             out.append(pltpu.make_async_copy(
                 grad.at[:, pl.ds(src, size)], own.at[slot, b, :, pl.ds(0, size)], own_sem.at[slot, b]))
         return out
@@ -101,14 +106,18 @@
         slot = i % SLOTS
         out = []
         for b, block in enumerate(blocks):
-            src = pl.multiple_of((block + shift) * shard_len + i * full, LANES)
+            src = pl.multiple_of((block + shift) * shard_len + row_of(i) * LANES, LANES)
             out.append(remote(
                 grad.at[:, pl.ds(src, size)], other.at[slot, b, :, pl.ds(0, size)],
                 part_ssem.at[slot, b], part_rsem.at[slot, b], part))
         return out
 
     def for_size(i, do):
-        @pl.when(i < chunks - 1)
+        @pl.when(i == 0)
+        def _():
+            do(edge)
+
+        @pl.when((i >= 1) & (i < chunks - 1))
         def _():
             do(full)
 
@@ -116,28 +125,34 @@
         def _():
             do(tail)
 
-    def hops(q, planes):
+    def hops(q, pieces):
         slot = q % SLOTS
-        return (remote(x_send.at[slot, planes], x_recv.at[slot, planes], x_ssem.at[slot], x_rsem.at[slot], along_x),
-                remote(y_send.at[slot, planes], y_recv.at[slot, planes], y_ssem.at[slot], y_rsem.at[slot], along_y))
-
-    def for_planes(q, do):
-        @pl.when((q >= 1) & (q < 3))
-        def _():
-            do(pl.ds(0, 2))
-
-        @pl.when((q >= 3) & (q <= chunks))
-        def _():
-            do(pl.ds(0, 3))
-
-        @pl.when((q > chunks) & (q <= chunks + 2))
-        def _():
-            do(pl.ds(2, 1))
-
-    for cp in loads(0, full):
+        out = []
+        for k, (plane, planes, rows) in enumerate(pieces):
+            at = (slot, pl.ds(plane, planes), pl.ds(0, rows))
+            out.append(remote(x_send.at[at], x_recv.at[at], x_ssem.at[slot, k], x_rsem.at[slot, k], along_x))
+            out.append(remote(y_send.at[at], y_recv.at[at], y_ssem.at[slot, k], y_rsem.at[slot, k], along_y))
+        return out
+
+    short = HALF_ROWS // 2
+
+    def for_pieces(q, do):
+        for test, pieces in (
+                (q == 1, [(0, 2, short)]),
+                (q == 2, [(0, 2, HALF_ROWS)]),
+                (q == 3, [(0, 2, HALF_ROWS), (2, 1, short)]),
+                ((q > 3) & (q < chunks), [(0, 3, HALF_ROWS)]),
+                (q == chunks, [(0, 2, short), (2, 1, HALF_ROWS)]),
+                (q == chunks + 1, [(2, 1, HALF_ROWS)]),
+                (q == chunks + 2, [(2, 1, short)])):
+            pl.when(test)(functools.partial(do, pieces))
+
+    for cp in loads(0, edge):
         cp.start()
-    meet(others)
-    for cp in swaps(0, full):
+    for peer in (part, along_x, along_y):
+        pl.semaphore_signal(barrier, inc=1, device_id=(peer,), device_id_type=MESH)
+    pl.semaphore_wait(barrier, 3)
+    for cp in swaps(0, edge):
         cp.start()
 
     def begin(i):
@@ -156,11 +171,12 @@
         slot = j % SLOTS
         out = (j + 1) % SLOTS
         kept = j % (SLOTS + 1)
+        tiles = half_of(j) // 8
 
         def tile(t, carry):
             for half in range(2):
                 row = pl.multiple_of(t * 8, 8)
-                col = pl.multiple_of((t + half * (HALF_ROWS // 8)) * 8 * LANES, 8 * LANES)
+                col = pl.multiple_of((t + half * tiles) * 8 * LANES, 8 * LANES)
 
                 def pair(b):
                     a = own[slot, b, :, pl.ds(col, 8 * LANES)].astype(jnp.float32)
@@ -178,14 +194,14 @@
                     y_send[out, 1, pl.ds(row, 8)] = pair(3)
             return carry
 
-        lax.fori_loop(0, HALF_ROWS // 8, tile, 0)
+        lax.fori_loop(0, tiles, tile, 0)
 
     def wait_for(q):
-        def do(planes):
-            for cp in hops(q, planes):
+        def do(pieces):
+            for cp in hops(q, pieces):
                 cp.wait()
 
-        for_planes(q, do)
+        for_pieces(q, do)
 
     def relay(j):
         slot = j % SLOTS
@@ -200,8 +216,9 @@
     def finish(j):
         got = (j + 3) % SLOTS
         kept = j % (SLOTS + 1)
-        base = j * CHUNK_ROWS
-        left = shard_rows - j * CHUNK_ROWS
+        base = row_of(j)
+        half = half_of(j)
+        left = shard_rows - base
         rows = lax.broadcasted_iota(jnp.int32, (8, LANES), 0)
 
         def tile(t, total):
@@ -209,11 +226,11 @@
             top = (mine[kept, 0, pl.ds(row, 8)] + y_recv[got, 2, pl.ds(row, 8)]) * 0.125
             low = (mine[kept, 1, pl.ds(row, 8)] + x_recv[got, 2, pl.ds(row, 8)]) * 0.125
             g_out[pl.ds(pl.multiple_of(base + t * 8, 8), 8)] = top
-            g_out[pl.ds(pl.multiple_of(base + HALF_ROWS + t * 8, 8), 8)] = low
+            g_out[pl.ds(pl.multiple_of(base + half + t * 8, 8), 8)] = low
             total = total + jnp.where(rows + t * 8 < left, top * top, 0.0)
-            return total + jnp.where(rows + (HALF_ROWS + t * 8) < left, low * low, 0.0)
-
-        acc[...] += lax.fori_loop(0, HALF_ROWS // 8, tile, jnp.zeros((8, LANES), jnp.float32))
+            return total + jnp.where(rows + (half + t * 8) < left, low * low, 0.0)
+
+        acc[...] += lax.fori_loop(0, half // 8, tile, jnp.zeros((8, LANES), jnp.float32))
 
     def step(i, carry):
         @pl.when((i >= 1) & (i < chunks))
@@ -234,11 +251,11 @@
         def _():
             finish(i - 5)
 
-        def go(planes):
-            for cp in hops(i, planes):
+        def go(pieces):
+            for cp in hops(i, pieces):
                 cp.start()
 
-        for_planes(i, go)
+        for_pieces(i, go)
 
         @pl.when(i == 4)
         def _():
@@ -280,13 +297,13 @@
 def reduce_scatter(lr, grad_row, w, m, v, mask, num_dev):
     f32, bf16 = jnp.float32, jnp.bfloat16
     shard_rows = w.shape[0]
-    chunks = -(-shard_rows // CHUNK_ROWS)
+    padded = (chunk_count(shard_rows) - 1) * CHUNK_ROWS
     ahead = PARTS[0] * ADAM_ROWS
     vm, dma = pltpu.VMEM, pltpu.SemaphoreType.DMA
     three = (SLOTS, 3, HALF_ROWS, LANES)
     one = (SLOTS, HALF_ROWS, LANES)
     raw = (SLOTS, 4, 1, CHUNK_ROWS * LANES)
-    state = vm((chunks * CHUNK_ROWS, LANES), f32)
+    state = vm((padded, LANES), f32)
     return pl.pallas_call(
         functools.partial(reduce_kernel, shard_rows),
         out_shape=(state, state, state, vm((ahead // 4, 4, LANES), bf16), jax.ShapeDtypeStruct((8, LANES), f32)),
@@ -297,7 +314,7 @@
             vm((SLOTS + 1, 2, HALF_ROWS, LANES), f32), vm(three, f32), vm(three, f32), vm((8, LANES), f32),
             vm((num_dev, 8, LANES), f32),
             dma((SLOTS, 4)), dma((SLOTS, 4)), dma((SLOTS, 4)),
-            dma((SLOTS,)), dma((SLOTS,)), dma((SLOTS,)), dma((SLOTS,)),
+            dma((SLOTS, 2)), dma((SLOTS, 2)), dma((SLOTS, 2)), dma((SLOTS, 2)),
             dma((num_dev - 1,)), dma((num_dev,)),
             vm((ahead, LANES), f32), vm((ahead, LANES), jnp.int32), dma((4,))],
         compiler_params=pltpu.CompilerParams(collective_id=0, has_side_effects=True,
@@ -425,12 +442,14 @@
             far.append(send(from_x, "y") if p % 2 == 0 else send(from_y, "x"))
             pieces = [packed, from_x, from_y, from_core, send(from_x, "core"), send(from_y, "core")]
             whole = put(pieces, [(k, starts[p]) for k in (0, 1, 2, 4, 5, 6)], whole)
+        pieces, spots = [], []
         for p in range(0, len(PARTS), 2):
-            pieces, spots = [], []
             for q in (p, p + 1):
                 pieces += [far[q], send(far[q], "core")]
                 spots += [(3, starts[q]), (7, starts[q])]
-            whole = put(pieces, spots, whole, p + 2 == len(PARTS))
+            if p + 4 != len(PARTS):
+                whole = put(pieces, spots, whole, p + 2 == len(PARTS))
+                pieces, spots = [], []
         new_w, new_m, new_v = state
         params = whole[0].reshape(num_dev * shard_len)
         return (params, new_w.reshape(shard_len), new_m.reshape(shard_len), new_v.reshape(shard_len),

time: 794 us -> 791 us (level)
    pallas_call x15 -> x14, Pallas kernels: 52.1 us -> 50.8 us  [store(): pl.pallas_call(functools.partial(store_kernel, [(which, start, min(p.shap...]
  transfers between devices with their start and end apart: 70 -> 70, of which waited for: 23 -> 19; matrix products, arithmetic and copies ran while one was open for 0% -> 0% of each run, Pallas kernels for 8% -> 7%
where the time goes in v6:
time: 791 us; the launch traced here: 790 us
  Pallas kernels  524 us (66%)
  waiting for transfers between devices  176 us (22%)
  local copies, waits for them, and re-layouts  51.6 us (7%)
  starting transfers between devices  36.4 us (5%)
    pallas_call x1, Pallas kernels, reduce_scatter(): pl.pallas_call(functools.partial(reduce_kernel, shard_rows), out_shape=(s...  425 us
    ppermute x70, waiting for transfers between devices, send(): return lax.ppermute(a, 'dp', hop[along])  176 us
    unnamed x248, local copies, waits for them, and re-layouts  51.6 us
    pallas_call x14, Pallas kernels, store(): pl.pallas_call(functools.partial(store_kernel, [(which, start, min(p.shap...  50.8 us
    pallas_call x10, Pallas kernels, adamw(): pl.pallas_call(adamw_kernel, grid=(steps,), out_shape=(state, state, stat...  48.1 us
    ppermute x70, starting transfers between devices, send(): return lax.ppermute(a, 'dp', hop[along])  36.4 us
  transfers between devices with their start and end apart: 70, of which 19 were waited for; matrix products, arithmetic and copies ran while one was open for 0% of the time, Pallas kernels for 7%

profile of v6, /device:TPU:0, one launch (start us, length us, event | category | flops | bytes accessed | tf_op | source)
XLA Modules:
  0.0 790.2 jit_solution(18282893128459380444)
XLA Ops:
  1.3 425.1 %shard_map.101 = (f32[24960,128]{1,0:T(8,128)S(1)}, f32[24960,128]{1,0:T(8,128)S(1)}, f32[24960,128]{1,0:T(8,128)S(1)}, bf16[480,4,128]{2,1,0:T(4,128)(2,1)S(1)}, f32[8,128]{1,0:T(8,128)}) custom-call(f32[1]{0:T(128)S(6)} %copy.91.lr, bf16[1,25530368]{1,0:T(2,128)(2,1)} %grad.1, f32[24932,128]{1,0:T(8,128)} %bitcast.34, f32[24932,128]{1,0:T(8,128)} %bitcast.35, ...), custom_call_target="tpu_custom_call" | custom-call | tf_op jit(solution)/shard_map/pallas_call | solution.py:307
  426.4 5.8 shard_map.102
  432.2 6.4 shard_map.103
  438.7 6.5 shard_map.104
  445.2 6.4 shard_map.105
  451.6 6.5 shard_map.106
  458.1 3.7 shard_map.107
  461.8 3.0 shard_map.108
  464.7 1.5 collective-permute-start.38
  466.8 3.0 shard_map.109
  469.8 1.4 collective-permute-start.6
  471.8 1.1 collective-permute-done.38.refs_1_
  472.9 1.5 collective-permute-start.24
  474.5 3.1 shard_map.110
  478.9 1.4 collective-permute-start.9
  481.6 12.6 %collective-permute-done.30.refs_1_ = bf16[240,4,128]{2,1,0:T(4,128)(2,1)S(1)} collective-permute-done((bf16[240,4,128]{2,1,0:T(4,128)(2,1)}, bf16[240,4,128]{2,1,0:T(4,128)(2,1)S(1)}, u32[]{:S(2)}, u32[]{:S(2)}) %collective-permute-start.30) | collective-permute-done | bytes 245792 | tf_op jit(solution)/shard_map/ppermute | solution.py:422
  494.2 1.4 collective-permute-start
  499.0 8.8 %collective-permute-done.refs_1_ = bf16[480,4,128]{2,1,0:T(4,128)(2,1)S(1)} collective-permute-done((bf16[480,4,128]{2,1,0:T(4,128)(2,1)S(1)}, bf16[480,4,128]{2,1,0:T(4,128)(2,1)S(1)}, u32[]{:S(2)}, u32[]{:S(2)}) %collective-permute-start) | collective-permute-done | bytes 491552 | tf_op jit(solution)/shard_map/ppermute | solution.py:422
  507.8 1.8 collective-permute-done.42.refs_2_
  515.1 1.5 collective-permute-start.62
  519.2 1.4 collective-permute-start.7
  522.7 17.2 %collective-permute-done.10.refs_6_ = bf16[240,4,128]{2,1,0:T(4,128)(2,1)} collective-permute-done((bf16[240,4,128]{2,1,0:T(4,128)(2,1)S(1)}, bf16[240,4,128]{2,1,0:T(4,128)(2,1)}, u32[]{:S(2)}, u32[]{:S(2)}) %collective-permute-start.10) | collective-permute-done | bytes 245792 | tf_op jit(solution)/shard_map/ppermute | solution.py:422
  539.8 1.5 collective-permute-start.18
  541.9 3.2 collective-permute-done.4.refs_2_
  549.1 1.5 collective-permute-start.54
  552.0 14.1 %collective-permute-done.18.refs_1_ = bf16[960,4,128]{2,1,0:T(4,128)(2,1)S(1)} collective-permute-done((bf16[960,4,128]{2,1,0:T(4,128)(2,1)S(1)}, bf16[960,4,128]{2,1,0:T(4,128)(2,1)S(1)}, u32[]{:S(2)}, u32[]{:S(2)}) %collective-permute-start.18) | collective-permute-done | bytes 983072 | tf_op jit(solution)/shard_map/ppermute | solution.py:422
  566.1 1.5 collective-permute-start.12
  568.1 19.0 %collective-permute-done.54.refs_1_ = bf16[960,4,128]{2,1,0:T(4,128)(2,1)S(1)} collective-permute-done((bf16[960,4,128]{2,1,0:T(4,128)(2,1)S(1)}, bf16[960,4,128]{2,1,0:T(4,128)(2,1)S(1)}, u32[]{:S(2)}, u32[]{:S(2)}) %collective-permute-start.54) | collective-permute-done | bytes 983072 | tf_op jit(solution)/shard_map/ppermute | solution.py:422
  587.1 1.5 collective-permute-start.46
  590.2 18.0 %collective-permute-done.12.refs_1_ = bf16[960,4,128]{2,1,0:T(4,128)(2,1)S(1)} collective-permute-done((bf16[960,4,128]{2,1,0:T(4,128)(2,1)S(1)}, bf16[960,4,128]{2,1,0:T(4,128)(2,1)S(1)}, u32[]{:S(2)}, u32[]{:S(2)}) %collective-permute-start.12) | collective-permute-done | bytes 983072 | tf_op jit(solution)/shard_map/ppermute | solution.py:422
  610.5 18.0 %collective-permute-done.46.refs_1_ = bf16[960,4,128]{2,1,0:T(4,128)(2,1)S(1)} collective-permute-done((bf16[960,4,128]{2,1,0:T(4,128)(2,1)S(1)}, bf16[960,4,128]{2,1,0:T(4,128)(2,1)S(1)}, u32[]{:S(2)}, u32[]{:S(2)}) %collective-permute-start.46) | collective-permute-done | bytes 983072 | tf_op jit(solution)/shard_map/ppermute | solution.py:422
  628.5 1.4 collective-permute-start.25
  634.4 8.4 %collective-permute-done.25.refs_0_ = bf16[480,4,128]{2,1,0:T(4,128)(2,1)S(1)} collective-permute-done((bf16[480,4,128]{2,1,0:T(4,128)(2,1)}, bf16[480,4,128]{2,1,0:T(4,128)(2,1)S(1)}, u32[]{:S(2)}, u32[]{:S(2)}) %collective-permute-start.25) | collective-permute-done | bytes 491552 | tf_op jit(solution)/shard_map/ppermute | solution.py:422
  643.7 8.2 %collective-permute-done.1.refs_0_ = bf16[480,4,128]{2,1,0:T(4,128)(2,1)} collective-permute-done((bf16[480,4,128]{2,1,0:T(4,128)(2,1)S(1)}, bf16[480,4,128]{2,1,0:T(4,128)(2,1)}, u32[]{:S(2)}, u32[]{:S(2)}) %collective-permute-start.1) | collective-permute-done | bytes 491552 | tf_op jit(solution)/shard_map/ppermute | solution.py:422
  651.9 1.5 collective-permute-start.28
  658.2 10.6 %collective-permute-done.28.refs_2_ = bf16[720,4,128]{2,1,0:T(4,128)(2,1)S(1)} collective-permute-done((bf16[720,4,128]{2,1,0:T(4,128)(2,1)S(1)}, bf16[720,4,128]{2,1,0:T(4,128)(2,1)S(1)}, u32[]{:S(2)}, u32[]{:S(2)}) %collective-permute-start.28) | collective-permute-done | bytes 737312 | tf_op jit(solution)/shard_map/ppermute | solution.py:422
  672.0 1.0 copy-done.26
  675.5 1.5 collective-permute-start.22
  680.4 1.4 collective-permute-start.16
  686.3 13.8 %collective-permute-done.22.refs_2_ = bf16[960,4,128]{2,1,0:T(4,128)(2,1)S(1)} collective-permute-done((bf16[960,4,128]{2,1,0:T(4,128)(2,1)S(1)}, bf16[960,4,128]{2,1,0:T(4,128)(2,1)S(1)}, u32[]{:S(2)}, u32[]{:S(2)}) %collective-permute-start.22) | collective-permute-done | bytes 983072 | tf_op jit(solution)/shard_map/ppermute | solution.py:422
  701.1 2.4 collective-permute-done.19.refs_0_
  704.5 15.7 %collective-permute-done.16.refs_2_ = bf16[960,4,128]{2,1,0:T(4,128)(2,1)S(1)} collective-permute-done((bf16[960,4,128]{2,1,0:T(4,128)(2,1)S(1)}, bf16[960,4,128]{2,1,0:T(4,128)(2,1)S(1)}, u32[]{:S(2)}, u32[]{:S(2)}) %collective-permute-start.16) | collective-permute-done | bytes 983072 | tf_op jit(solution)/shard_map/ppermute | solution.py:422
  720.2 1.0 copy-done.28
  725.8 1.0 copy-done.38
  729.4 3.7 shard_map.125
  733.1 1.0 copy-done.82
  734.1 1.0 copy-done.84
  735.1 1.0 copy-done.86
  736.2 1.0 copy-done.88
  737.2 1.0 copy-done.90
  738.2 3.3 shard_map.111.refs_6_
  741.6 4.1 shard_map.112.refs_6_
  745.7 4.5 shard_map.113.refs_6_
  750.4 4.5 shard_map.114.refs_6_
  755.0 4.5 shard_map.115.refs_6_
  759.7 4.5 shard_map.116.refs_6_
  764.3 3.6 shard_map.117.refs_6_
  768.1 3.1 shard_map.118.refs_6_
  771.3 3.1 shard_map.119.refs_6_
  774.5 3.0 shard_map.120.refs_4_
  777.7 2.8 shard_map.121.refs_4_
  780.5 3.2 shard_map.122.refs_4_
  783.8 3.2 shard_map.123.refs_8_
  787.0 3.2 shard_map.124
  (349 shorter events, 61.1 us)
Async XLA Ops:
  464.7 8.2 %collective-permute-start.38 = (bf16[240,4,128]{2,1,0:T(4,128)(2,1)}, bf16[240,4,128]{2,1,0:T(4,128)(2,1)S(1)}, u32[]{:S(2)}, u32[]{:S(2)}) collective-permute-start(bf16[240,4,128]{2,1,0:T(4,128)(2,1)} %get-tuple-element.73.refs_0_), channel_id=1, source_target_pairs={{0,2},{1,3},{2,0},{3,1},{4,6},{5,7},{6,4},{7,5}} | collective-permute-start | bytes 737288 | tf_op jit(solution)/shard_map/ppermute | solution.py:422
  466.2 8.2 %collective-permute-start.3 = (bf16[240,4,128]{2,1,0:T(4,128)(2,1)}, bf16[240,4,128]{2,1,0:T(4,128)(2,1)S(1)}, u32[]{:S(2)}, u32[]{:S(2)}) collective-permute-start(bf16[240,4,128]{2,1,0:T(4,128)(2,1)} %get-tuple-element.73.refs_0_), channel_id=1, source_target_pairs={{0,4},{1,5},{2,6},{3,7},{4,0},{5,1},{6,2},{7,3}} | collective-permute-start | bytes 737288 | tf_op jit(solution)/shard_map/ppermute | solution.py:422
  466.8 10.8 %collective-permute-start.39 = (bf16[240,4,128]{2,1,0:T(4,128)(2,1)}, bf16[240,4,128]{2,1,0:T(4,128)(2,1)S(1)}, u32[]{:S(2)}, u32[]{:S(2)}) collective-permute-start(bf16[240,4,128]{2,1,0:T(4,128)(2,1)} %get-tuple-element.73.refs_0_), channel_id=1, source_target_pairs={{0,1},{1,0},{2,3},{3,2},{4,5},{5,4},{6,7},{7,6}} | collective-permute-start | bytes 737288 | tf_op jit(solution)/shard_map/ppermute | solution.py:422
  469.8 9.1 %collective-permute-start.6 = (bf16[240,4,128]{2,1,0:T(4,128)(2,1)}, bf16[240,4,128]{2,1,0:T(4,128)(2,1)S(1)}, u32[]{:S(2)}, u32[]{:S(2)}) collective-permute-start(bf16[240,4,128]{2,1,0:T(4,128)(2,1)} %get-tuple-element.77.refs_0_), channel_id=1, source_target_pairs={{0,2},{1,3},{2,0},{3,1},{4,6},{5,7},{6,4},{7,5}} | collective-permute-start | bytes 737288 | tf_op jit(solution)/shard_map/ppermute | solution.py:422
  471.1 9.1 %collective-permute-start.34 = (bf16[240,4,128]{2,1,0:T(4,128)(2,1)}, bf16[240,4,128]{2,1,0:T(4,128)(2,1)S(1)}, u32[]{:S(2)}, u32[]{:S(2)}) collective-permute-start(bf16[240,4,128]{2,1,0:T(4,128)(2,1)} %get-tuple-element.77.refs_0_), channel_id=1, source_target_pairs={{0,4},{1,5},{2,6},{3,7},{4,0},{5,1},{6,2},{7,3}} | collective-permute-start | bytes 737288 | tf_op jit(solution)/shard_map/ppermute | solution.py:422
  472.9 24.0 %collective-permute-start.24 = (bf16[480,4,128]{2,1,0:T(4,128)(2,1)S(1)}, bf16[480,4,128]{2,1,0:T(4,128)(2,1)}, u32[]{:S(2)}, u32[]{:S(2)}) collective-permute-start(bf16[480,4,128]{2,1,0:T(4,128)(2,1)S(1)} %get-tuple-element.86.refs_0_), channel_id=1, source_target_pairs={{0,2},{1,3},{2,0},{3,1},{4,6},{5,7},{6,4},{7,5}} | collective-permute-start | bytes 1474568 | tf_op jit(solution)/shard_map/ppermute | solution.py:422
  478.3 15.8 %collective-permute-start.30 = (bf16[240,4,128]{2,1,0:T(4,128)(2,1)}, bf16[240,4,128]{2,1,0:T(4,128)(2,1)S(1)}, u32[]{:S(2)}, u32[]{:S(2)}) collective-permute-start(bf16[240,4,128]{2,1,0:T(4,128)(2,1)} %get-tuple-element.81.refs_0_), channel_id=1, source_target_pairs={{0,2},{1,3},{2,0},{3,1},{4,6},{5,7},{6,4},{7,5}} | collective-permute-start | bytes 737288 | tf_op jit(solution)/shard_map/ppermute | solution.py:422
  478.9 15.3 %collective-permute-start.9 = (bf16[240,4,128]{2,1,0:T(4,128)(2,1)}, bf16[240,4,128]{2,1,0:T(4,128)(2,1)S(1)}, u32[]{:S(2)}, u32[]{:S(2)}) collective-permute-start(bf16[240,4,128]{2,1,0:T(4,128)(2,1)} %get-tuple-element.81.refs_0_), channel_id=1, source_target_pairs={{0,4},{1,5},{2,6},{3,7},{4,0},{5,1},{6,2},{7,3}} | collective-permute-start | bytes 737288 | tf_op jit(solution)/shard_map/ppermute | solution.py:422
  480.3 15.3 %collective-permute-start.31 = (bf16[240,4,128]{2,1,0:T(4,128)(2,1)}, bf16[240,4,128]{2,1,0:T(4,128)(2,1)S(1)}, u32[]{:S(2)}, u32[]{:S(2)}) collective-permute-start(bf16[240,4,128]{2,1,0:T(4,128)(2,1)} %get-tuple-element.81.refs_0_), channel_id=1, source_target_pairs={{0,1},{1,0},{2,3},{3,2},{4,5},{5,4},{6,7},{7,6}} | collective-permute-start | bytes 737288 | tf_op jit(solution)/shard_map/ppermute | solution.py:422
  481.0 16.7 %collective-permute-start.66 = (bf16[480,4,128]{2,1,0:T(4,128)(2,1)S(1)}, bf16[480,4,128]{2,1,0:T(4,128)(2,1)S(1)}, u32[]{:S(2)}, u32[]{:S(2)}) collective-permute-start(bf16[480,4,128]{2,1,0:T(4,128)(2,1)S(1)} %get-tuple-element.86.refs_0_), channel_id=1, source_target_pairs={{0,4},{1,5},{2,6},{3,7},{4,0},{5,1},{6,2},{7,3}} | collective-permute-start | bytes 1474568 | tf_op jit(solution)/shard_map/ppermute | solution.py:422
  494.2 13.6 %collective-permute-start = (bf16[480,4,128]{2,1,0:T(4,128)(2,1)S(1)}, bf16[480,4,128]{2,1,0:T(4,128)(2,1)S(1)}, u32[]{:S(2)}, u32[]{:S(2)}) collective-permute-start(bf16[480,4,128]{2,1,0:T(4,128)(2,1)S(1)} %copy-done.65), channel_id=1, source_target_pairs={{0,2},{1,3},{2,0},{3,1},{4,6},{5,7},{6,4},{7,5}} | collective-permute-start | bytes 1474568 | tf_op jit(solution)/shard_map/ppermute | solution.py:422
  496.3 13.3 %collective-permute-start.42 = (bf16[480,4,128]{2,1,0:T(4,128)(2,1)S(1)}, bf16[480,4,128]{2,1,0:T(4,128)(2,1)S(1)}, u32[]{:S(2)}, u32[]{:S(2)}) collective-permute-start(bf16[480,4,128]{2,1,0:T(4,128)(2,1)S(1)} %copy-done.65), channel_id=1, source_target_pairs={{0,4},{1,5},{2,6},{3,7},{4,0},{5,1},{6,2},{7,3}} | collective-permute-start | bytes 1474568 | tf_op jit(solution)/shard_map/ppermute | solution.py:422
  496.9 13.4 %collective-permute-start.43 = (bf16[480,4,128]{2,1,0:T(4,128)(2,1)S(1)}, bf16[480,4,128]{2,1,0:T(4,128)(2,1)S(1)}, u32[]{:S(2)}, u32[]{:S(2)}) collective-permute-start(bf16[480,4,128]{2,1,0:T(4,128)(2,1)S(1)} %copy-done.65), channel_id=1, source_target_pairs={{0,1},{1,0},{2,3},{3,2},{4,5},{5,4},{6,7},{7,6}} | collective-permute-start | bytes 1474568 | tf_op jit(solution)/shard_map/ppermute | solution.py:422
  497.7 14.6 %collective-permute-start.40 = (bf16[240,4,128]{2,1,0:T(4,128)(2,1)S(1)}, bf16[240,4,128]{2,1,0:T(4,128)(2,1)S(1)}, u32[]{:S(2)}, u32[]{:S(2)}) collective-permute-start(bf16[240,4,128]{2,1,0:T(4,128)(2,1)S(1)} %collective-permute-done.38.refs_1_), channel_id=1, source_target_pairs={{0,1},{1,0},{2,3},{3,2},{4,5},{5,4},{6,7},{7,6}} | collective-permute-start | bytes 737288 | tf_op jit(solution)/shard_map/ppermute | solution.py:422
  498.5 14.6 %collective-permute-start.41 = (bf16[240,4,128]{2,1,0:T(4,128)(2,1)S(1)}, bf16[240,4,128]{2,1,0:T(4,128)(2,1)S(1)}, u32[]{:S(2)}, u32[]{:S(2)}) collective-permute-start(bf16[240,4,128]{2,1,0:T(4,128)(2,1)S(1)} %collective-permute-done.3.refs_2_), channel_id=1, source_target_pairs={{0,1},{1,0},{2,3},{3,2},{4,5},{5,4},{6,7},{7,6}} | collective-permute-start | bytes 737288 | tf_op jit(solution)/shard_map/ppermute | solution.py:422
  507.8 6.6 collective-permute-start.36
  509.6 7.0 collective-permute-start.37
  511.1 7.4 collective-permute-start.32
  513.0 8.3 %collective-permute-start.33 = (bf16[240,4,128]{2,1,0:T(4,128)(2,1)S(1)}, bf16[240,4,128]{2,1,0:T(4,128)(2,1)S(1)}, u32[]{:S(2)}, u32[]{:S(2)}) collective-permute-start(bf16[240,4,128]{2,1,0:T(4,128)(2,1)S(1)} %collective-permute-done.9.refs_2_), channel_id=1, source_target_pairs={{0,1},{1,0},{2,3},{3,2},{4,5},{5,4},{6,7},{7,6}} | collective-permute-start | bytes 737288 | tf_op jit(solution)/shard_map/ppermute | solution.py:422
  513.7 31.4 %collective-permute-start.27 = (bf16[720,4,128]{2,1,0:T(4,128)(2,1)S(1)}, bf16[720,4,128]{2,1,0:T(4,128)(2,1)S(1)}, u32[]{:S(2)}, u32[]{:S(2)}) collective-permute-start(bf16[720,4,128]{2,1,0:T(4,128)(2,1)S(1)} %copy-done.50), channel_id=1, source_target_pairs={{0,4},{1,5},{2,6},{3,7},{4,0},{5,1},{6,2},{7,3}} | collective-permute-start | bytes 2211848 | tf_op jit(solution)/shard_map/ppermute | solution.py:422
  515.1 30.5 %collective-permute-start.62 = (bf16[720,4,128]{2,1,0:T(4,128)(2,1)S(1)}, bf16[720,4,128]{2,1,0:T(4,128)(2,1)S(1)}, u32[]{:S(2)}, u32[]{:S(2)}) collective-permute-start(bf16[720,4,128]{2,1,0:T(4,128)(2,1)S(1)} %copy-done.50), channel_id=1, source_target_pairs={{0,2},{1,3},{2,0},{3,1},{4,6},{5,7},{6,4},{7,5}} | collective-permute-start | bytes 2211848 | tf_op jit(solution)/shard_map/ppermute | solution.py:422
  517.3 22.6 %collective-permute-start.10 = (bf16[240,4,128]{2,1,0:T(4,128)(2,1)S(1)}, bf16[240,4,128]{2,1,0:T(4,128)(2,1)}, u32[]{:S(2)}, u32[]{:S(2)}) collective-permute-start(bf16[240,4,128]{2,1,0:T(4,128)(2,1)S(1)} %collective-permute-done.9.refs_2_), channel_id=1, source_target_pairs={{0,2},{1,3},{2,0},{3,1},{4,6},{5,7},{6,4},{7,5}} | collective-permute-start | bytes 737288 | tf_op jit(solution)/shard_map/ppermute | solution.py:422
  519.2 22.1 %collective-permute-start.7 = (bf16[240,4,128]{2,1,0:T(4,128)(2,1)S(1)}, bf16[240,4,128]{2,1,0:T(4,128)(2,1)}, u32[]{:S(2)}, u32[]{:S(2)}) collective-permute-start(bf16[240,4,128]{2,1,0:T(4,128)(2,1)S(1)} %collective-permute-done.6.refs_1_), channel_id=1, source_target_pairs={{0,4},{1,5},{2,6},{3,7},{4,0},{5,1},{6,2},{7,3}} | collective-permute-start | bytes 737288 | tf_op jit(solution)/shard_map/ppermute | solution.py:422
  522.0 23.1 %collective-permute-start.4 = (bf16[240,4,128]{2,1,0:T(4,128)(2,1)S(1)}, bf16[240,4,128]{2,1,0:T(4,128)(2,1)}, u32[]{:S(2)}, u32[]{:S(2)}) collective-permute-start(bf16[240,4,128]{2,1,0:T(4,128)(2,1)S(1)} %collective-permute-done.3.refs_2_), channel_id=1, source_target_pairs={{0,2},{1,3},{2,0},{3,1},{4,6},{5,7},{6,4},{7,5}} | collective-permute-start | bytes 737288 | tf_op jit(solution)/shard_map/ppermute | solution.py:422
  539.8 26.2 %collective-permute-start.18 = (bf16[960,4,128]{2,1,0:T(4,128)(2,1)S(1)}, bf16[960,4,128]{2,1,0:T(4,128)(2,1)S(1)}, u32[]{:S(2)}, u32[]{:S(2)}) collective-permute-start(bf16[960,4,128]{2,1,0:T(4,128)(2,1)S(1)} %copy-done), channel_id=1, source_target_pairs={{0,2},{1,3},{2,0},{3,1},{4,6},{5,7},{6,4},{7,5}} | collective-permute-start | bytes 2949128 | tf_op jit(solution)/shard_map/ppermute | solution.py:422
  541.3 24.8 %collective-permute-start.58 = (bf16[960,4,128]{2,1,0:T(4,128)(2,1)S(1)}, bf16[960,4,128]{2,1,0:T(4,128)(2,1)S(1)}, u32[]{:S(2)}, u32[]{:S(2)}) collective-permute-start(bf16[960,4,128]{2,1,0:T(4,128)(2,1)S(1)} %copy-done), channel_id=1, source_target_pairs={{0,4},{1,5},{2,6},{3,7},{4,0},{5,1},{6,2},{7,3}} | collective-permute-start | bytes 2949128 | tf_op jit(solution)/shard_map/ppermute | solution.py:422
  548.2 19.3 %collective-permute-start.59 = (bf16[960,4,128]{2,1,0:T(4,128)(2,1)S(1)}, bf16[960,4,128]{2,1,0:T(4,128)(2,1)S(1)}, u32[]{:S(2)}, u32[]{:S(2)}) collective-permute-start(bf16[960,4,128]{2,1,0:T(4,128)(2,1)S(1)} %copy-done), channel_id=1, source_target_pairs={{0,1},{1,0},{2,3},{3,2},{4,5},{5,4},{6,7},{7,6}} | collective-permute-start | bytes 2949128 | tf_op jit(solution)/shard_map/ppermute | solution.py:422
  549.1 38.0 %collective-permute-start.54 = (bf16[960,4,128]{2,1,0:T(4,128)(2,1)S(1)}, bf16[960,4,128]{2,1,0:T(4,128)(2,1)S(1)}, u32[]{:S(2)}, u32[]{:S(2)}) collective-permute-start(bf16[960,4,128]{2,1,0:T(4,128)(2,1)S(1)} %copy-done.1), channel_id=1, source_target_pairs={{0,2},{1,3},{2,0},{3,1},{4,6},{5,7},{6,4},{7,5}} | collective-permute-start | bytes 2949128 | tf_op jit(solution)/shard_map/ppermute | solution.py:422
  551.4 35.7 %collective-permute-start.21 = (bf16[960,4,128]{2,1,0:T(4,128)(2,1)S(1)}, bf16[960,4,128]{2,1,0:T(4,128)(2,1)S(1)}, u32[]{:S(2)}, u32[]{:S(2)}) collective-permute-start(bf16[960,4,128]{2,1,0:T(4,128)(2,1)S(1)} %copy-done.1), channel_id=1, source_target_pairs={{0,4},{1,5},{2,6},{3,7},{4,0},{5,1},{6,2},{7,3}} | collective-permute-start | bytes 2949128 | tf_op jit(solution)/shard_map/ppermute | solution.py:422
  566.1 22.6 %collective-permute-start.55 = (bf16[960,4,128]{2,1,0:T(4,128)(2,1)S(1)}, bf16[960,4,128]{2,1,0:T(4,128)(2,1)S(1)}, u32[]{:S(2)}, u32[]{:S(2)}) collective-permute-start(bf16[960,4,128]{2,1,0:T(4,128)(2,1)S(1)} %copy-done.1), channel_id=1, source_target_pairs={{0,1},{1,0},{2,3},{3,2},{4,5},{5,4},{6,7},{7,6}} | collective-permute-start | bytes 2949128 | tf_op jit(solution)/shard_map/ppermute | solution.py:422
  566.1 42.1 %collective-permute-start.12 = (bf16[960,4,128]{2,1,0:T(4,128)(2,1)S(1)}, bf16[960,4,128]{2,1,0:T(4,128)(2,1)S(1)}, u32[]{:S(2)}, u32[]{:S(2)}) collective-permute-start(bf16[960,4,128]{2,1,0:T(4,128)(2,1)S(1)} %copy-done.2), channel_id=1, source_target_pairs={{0,2},{1,3},{2,0},{3,1},{4,6},{5,7},{6,4},{7,5}} | collective-permute-start | bytes 2949128 | tf_op jit(solution)/shard_map/ppermute | solution.py:422
  567.6 40.6 %collective-permute-start.50 = (bf16[960,4,128]{2,1,0:T(4,128)(2,1)S(1)}, bf16[960,4,128]{2,1,0:T(4,128)(2,1)S(1)}, u32[]{:S(2)}, u32[]{:S(2)}) collective-permute-start(bf16[960,4,128]{2,1,0:T(4,128)(2,1)S(1)} %copy-done.2), channel_id=1, source_target_pairs={{0,4},{1,5},{2,6},{3,7},{4,0},{5,1},{6,2},{7,3}} | collective-permute-start | bytes 2949128 | tf_op jit(solution)/shard_map/ppermute | solution.py:422
  587.1 21.6 %collective-permute-start.51 = (bf16[960,4,128]{2,1,0:T(4,128)(2,1)S(1)}, bf16[960,4,128]{2,1,0:T(4,128)(2,1)S(1)}, u32[]{:S(2)}, u32[]{:S(2)}) collective-permute-start(bf16[960,4,128]{2,1,0:T(4,128)(2,1)S(1)} %copy-done.2), channel_id=1, source_target_pairs={{0,1},{1,0},{2,3},{3,2},{4,5},{5,4},{6,7},{7,6}} | collective-permute-start | bytes 2949128 | tf_op jit(solution)/shard_map/ppermute | solution.py:422
  587.1 41.4 %collective-permute-start.46 = (bf16[960,4,128]{2,1,0:T(4,128)(2,1)S(1)}, bf16[960,4,128]{2,1,0:T(4,128)(2,1)S(1)}, u32[]{:S(2)}, u32[]{:S(2)}) collective-permute-start(bf16[960,4,128]{2,1,0:T(4,128)(2,1)S(1)} %copy-done.3), channel_id=1, source_target_pairs={{0,2},{1,3},{2,0},{3,1},{4,6},{5,7},{6,4},{7,5}} | collective-permute-start | bytes 2949128 | tf_op jit(solution)/shard_map/ppermute | solution.py:422
  589.6 40.3 %collective-permute-start.15 = (bf16[960,4,128]{2,1,0:T(4,128)(2,1)S(1)}, bf16[960,4,128]{2,1,0:T(4,128)(2,1)S(1)}, u32[]{:S(2)}, u32[]{:S(2)}) collective-permute-start(bf16[960,4,128]{2,1,0:T(4,128)(2,1)S(1)} %copy-done.3), channel_id=1, source_target_pairs={{0,4},{1,5},{2,6},{3,7},{4,0},{5,1},{6,2},{7,3}} | collective-permute-start | bytes 2949128 | tf_op jit(solution)/shard_map/ppermute | solution.py:422
  608.2 23.2 %collective-permute-start.47 = (bf16[960,4,128]{2,1,0:T(4,128)(2,1)S(1)}, bf16[960,4,128]{2,1,0:T(4,128)(2,1)S(1)}, u32[]{:S(2)}, u32[]{:S(2)}) collective-permute-start(bf16[960,4,128]{2,1,0:T(4,128)(2,1)S(1)} %copy-done.3), channel_id=1, source_target_pairs={{0,1},{1,0},{2,3},{3,2},{4,5},{5,4},{6,7},{7,6}} | collective-permute-start | bytes 2949128 | tf_op jit(solution)/shard_map/ppermute | solution.py:422
  608.2 24.1 %collective-permute-start.44 = (bf16[480,4,128]{2,1,0:T(4,128)(2,1)S(1)}, bf16[480,4,128]{2,1,0:T(4,128)(2,1)S(1)}, u32[]{:S(2)}, u32[]{:S(2)}) collective-permute-start(bf16[480,4,128]{2,1,0:T(4,128)(2,1)S(1)} %collective-permute-done.refs_1_), channel_id=1, source_target_pairs={{0,1},{1,0},{2,3},{3,2},{4,5},{5,4},{6,7},{7,6}} | collective-permute-start | bytes 1474568 | tf_op jit(solution)/shard_map/ppermute | solution.py:422
  609.7 23.9 %collective-permute-start.45 = (bf16[480,4,128]{2,1,0:T(4,128)(2,1)S(1)}, bf16[480,4,128]{2,1,0:T(4,128)(2,1)S(1)}, u32[]{:S(2)}, u32[]{:S(2)}) collective-permute-start(bf16[480,4,128]{2,1,0:T(4,128)(2,1)S(1)} %collective-permute-done.42.refs_2_), channel_id=1, source_target_pairs={{0,1},{1,0},{2,3},{3,2},{4,5},{5,4},{6,7},{7,6}} | collective-permute-start | bytes 1474568 | tf_op jit(solution)/shard_map/ppermute | solution.py:422
  628.5 14.3 %collective-permute-start.25 = (bf16[480,4,128]{2,1,0:T(4,128)(2,1)}, bf16[480,4,128]{2,1,0:T(4,128)(2,1)S(1)}, u32[]{:S(2)}, u32[]{:S(2)}) collective-permute-start(bf16[480,4,128]{2,1,0:T(4,128)(2,1)} %collective-permute-done.24.refs_1_), channel_id=1, source_target_pairs={{0,4},{1,5},{2,6},{3,7},{4,0},{5,1},{6,2},{7,3}} | collective-permute-start | bytes 1474568 | tf_op jit(solution)/shard_map/ppermute | solution.py:422
  629.9 22.0 %collective-permute-start.1 = (bf16[480,4,128]{2,1,0:T(4,128)(2,1)S(1)}, bf16[480,4,128]{2,1,0:T(4,128)(2,1)}, u32[]{:S(2)}, u32[]{:S(2)}) collective-permute-start(bf16[480,4,128]{2,1,0:T(4,128)(2,1)S(1)} %collective-permute-done.refs_1_), channel_id=1, source_target_pairs={{0,4},{1,5},{2,6},{3,7},{4,0},{5,1},{6,2},{7,3}} | collective-permute-start | bytes 1474568 | tf_op jit(solution)/shard_map/ppermute | solution.py:422
  632.3 21.9 %collective-permute-start.65 = (bf16[720,4,128]{2,1,0:T(4,128)(2,1)S(1)}, bf16[720,4,128]{2,1,0:T(4,128)(2,1)S(1)}, u32[]{:S(2)}, u32[]{:S(2)}) collective-permute-start(bf16[720,4,128]{2,1,0:T(4,128)(2,1)S(1)} %collective-permute-done.27.refs_2_), channel_id=1, source_target_pairs={{0,1},{1,0},{2,3},{3,2},{4,5},{5,4},{6,7},{7,6}} | collective-permute-start | bytes 2211848 | tf_op jit(solution)/shard_map/ppermute | solution.py:422
  633.1 37.0 %collective-permute-start.60 = (bf16[960,4,128]{2,1,0:T(4,128)(2,1)S(1)}, bf16[960,4,128]{2,1,0:T(4,128)(2,1)S(1)}, u32[]{:S(2)}, u32[]{:S(2)}) collective-permute-start(bf16[960,4,128]{2,1,0:T(4,128)(2,1)S(1)} %collective-permute-done.18.refs_1_), channel_id=1, source_target_pairs={{0,1},{1,0},{2,3},{3,2},{4,5},{5,4},{6,7},{7,6}} | collective-permute-start | bytes 2949128 | tf_op jit(solution)/shard_map/ppermute | solution.py:422
  634.4 37.6 %collective-permute-start.61 = (bf16[960,4,128]{2,1,0:T(4,128)(2,1)S(1)}, bf16[960,4,128]{2,1,0:T(4,128)(2,1)S(1)}, u32[]{:S(2)}, u32[]{:S(2)}) collective-permute-start(bf16[960,4,128]{2,1,0:T(4,128)(2,1)S(1)} %collective-permute-done.58.refs_2_), channel_id=1, source_target_pairs={{0,1},{1,0},{2,3},{3,2},{4,5},{5,4},{6,7},{7,6}} | collective-permute-start | bytes 2949128 | tf_op jit(solution)/shard_map/ppermute | solution.py:422
  642.8 13.0 %collective-permute-start.64 = (bf16[720,4,128]{2,1,0:T(4,128)(2,1)S(1)}, bf16[720,4,128]{2,1,0:T(4,128)(2,1)S(1)}, u32[]{:S(2)}, u32[]{:S(2)}) collective-permute-start(bf16[720,4,128]{2,1,0:T(4,128)(2,1)S(1)} %collective-permute-done.62.refs_1_), channel_id=1, source_target_pairs={{0,1},{1,0},{2,3},{3,2},{4,5},{5,4},{6,7},{7,6}} | collective-permute-start | bytes 2211848 | tf_op jit(solution)/shard_map/ppermute | solution.py:422
  651.9 16.9 %collective-permute-start.28 = (bf16[720,4,128]{2,1,0:T(4,128)(2,1)S(1)}, bf16[720,4,128]{2,1,0:T(4,128)(2,1)S(1)}, u32[]{:S(2)}, u32[]{:S(2)}) collective-permute-start(bf16[720,4,128]{2,1,0:T(4,128)(2,1)S(1)} %collective-permute-done.27.refs_2_), channel_id=1, source_target_pairs={{0,2},{1,3},{2,0},{3,1},{4,6},{5,7},{6,4},{7,5}} | collective-permute-start | bytes 2211848 | tf_op jit(solution)/shard_map/ppermute | solution.py:422
  655.1 13.7 %collective-permute-start.26 = (bf16[480,4,128]{2,1,0:T(4,128)(2,1)S(1)}, bf16[480,4,128]{2,1,0:T(4,128)(2,1)S(1)}, u32[]{:S(2)}, u32[]{:S(2)}) collective-permute-start(bf16[480,4,128]{2,1,0:T(4,128)(2,1)S(1)} %collective-permute-done.25.refs_0_), channel_id=1, source_target_pairs={{0,1},{1,0},{2,3},{3,2},{4,5},{5,4},{6,7},{7,6}} | collective-permute-start | bytes 1474568 | tf_op jit(solution)/shard_map/ppermute | solution.py:422
  656.7 17.8 %collective-permute-start.56 = (bf16[960,4,128]{2,1,0:T(4,128)(2,1)S(1)}, bf16[960,4,128]{2,1,0:T(4,128)(2,1)S(1)}, u32[]{:S(2)}, u32[]{:S(2)}) collective-permute-start(bf16[960,4,128]{2,1,0:T(4,128)(2,1)S(1)} %collective-permute-done.54.refs_1_), channel_id=1, source_target_pairs={{0,1},{1,0},{2,3},{3,2},{4,5},{5,4},{6,7},{7,6}} | collective-permute-start | bytes 2949128 | tf_op jit(solution)/shard_map/ppermute | solution.py:422
  668.8 9.1 %collective-permute-start.57 = (bf16[960,4,128]{2,1,0:T(4,128)(2,1)S(1)}, bf16[960,4,128]{2,1,0:T(4,128)(2,1)S(1)}, u32[]{:S(2)}, u32[]{:S(2)}) collective-permute-start(bf16[960,4,128]{2,1,0:T(4,128)(2,1)S(1)} %collective-permute-done.21.refs_2_), channel_id=1, source_target_pairs={{0,1},{1,0},{2,3},{3,2},{4,5},{5,4},{6,7},{7,6}} | collective-permute-start | bytes 2949128 | tf_op jit(solution)/shard_map/ppermute | solution.py:422
  669.6 9.8 %collective-permute-start.52 = (bf16[960,4,128]{2,1,0:T(4,128)(2,1)S(1)}, bf16[960,4,128]{2,1,0:T(4,128)(2,1)S(1)}, u32[]{:S(2)}, u32[]{:S(2)}) collective-permute-start(bf16[960,4,128]{2,1,0:T(4,128)(2,1)S(1)} %collective-permute-done.12.refs_1_), channel_id=1, source_target_pairs={{0,1},{1,0},{2,3},{3,2},{4,5},{5,4},{6,7},{7,6}} | collective-permute-start | bytes 2949128 | tf_op jit(solution)/shard_map/ppermute | solution.py:422
  671.0 10.7 %collective-permute-start.53 = (bf16[960,4,128]{2,1,0:T(4,128)(2,1)S(1)}, bf16[960,4,128]{2,1,0:T(4,128)(2,1)S(1)}, u32[]{:S(2)}, u32[]{:S(2)}) collective-permute-start(bf16[960,4,128]{2,1,0:T(4,128)(2,1)S(1)} %collective-permute-done.50.refs_2_), channel_id=1, source_target_pairs={{0,1},{1,0},{2,3},{3,2},{4,5},{5,4},{6,7},{7,6}} | collective-permute-start | bytes 2949128 | tf_op jit(solution)/shard_map/ppermute | solution.py:422
  673.0 10.6 %collective-permute-start.48 = (bf16[960,4,128]{2,1,0:T(4,128)(2,1)S(1)}, bf16[960,4,128]{2,1,0:T(4,128)(2,1)S(1)}, u32[]{:S(2)}, u32[]{:S(2)}) collective-permute-start(bf16[960,4,128]{2,1,0:T(4,128)(2,1)S(1)} %collective-permute-done.46.refs_1_), channel_id=1, source_target_pairs={{0,1},{1,0},{2,3},{3,2},{4,5},{5,4},{6,7},{7,6}} | collective-permute-start | bytes 2949128 | tf_op jit(solution)/shard_map/ppermute | solution.py:422
  675.5 24.6 %collective-permute-start.22 = (bf16[960,4,128]{2,1,0:T(4,128)(2,1)S(1)}, bf16[960,4,128]{2,1,0:T(4,128)(2,1)S(1)}, u32[]{:S(2)}, u32[]{:S(2)}) collective-permute-start(bf16[960,4,128]{2,1,0:T(4,128)(2,1)S(1)} %collective-permute-done.21.refs_2_), channel_id=1, source_target_pairs={{0,2},{1,3},{2,0},{3,1},{4,6},{5,7},{6,4},{7,5}} | collective-permute-start | bytes 2949128 | tf_op jit(solution)/shard_map/ppermute | solution.py:422
  678.9 24.6 %collective-permute-start.19 = (bf16[960,4,128]{2,1,0:T(4,128)(2,1)S(1)}, bf16[960,4,128]{2,1,0:T(4,128)(2,1)S(1)}, u32[]{:S(2)}, u32[]{:S(2)}) collective-permute-start(bf16[960,4,128]{2,1,0:T(4,128)(2,1)S(1)} %collective-permute-done.18.refs_1_), channel_id=1, source_target_pairs={{0,4},{1,5},{2,6},{3,7},{4,0},{5,1},{6,2},{7,3}} | collective-permute-start | bytes 2949128 | tf_op jit(solution)/shard_map/ppermute | solution.py:422
  680.4 39.8 %collective-permute-start.16 = (bf16[960,4,128]{2,1,0:T(4,128)(2,1)S(1)}, bf16[960,4,128]{2,1,0:T(4,128)(2,1)S(1)}, u32[]{:S(2)}, u32[]{:S(2)}) collective-permute-start(bf16[960,4,128]{2,1,0:T(4,128)(2,1)S(1)} %collective-permute-done.15.refs_2_), channel_id=1, source_target_pairs={{0,2},{1,3},{2,0},{3,1},{4,6},{5,7},{6,4},{7,5}} | collective-permute-start | bytes 2949128 | tf_op jit(solution)/shard_map/ppermute | solution.py:422
  682.7 38.5 %collective-permute-start.49 = (bf16[960,4,128]{2,1,0:T(4,128)(2,1)S(1)}, bf16[960,4,128]{2,1,0:T(4,128)(2,1)S(1)}, u32[]{:S(2)}, u32[]{:S(2)}) collective-permute-start(bf16[960,4,128]{2,1,0:T(4,128)(2,1)S(1)} %collective-permute-done.15.refs_2_), channel_id=1, source_target_pairs={{0,1},{1,0},{2,3},{3,2},{4,5},{5,4},{6,7},{7,6}} | collective-permute-start | bytes 2949128 | tf_op jit(solution)/shard_map/ppermute | solution.py:422
  684.6 38.9 %collective-permute-start.13 = (bf16[960,4,128]{2,1,0:T(4,128)(2,1)S(1)}, bf16[960,4,128]{2,1,0:T(4,128)(2,1)}, u32[]{:S(2)}, u32[]{:S(2)}) collective-permute-start(bf16[960,4,128]{2,1,0:T(4,128)(2,1)S(1)} %collective-permute-done.12.refs_1_), channel_id=1, source_target_pairs={{0,4},{1,5},{2,6},{3,7},{4,0},{5,1},{6,2},{7,3}} | collective-permute-start | bytes 2949128 | tf_op jit(solution)/shard_map/ppermute | solution.py:422
  700.1 25.7 %collective-permute-start.23 = (bf16[960,4,128]{2,1,0:T(4,128)(2,1)S(1)}, bf16[960,4,128]{2,1,0:T(4,128)(2,1)S(1)}, u32[]{:S(2)}, u32[]{:S(2)}) collective-permute-start(bf16[960,4,128]{2,1,0:T(4,128)(2,1)S(1)} %collective-permute-done.22.refs_2_), channel_id=1, source_target_pairs={{0,1},{1,0},{2,3},{3,2},{4,5},{5,4},{6,7},{7,6}} | collective-permute-start | bytes 2949128 | tf_op jit(solution)/shard_map/ppermute | solution.py:422
  703.5 23.5 %collective-permute-start.20 = (bf16[960,4,128]{2,1,0:T(4,128)(2,1)S(1)}, bf16[960,4,128]{2,1,0:T(4,128)(2,1)S(1)}, u32[]{:S(2)}, u32[]{:S(2)}) collective-permute-start(bf16[960,4,128]{2,1,0:T(4,128)(2,1)S(1)} %collective-permute-done.19.refs_0_), channel_id=1, source_target_pairs={{0,1},{1,0},{2,3},{3,2},{4,5},{5,4},{6,7},{7,6}} | collective-permute-start | bytes 2949128 | tf_op jit(solution)/shard_map/ppermute | solution.py:422
  720.2 8.1 %collective-permute-start.17 = (bf16[960,4,128]{2,1,0:T(4,128)(2,1)S(1)}, bf16[960,4,128]{2,1,0:T(4,128)(2,1)S(1)}, u32[]{:S(2)}, u32[]{:S(2)}) collective-permute-start(bf16[960,4,128]{2,1,0:T(4,128)(2,1)S(1)} %collective-permute-done.16.refs_2_), channel_id=1, source_target_pairs={{0,1},{1,0},{2,3},{3,2},{4,5},{5,4},{6,7},{7,6}} | collective-permute-start | bytes 2949128 | tf_op jit(solution)/shard_map/ppermute | solution.py:422
  723.6 60.2 %collective-permute-start.14 = (bf16[960,4,128]{2,1,0:T(4,128)(2,1)}, bf16[960,4,128]{2,1,0:T(4,128)(2,1)}, u32[]{:S(2)}, u32[]{:S(2)}) collective-permute-start(bf16[960,4,128]{2,1,0:T(4,128)(2,1)} %collective-permute-done.13.refs_0_), channel_id=1, source_target_pairs={{0,1},{1,0},{2,3},{3,2},{4,5},{5,4},{6,7},{7,6}} | collective-permute-start | bytes 2949128 | tf_op jit(solution)/shard_map/ppermute | solution.py:422
  725.4 61.6 %collective-permute-start.2 = (bf16[480,4,128]{2,1,0:T(4,128)(2,1)}, bf16[480,4,128]{2,1,0:T(4,128)(2,1)}, u32[]{:S(2)}, u32[]{:S(2)}) collective-permute-start(bf16[480,4,128]{2,1,0:T(4,128)(2,1)} %collective-permute-done.1.refs_0_), channel_id=1, source_target_pairs={{0,1},{1,0},{2,3},{3,2},{4,5},{5,4},{6,7},{7,6}} | collective-permute-start | bytes 1474568 | tf_op jit(solution)/shard_map/ppermute | solution.py:422
  726.8 60.2 %collective-permute-start.11 = (bf16[240,4,128]{2,1,0:T(4,128)(2,1)}, bf16[240,4,128]{2,1,0:T(4,128)(2,1)}, u32[]{:S(2)}, u32[]{:S(2)}) collective-permute-start(bf16[240,4,128]{2,1,0:T(4,128)(2,1)} %collective-permute-done.10.refs_6_), channel_id=1, source_target_pairs={{0,1},{1,0},{2,3},{3,2},{4,5},{5,4},{6,7},{7,6}} | collective-permute-start | bytes 737288 | tf_op jit(solution)/shard_map/ppermute | solution.py:422
  727.9 59.1 %collective-permute-start.8 = (bf16[240,4,128]{2,1,0:T(4,128)(2,1)}, bf16[240,4,128]{2,1,0:T(4,128)(2,1)}, u32[]{:S(2)}, u32[]{:S(2)}) collective-permute-start(bf16[240,4,128]{2,1,0:T(4,128)(2,1)} %collective-permute-done.7.refs_4_), channel_id=1, source_target_pairs={{0,1},{1,0},{2,3},{3,2},{4,5},{5,4},{6,7},{7,6}} | collective-permute-start | bytes 737288 | tf_op jit(solution)/shard_map/ppermute | solution.py:422
  729.2 57.8 %collective-permute-start.5 = (bf16[240,4,128]{2,1,0:T(4,128)(2,1)}, bf16[240,4,128]{2,1,0:T(4,128)(2,1)}, u32[]{:S(2)}, u32[]{:S(2)}) collective-permute-start(bf16[240,4,128]{2,1,0:T(4,128)(2,1)} %collective-permute-done.4.refs_2_), channel_id=1, source_target_pairs={{0,1},{1,0},{2,3},{3,2},{4,5},{5,4},{6,7},{7,6}} | collective-permute-start | bytes 737288 | tf_op jit(solution)/shard_map/ppermute | solution.py:422
  (130 other events, 828.1 us)

commit v7 on v6

--- a/solution.py
+++ b/solution.py
@@ -17,12 +17,12 @@
 
 MESH = pl.DeviceIdType.MESH
 LANES = 128
-CHUNK_ROWS = 384
+CHUNK_ROWS = 480
 HALF_ROWS = CHUNK_ROWS // 2
 SLOTS = 4
 VMEM_LIMIT = 20 << 20
-ADAM_ROWS = 960
-PARTS = (2, 3, 4, 4, 4, 4, 2, 1, 1, 1)
+ADAM_ROWS = 480
+PARTS = (3, 5, 8, 8, 8, 7, 4, 3, 3, 3)
 TILE_ROWS = 120
 
 
@@ -442,14 +442,12 @@
             far.append(send(from_x, "y") if p % 2 == 0 else send(from_y, "x"))
             pieces = [packed, from_x, from_y, from_core, send(from_x, "core"), send(from_y, "core")]
             whole = put(pieces, [(k, starts[p]) for k in (0, 1, 2, 4, 5, 6)], whole)
-        pieces, spots = [], []
         for p in range(0, len(PARTS), 2):
+            pieces, spots = [], []
             for q in (p, p + 1):
                 pieces += [far[q], send(far[q], "core")]
                 spots += [(3, starts[q]), (7, starts[q])]
-            if p + 4 != len(PARTS):
-                whole = put(pieces, spots, whole, p + 2 == len(PARTS))
-                pieces, spots = [], []
+            whole = put(pieces, spots, whole, p + 2 == len(PARTS))
         new_w, new_m, new_v = state
         params = whole[0].reshape(num_dev * shard_len)
         return (params, new_w.reshape(shard_len), new_m.reshape(shard_len), new_v.reshape(shard_len),

time: 791 us -> 796 us (level)
  Pallas kernels: 524 us -> 535 us
    pallas_call x10, Pallas kernels: 48.1 us -> 63.3 us  [adamw(): pl.pallas_call(adamw_kernel, grid=(steps,), out_shape=(state, state, stat...]
    unnamed x248 -> x232, local copies, waits for them, and re-layouts: 51.6 us -> 46.6 us
    pallas_call x14 -> x15, Pallas kernels: 50.8 us -> 46.6 us  [store(): pl.pallas_call(functools.partial(store_kernel, [(which, start, min(p.shap...]
  transfers between devices with their start and end apart: 70 -> 70, of which waited for: 19 -> 20; matrix products, arithmetic and copies ran while one was open for 0% -> 0% of each run, Pallas kernels for 7% -> 14%
where the time goes in v7:
time: 796 us; the launch traced here: 794 us
  Pallas kernels  535 us (67%)
  waiting for transfers between devices  173 us (22%)
  local copies, waits for them, and re-layouts  46.6 us (6%)
  starting transfers between devices  37.1 us (5%)
    pallas_call x1, Pallas kernels, reduce_scatter(): pl.pallas_call(functools.partial(reduce_kernel, shard_rows), out_shape=(s...  425 us
    ppermute x70, waiting for transfers between devices, send(): return lax.ppermute(a, 'dp', hop[along])  173 us
    pallas_call x10, Pallas kernels, adamw(): pl.pallas_call(adamw_kernel, grid=(steps,), out_shape=(state, state, stat...  63.3 us
    unnamed x232, local copies, waits for them, and re-layouts  46.6 us
    pallas_call x15, Pallas kernels, store(): pl.pallas_call(functools.partial(store_kernel, [(which, start, min(p.shap...  46.6 us
    ppermute x70, starting transfers between devices, send(): return lax.ppermute(a, 'dp', hop[along])  37.1 us
  transfers between devices with their start and end apart: 70, of which 20 were waited for; matrix products, arithmetic and copies ran while one was open for 0% of the time, Pallas kernels for 14%

profile of v7, /device:TPU:0, one launch (start us, length us, event | category | flops | bytes accessed | tf_op | source)
XLA Modules:
  0.0 794.4 jit_solution(3594174309826447494)
XLA Ops:
  1.3 425.1 %shard_map.101 = (f32[24960,128]{1,0:T(8,128)S(1)}, f32[24960,128]{1,0:T(8,128)S(1)}, f32[24960,128]{1,0:T(8,128)S(1)}, bf16[360,4,128]{2,1,0:T(4,128)(2,1)}, f32[8,128]{1,0:T(8,128)}) custom-call(f32[1]{0:T(128)S(6)} %copy.93.lr, bf16[1,25530368]{1,0:T(2,128)(2,1)} %grad.1, f32[24932,128]{1,0:T(8,128)} %bitcast.34, f32[24932,128]{1,0:T(8,128)} %bitcast.35, ...), custom_call_target="tpu_custom_call" | custom-call | tf_op jit(solution)/shard_map/pallas_call | solution.py:307
  426.4 1.1 collective-permute-start.24
  427.5 1.0 collective-permute-start.66
  428.5 6.4 shard_map.102
  434.9 8.8 %shard_map.103 = (f32[24932,128]{1,0:T(8,128)}, f32[24932,128]{1,0:T(8,128)}, f32[24932,128]{1,0:T(8,128)}, bf16[960,4,128]{2,1,0:T(4,128)(2,1)}, f32[1]{0:T(128)}) custom-call(f32[1]{0:T(128)S(6)} %copy.93.lr, f32[8,128]{1,0:T(8,128)} %get-tuple-element.50.norm, ...), custom_call_target="tpu_custom_call", output_to_operand_aliasing={{0}: (7, {}), {1}: (8, {}), {2}: (9, {})} | custom-call | flops 589824000 | bytes 9830400 | tf_op jit(solution)/shard_map/pallas_call | solution.py:347
  443.7 8.8 %shard_map.104 = (f32[24932,128]{1,0:T(8,128)}, f32[24932,128]{1,0:T(8,128)}, f32[24932,128]{1,0:T(8,128)}, bf16[960,4,128]{2,1,0:T(4,128)(2,1)}, f32[1]{0:T(128)}) custom-call(f32[1]{0:T(128)S(6)} %copy.93.lr, f32[8,128]{1,0:T(8,128)} %get-tuple-element.50.norm, ...), custom_call_target="tpu_custom_call", output_to_operand_aliasing={{0}: (7, {}), {1}: (8, {}), {2}: (9, {})} | custom-call | flops 589824000 | bytes 9830400 | tf_op jit(solution)/shard_map/pallas_call | solution.py:347
  452.4 8.8 %shard_map.105 = (f32[24932,128]{1,0:T(8,128)}, f32[24932,128]{1,0:T(8,128)}, f32[24932,128]{1,0:T(8,128)}, bf16[960,4,128]{2,1,0:T(4,128)(2,1)}, f32[1]{0:T(128)}) custom-call(f32[1]{0:T(128)S(6)} %copy.93.lr, f32[8,128]{1,0:T(8,128)} %get-tuple-element.50.norm, ...), custom_call_target="tpu_custom_call", output_to_operand_aliasing={{0}: (7, {}), {1}: (8, {}), {2}: (9, {})} | custom-call | flops 589824000 | bytes 9830400 | tf_op jit(solution)/shard_map/pallas_call | solution.py:347
  461.2 8.4 %shard_map.106 = (f32[24932,128]{1,0:T(8,128)}, f32[24932,128]{1,0:T(8,128)}, f32[24932,128]{1,0:T(8,128)}, bf16[840,4,128]{2,1,0:T(4,128)(2,1)}, f32[1]{0:T(128)}) custom-call(f32[1]{0:T(128)S(6)} %copy.93.lr, f32[8,128]{1,0:T(8,128)} %get-tuple-element.50.norm, ...), custom_call_target="tpu_custom_call", output_to_operand_aliasing={{0}: (7, {}), {1}: (8, {}), {2}: (9, {})} | custom-call | flops 516096000 | bytes 8601600 | tf_op jit(solution)/shard_map/pallas_call | solution.py:347
  469.6 4.7 shard_map.107
  474.3 4.3 shard_map.108
  479.5 1.0 collective-permute-start.9
  480.6 4.4 shard_map.109
  485.0 1.1 collective-permute-start
  486.1 1.0 collective-permute-start.34
  487.1 3.2 collective-permute-done.38.refs_1_
  491.2 4.4 shard_map.110
  496.5 1.1 collective-permute-start.30
  498.2 1.0 collective-permute-start.3
  500.0 1.0 collective-permute-start.27
  501.0 15.2 %collective-permute-done.30.refs_1_ = bf16[360,4,128]{2,1,0:T(4,128)(2,1)S(1)} collective-permute-done((bf16[360,4,128]{2,1,0:T(4,128)(2,1)}, bf16[360,4,128]{2,1,0:T(4,128)(2,1)S(1)}, u32[]{:S(2)}, u32[]{:S(2)}) %collective-permute-start.30) | collective-permute-done | bytes 368672 | tf_op jit(solution)/shard_map/ppermute | solution.py:422
  516.2 1.0 collective-permute-start.42
  519.4 12.9 %collective-permute-done.42.refs_2_ = bf16[480,4,128]{2,1,0:T(4,128)(2,1)S(1)} collective-permute-done((bf16[480,4,128]{2,1,0:T(4,128)(2,1)S(1)}, bf16[480,4,128]{2,1,0:T(4,128)(2,1)S(1)}, u32[]{:S(2)}, u32[]{:S(2)}) %collective-permute-start.42) | collective-permute-done | bytes 491552 | tf_op jit(solution)/shard_map/ppermute | solution.py:422
  542.1 1.0 collective-permute-start.25
  545.6 1.1 collective-permute-start.10
  549.9 3.9 collective-permute-done.25.refs_0_
  553.7 1.0 collective-permute-start.1
  555.5 15.1 %collective-permute-done.10.refs_2_ = bf16[360,4,128]{2,1,0:T(4,128)(2,1)} collective-permute-done((bf16[360,4,128]{2,1,0:T(4,128)(2,1)S(1)}, bf16[360,4,128]{2,1,0:T(4,128)(2,1)}, u32[]{:S(2)}, u32[]{:S(2)}) %collective-permute-start.10) | collective-permute-done | bytes 368672 | tf_op jit(solution)/shard_map/ppermute | solution.py:422
  571.5 7.0 collective-permute-done.4.refs_2_
  578.5 1.0 collective-permute-start.58
  581.0 1.2 collective-permute-done.47.refs_3_
  583.0 1.0 collective-permute-start.21
  584.1 15.4 %collective-permute-done.18.refs_1_ = bf16[960,4,128]{2,1,0:T(4,128)(2,1)S(1)} collective-permute-done((bf16[960,4,128]{2,1,0:T(4,128)(2,1)S(1)}, bf16[960,4,128]{2,1,0:T(4,128)(2,1)S(1)}, u32[]{:S(2)}, u32[]{:S(2)}) %collective-permute-start.18) | collective-permute-done | bytes 983072 | tf_op jit(solution)/shard_map/ppermute | solution.py:422
  599.5 3.7 collective-permute-done.58.refs_2_
  604.1 1.0 collective-permute-start.50
  605.1 15.5 %collective-permute-done.54.refs_1_ = bf16[960,4,128]{2,1,0:T(4,128)(2,1)S(1)} collective-permute-done((bf16[960,4,128]{2,1,0:T(4,128)(2,1)S(1)}, bf16[960,4,128]{2,1,0:T(4,128)(2,1)S(1)}, u32[]{:S(2)}, u32[]{:S(2)}) %collective-permute-start.54) | collective-permute-done | bytes 983072 | tf_op jit(solution)/shard_map/ppermute | solution.py:422
  620.5 3.7 collective-permute-done.21.refs_2_
  626.5 14.2 %collective-permute-done.12.refs_1_ = bf16[960,4,128]{2,1,0:T(4,128)(2,1)S(1)} collective-permute-done((bf16[960,4,128]{2,1,0:T(4,128)(2,1)S(1)}, bf16[960,4,128]{2,1,0:T(4,128)(2,1)S(1)}, u32[]{:S(2)}, u32[]{:S(2)}) %collective-permute-start.12) | collective-permute-done | bytes 983072 | tf_op jit(solution)/shard_map/ppermute | solution.py:422
  640.7 1.0 collective-permute-start.7
  648.6 4.7 collective-permute-done.7.refs_0_
  656.7 1.1 collective-permute-start.16
  659.8 10.2 %collective-permute-done.28.refs_2_ = bf16[600,4,128]{2,1,0:T(4,128)(2,1)S(1)} collective-permute-done((bf16[600,4,128]{2,1,0:T(4,128)(2,1)S(1)}, bf16[600,4,128]{2,1,0:T(4,128)(2,1)S(1)}, u32[]{:S(2)}, u32[]{:S(2)}) %collective-permute-start.28) | collective-permute-done | bytes 614432 | tf_op jit(solution)/shard_map/ppermute | solution.py:422
  673.2 12.6 %collective-permute-done.16.refs_2_ = bf16[840,4,128]{2,1,0:T(4,128)(2,1)S(1)} collective-permute-done((bf16[840,4,128]{2,1,0:T(4,128)(2,1)S(1)}, bf16[840,4,128]{2,1,0:T(4,128)(2,1)S(1)}, u32[]{:S(2)}, u32[]{:S(2)}) %collective-permute-start.16) | collective-permute-done | bytes 860192 | tf_op jit(solution)/shard_map/ppermute | solution.py:422
  689.5 1.0 collective-permute-start.19
  691.5 1.0 copy-done.23
  696.6 14.2 %collective-permute-done.22.refs_2_ = bf16[960,4,128]{2,1,0:T(4,128)(2,1)S(1)} collective-permute-done((bf16[960,4,128]{2,1,0:T(4,128)(2,1)S(1)}, bf16[960,4,128]{2,1,0:T(4,128)(2,1)S(1)}, u32[]{:S(2)}, u32[]{:S(2)}) %collective-permute-start.22) | collective-permute-done | bytes 983072 | tf_op jit(solution)/shard_map/ppermute | solution.py:422
  711.7 2.4 collective-permute-done.19.refs_0_
  717.5 17.0 %collective-permute-done.13.refs_0_ = bf16[960,4,128]{2,1,0:T(4,128)(2,1)} collective-permute-done((bf16[960,4,128]{2,1,0:T(4,128)(2,1)S(1)}, bf16[960,4,128]{2,1,0:T(4,128)(2,1)}, u32[]{:S(2)}, u32[]{:S(2)}) %collective-permute-start.13) | collective-permute-done | bytes 983072 | tf_op jit(solution)/shard_map/ppermute | solution.py:422
  738.5 1.0 copy-done.25
  739.5 4.3 shard_map.126
  745.8 2.6 shard_map.111.refs_6_
  748.5 2.8 shard_map.112.refs_6_
  751.4 4.5 shard_map.113.refs_6_
  756.1 4.5 shard_map.114.refs_6_
  760.7 4.5 shard_map.115.refs_6_
  765.4 3.7 shard_map.116.refs_6_
  769.2 3.6 shard_map.117.refs_6_
  772.9 2.4 shard_map.118.refs_6_
  775.5 2.4 shard_map.119.refs_6_
  778.0 2.3 shard_map.120.refs_4_
  780.4 2.0 shard_map.121.refs_4_
  783.2 3.2 shard_map.122.refs_4_
  786.4 3.1 shard_map.123.refs_4_
  789.6 2.3 shard_map.124.refs_4_
  791.9 2.5 shard_map.125
  (334 shorter events, 64.4 us)
Async XLA Ops:
  426.4 54.2 %collective-permute-start.24 = (bf16[360,4,128]{2,1,0:T(4,128)(2,1)}, bf16[360,4,128]{2,1,0:T(4,128)(2,1)}, u32[]{:S(2)}, u32[]{:S(2)}) collective-permute-start(bf16[360,4,128]{2,1,0:T(4,128)(2,1)} %get-tuple-element.86.refs_0_), channel_id=1, source_target_pairs={{0,2},{1,3},{2,0},{3,1},{4,6},{5,7},{6,4},{7,5}} | collective-permute-start | bytes 1105928 | tf_op jit(solution)/shard_map/ppermute | solution.py:422
  427.5 57.5 %collective-permute-start.66 = (bf16[360,4,128]{2,1,0:T(4,128)(2,1)}, bf16[360,4,128]{2,1,0:T(4,128)(2,1)}, u32[]{:S(2)}, u32[]{:S(2)}) collective-permute-start(bf16[360,4,128]{2,1,0:T(4,128)(2,1)} %get-tuple-element.86.refs_0_), channel_id=1, source_target_pairs={{0,4},{1,5},{2,6},{3,7},{4,0},{5,1},{6,2},{7,3}} | collective-permute-start | bytes 1105928 | tf_op jit(solution)/shard_map/ppermute | solution.py:422
  428.5 57.6 %collective-permute-start.67 = (bf16[360,4,128]{2,1,0:T(4,128)(2,1)}, bf16[360,4,128]{2,1,0:T(4,128)(2,1)}, u32[]{:S(2)}, u32[]{:S(2)}) collective-permute-start(bf16[360,4,128]{2,1,0:T(4,128)(2,1)} %get-tuple-element.86.refs_0_), channel_id=1, source_target_pairs={{0,1},{1,0},{2,3},{3,2},{4,5},{5,4},{6,7},{7,6}} | collective-permute-start | bytes 1105928 | tf_op jit(solution)/shard_map/ppermute | solution.py:422
  478.6 11.7 %collective-permute-start.38 = (bf16[360,4,128]{2,1,0:T(4,128)(2,1)}, bf16[360,4,128]{2,1,0:T(4,128)(2,1)S(1)}, u32[]{:S(2)}, u32[]{:S(2)}) collective-permute-start(bf16[360,4,128]{2,1,0:T(4,128)(2,1)} %get-tuple-element.81.refs_0_), channel_id=1, source_target_pairs={{0,2},{1,3},{2,0},{3,1},{4,6},{5,7},{6,4},{7,5}} | collective-permute-start | bytes 1105928 | tf_op jit(solution)/shard_map/ppermute | solution.py:422
  479.5 16.2 %collective-permute-start.9 = (bf16[360,4,128]{2,1,0:T(4,128)(2,1)}, bf16[360,4,128]{2,1,0:T(4,128)(2,1)S(1)}, u32[]{:S(2)}, u32[]{:S(2)}) collective-permute-start(bf16[360,4,128]{2,1,0:T(4,128)(2,1)} %get-tuple-element.81.refs_0_), channel_id=1, source_target_pairs={{0,4},{1,5},{2,6},{3,7},{4,0},{5,1},{6,2},{7,3}} | collective-permute-start | bytes 1105928 | tf_op jit(solution)/shard_map/ppermute | solution.py:422
  480.6 15.2 %collective-permute-start.39 = (bf16[360,4,128]{2,1,0:T(4,128)(2,1)}, bf16[360,4,128]{2,1,0:T(4,128)(2,1)S(1)}, u32[]{:S(2)}, u32[]{:S(2)}) collective-permute-start(bf16[360,4,128]{2,1,0:T(4,128)(2,1)} %get-tuple-element.81.refs_0_), channel_id=1, source_target_pairs={{0,1},{1,0},{2,3},{3,2},{4,5},{5,4},{6,7},{7,6}} | collective-permute-start | bytes 1105928 | tf_op jit(solution)/shard_map/ppermute | solution.py:422
  485.0 13.2 %collective-permute-start = (bf16[360,4,128]{2,1,0:T(4,128)(2,1)}, bf16[360,4,128]{2,1,0:T(4,128)(2,1)S(1)}, u32[]{:S(2)}, u32[]{:S(2)}) collective-permute-start(bf16[360,4,128]{2,1,0:T(4,128)(2,1)} %get-tuple-element.75.refs_0_), channel_id=1, source_target_pairs={{0,2},{1,3},{2,0},{3,1},{4,6},{5,7},{6,4},{7,5}} | collective-permute-start | bytes 1105928 | tf_op jit(solution)/shard_map/ppermute | solution.py:422
  486.1 13.1 %collective-permute-start.34 = (bf16[360,4,128]{2,1,0:T(4,128)(2,1)}, bf16[360,4,128]{2,1,0:T(4,128)(2,1)S(1)}, u32[]{:S(2)}, u32[]{:S(2)}) collective-permute-start(bf16[360,4,128]{2,1,0:T(4,128)(2,1)} %get-tuple-element.75.refs_0_), channel_id=1, source_target_pairs={{0,4},{1,5},{2,6},{3,7},{4,0},{5,1},{6,2},{7,3}} | collective-permute-start | bytes 1105928 | tf_op jit(solution)/shard_map/ppermute | solution.py:422
  490.3 28.5 %collective-permute-start.6 = (bf16[480,4,128]{2,1,0:T(4,128)(2,1)S(1)}, bf16[480,4,128]{2,1,0:T(4,128)(2,1)S(1)}, u32[]{:S(2)}, u32[]{:S(2)}) collective-permute-start(bf16[480,4,128]{2,1,0:T(4,128)(2,1)S(1)} %copy-done.62), channel_id=1, source_target_pairs={{0,2},{1,3},{2,0},{3,1},{4,6},{5,7},{6,4},{7,5}} | collective-permute-start | bytes 1474568 | tf_op jit(solution)/shard_map/ppermute | solution.py:422
  496.5 19.7 %collective-permute-start.30 = (bf16[360,4,128]{2,1,0:T(4,128)(2,1)}, bf16[360,4,128]{2,1,0:T(4,128)(2,1)S(1)}, u32[]{:S(2)}, u32[]{:S(2)}) collective-permute-start(bf16[360,4,128]{2,1,0:T(4,128)(2,1)} %get-tuple-element.79.refs_0_), channel_id=1, source_target_pairs={{0,2},{1,3},{2,0},{3,1},{4,6},{5,7},{6,4},{7,5}} | collective-permute-start | bytes 1105928 | tf_op jit(solution)/shard_map/ppermute | solution.py:422
  498.2 19.0 %collective-permute-start.3 = (bf16[360,4,128]{2,1,0:T(4,128)(2,1)}, bf16[360,4,128]{2,1,0:T(4,128)(2,1)S(1)}, u32[]{:S(2)}, u32[]{:S(2)}) collective-permute-start(bf16[360,4,128]{2,1,0:T(4,128)(2,1)} %get-tuple-element.79.refs_0_), channel_id=1, source_target_pairs={{0,4},{1,5},{2,6},{3,7},{4,0},{5,1},{6,2},{7,3}} | collective-permute-start | bytes 1105928 | tf_op jit(solution)/shard_map/ppermute | solution.py:422
  499.2 18.9 %collective-permute-start.31 = (bf16[360,4,128]{2,1,0:T(4,128)(2,1)}, bf16[360,4,128]{2,1,0:T(4,128)(2,1)S(1)}, u32[]{:S(2)}, u32[]{:S(2)}) collective-permute-start(bf16[360,4,128]{2,1,0:T(4,128)(2,1)} %get-tuple-element.79.refs_0_), channel_id=1, source_target_pairs={{0,1},{1,0},{2,3},{3,2},{4,5},{5,4},{6,7},{7,6}} | collective-permute-start | bytes 1105928 | tf_op jit(solution)/shard_map/ppermute | solution.py:422
  500.0 33.6 %collective-permute-start.27 = (bf16[600,4,128]{2,1,0:T(4,128)(2,1)S(1)}, bf16[600,4,128]{2,1,0:T(4,128)(2,1)S(1)}, u32[]{:S(2)}, u32[]{:S(2)}) collective-permute-start(bf16[600,4,128]{2,1,0:T(4,128)(2,1)S(1)} %copy-done.47), channel_id=1, source_target_pairs={{0,4},{1,5},{2,6},{3,7},{4,0},{5,1},{6,2},{7,3}} | collective-permute-start | bytes 1843208 | tf_op jit(solution)/shard_map/ppermute | solution.py:422
  516.2 16.1 %collective-permute-start.42 = (bf16[480,4,128]{2,1,0:T(4,128)(2,1)S(1)}, bf16[480,4,128]{2,1,0:T(4,128)(2,1)S(1)}, u32[]{:S(2)}, u32[]{:S(2)}) collective-permute-start(bf16[480,4,128]{2,1,0:T(4,128)(2,1)S(1)} %copy-done.62), channel_id=1, source_target_pairs={{0,4},{1,5},{2,6},{3,7},{4,0},{5,1},{6,2},{7,3}} | collective-permute-start | bytes 1474568 | tf_op jit(solution)/shard_map/ppermute | solution.py:422
  517.2 16.4 %collective-permute-start.62 = (bf16[600,4,128]{2,1,0:T(4,128)(2,1)S(1)}, bf16[600,4,128]{2,1,0:T(4,128)(2,1)S(1)}, u32[]{:S(2)}, u32[]{:S(2)}) collective-permute-start(bf16[600,4,128]{2,1,0:T(4,128)(2,1)S(1)} %copy-done.47), channel_id=1, source_target_pairs={{0,2},{1,3},{2,0},{3,1},{4,6},{5,7},{6,4},{7,5}} | collective-permute-start | bytes 1843208 | tf_op jit(solution)/shard_map/ppermute | solution.py:422
  518.9 15.2 %collective-permute-start.63 = (bf16[600,4,128]{2,1,0:T(4,128)(2,1)S(1)}, bf16[600,4,128]{2,1,0:T(4,128)(2,1)S(1)}, u32[]{:S(2)}, u32[]{:S(2)}) collective-permute-start(bf16[600,4,128]{2,1,0:T(4,128)(2,1)S(1)} %copy-done.47), channel_id=1, source_target_pairs={{0,1},{1,0},{2,3},{3,2},{4,5},{5,4},{6,7},{7,6}} | collective-permute-start | bytes 1843208 | tf_op jit(solution)/shard_map/ppermute | solution.py:422
  518.9 13.4 %collective-permute-start.43 = (bf16[480,4,128]{2,1,0:T(4,128)(2,1)S(1)}, bf16[480,4,128]{2,1,0:T(4,128)(2,1)S(1)}, u32[]{:S(2)}, u32[]{:S(2)}) collective-permute-start(bf16[480,4,128]{2,1,0:T(4,128)(2,1)S(1)} %copy-done.62), channel_id=1, source_target_pairs={{0,1},{1,0},{2,3},{3,2},{4,5},{5,4},{6,7},{7,6}} | collective-permute-start | bytes 1474568 | tf_op jit(solution)/shard_map/ppermute | solution.py:422
  534.9 6.4 collective-permute-start.36
  535.7 7.4 collective-permute-start.37
  537.6 7.2 collective-permute-start.32
  539.2 8.3 %collective-permute-start.33 = (bf16[360,4,128]{2,1,0:T(4,128)(2,1)S(1)}, bf16[360,4,128]{2,1,0:T(4,128)(2,1)S(1)}, u32[]{:S(2)}, u32[]{:S(2)}) collective-permute-start(bf16[360,4,128]{2,1,0:T(4,128)(2,1)S(1)} %collective-permute-done.3.refs_2_), channel_id=1, source_target_pairs={{0,1},{1,0},{2,3},{3,2},{4,5},{5,4},{6,7},{7,6}} | collective-permute-start | bytes 1105928 | tf_op jit(solution)/shard_map/ppermute | solution.py:422
  540.4 39.1 %collective-permute-start.46 = (bf16[840,4,128]{2,1,0:T(4,128)(2,1)}, bf16[840,4,128]{2,1,0:T(4,128)(2,1)S(1)}, u32[]{:S(2)}, u32[]{:S(2)}) collective-permute-start(bf16[840,4,128]{2,1,0:T(4,128)(2,1)} %get-tuple-element.83.refs_0_), channel_id=1, source_target_pairs={{0,2},{1,3},{2,0},{3,1},{4,6},{5,7},{6,4},{7,5}} | collective-permute-start | bytes 2580488 | tf_op jit(solution)/shard_map/ppermute | solution.py:422
  542.1 11.7 %collective-permute-start.25 = (bf16[360,4,128]{2,1,0:T(4,128)(2,1)}, bf16[360,4,128]{2,1,0:T(4,128)(2,1)S(1)}, u32[]{:S(2)}, u32[]{:S(2)}) collective-permute-start(bf16[360,4,128]{2,1,0:T(4,128)(2,1)} %collective-permute-done.24.refs_1_), channel_id=1, source_target_pairs={{0,4},{1,5},{2,6},{3,7},{4,0},{5,1},{6,2},{7,3}} | collective-permute-start | bytes 1105928 | tf_op jit(solution)/shard_map/ppermute | solution.py:422
  543.8 36.2 %collective-permute-start.15 = (bf16[840,4,128]{2,1,0:T(4,128)(2,1)}, bf16[840,4,128]{2,1,0:T(4,128)(2,1)S(1)}, u32[]{:S(2)}, u32[]{:S(2)}) collective-permute-start(bf16[840,4,128]{2,1,0:T(4,128)(2,1)} %get-tuple-element.83.refs_0_), channel_id=1, source_target_pairs={{0,4},{1,5},{2,6},{3,7},{4,0},{5,1},{6,2},{7,3}} | collective-permute-start | bytes 2580488 | tf_op jit(solution)/shard_map/ppermute | solution.py:422
  545.6 25.1 %collective-permute-start.10 = (bf16[360,4,128]{2,1,0:T(4,128)(2,1)S(1)}, bf16[360,4,128]{2,1,0:T(4,128)(2,1)}, u32[]{:S(2)}, u32[]{:S(2)}) collective-permute-start(bf16[360,4,128]{2,1,0:T(4,128)(2,1)S(1)} %collective-permute-done.9.refs_2_), channel_id=1, source_target_pairs={{0,2},{1,3},{2,0},{3,1},{4,6},{5,7},{6,4},{7,5}} | collective-permute-start | bytes 1105928 | tf_op jit(solution)/shard_map/ppermute | solution.py:422
  548.2 30.3 %collective-permute-start.4 = (bf16[360,4,128]{2,1,0:T(4,128)(2,1)S(1)}, bf16[360,4,128]{2,1,0:T(4,128)(2,1)}, u32[]{:S(2)}, u32[]{:S(2)}) collective-permute-start(bf16[360,4,128]{2,1,0:T(4,128)(2,1)S(1)} %collective-permute-done.3.refs_2_), channel_id=1, source_target_pairs={{0,2},{1,3},{2,0},{3,1},{4,6},{5,7},{6,4},{7,5}} | collective-permute-start | bytes 1105928 | tf_op jit(solution)/shard_map/ppermute | solution.py:422
  553.7 25.8 %collective-permute-start.1 = (bf16[360,4,128]{2,1,0:T(4,128)(2,1)S(1)}, bf16[360,4,128]{2,1,0:T(4,128)(2,1)}, u32[]{:S(2)}, u32[]{:S(2)}) collective-permute-start(bf16[360,4,128]{2,1,0:T(4,128)(2,1)S(1)} %collective-permute-done.refs_1_), channel_id=1, source_target_pairs={{0,4},{1,5},{2,6},{3,7},{4,0},{5,1},{6,2},{7,3}} | collective-permute-start | bytes 1105928 | tf_op jit(solution)/shard_map/ppermute | solution.py:422
  570.6 28.9 %collective-permute-start.18 = (bf16[960,4,128]{2,1,0:T(4,128)(2,1)S(1)}, bf16[960,4,128]{2,1,0:T(4,128)(2,1)S(1)}, u32[]{:S(2)}, u32[]{:S(2)}) collective-permute-start(bf16[960,4,128]{2,1,0:T(4,128)(2,1)S(1)} %copy-done), channel_id=1, source_target_pairs={{0,2},{1,3},{2,0},{3,1},{4,6},{5,7},{6,4},{7,5}} | collective-permute-start | bytes 2949128 | tf_op jit(solution)/shard_map/ppermute | solution.py:422
  578.5 24.6 %collective-permute-start.58 = (bf16[960,4,128]{2,1,0:T(4,128)(2,1)S(1)}, bf16[960,4,128]{2,1,0:T(4,128)(2,1)S(1)}, u32[]{:S(2)}, u32[]{:S(2)}) collective-permute-start(bf16[960,4,128]{2,1,0:T(4,128)(2,1)S(1)} %copy-done), channel_id=1, source_target_pairs={{0,4},{1,5},{2,6},{3,7},{4,0},{5,1},{6,2},{7,3}} | collective-permute-start | bytes 2949128 | tf_op jit(solution)/shard_map/ppermute | solution.py:422
  579.5 24.5 %collective-permute-start.59 = (bf16[960,4,128]{2,1,0:T(4,128)(2,1)S(1)}, bf16[960,4,128]{2,1,0:T(4,128)(2,1)S(1)}, u32[]{:S(2)}, u32[]{:S(2)}) collective-permute-start(bf16[960,4,128]{2,1,0:T(4,128)(2,1)S(1)} %copy-done), channel_id=1, source_target_pairs={{0,1},{1,0},{2,3},{3,2},{4,5},{5,4},{6,7},{7,6}} | collective-permute-start | bytes 2949128 | tf_op jit(solution)/shard_map/ppermute | solution.py:422
  580.0 40.5 %collective-permute-start.54 = (bf16[960,4,128]{2,1,0:T(4,128)(2,1)S(1)}, bf16[960,4,128]{2,1,0:T(4,128)(2,1)S(1)}, u32[]{:S(2)}, u32[]{:S(2)}) collective-permute-start(bf16[960,4,128]{2,1,0:T(4,128)(2,1)S(1)} %copy-done.1), channel_id=1, source_target_pairs={{0,2},{1,3},{2,0},{3,1},{4,6},{5,7},{6,4},{7,5}} | collective-permute-start | bytes 2949128 | tf_op jit(solution)/shard_map/ppermute | solution.py:422
  583.0 41.2 %collective-permute-start.21 = (bf16[960,4,128]{2,1,0:T(4,128)(2,1)S(1)}, bf16[960,4,128]{2,1,0:T(4,128)(2,1)S(1)}, u32[]{:S(2)}, u32[]{:S(2)}) collective-permute-start(bf16[960,4,128]{2,1,0:T(4,128)(2,1)S(1)} %copy-done.1), channel_id=1, source_target_pairs={{0,4},{1,5},{2,6},{3,7},{4,0},{5,1},{6,2},{7,3}} | collective-permute-start | bytes 2949128 | tf_op jit(solution)/shard_map/ppermute | solution.py:422
  599.5 24.7 %collective-permute-start.55 = (bf16[960,4,128]{2,1,0:T(4,128)(2,1)S(1)}, bf16[960,4,128]{2,1,0:T(4,128)(2,1)S(1)}, u32[]{:S(2)}, u32[]{:S(2)}) collective-permute-start(bf16[960,4,128]{2,1,0:T(4,128)(2,1)S(1)} %copy-done.1), channel_id=1, source_target_pairs={{0,1},{1,0},{2,3},{3,2},{4,5},{5,4},{6,7},{7,6}} | collective-permute-start | bytes 2949128 | tf_op jit(solution)/shard_map/ppermute | solution.py:422
  603.1 37.5 %collective-permute-start.12 = (bf16[960,4,128]{2,1,0:T(4,128)(2,1)S(1)}, bf16[960,4,128]{2,1,0:T(4,128)(2,1)S(1)}, u32[]{:S(2)}, u32[]{:S(2)}) collective-permute-start(bf16[960,4,128]{2,1,0:T(4,128)(2,1)S(1)} %copy-done.2), channel_id=1, source_target_pairs={{0,2},{1,3},{2,0},{3,1},{4,6},{5,7},{6,4},{7,5}} | collective-permute-start | bytes 2949128 | tf_op jit(solution)/shard_map/ppermute | solution.py:422
  604.1 38.5 %collective-permute-start.50 = (bf16[960,4,128]{2,1,0:T(4,128)(2,1)S(1)}, bf16[960,4,128]{2,1,0:T(4,128)(2,1)S(1)}, u32[]{:S(2)}, u32[]{:S(2)}) collective-permute-start(bf16[960,4,128]{2,1,0:T(4,128)(2,1)S(1)} %copy-done.2), channel_id=1, source_target_pairs={{0,4},{1,5},{2,6},{3,7},{4,0},{5,1},{6,2},{7,3}} | collective-permute-start | bytes 2949128 | tf_op jit(solution)/shard_map/ppermute | solution.py:422
  620.5 22.8 %collective-permute-start.51 = (bf16[960,4,128]{2,1,0:T(4,128)(2,1)S(1)}, bf16[960,4,128]{2,1,0:T(4,128)(2,1)S(1)}, u32[]{:S(2)}, u32[]{:S(2)}) collective-permute-start(bf16[960,4,128]{2,1,0:T(4,128)(2,1)S(1)} %copy-done.2), channel_id=1, source_target_pairs={{0,1},{1,0},{2,3},{3,2},{4,5},{5,4},{6,7},{7,6}} | collective-permute-start | bytes 2949128 | tf_op jit(solution)/shard_map/ppermute | solution.py:422
  624.2 20.5 %collective-permute-start.44 = (bf16[480,4,128]{2,1,0:T(4,128)(2,1)}, bf16[480,4,128]{2,1,0:T(4,128)(2,1)S(1)}, u32[]{:S(2)}, u32[]{:S(2)}) collective-permute-start(bf16[480,4,128]{2,1,0:T(4,128)(2,1)} %copy-done.64), channel_id=1, source_target_pairs={{0,1},{1,0},{2,3},{3,2},{4,5},{5,4},{6,7},{7,6}} | collective-permute-start | bytes 1474568 | tf_op jit(solution)/shard_map/ppermute | solution.py:422
  625.2 21.2 %collective-permute-start.45 = (bf16[480,4,128]{2,1,0:T(4,128)(2,1)S(1)}, bf16[480,4,128]{2,1,0:T(4,128)(2,1)S(1)}, u32[]{:S(2)}, u32[]{:S(2)}) collective-permute-start(bf16[480,4,128]{2,1,0:T(4,128)(2,1)S(1)} %collective-permute-done.42.refs_2_), channel_id=1, source_target_pairs={{0,1},{1,0},{2,3},{3,2},{4,5},{5,4},{6,7},{7,6}} | collective-permute-start | bytes 1474568 | tf_op jit(solution)/shard_map/ppermute | solution.py:422
  640.7 12.6 %collective-permute-start.7 = (bf16[480,4,128]{2,1,0:T(4,128)(2,1)}, bf16[480,4,128]{2,1,0:T(4,128)(2,1)}, u32[]{:S(2)}, u32[]{:S(2)}) collective-permute-start(bf16[480,4,128]{2,1,0:T(4,128)(2,1)} %copy-done.64), channel_id=1, source_target_pairs={{0,4},{1,5},{2,6},{3,7},{4,0},{5,1},{6,2},{7,3}} | collective-permute-start | bytes 1474568 | tf_op jit(solution)/shard_map/ppermute | solution.py:422
  642.6 12.5 %collective-permute-start.26 = (bf16[360,4,128]{2,1,0:T(4,128)(2,1)S(1)}, bf16[360,4,128]{2,1,0:T(4,128)(2,1)S(1)}, u32[]{:S(2)}, u32[]{:S(2)}) collective-permute-start(bf16[360,4,128]{2,1,0:T(4,128)(2,1)S(1)} %collective-permute-done.25.refs_0_), channel_id=1, source_target_pairs={{0,1},{1,0},{2,3},{3,2},{4,5},{5,4},{6,7},{7,6}} | collective-permute-start | bytes 1105928 | tf_op jit(solution)/shard_map/ppermute | solution.py:422
  644.2 11.6 %collective-permute-start.65 = (bf16[600,4,128]{2,1,0:T(4,128)(2,1)S(1)}, bf16[600,4,128]{2,1,0:T(4,128)(2,1)S(1)}, u32[]{:S(2)}, u32[]{:S(2)}) collective-permute-start(bf16[600,4,128]{2,1,0:T(4,128)(2,1)S(1)} %collective-permute-done.27.refs_2_), channel_id=1, source_target_pairs={{0,1},{1,0},{2,3},{3,2},{4,5},{5,4},{6,7},{7,6}} | collective-permute-start | bytes 1843208 | tf_op jit(solution)/shard_map/ppermute | solution.py:422
  645.6 13.2 %collective-permute-start.64 = (bf16[600,4,128]{2,1,0:T(4,128)(2,1)S(1)}, bf16[600,4,128]{2,1,0:T(4,128)(2,1)S(1)}, u32[]{:S(2)}, u32[]{:S(2)}) collective-permute-start(bf16[600,4,128]{2,1,0:T(4,128)(2,1)S(1)} %collective-permute-done.62.refs_1_), channel_id=1, source_target_pairs={{0,1},{1,0},{2,3},{3,2},{4,5},{5,4},{6,7},{7,6}} | collective-permute-start | bytes 1843208 | tf_op jit(solution)/shard_map/ppermute | solution.py:422
  647.2 22.8 %collective-permute-start.48 = (bf16[840,4,128]{2,1,0:T(4,128)(2,1)S(1)}, bf16[840,4,128]{2,1,0:T(4,128)(2,1)S(1)}, u32[]{:S(2)}, u32[]{:S(2)}) collective-permute-start(bf16[840,4,128]{2,1,0:T(4,128)(2,1)S(1)} %collective-permute-done.46.refs_1_), channel_id=1, source_target_pairs={{0,1},{1,0},{2,3},{3,2},{4,5},{5,4},{6,7},{7,6}} | collective-permute-start | bytes 2580488 | tf_op jit(solution)/shard_map/ppermute | solution.py:422
  653.3 16.7 %collective-permute-start.28 = (bf16[600,4,128]{2,1,0:T(4,128)(2,1)S(1)}, bf16[600,4,128]{2,1,0:T(4,128)(2,1)S(1)}, u32[]{:S(2)}, u32[]{:S(2)}) collective-permute-start(bf16[600,4,128]{2,1,0:T(4,128)(2,1)S(1)} %collective-permute-done.27.refs_2_), channel_id=1, source_target_pairs={{0,2},{1,3},{2,0},{3,1},{4,6},{5,7},{6,4},{7,5}} | collective-permute-start | bytes 1843208 | tf_op jit(solution)/shard_map/ppermute | solution.py:422
  655.8 15.7 %collective-permute-start.49 = (bf16[840,4,128]{2,1,0:T(4,128)(2,1)S(1)}, bf16[840,4,128]{2,1,0:T(4,128)(2,1)S(1)}, u32[]{:S(2)}, u32[]{:S(2)}) collective-permute-start(bf16[840,4,128]{2,1,0:T(4,128)(2,1)S(1)} %collective-permute-done.15.refs_2_), channel_id=1, source_target_pairs={{0,1},{1,0},{2,3},{3,2},{4,5},{5,4},{6,7},{7,6}} | collective-permute-start | bytes 2580488 | tf_op jit(solution)/shard_map/ppermute | solution.py:422
  656.7 29.1 %collective-permute-start.16 = (bf16[840,4,128]{2,1,0:T(4,128)(2,1)S(1)}, bf16[840,4,128]{2,1,0:T(4,128)(2,1)S(1)}, u32[]{:S(2)}, u32[]{:S(2)}) collective-permute-start(bf16[840,4,128]{2,1,0:T(4,128)(2,1)S(1)} %collective-permute-done.15.refs_2_), channel_id=1, source_target_pairs={{0,2},{1,3},{2,0},{3,1},{4,6},{5,7},{6,4},{7,5}} | collective-permute-start | bytes 2580488 | tf_op jit(solution)/shard_map/ppermute | solution.py:422
  659.6 28.9 %collective-permute-start.60 = (bf16[960,4,128]{2,1,0:T(4,128)(2,1)S(1)}, bf16[960,4,128]{2,1,0:T(4,128)(2,1)S(1)}, u32[]{:S(2)}, u32[]{:S(2)}) collective-permute-start(bf16[960,4,128]{2,1,0:T(4,128)(2,1)S(1)} %collective-permute-done.18.refs_1_), channel_id=1, source_target_pairs={{0,1},{1,0},{2,3},{3,2},{4,5},{5,4},{6,7},{7,6}} | collective-permute-start | bytes 2949128 | tf_op jit(solution)/shard_map/ppermute | solution.py:422
  670.0 20.5 %collective-permute-start.61 = (bf16[960,4,128]{2,1,0:T(4,128)(2,1)S(1)}, bf16[960,4,128]{2,1,0:T(4,128)(2,1)S(1)}, u32[]{:S(2)}, u32[]{:S(2)}) collective-permute-start(bf16[960,4,128]{2,1,0:T(4,128)(2,1)S(1)} %collective-permute-done.58.refs_2_), channel_id=1, source_target_pairs={{0,1},{1,0},{2,3},{3,2},{4,5},{5,4},{6,7},{7,6}} | collective-permute-start | bytes 2949128 | tf_op jit(solution)/shard_map/ppermute | solution.py:422
  671.0 20.5 %collective-permute-start.56 = (bf16[960,4,128]{2,1,0:T(4,128)(2,1)S(1)}, bf16[960,4,128]{2,1,0:T(4,128)(2,1)S(1)}, u32[]{:S(2)}, u32[]{:S(2)}) collective-permute-start(bf16[960,4,128]{2,1,0:T(4,128)(2,1)S(1)} %collective-permute-done.54.refs_1_), channel_id=1, source_target_pairs={{0,1},{1,0},{2,3},{3,2},{4,5},{5,4},{6,7},{7,6}} | collective-permute-start | bytes 2949128 | tf_op jit(solution)/shard_map/ppermute | solution.py:422
  672.4 13.4 %collective-permute-start.29 = (bf16[600,4,128]{2,1,0:T(4,128)(2,1)S(1)}, bf16[600,4,128]{2,1,0:T(4,128)(2,1)S(1)}, u32[]{:S(2)}, u32[]{:S(2)}) collective-permute-start(bf16[600,4,128]{2,1,0:T(4,128)(2,1)S(1)} %collective-permute-done.28.refs_2_), channel_id=1, source_target_pairs={{0,1},{1,0},{2,3},{3,2},{4,5},{5,4},{6,7},{7,6}} | collective-permute-start | bytes 1843208 | tf_op jit(solution)/shard_map/ppermute | solution.py:422
  685.8 8.7 %collective-permute-start.57 = (bf16[960,4,128]{2,1,0:T(4,128)(2,1)S(1)}, bf16[960,4,128]{2,1,0:T(4,128)(2,1)S(1)}, u32[]{:S(2)}, u32[]{:S(2)}) collective-permute-start(bf16[960,4,128]{2,1,0:T(4,128)(2,1)S(1)} %collective-permute-done.21.refs_2_), channel_id=1, source_target_pairs={{0,1},{1,0},{2,3},{3,2},{4,5},{5,4},{6,7},{7,6}} | collective-permute-start | bytes 2949128 | tf_op jit(solution)/shard_map/ppermute | solution.py:422
  686.6 24.2 %collective-permute-start.22 = (bf16[960,4,128]{2,1,0:T(4,128)(2,1)S(1)}, bf16[960,4,128]{2,1,0:T(4,128)(2,1)S(1)}, u32[]{:S(2)}, u32[]{:S(2)}) collective-permute-start(bf16[960,4,128]{2,1,0:T(4,128)(2,1)S(1)} %collective-permute-done.21.refs_2_), channel_id=1, source_target_pairs={{0,2},{1,3},{2,0},{3,1},{4,6},{5,7},{6,4},{7,5}} | collective-permute-start | bytes 2949128 | tf_op jit(solution)/shard_map/ppermute | solution.py:422
  689.5 24.6 %collective-permute-start.19 = (bf16[960,4,128]{2,1,0:T(4,128)(2,1)S(1)}, bf16[960,4,128]{2,1,0:T(4,128)(2,1)S(1)}, u32[]{:S(2)}, u32[]{:S(2)}) collective-permute-start(bf16[960,4,128]{2,1,0:T(4,128)(2,1)S(1)} %collective-permute-done.18.refs_1_), channel_id=1, source_target_pairs={{0,4},{1,5},{2,6},{3,7},{4,0},{5,1},{6,2},{7,3}} | collective-permute-start | bytes 2949128 | tf_op jit(solution)/shard_map/ppermute | solution.py:422
  691.5 23.6 %collective-permute-start.52 = (bf16[960,4,128]{2,1,0:T(4,128)(2,1)S(1)}, bf16[960,4,128]{2,1,0:T(4,128)(2,1)S(1)}, u32[]{:S(2)}, u32[]{:S(2)}) collective-permute-start(bf16[960,4,128]{2,1,0:T(4,128)(2,1)S(1)} %collective-permute-done.12.refs_1_), channel_id=1, source_target_pairs={{0,1},{1,0},{2,3},{3,2},{4,5},{5,4},{6,7},{7,6}} | collective-permute-start | bytes 2949128 | tf_op jit(solution)/shard_map/ppermute | solution.py:422
  692.5 42.0 %collective-permute-start.13 = (bf16[960,4,128]{2,1,0:T(4,128)(2,1)S(1)}, bf16[960,4,128]{2,1,0:T(4,128)(2,1)}, u32[]{:S(2)}, u32[]{:S(2)}) collective-permute-start(bf16[960,4,128]{2,1,0:T(4,128)(2,1)S(1)} %collective-permute-done.12.refs_1_), channel_id=1, source_target_pairs={{0,4},{1,5},{2,6},{3,7},{4,0},{5,1},{6,2},{7,3}} | collective-permute-start | bytes 2949128 | tf_op jit(solution)/shard_map/ppermute | solution.py:422
  695.4 39.1 %collective-permute-start.53 = (bf16[960,4,128]{2,1,0:T(4,128)(2,1)S(1)}, bf16[960,4,128]{2,1,0:T(4,128)(2,1)S(1)}, u32[]{:S(2)}, u32[]{:S(2)}) collective-permute-start(bf16[960,4,128]{2,1,0:T(4,128)(2,1)S(1)} %collective-permute-done.50.refs_2_), channel_id=1, source_target_pairs={{0,1},{1,0},{2,3},{3,2},{4,5},{5,4},{6,7},{7,6}} | collective-permute-start | bytes 2949128 | tf_op jit(solution)/shard_map/ppermute | solution.py:422
  710.8 26.2 %collective-permute-start.23 = (bf16[960,4,128]{2,1,0:T(4,128)(2,1)S(1)}, bf16[960,4,128]{2,1,0:T(4,128)(2,1)S(1)}, u32[]{:S(2)}, u32[]{:S(2)}) collective-permute-start(bf16[960,4,128]{2,1,0:T(4,128)(2,1)S(1)} %collective-permute-done.22.refs_2_), channel_id=1, source_target_pairs={{0,1},{1,0},{2,3},{3,2},{4,5},{5,4},{6,7},{7,6}} | collective-permute-start | bytes 2949128 | tf_op jit(solution)/shard_map/ppermute | solution.py:422
  714.1 24.4 %collective-permute-start.20 = (bf16[960,4,128]{2,1,0:T(4,128)(2,1)S(1)}, bf16[960,4,128]{2,1,0:T(4,128)(2,1)S(1)}, u32[]{:S(2)}, u32[]{:S(2)}) collective-permute-start(bf16[960,4,128]{2,1,0:T(4,128)(2,1)S(1)} %collective-permute-done.19.refs_0_), channel_id=1, source_target_pairs={{0,1},{1,0},{2,3},{3,2},{4,5},{5,4},{6,7},{7,6}} | collective-permute-start | bytes 2949128 | tf_op jit(solution)/shard_map/ppermute | solution.py:422
  716.1 20.0 %collective-permute-start.17 = (bf16[840,4,128]{2,1,0:T(4,128)(2,1)S(1)}, bf16[840,4,128]{2,1,0:T(4,128)(2,1)S(1)}, u32[]{:S(2)}, u32[]{:S(2)}) collective-permute-start(bf16[840,4,128]{2,1,0:T(4,128)(2,1)S(1)} %collective-permute-done.16.refs_2_), channel_id=1, source_target_pairs={{0,1},{1,0},{2,3},{3,2},{4,5},{5,4},{6,7},{7,6}} | collective-permute-start | bytes 2580488 | tf_op jit(solution)/shard_map/ppermute | solution.py:422
  734.5 51.9 %collective-permute-start.14 = (bf16[960,4,128]{2,1,0:T(4,128)(2,1)}, bf16[960,4,128]{2,1,0:T(4,128)(2,1)}, u32[]{:S(2)}, u32[]{:S(2)}) collective-permute-start(bf16[960,4,128]{2,1,0:T(4,128)(2,1)} %collective-permute-done.13.refs_0_), channel_id=1, source_target_pairs={{0,1},{1,0},{2,3},{3,2},{4,5},{5,4},{6,7},{7,6}} | collective-permute-start | bytes 2949128 | tf_op jit(solution)/shard_map/ppermute | solution.py:422
  735.5 54.0 %collective-permute-start.8 = (bf16[480,4,128]{2,1,0:T(4,128)(2,1)}, bf16[480,4,128]{2,1,0:T(4,128)(2,1)}, u32[]{:S(2)}, u32[]{:S(2)}) collective-permute-start(bf16[480,4,128]{2,1,0:T(4,128)(2,1)} %collective-permute-done.7.refs_0_), channel_id=1, source_target_pairs={{0,1},{1,0},{2,3},{3,2},{4,5},{5,4},{6,7},{7,6}} | collective-permute-start | bytes 1474568 | tf_op jit(solution)/shard_map/ppermute | solution.py:422
  737.0 52.5 %collective-permute-start.11 = (bf16[360,4,128]{2,1,0:T(4,128)(2,1)}, bf16[360,4,128]{2,1,0:T(4,128)(2,1)}, u32[]{:S(2)}, u32[]{:S(2)}) collective-permute-start(bf16[360,4,128]{2,1,0:T(4,128)(2,1)} %collective-permute-done.10.refs_2_), channel_id=1, source_target_pairs={{0,1},{1,0},{2,3},{3,2},{4,5},{5,4},{6,7},{7,6}} | collective-permute-start | bytes 1105928 | tf_op jit(solution)/shard_map/ppermute | solution.py:422
  738.0 53.9 %collective-permute-start.5 = (bf16[360,4,128]{2,1,0:T(4,128)(2,1)}, bf16[360,4,128]{2,1,0:T(4,128)(2,1)}, u32[]{:S(2)}, u32[]{:S(2)}) collective-permute-start(bf16[360,4,128]{2,1,0:T(4,128)(2,1)} %collective-permute-done.4.refs_2_), channel_id=1, source_target_pairs={{0,1},{1,0},{2,3},{3,2},{4,5},{5,4},{6,7},{7,6}} | collective-permute-start | bytes 1105928 | tf_op jit(solution)/shard_map/ppermute | solution.py:422
  739.5 52.4 %collective-permute-start.2 = (bf16[360,4,128]{2,1,0:T(4,128)(2,1)}, bf16[360,4,128]{2,1,0:T(4,128)(2,1)}, u32[]{:S(2)}, u32[]{:S(2)}) collective-permute-start(bf16[360,4,128]{2,1,0:T(4,128)(2,1)} %collective-permute-done.1.refs_0_), channel_id=1, source_target_pairs={{0,1},{1,0},{2,3},{3,2},{4,5},{5,4},{6,7},{7,6}} | collective-permute-start | bytes 1105928 | tf_op jit(solution)/shard_map/ppermute | solution.py:422
  (122 other events, 650.1 us)
